TPU v7x, 32 devices: a whole 2x2x4 slice. The times are simulated.
32 devices in a mesh: groups: 2 (over y), col: 4 (over x, core), row: 4 (over z).
Axes of the slice: x: 2, y: 2, z: 4, core: 2. Of those that a mesh axis runs over, the one named last changes fastest.
Arguments:
- features: bfloat16 [128, 128, 256], P(('groups', 'row'), 'col'), parts along dimension 0, may hold values from -6 to 6
- tissue: int32 [128, 128], P(('groups', 'row'), 'col'), parts along dimension 0, may hold values from 0 to 1, as said below
- conv_first: bfloat16 [3, 3, 256, 256], replicated, may hold values from -0.1875 to 0.1875
- bias_first: float32 [256], replicated, may hold values from -3 to 3
- conv_second: bfloat16 [3, 3, 256, 256], replicated, may hold values from -0.1875 to 0.1875
- bias_second: float32 [256], replicated, may hold values from -3 to 3
- key_weight: bfloat16 [256, 1280], replicated, may hold values from -0.375 to 0.375
- value_weight: bfloat16 [256, 1280], replicated, may hold values from -0.375 to 0.375
- latent_queries: bfloat16 [512, 1280], P(('col', 'row')), may hold values from -70 to 70
- out_weight: bfloat16 [1280, 1280], P(None, 'col'), may hold values from -0.15625 to 0.15625
Outputs:
- encoded: bfloat16 [1024, 1280], P(('groups', 'row'), 'col'), parts along dimension 0
There are 2 independent parts, one for each index of `groups`. A program takes and returns all parts, laid end to end along the dimension named above; an argument that names none is the same for every part. Nothing has to cross between parts.
Inputs may be any that keep to these rules, and one draw needn't show every extreme that they name: Every region of 16 x 32 patches of one device holds at least one tissue patch; the share of tissue differs widely from region to region.
All inputs are finite; a program needn't handle non-finite values.
Results may differ from a plain program's by a relative error of at most 0.007.
The roundings to bfloat16 on the way count: a program that leaves them out, or rounds other values in their place, can miss the bound.
Values may be sent and summed in bfloat16 or wider, within the bound.
No kernel may reach another device: no remote copies, remote signals or barrier semaphores. Data moves between devices by JAX's collectives and lax.ppermute only.
A program may use at most 64 MiB of HBM per device.

v0:
```python
import math

import jax
import jax.numpy as jnp
from jax import lax
from jax.sharding import PartitionSpec as P


def padded_2(cells, sides, width):
    for axis, dim in sides:
        count = lax.axis_size(axis)
        ends = count - 1
        head = lax.slice_in_dim(cells, 0, width, axis=dim)
        tail = lax.slice_in_dim(cells, cells.shape[dim] - width, cells.shape[dim], axis=dim)
        cells = jnp.concatenate(
            [
                lax.ppermute(tail, axis, [(i, (i + 1) % count) for i in range(ends)]),
                cells,
                lax.ppermute(head, axis, [((i + 1) % count, i) for i in range(ends)]),
            ],
            axis=dim,
        )
    return cells


def convolve_valid(padded, weight, height, breadth):
    channels = padded.shape[2]
    summed = jnp.zeros((height * breadth, weight.shape[3]), jnp.float32)
    for offset_row in range(3):
        for offset_col in range(3):
            window = padded[offset_row : offset_row + height, offset_col : offset_col + breadth]
            summed = summed + jnp.dot(
                window.reshape(height * breadth, channels),
                weight[offset_row, offset_col],
                preferred_element_type=jnp.float32,
            )
    return summed.reshape(height, breadth, weight.shape[3])


def shards(
    features,
    tissue,
    conv_first,
    bias_first,
    conv_second,
    bias_second,
    key_weight,
    value_weight,
    latent_queries,
    out_weight,
):
    height, breadth, channels = features.shape
    keep_half = tissue.astype(jnp.bfloat16)
    keep_float = tissue.astype(jnp.float32)[:, :, None]
    inputs = features * keep_half[:, :, None]
    padded = padded_2(inputs, (("row", 0), ("col", 1)), 1)
    hidden = (
        jax.nn.gelu(
            convolve_valid(padded, conv_first, height, breadth) + bias_first, approximate=False
        )
        * keep_float
    ).astype(jnp.bfloat16)
    beside_all = padded_2(hidden, (("row", 0), ("col", 1)), 1)
    second = (
        jax.nn.gelu(
            convolve_valid(beside_all, conv_second, height, breadth) + bias_second,
            approximate=False,
        )
        * keep_float
    ).astype(jnp.bfloat16)
    flattened = second.reshape(height * breadth, channels)
    key_rows = jnp.dot(flattened, key_weight, preferred_element_type=jnp.float32).astype(
        jnp.bfloat16
    )
    queries = lax.all_gather(latent_queries, ("col", "row"), axis=0, tiled=True)
    latent_size = queries.shape[1]
    scale = 1.0 / math.sqrt(latent_size)
    scores = (
        lax.dot_general(
            queries, key_rows, (((1,), (1,)), ((), ())), preferred_element_type=jnp.float32
        )
        * scale
    )
    living = tissue.reshape(-1) > 0
    scores = jnp.where(living[None, :], scores, -1e30)
    local_top = jnp.max(scores, axis=1)
    top_score = lax.pmax(local_top, ("col", "row"))
    weights = jnp.exp(scores - top_score[:, None])
    denominator = jnp.sum(weights, axis=1)
    pooled = jnp.dot(weights.astype(jnp.bfloat16), flattened, preferred_element_type=jnp.float32)
    pooled_part, denom_part = (
        lax.psum_scatter(pooled, "row", scatter_dimension=0, tiled=True),
        lax.psum_scatter(denominator, "row", scatter_dimension=0, tiled=True),
    )
    pooled_whole, denom_whole = lax.psum((pooled_part, denom_part), "col")
    normalized = (pooled_whole / denom_whole[:, None]).astype(jnp.bfloat16)
    attended = jnp.dot(normalized, value_weight, preferred_element_type=jnp.float32).astype(
        jnp.bfloat16
    )
    return jnp.dot(attended, out_weight, preferred_element_type=jnp.float32).astype(jnp.bfloat16)


def solution(mesh):
    placed = (
        P(("groups", "row"), "col", None),
        P(("groups", "row"), "col"),
        P(),
        P(),
        P(),
        P(),
        P(),
        P(),
        P(("col", "row"), None),
        P(None, "col"),
    )
    return jax.shard_map(
        shards, mesh=mesh, in_specs=placed, out_specs=P(("groups", "row"), "col"), check_vma=False
    )
```

profile of v0, /device:TPU:0, one launch (start us, length us, event | category | flops | bytes accessed | tf_op | source)
XLA Modules:
  0.0 152.8 jit_solution(1866470164505878585)
XLA Ops:
  6.5 0.9 fusion.157
  7.4 1.1 broadcast_multiply_fusion
  8.5 5.0 %collective-permute-start = (bf16[1,32,256]{2,1,0:T(8,128)(2,1)S(1)}, bf16[1,32,256]{2,1,0:T(8,128)(2,1)S(1)}, u32[]{:S(2)}, u32[]{:S(2)}) collective-permute-start(bf16[1,32,256]{2,1,0:T(8,128)(2,1)S(1)} %get-tuple-element.31), channel_id=1, source_target_pairs={{0,1},{1,2},{2,3},{4,5},{5,6},{6,7},{8,9},{9,10},{10,11},{12,13},{... | collective-permute-start | bytes 49160 | tf_op jit(solution)/shard_map/ppermute | solution.py:17
  13.5 1.3 collective-permute-start.1
  14.9 4.2 %collective-permute-done.1 = bf16[1,32,256]{2,1,0:T(8,128)(2,1)S(1)} collective-permute-done((bf16[1,32,256]{2,1,0:T(8,128)(2,1)S(1)}, bf16[1,32,256]{2,1,0:T(8,128)(2,1)S(1)}, u32[]{:S(2)}, u32[]{:S(2)}) %collective-permute-start.1) | collective-permute-done | bytes 16416 | tf_op jit(solution)/shard_map/ppermute | solution.py:19
  19.1 1.3 collective-permute-start.2
  20.4 1.3 collective-permute-start.3
  22.0 3.2 %collective-permute-done.3 = bf16[18,1,256]{2,1,0:T(2,128)(2,1)S(1)} collective-permute-done((bf16[18,1,256]{2,1,0:T(2,128)(2,1)S(1)}, bf16[18,1,256]{2,1,0:T(2,128)(2,1)S(1)}, u32[]{:S(2)}, u32[]{:S(2)}) %collective-permute-start.3) | collective-permute-done | bytes 9248 | tf_op jit(solution)/shard_map/ppermute | solution.py:19
  25.9 0.2 convolution_add_fusion.13
  27.3 0.2 fusion.5
  27.6 0.4 copy-done.4
  28.0 1.2 fusion.13
  29.2 3.5 %collective-permute-start.4 = (bf16[1,32,256]{2,1,0:T(8,128)(2,1)S(1)}, bf16[1,32,256]{2,1,0:T(8,128)(2,1)S(1)}, u32[]{:S(2)}, u32[]{:S(2)}) collective-permute-start(bf16[1,32,256]{2,1,0:T(8,128)(2,1)S(1)} %get-tuple-element.27), channel_id=1, source_target_pairs={{0,1},{1,2},{2,3},{4,5},{5,6},{6,7},{8,9},{9,10},{10,11},{12,13},{... | collective-permute-start | bytes 49160 | tf_op jit(solution)/shard_map/ppermute | solution.py:17
  32.6 1.3 collective-permute-start.5
  34.1 4.1 %collective-permute-done.5 = bf16[1,32,256]{2,1,0:T(8,128)(2,1)S(1)} collective-permute-done((bf16[1,32,256]{2,1,0:T(8,128)(2,1)S(1)}, bf16[1,32,256]{2,1,0:T(8,128)(2,1)S(1)}, u32[]{:S(2)}, u32[]{:S(2)}) %collective-permute-start.5) | collective-permute-done | bytes 16416 | tf_op jit(solution)/shard_map/ppermute | solution.py:19
  38.3 3.4 %collective-permute-start.6 = (bf16[18,1,256]{2,1,0:T(2,128)(2,1)S(1)}, bf16[18,1,256]{2,1,0:T(2,128)(2,1)S(1)}, u32[]{:S(2)}, u32[]{:S(2)}) collective-permute-start(bf16[18,1,256]{2,1,0:T(2,128)(2,1)S(1)} %get-tuple-element.19), channel_id=1, source_target_pairs={{0,4},{4,8},{8,12},{1,5},{5,9},{9,13},{2,6},{6,10},{10,14},{3,7},{... | collective-permute-start | bytes 27656 | tf_op jit(solution)/shard_map/ppermute | solution.py:17
  41.7 1.3 collective-permute-start.7
  43.3 2.0 %collective-permute-done.7 = bf16[18,1,256]{2,1,0:T(2,128)(2,1)S(1)} collective-permute-done((bf16[18,1,256]{2,1,0:T(2,128)(2,1)S(1)}, bf16[18,1,256]{2,1,0:T(2,128)(2,1)S(1)}, u32[]{:S(2)}, u32[]{:S(2)}) %collective-permute-start.7) | collective-permute-done | bytes 9248 | tf_op jit(solution)/shard_map/ppermute | solution.py:19
  46.0 0.2 convolution_add_fusion.6
  46.7 1.3 convolution_add_fusion.3
  48.0 0.2 convolution_add_fusion.2
  48.7 1.4 fusion.21
  50.1 6.1 %all-gather.2.cloned.1.call-done = bf16[512,1280]{1,0:T(8,128)(2,1)} async-done(((bf16[32,1280]{1,0:T(8,128)(2,1)}), bf16[512,1280]{1,0:T(8,128)(2,1)}) %all-gather.2.cloned.1.call-update) | async-done | bytes 1310736 | tf_op jit(solution)/shard_map/all_gather | solution.py:75
  56.2 2.5 %fusion.158 = (f32[512]{0:T(512)S(1)}, f32[512,512]{1,0:T(8,128)S(1)}) fusion(bf16[512,1280]{1,0:T(8,128)(2,1)} %all-gather.2.cloned.1.call-done, bf16[512,256]{1,0:T(8,128)(2,1)S(1)} %fusion.21, bf16[256,1280]{1,0:T(8,128)(2,1)S(1)} %copy-done.5, pred[512]{0:T(512)(128)(4,1)S(1)} %gt.15), kind=kOutput, calls=%fused_computation.216 | convolution fusion | flops 1008074240 | bytes 3279360 | tf_op jit(solution)/shard_map/dot_general | solution.py:79
  58.7 31.4 %pmax.7 = f32[512]{0:T(512)S(1)} all-reduce(f32[512]{0:T(512)S(1)} %get-tuple-element.35), channel_id=1, replica_groups=mesh['groups'=2,'col'=4,'row'=4] {'col','row'}, use_global_device_ids=true, to_apply=%region_1.2 | all-reduce | flops 512 | bytes 4096 | tf_op jit(solution)/shard_map/pmax | solution.py:87
  90.1 1.2 fusion.22
  91.4 0.6 dynamic-slice
  92.6 19.0 %reduce-scatter.2.cloned.1.call-done = f32[128,256]{1,0:T(8,128)} async-done(((f32[512,256]{1,0:T(8,128)}), f32[128,256]{1,0:T(8,128)}) %reduce-scatter.2.cloned.1.call-update) | async-done | bytes 131088 | tf_op jit(solution)/shard_map/reduce_scatter | solution.py:92
  111.9 8.6 %all-reduce = f32[512]{0:T(512)S(1)} all-reduce(f32[512]{0:T(512)S(1)} %fusion.8), channel_id=3, replica_groups=mesh['groups'=2,'col'=4,'row'=4] {'row'}, use_global_device_ids=true, to_apply=%region_5.6.clone | all-reduce | flops 512 | bytes 4096
  120.6 5.6 %psum.15 = f32[128]{0:T(128)S(1)} all-reduce(f32[128]{0:T(128)S(1)} %dynamic-slice.1), channel_id=1, replica_groups=mesh['groups'=2,'col'=4,'row'=4] {'col'}, use_global_device_ids=true, to_apply=%region_6.7 | all-reduce | flops 128 | bytes 1024 | tf_op jit(solution)/shard_map/psum | solution.py:95
  126.2 17.9 %all-reduce.3.cloned.1.call-done = f32[128,256]{1,0:T(8,128)} async-done(((f32[128,256]{1,0:T(8,128)}), f32[128,256]{1,0:T(8,128)}) %all-reduce.3.cloned.1.call-update) | async-done | bytes 131088 | tf_op jit(solution)/shard_map/psum | solution.py:95
  144.1 2.2 %fusion.7 = bf16[128,320]{0,1:T(8,128)(2,1)} fusion(bf16[1280,320]{0,1:T(8,128)(2,1)S(1)} %copy-done, bf16[256,1280]{1,0:T(8,128)(2,1)S(1)} %copy-done.6, f32[128,256]{1,0:T(8,128)} %all-reduce.3.cloned.1.call-done, f32[128]{0:T(128)S(1)} %psum.15), kind=kOutput, calls=%fused_computation.23 | convolution fusion | flops 189014016 | bytes 1688064 | tf_op jit(solution)/shard_map/dot_general | solution.py:100
  (55 shorter events, 4.5 us)
Async XLA Ops:
  6.5 137.6 %copy-start = (bf16[1280,320]{0,1:T(8,128)(2,1)S(1)}, bf16[1280,320]{0,1:T(8,128)(2,1)}, u32[]{:S(2)}) copy-start(bf16[1280,320]{0,1:T(8,128)(2,1)} %param.19) | copy-start | bytes 2457604
  6.5 15.2 %copy-start.1 = (bf16[3,3,256,256]{3,2,1,0:T(8,128)(2,1)S(1)}, bf16[3,3,256,256]{3,2,1,0:T(8,128)(2,1)}, u32[]{:S(2)}) copy-start(bf16[3,3,256,256]{3,2,1,0:T(8,128)(2,1)} %param.12) | copy-start | bytes 3538948
  6.5 49.6 %all-gather.2.cloned.1.call-start = ((), (), s32[]{:S(2)}) async-start(), calls=%async_computation.1 | async-start | bytes 1392640 | tf_op jit(solution)/shard_map/all_gather | solution.py:75
  8.5 6.4 %collective-permute-start = (bf16[1,32,256]{2,1,0:T(8,128)(2,1)S(1)}, bf16[1,32,256]{2,1,0:T(8,128)(2,1)S(1)}, u32[]{:S(2)}, u32[]{:S(2)}) collective-permute-start(bf16[1,32,256]{2,1,0:T(8,128)(2,1)S(1)} %get-tuple-element.31), channel_id=1, source_target_pairs={{0,1},{1,2},{2,3},{4,5},{5,6},{6,7},{8,9},{9,10},{10,11},{12,13},{... | collective-permute-start | bytes 49160 | tf_op jit(solution)/shard_map/ppermute | solution.py:17
  13.5 5.6 %collective-permute-start.1 = (bf16[1,32,256]{2,1,0:T(8,128)(2,1)S(1)}, bf16[1,32,256]{2,1,0:T(8,128)(2,1)S(1)}, u32[]{:S(2)}, u32[]{:S(2)}) collective-permute-start(bf16[1,32,256]{2,1,0:T(8,128)(2,1)S(1)} %get-tuple-element.32), channel_id=1, source_target_pairs={{1,0},{2,1},{3,2},{5,4},{6,5},{7,6},{9,8},{10,9},{11,10},{13,12},{... | collective-permute-start | bytes 49160 | tf_op jit(solution)/shard_map/ppermute | solution.py:19
  14.8 96.9 %reduce-scatter.2.cloned.1.call-start = ((), (), s32[]{:S(2)}) async-start(), calls=%async_computation.2 | async-start | bytes 655360 | tf_op jit(solution)/shard_map/reduce_scatter | solution.py:92
  19.1 2.9 %collective-permute-start.2 = (bf16[18,1,256]{2,1,0:T(2,128)(2,1)S(1)}, bf16[18,1,256]{2,1,0:T(2,128)(2,1)S(1)}, u32[]{:S(2)}, u32[]{:S(2)}) collective-permute-start(bf16[18,1,256]{2,1,0:T(2,128)(2,1)S(1)} %get-tuple-element.23), channel_id=1, source_target_pairs={{0,4},{4,8},{8,12},{1,5},{5,9},{9,13},{2,6},{6,10},{10,14},{3,7},{... | collective-permute-start | bytes 27656 | tf_op jit(solution)/shard_map/ppermute | solution.py:17
  20.4 4.8 %collective-permute-start.3 = (bf16[18,1,256]{2,1,0:T(2,128)(2,1)S(1)}, bf16[18,1,256]{2,1,0:T(2,128)(2,1)S(1)}, u32[]{:S(2)}, u32[]{:S(2)}) collective-permute-start(bf16[18,1,256]{2,1,0:T(2,128)(2,1)S(1)} %get-tuple-element.24), channel_id=1, source_target_pairs={{4,0},{8,4},{12,8},{5,1},{9,5},{13,9},{6,2},{10,6},{14,10},{7,3},{... | collective-permute-start | bytes 27656 | tf_op jit(solution)/shard_map/ppermute | solution.py:19
  27.3 0.7 copy-start.4
  27.3 6.7 %copy-start.3 = (s32[16,32]{1,0:T(8,128)S(1)}, s32[16,32]{1,0:T(8,128)}, u32[]{:S(2)}) copy-start(s32[16,32]{1,0:T(8,128)} %param.11) | copy-start | bytes 6148
  27.5 15.5 %copy-start.2 = (bf16[3,3,256,256]{3,2,1,0:T(8,128)(2,1)S(1)}, bf16[3,3,256,256]{3,2,1,0:T(8,128)(2,1)}, u32[]{:S(2)}) copy-start(bf16[3,3,256,256]{3,2,1,0:T(8,128)(2,1)} %param.14) | copy-start | bytes 3538948
  29.2 5.0 %collective-permute-start.4 = (bf16[1,32,256]{2,1,0:T(8,128)(2,1)S(1)}, bf16[1,32,256]{2,1,0:T(8,128)(2,1)S(1)}, u32[]{:S(2)}, u32[]{:S(2)}) collective-permute-start(bf16[1,32,256]{2,1,0:T(8,128)(2,1)S(1)} %get-tuple-element.27), channel_id=1, source_target_pairs={{0,1},{1,2},{2,3},{4,5},{5,6},{6,7},{8,9},{9,10},{10,11},{12,13},{... | collective-permute-start | bytes 49160 | tf_op jit(solution)/shard_map/ppermute | solution.py:17
  32.6 5.6 %collective-permute-start.5 = (bf16[1,32,256]{2,1,0:T(8,128)(2,1)S(1)}, bf16[1,32,256]{2,1,0:T(8,128)(2,1)S(1)}, u32[]{:S(2)}, u32[]{:S(2)}) collective-permute-start(bf16[1,32,256]{2,1,0:T(8,128)(2,1)S(1)} %get-tuple-element.28), channel_id=1, source_target_pairs={{1,0},{2,1},{3,2},{5,4},{6,5},{7,6},{9,8},{10,9},{11,10},{13,12},{... | collective-permute-start | bytes 49160 | tf_op jit(solution)/shard_map/ppermute | solution.py:19
  38.3 5.0 %collective-permute-start.6 = (bf16[18,1,256]{2,1,0:T(2,128)(2,1)S(1)}, bf16[18,1,256]{2,1,0:T(2,128)(2,1)S(1)}, u32[]{:S(2)}, u32[]{:S(2)}) collective-permute-start(bf16[18,1,256]{2,1,0:T(2,128)(2,1)S(1)} %get-tuple-element.19), channel_id=1, source_target_pairs={{0,4},{4,8},{8,12},{1,5},{5,9},{9,13},{2,6},{6,10},{10,14},{3,7},{... | collective-permute-start | bytes 27656 | tf_op jit(solution)/shard_map/ppermute | solution.py:17
  41.7 3.6 %collective-permute-start.7 = (bf16[18,1,256]{2,1,0:T(2,128)(2,1)S(1)}, bf16[18,1,256]{2,1,0:T(2,128)(2,1)S(1)}, u32[]{:S(2)}, u32[]{:S(2)}) collective-permute-start(bf16[18,1,256]{2,1,0:T(2,128)(2,1)S(1)} %get-tuple-element.20), channel_id=1, source_target_pairs={{4,0},{8,4},{12,8},{5,1},{9,5},{13,9},{6,2},{10,6},{14,10},{7,3},{... | collective-permute-start | bytes 27656 | tf_op jit(solution)/shard_map/ppermute | solution.py:19
  48.0 0.7 copy-start.7
  48.7 7.5 %copy-start.5 = (bf16[256,1280]{1,0:T(8,128)(2,1)S(1)}, bf16[256,1280]{1,0:T(8,128)(2,1)}, u32[]{:S(2)}) copy-start(bf16[256,1280]{1,0:T(8,128)(2,1)} %param.16) | copy-start | bytes 1966084
  90.1 1.2 copy-start.8
  91.3 52.8 %copy-start.6 = (bf16[256,1280]{1,0:T(8,128)(2,1)S(1)}, bf16[256,1280]{1,0:T(8,128)(2,1)}, u32[]{:S(2)}) copy-start(bf16[256,1280]{1,0:T(8,128)(2,1)} %param.17) | copy-start | bytes 1966084
  91.3 52.8 %all-reduce.3.cloned.1.call-start = ((), (), s32[]{:S(2)}) async-start(), calls=%async_computation.3 | async-start | bytes 262144 | tf_op jit(solution)/shard_map/psum | solution.py:95
Sparse Core Ops, SparseCore 0:
  14.9 41.2 all-gather.1
  91.4 20.1 reduce-scatter.1
  114.0 30.0 all-reduce.2
where the time goes:
time: 153 us
  waiting for transfers between devices  56.6 us (37%)
  blocking collectives  45.7 us (30%)
  starting transfers between devices  18.4 us (12%)
  between operations  14.1 us (9%)
  matrix products  12.2 us (8%)
  other arithmetic  3.89 us (3%)
  local copies, waits for them, and re-layouts  1.86 us (1%)
    pmax x1, blocking collectives, shards(): top_score = lax.pmax(local_top, ('col', 'row'))  31.4 us
    reduce_scatter x1, waiting for transfers between devices, shards(): lax.psum_scatter(pooled, 'row', scatter_dimension=0, tiled=True)  19 us
    psum x1, waiting for transfers between devices, shards(): pooled_whole, denom_whole = lax.psum((pooled_part, denom_part), 'col')  17.9 us
    ppermute x4, waiting for transfers between devices, padded_2(): lax.ppermute(head, axis, [((i + 1) % count, i) for i in range(ends)])  13.6 us
    ppermute x4, starting transfers between devices, padded_2(): lax.ppermute(tail, axis, [(i, (i + 1) % count) for i in range(ends)])  13.1 us
    unnamed x1, blocking collectives  8.63 us
    dot_general x18, matrix products, convolve_valid(): jnp.dot(window.reshape(height * breadth, channels), weight[offset_row, of...  6.36 us
    all_gather x1, waiting for transfers between devices, shards(): queries = lax.all_gather(latent_queries, ('col', 'row'), axis=0, tiled=True)  6.07 us
  transfers between devices with their start and end apart: 11, of which 8 were waited for; matrix products, arithmetic and copies ran while one was open for 6% of the time, Pallas kernels for 0%

commit v1 on v0

v1 whole, which is shorter than its diff:
```python
import math

import jax
import jax.numpy as jnp
from jax import lax
from jax.sharding import PartitionSpec as P

HALO = 2
FAR = float("inf")


def shifted(array, axis, step):
    count = lax.axis_size(axis)
    return lax.ppermute(array, axis, [(i, (i + step) % count) for i in range(count)])


def flipped(array, axis, bit):
    count = lax.axis_size(axis)
    return lax.ppermute(array, axis, [(i, i ^ bit) for i in range(count)])


def with_halo(cells, axis, dim):
    size = cells.shape[dim]
    index, last = lax.axis_index(axis), lax.axis_size(axis) - 1
    before = shifted(lax.slice_in_dim(cells, size - HALO, size, axis=dim), axis, 1)
    after = shifted(lax.slice_in_dim(cells, 0, HALO, axis=dim), axis, -1)
    far = jnp.asarray(FAR, cells.dtype)
    return jnp.concatenate(
        [jnp.where(index == 0, far, before), cells, jnp.where(index == last, far, after)], axis=dim
    )


def convolve_valid(padded, weight):
    height, breadth = padded.shape[0] - 2, padded.shape[1] - 2
    channels = padded.shape[2]
    summed = jnp.zeros((height * breadth, weight.shape[3]), jnp.float32)
    for offset_row in range(3):
        for offset_col in range(3):
            window = padded[offset_row : offset_row + height, offset_col : offset_col + breadth]
            summed = summed + jnp.dot(
                window.reshape(height * breadth, channels),
                weight[offset_row, offset_col],
                preferred_element_type=jnp.float32,
            )
    return summed.reshape(height, breadth, weight.shape[3])


def rotated(parts, offset, step):
    count = len(parts)
    size = parts[0].shape[0]
    ordered = [parts[(step * k) % count] for k in range(count)]
    twice = jnp.concatenate(ordered + ordered[:-1], axis=0)
    return lax.dynamic_slice_in_dim(twice, ((count - offset) % count) * size, count * size, axis=0)


def gathered_queries(latent_queries):
    rows, cols = lax.axis_size("row"), lax.axis_size("col")
    parts = [latent_queries] + [shifted(latent_queries, "row", k) for k in range(1, rows)]
    queries = rotated(parts, lax.axis_index("row"), -1)
    own = lax.axis_index("col")
    bit = cols // 2
    groups = [queries]
    order = [0]
    while bit > 0:
        groups = groups + list(flipped(jnp.concatenate(groups, axis=0), "col", bit).reshape(len(groups), -1, queries.shape[1]))
        order = order + [place ^ bit for place in order]
        bit //= 2
    stacked = jnp.stack(groups)
    place = jnp.asarray([order.index(k) for k in range(cols)], jnp.int32)
    return stacked[place[own ^ jnp.arange(cols)]].reshape(-1, queries.shape[1])


def in_parts(values, count):
    parts = []
    for _ in range(count):
        part = lax.reduce_precision(values, exponent_bits=8, mantissa_bits=7)
        parts.append(part.astype(jnp.bfloat16))
        values = values - part
    return parts


def packed(pooled, top, total):
    rest = jnp.zeros((11, pooled.shape[1]), jnp.bfloat16)
    return jnp.concatenate(
        [pooled.astype(jnp.bfloat16)] + in_parts(top, 3) + in_parts(total, 2) + [rest], axis=0
    )


def unpacked(block, channels):
    wide = block.astype(jnp.float32)
    row = lambda k: wide[channels + k : channels + k + 1]
    return wide[:channels], row(0) + row(1) + row(2), row(3) + row(4)


def merged(partials):
    top = partials[0][1]
    for _, other, _ in partials[1:]:
        top = jnp.maximum(top, other)
    pooled = total = 0.0
    for part, shift, count in partials:
        factor = jnp.exp(shift - top)
        pooled = pooled + part * factor
        total = total + count * factor
    return pooled, top, total


def shards(
    features,
    tissue,
    conv_first,
    bias_first,
    conv_second,
    bias_second,
    key_weight,
    value_weight,
    latent_queries,
    out_weight,
):
    height, breadth, channels = features.shape
    rows = lax.axis_size("row")
    marked = jnp.where(tissue[:, :, None] > 0, features, jnp.asarray(FAR, features.dtype))
    marked = with_halo(with_halo(marked, "row", 0), "col", 1)
    queries = gathered_queries(latent_queries)
    alive = marked < FAR
    inputs = jnp.where(alive, marked, jnp.zeros_like(marked))
    hidden = jax.nn.gelu(convolve_valid(inputs, conv_first) + bias_first, approximate=False)
    hidden = jnp.where(alive[1:-1, 1:-1], hidden, 0.0).astype(jnp.bfloat16)
    second = jax.nn.gelu(convolve_valid(hidden, conv_second) + bias_second, approximate=False)
    second = jnp.where(alive[HALO:-HALO, HALO:-HALO], second, 0.0).astype(jnp.bfloat16)
    flattened = second.reshape(height * breadth, channels)
    key_rows = jnp.dot(flattened, key_weight, preferred_element_type=jnp.float32).astype(
        jnp.bfloat16
    )
    scale = 1.0 / math.sqrt(latent_queries.shape[1])
    scores = (
        lax.dot_general(
            key_rows, queries, (((1,), (1,)), ((), ())), preferred_element_type=jnp.float32
        )
        * scale
    )
    scores = jnp.where(tissue.reshape(-1, 1) > 0, scores, -1e30)
    shift = jnp.max(scores, axis=0, keepdims=True)
    weights = jnp.exp(scores - shift)
    total = jnp.sum(weights, axis=0, keepdims=True)
    pooled = lax.dot_general(
        flattened,
        weights.astype(jnp.bfloat16),
        (((0,), (0,)), ((), ())),
        preferred_element_type=jnp.float32,
    )

    own_row = lax.axis_index("row")
    size = pooled.shape[1] // rows

    def block_of(step):
        start = ((own_row + step) % rows) * size
        cut = lambda array: lax.dynamic_slice_in_dim(array, start, size, axis=1)
        return cut(pooled), cut(shift), cut(total)

    arrived = [shifted(packed(*block_of(k)), "row", k) for k in range(1, rows)]
    partial = merged([block_of(0)] + [unpacked(block, channels) for block in arrived])
    bit = lax.axis_size("col") // 2
    while bit > 0:
        other = flipped(packed(*partial), "col", bit)
        partial = merged([partial, unpacked(other, channels)])
        bit //= 2
    normalized = (partial[0] / partial[2]).astype(jnp.bfloat16)
    attended = lax.dot_general(
        normalized, value_weight, (((0,), (0,)), ((), ())), preferred_element_type=jnp.float32
    ).astype(jnp.bfloat16)
    return jnp.dot(attended, out_weight, preferred_element_type=jnp.float32).astype(jnp.bfloat16)


def solution(mesh):
    placed = (
        P(("groups", "row"), "col", None),
        P(("groups", "row"), "col"),
        P(),
        P(),
        P(),
        P(),
        P(),
        P(),
        P(("col", "row"), None),
        P(None, "col"),
    )
    return jax.shard_map(
        shards, mesh=mesh, in_specs=placed, out_specs=P(("groups", "row"), "col"), check_vma=False
    )
```

time: 153 us -> 74.8 us (0.49)
  blocking collectives: 45.7 us -> 0 us
  waiting for transfers between devices: 56.6 us -> 25.7 us
  between operations: 14.1 us -> 0.62 us
  local copies, waits for them, and re-layouts: 1.86 us -> 15.2 us
  starting transfers between devices: 18.4 us -> 13.7 us
  other arithmetic: 3.89 us -> 7.76 us
    pmax x1 -> x0, blocking collectives: 31.4 us -> none  [shards(): top_score = lax.pmax(local_top, ('col', 'row'))]
    reduce_scatter x1 -> x0, waiting for transfers between devices: 19 us -> none  [shards(): lax.psum_scatter(pooled, 'row', scatter_dimension=0, tiled=True)]
    psum x1 -> x0, waiting for transfers between devices: 17.9 us -> none  [shards(): pooled_whole, denom_whole = lax.psum((pooled_part, denom_part), 'col')]
    ppermute x8 -> x14, waiting for transfers between devices: 13.6 us -> 25.7 us  [the longest x4 13.1 us: flipped(): return lax.ppermute(array, axis, [(i, i ^ bit) for i in range(count)])]
    unnamed x1 -> x0, blocking collectives: 8.63 us -> none
    all_gather x1 -> x0, waiting for transfers between devices: 6.07 us -> none  [shards(): queries = lax.all_gather(latent_queries, ('col', 'row'), axis=0, tiled=True)]
    psum x1 -> x0, blocking collectives: 5.64 us -> none  [shards(): pooled_whole, denom_whole = lax.psum((pooled_part, denom_part), 'col')]
    reshape x0 -> x10, local copies, waits for them, and re-layouts: none -> 5.01 us  [the longest x9 4.93 us: convolve_valid(): window.reshape(height * breadth, channels)]
  transfers between devices with their start and end apart: 11 -> 14, of which waited for: 8 -> 10; matrix products, arithmetic and copies ran while one was open for 6% -> 31% of each run, Pallas kernels for 0% -> 0%
where the time goes in v1:
time: 74.8 us; the launch traced here: 74.2 us
  waiting for transfers between devices  25.7 us (34%)
  local copies, waits for them, and re-layouts  15.2 us (20%)
  starting transfers between devices  13.7 us (18%)
  matrix products  11.3 us (15%)
  other arithmetic  7.76 us (10%)
    ppermute x4, waiting for transfers between devices, flipped(): return lax.ppermute(array, axis, [(i, i ^ bit) for i in range(count)])  13.1 us
    ppermute x10, waiting for transfers between devices, shifted(): lax.ppermute(array, axis, [(i, (i + step) % count) for i in range(count)])  12.6 us
    ppermute x10, starting transfers between devices, shifted(): lax.ppermute(array, axis, [(i, (i + step) % count) for i in range(count)])  11.7 us
    dot_general x18, matrix products, convolve_valid(): jnp.dot(window.reshape(height * breadth, channels), weight[offset_row, of...  6.33 us
    unnamed x28, local copies, waits for them, and re-layouts  5.43 us
    reshape x9, local copies, waits for them, and re-layouts, convolve_valid(): window.reshape(height * breadth, channels)  4.93 us
    dot_general x1, matrix products, shards(): lax.dot_general(key_rows, queries, (((1,), (1,)), ((), ())), preferred_el...  2.37 us
    convert_element_type x1, other arithmetic, shards(): jnp.where(alive[HALO:-HALO, HALO:-HALO], second, 0.0).astype(jnp.bfloat16)  1.99 us
  transfers between devices with their start and end apart: 14, of which 10 were waited for; matrix products, arithmetic and copies ran while one was open for 31% of the time, Pallas kernels for 0%

profile of v1, /device:TPU:0, one launch (start us, length us, event | category | flops | bytes accessed | tf_op | source)
XLA Modules:
  0.0 74.2 jit_solution(11959782587460504649)
XLA Ops:
  0.0 5.1 %collective-permute-start.4 = (bf16[32,1280]{1,0:T(8,128)(2,1)}, bf16[32,1280]{1,0:T(8,128)(2,1)S(1)}, u32[]{:S(2)}, u32[]{:S(2)}) collective-permute-start(bf16[32,1280]{1,0:T(8,128)(2,1)} %param.19), channel_id=1, source_target_pairs={{0,3},{1,0},{2,1},{3,2},{4,7},{5,4},{6,5},{7,6},{8,11},{9,8},{10,9... | collective-permute-start | bytes 245768 | tf_op jit(solution)/shard_map/ppermute | solution.py:14
  5.1 1.0 %collective-permute-start.6 = (bf16[32,1280]{1,0:T(8,128)(2,1)}, bf16[32,1280]{1,0:T(8,128)(2,1)}, u32[]{:S(2)}, u32[]{:S(2)}) collective-permute-start(bf16[32,1280]{1,0:T(8,128)(2,1)} %param.19), channel_id=1, source_target_pairs={{0,1},{1,2},{2,3},{3,0},{4,5},{5,6},{6,7},{7,4},{8,9},{9,10},{10,1... | collective-permute-start | bytes 245768 | tf_op jit(solution)/shard_map/ppermute | solution.py:14
  6.1 0.7 broadcast_compare_fusion.1
  6.8 1.1 %broadcast_select_fusion = bf16[16,32,256]{2,1,0:T(8,128)(2,1)S(1)} fusion(bf16[16,32,256]{2,1,0:T(8,128)(2,1)} %param.11, pred[16,32]{1,0:T(8,128)(4,1)S(1)} %broadcast_compare_fusion.1), kind=kLoop, calls=%fused_computation.75 | loop fusion | flops 131072 | bytes 524800 | tf_op jit(solution)/shard_map/jit(_where)/select_n | solution.py:121
  7.9 2.9 %collective-permute-start.1 = (bf16[2,32,256]{2,1,0:T(8,128)(2,1)S(1)}, bf16[2,32,256]{2,1,0:T(8,128)(2,1)S(1)}, u32[]{:S(2)}, u32[]{:S(2)}) collective-permute-start(bf16[2,32,256]{2,1,0:T(8,128)(2,1)S(1)} %get-tuple-element.45), channel_id=1, source_target_pairs={{0,3},{1,0},{2,1},{3,2},{4,7},{5,4},{6,5},{7,6},{8,11},{9,8},{10,9... | collective-permute-start | bytes 98312 | tf_op jit(solution)/shard_map/ppermute | solution.py:14
  10.8 1.5 %constant_dynamic-update-slice_fusion.6 = bf16[224,1280]{1,0:T(8,128)(2,1)} fusion(bf16[32,1280]{1,0:T(8,128)(2,1)} %param.19), kind=kLoop, calls=%fused_computation.148 | loop fusion | bytes 163840
  13.5 3.0 %collective-permute-done = bf16[2,32,256]{2,1,0:T(8,128)(2,1)S(1)} collective-permute-done((bf16[2,32,256]{2,1,0:T(8,128)(2,1)S(1)}, bf16[2,32,256]{2,1,0:T(8,128)(2,1)S(1)}, u32[]{:S(2)}, u32[]{:S(2)}) %collective-permute-start) | collective-permute-done | bytes 32800 | tf_op jit(solution)/shard_map/ppermute | solution.py:14
  17.2 0.8 %collective-permute-done.3 = bf16[20,2,256]{2,1,0:T(2,128)(2,1)S(1)} collective-permute-done((bf16[20,2,256]{2,1,0:T(2,128)(2,1)S(1)}, bf16[20,2,256]{2,1,0:T(2,128)(2,1)S(1)}, u32[]{:S(2)}, u32[]{:S(2)}) %collective-permute-start.3) | collective-permute-done | bytes 20512 | tf_op jit(solution)/shard_map/ppermute | solution.py:14
  18.1 2.0 %collective-permute-done.2 = bf16[20,2,256]{2,1,0:T(2,128)(2,1)S(1)} collective-permute-done((bf16[20,2,256]{2,1,0:T(2,128)(2,1)S(1)}, bf16[20,2,256]{2,1,0:T(2,128)(2,1)S(1)}, u32[]{:S(2)}, u32[]{:S(2)}) %collective-permute-start.2) | collective-permute-done | bytes 20512 | tf_op jit(solution)/shard_map/ppermute | solution.py:14
  20.1 0.9 %broadcast_compare_fusion = pred[20,36,256]{2,1,0:T(8,128)(4,1)} fusion(bf16[20,2,256]{2,1,0:T(2,128)(2,1)S(1)} %broadcast_select_fusion.1, bf16[2,32,256]{2,1,0:T(8,128)(2,1)S(1)} %broadcast_select_fusion.3, bf16[16,32,256]{2,1,0:T(8,128)(2,1)S(1)} %broadcast_select_fusion, bf16[2,32,256]{2,1,0:T(8,128)(2,1)S(1)} %broadcast_select_fusion.4, ...), kind=kLoop, calls=%fused_computation.77 | loop fusion | flops 2027520 | bytes 552960 | tf_op jit(solution)/shard_map/lt | solution.py:124
  21.3 1.2 %fusion.154 = (bf16[18,34,256]{2,1,0:T(8,128)(2,1)S(1)}, bf16[18,34,256]{2,1,0:T(8,128)(2,1)S(1)}, bf16[18,34,256]{2,1,0:T(8,128)(2,1)S(1)}, bf16[18,34,256]{2,1...) fusion(bf16[20,36,256]{2,1,0:T(8,128)(2,1)S(1)} %compare_select, ...), kind=kLoop, calls=%fused_computation.272 | loop fusion | bytes 5640192 | tf_op jit(solution)/shard_map/slice | solution.py:39
  22.4 1.8 %reshape.163 = bf16[612,256]{1,0:T(8,128)(2,1)} reshape(bf16[18,34,256]{2,1,0:T(8,128)(2,1)} %get-tuple-element.32) | data formatting | bytes 626688 | tf_op jit(solution)/shard_map/reshape | solution.py:41
  24.2 1.8 %reshape.164 = bf16[612,256]{1,0:T(8,128)(2,1)} reshape(bf16[18,34,256]{2,1,0:T(8,128)(2,1)} %get-tuple-element.31) | data formatting | bytes 626688 | tf_op jit(solution)/shard_map/reshape | solution.py:41
  26.0 0.8 %reshape.165 = bf16[612,256]{1,0:T(8,128)(2,1)} reshape(bf16[18,34,256]{2,1,0:T(8,128)(2,1)S(1)} %get-tuple-element.30) | data formatting | bytes 626688 | tf_op jit(solution)/shard_map/reshape | solution.py:41
  27.4 1.3 %fusion.56 = f32[612,256]{1,0:T(8,128)S(1)} fusion(bf16[612,256]{1,0:T(8,128)(2,1)} %reshape.163, bf16[3,3,256,256]{3,2,1,0:T(8,128)(2,1)} %param.13), kind=kOutput, calls=%fused_computation.107 | convolution fusion | flops 80216064 | bytes 1073152 | tf_op jit(solution)/shard_map/dot_general | solution.py:40
  28.8 1.2 %convolution_add_fusion.7 = f32[612,256]{1,0:T(8,128)S(1)} fusion(f32[612,256]{1,0:T(8,128)S(1)} %fusion.56, bf16[612,256]{1,0:T(8,128)(2,1)} %reshape.164, bf16[3,3,256,256]{3,2,1,0:T(8,128)(2,1)} %param.13), kind=kOutput, calls=%fused_computation.15 | convolution fusion | flops 80372736 | bytes 1699840 | tf_op jit(solution)/shard_map/dot_general | solution.py:40
  32.5 1.8 %fusion.10 = bf16[18,34,256]{2,1,0:T(8,128)(2,1)S(1)} fusion(pred[20,36,256]{2,1,0:T(8,128)(4,1)S(1)} %copy-done.2, f32[18,34,256]{2,1,0:T(8,128)S(1)} %reshape.172, f32[256]{0:T(256)S(1)} %copy-done.9), kind=kLoop, calls=%fused_computation.34 | loop fusion | flops 10497024 | bytes 1097728 | tf_op jit(solution)/shard_map/convert_element_type | solution.py:127
  34.7 0.9 %copy-done.5 = bf16[3,3,256,256]{3,2,1,0:T(8,128)(2,1)S(1)} copy-done((bf16[3,3,256,256]{3,2,1,0:T(8,128)(2,1)S(1)}, bf16[3,3,256,256]{3,2,1,0:T(8,128)(2,1)}, u32[]{:S(2)}) %copy-start.5) | copy-done | bytes 1179672
  37.8 0.9 %constant_dynamic-update-slice_fusion.4 = bf16[224,1280]{1,0:T(8,128)(2,1)S(1)} fusion(bf16[224,1280]{1,0:T(8,128)(2,1)S(1)} %constant_dynamic-update-slice_fusion.5, bf16[32,1280]{1,0:T(8,128)(2,1)} %collective-permute-done.5), kind=kLoop, calls=%fused_computation.146 | loop fusion | bytes 163840
  38.7 0.9 %constant_dynamic-update-slice_fusion.3 = bf16[224,1280]{1,0:T(8,128)(2,1)S(1)} fusion(bf16[224,1280]{1,0:T(8,128)(2,1)S(1)} %constant_dynamic-update-slice_fusion.4, bf16[32,1280]{1,0:T(8,128)(2,1)} %collective-permute-done.6), kind=kLoop, calls=%fused_computation.145 | loop fusion | bytes 163840
  39.6 0.9 %constant_dynamic-update-slice_fusion = bf16[224,1280]{1,0:T(8,128)(2,1)S(1)} fusion(bf16[224,1280]{1,0:T(8,128)(2,1)S(1)} %constant_dynamic-update-slice_fusion.1, bf16[32,1280]{1,0:T(8,128)(2,1)} %collective-permute-done.5), kind=kLoop, calls=%fused_computation.142 | loop fusion | bytes 163840 | tf_op jit(solution)/shard_map/concatenate | solution.py:52
  40.6 1.5 %collective-permute-start.7 = (bf16[128,1280]{1,0:T(8,128)(2,1)S(1)}, bf16[128,1280]{1,0:T(8,128)(2,1)S(1)}, u32[]{:S(2)}, u32[]{:S(2)}) collective-permute-start(bf16[128,1280]{1,0:T(8,128)(2,1)S(1)} %constant_dynamic-slice_fusion), channel_id=1, source_target_pairs={{0,8},{4,12},{8,0},{12,4},{1,9},{5,13},{9,1},{13,5},{2,10},{6,14},... | collective-permute-start | bytes 983048 | tf_op jit(solution)/shard_map/ppermute | solution.py:19
  42.5 7.8 %collective-permute-done.7 = bf16[128,1280]{1,0:T(8,128)(2,1)S(1)} collective-permute-done((bf16[128,1280]{1,0:T(8,128)(2,1)S(1)}, bf16[128,1280]{1,0:T(8,128)(2,1)S(1)}, u32[]{:S(2)}, u32[]{:S(2)}) %collective-permute-start.7) | collective-permute-done | bytes 327712 | tf_op jit(solution)/shard_map/ppermute | solution.py:19
  50.4 2.0 %fusion.21 = bf16[16,32,256]{2,1,0:T(8,128)(2,1)} fusion(pred[20,36,256]{2,1,0:T(8,128)(4,1)S(1)} %copy-done.2, f32[16,32,256]{2,1,0:T(8,128)S(1)} %bitcast.171, f32[256]{0:T(256)S(1)} %copy-done.10), kind=kLoop, calls=%fused_computation.54 | loop fusion | flops 8781824 | bytes 918528 | tf_op jit(solution)/shard_map/convert_element_type | solution.py:129
  53.3 2.4 %fusion.157 = (f32[512]{0:T(512)S(1)}, f32[512,512]{1,0:T(8,128)S(1)}) fusion(bf16[512,1280]{1,0:T(8,128)(2,1)S(1)} %bitcast.173, bf16[512,256]{1,0:T(8,128)(2,1)} %bitcast.183, bf16[256,1280]{1,0:T(8,128)(2,1)} %param.17, pred[512]{0:T(512)(128)(4,1)S(1)} %gt.19), kind=kOutput, calls=%fused_computation.275 | convolution fusion | flops 1008074240 | bytes 3279360 | tf_op jit(solution)/shard_map/dot_general | solution.py:136
  55.7 1.3 %fusion.22 = f32[256,512]{1,0:T(8,128)S(1)} fusion(bf16[512,256]{1,0:T(8,128)(2,1)} %bitcast.184, f32[512,512]{1,0:T(8,128)S(1)} %get-tuple-element.76, f32[512]{0:T(512)S(1)} %get-tuple-element.75), kind=kOutput, calls=%fused_computation.55 | convolution fusion | flops 134742016 | bytes 1837056 | tf_op jit(solution)/shard_map/dot_general | solution.py:145
  58.4 1.7 %collective-permute-start.9 = (bf16[272,128]{1,0:T(8,128)(2,1)S(1)}, bf16[272,128]{1,0:T(8,128)(2,1)S(1)}, u32[]{:S(2)}, u32[]{:S(2)}) collective-permute-start(bf16[272,128]{1,0:T(8,128)(2,1)S(1)} %concatenate.31), channel_id=1, source_target_pairs={{0,1},{1,2},{2,3},{3,0},{4,5},{5,6},{6,7},{7,4},{8,9},{9,10},{10,1... | collective-permute-start | bytes 208904 | tf_op jit(solution)/shard_map/ppermute | solution.py:14
  60.1 3.2 %collective-permute-done.11 = bf16[272,128]{1,0:T(8,128)(2,1)S(1)} collective-permute-done((bf16[272,128]{1,0:T(8,128)(2,1)S(1)}, bf16[272,128]{1,0:T(8,128)(2,1)S(1)}, u32[]{:S(2)}, u32[]{:S(2)}) %collective-permute-start.11) | collective-permute-done | bytes 69664 | tf_op jit(solution)/shard_map/ppermute | solution.py:14
  63.3 3.0 %collective-permute-done.10 = bf16[272,128]{1,0:T(8,128)(2,1)S(1)} collective-permute-done((bf16[272,128]{1,0:T(8,128)(2,1)S(1)}, bf16[272,128]{1,0:T(8,128)(2,1)S(1)}, u32[]{:S(2)}, u32[]{:S(2)}) %collective-permute-start.10) | collective-permute-done | bytes 69664 | tf_op jit(solution)/shard_map/ppermute | solution.py:14
  67.2 4.0 %collective-permute-done.12 = bf16[272,128]{1,0:T(8,128)(2,1)S(1)} collective-permute-done((bf16[272,128]{1,0:T(8,128)(2,1)S(1)}, bf16[272,128]{1,0:T(8,128)(2,1)S(1)}, u32[]{:S(2)}, u32[]{:S(2)}) %collective-permute-start.12) | collective-permute-done | bytes 69664 | tf_op jit(solution)/shard_map/ppermute | solution.py:19
  71.6 1.2 %collective-permute-done.13 = bf16[272,128]{1,0:T(8,128)(2,1)S(1)} collective-permute-done((bf16[272,128]{1,0:T(8,128)(2,1)S(1)}, bf16[272,128]{1,0:T(8,128)(2,1)S(1)}, u32[]{:S(2)}, u32[]{:S(2)}) %collective-permute-start.13) | collective-permute-done | bytes 69664 | tf_op jit(solution)/shard_map/ppermute | solution.py:19
  72.9 1.3 %fusion.4 = bf16[128,320]{0,1:T(8,128)(2,1)} fusion(bf16[1280,320]{0,1:T(8,128)(2,1)S(1)} %copy-done, bf16[256,1280]{1,0:T(8,128)(2,1)S(1)} %copy-done.7, f32[272,128]{1,0:T(8,128)S(1)} %convert_element_type.224, f32[128]{0:T(128)S(1)} %get-tuple-element.62, f32[128]{0:T(128)S(1)} %get-tuple-element.61, f32[128]{0:T(128)S(1)} %get-tuple-element.5, ...), kind=kOutput, calls=%fused_computation.25 | convolution fusion | flops 189210624 | bytes 1952256 | tf_op jit(solution)/shard_map/dot_general | solution.py:171
  (106 shorter events, 11.6 us)
Async XLA Ops:
  0.0 72.9 %copy-start = (bf16[1280,320]{0,1:T(8,128)(2,1)S(1)}, bf16[1280,320]{0,1:T(8,128)(2,1)}, u32[]{:S(2)}) copy-start(bf16[1280,320]{0,1:T(8,128)(2,1)} %param.20) | copy-start | bytes 2457604
  0.0 12.3 %copy-start.1 = (s32[4]{0:T(128)S(1)}, s32[4]{0:T(128)}, u32[]{:S(2)}) copy-start(s32[4]{0:T(128)} %constant.34.clone) | copy-start | bytes 52
  0.0 37.2 %collective-permute-start.4 = (bf16[32,1280]{1,0:T(8,128)(2,1)}, bf16[32,1280]{1,0:T(8,128)(2,1)S(1)}, u32[]{:S(2)}, u32[]{:S(2)}) collective-permute-start(bf16[32,1280]{1,0:T(8,128)(2,1)} %param.19), channel_id=1, source_target_pairs={{0,3},{1,0},{2,1},{3,2},{4,7},{5,4},{6,5},{7,6},{8,11},{9,8},{10,9... | collective-permute-start | bytes 245768 | tf_op jit(solution)/shard_map/ppermute | solution.py:14
  5.1 32.7 %collective-permute-start.5 = (bf16[32,1280]{1,0:T(8,128)(2,1)}, bf16[32,1280]{1,0:T(8,128)(2,1)}, u32[]{:S(2)}, u32[]{:S(2)}) collective-permute-start(bf16[32,1280]{1,0:T(8,128)(2,1)} %param.19), channel_id=1, source_target_pairs={{0,2},{1,3},{2,0},{3,1},{4,6},{5,7},{6,4},{7,5},{8,10},{9,11},{10,... | collective-permute-start | bytes 245768 | tf_op jit(solution)/shard_map/ppermute | solution.py:14
  5.1 33.6 %collective-permute-start.6 = (bf16[32,1280]{1,0:T(8,128)(2,1)}, bf16[32,1280]{1,0:T(8,128)(2,1)}, u32[]{:S(2)}, u32[]{:S(2)}) collective-permute-start(bf16[32,1280]{1,0:T(8,128)(2,1)} %param.19), channel_id=1, source_target_pairs={{0,1},{1,2},{2,3},{3,0},{4,5},{5,6},{6,7},{7,4},{8,9},{9,10},{10,1... | collective-permute-start | bytes 245768 | tf_op jit(solution)/shard_map/ppermute | solution.py:14
  7.9 5.6 %collective-permute-start.1 = (bf16[2,32,256]{2,1,0:T(8,128)(2,1)S(1)}, bf16[2,32,256]{2,1,0:T(8,128)(2,1)S(1)}, u32[]{:S(2)}, u32[]{:S(2)}) collective-permute-start(bf16[2,32,256]{2,1,0:T(8,128)(2,1)S(1)} %get-tuple-element.45), channel_id=1, source_target_pairs={{0,3},{1,0},{2,1},{3,2},{4,7},{5,4},{6,5},{7,6},{8,11},{9,8},{10,9... | collective-permute-start | bytes 98312 | tf_op jit(solution)/shard_map/ppermute | solution.py:14
  10.8 5.7 %collective-permute-start = (bf16[2,32,256]{2,1,0:T(8,128)(2,1)S(1)}, bf16[2,32,256]{2,1,0:T(8,128)(2,1)S(1)}, u32[]{:S(2)}, u32[]{:S(2)}) collective-permute-start(bf16[2,32,256]{2,1,0:T(8,128)(2,1)S(1)} %get-tuple-element.44), channel_id=1, source_target_pairs={{0,1},{1,2},{2,3},{3,0},{4,5},{5,6},{6,7},{7,4},{8,9},{9,10},{10,1... | collective-permute-start | bytes 98312 | tf_op jit(solution)/shard_map/ppermute | solution.py:14
  16.5 1.5 %collective-permute-start.3 = (bf16[20,2,256]{2,1,0:T(2,128)(2,1)S(1)}, bf16[20,2,256]{2,1,0:T(2,128)(2,1)S(1)}, u32[]{:S(2)}, u32[]{:S(2)}) collective-permute-start(bf16[20,2,256]{2,1,0:T(2,128)(2,1)S(1)} %get-tuple-element.43), channel_id=1, source_target_pairs={{0,12},{4,0},{8,4},{12,8},{1,13},{5,1},{9,5},{13,9},{2,14},{6,2},{... | collective-permute-start | bytes 61448 | tf_op jit(solution)/shard_map/ppermute | solution.py:14
  16.7 3.3 %collective-permute-start.2 = (bf16[20,2,256]{2,1,0:T(2,128)(2,1)S(1)}, bf16[20,2,256]{2,1,0:T(2,128)(2,1)S(1)}, u32[]{:S(2)}, u32[]{:S(2)}) collective-permute-start(bf16[20,2,256]{2,1,0:T(2,128)(2,1)S(1)} %get-tuple-element.42), channel_id=1, source_target_pairs={{0,4},{4,8},{8,12},{12,0},{1,5},{5,9},{9,13},{13,1},{2,6},{6,10},{... | collective-permute-start | bytes 61448 | tf_op jit(solution)/shard_map/ppermute | solution.py:14
  27.4 2.6 %copy-start.3 = (bf16[612,256]{1,0:T(8,128)(2,1)S(1)}, bf16[612,256]{1,0:T(8,128)(2,1)}, u32[]{:S(2)}) copy-start(bf16[612,256]{1,0:T(8,128)(2,1)} %reshape.165) | copy-start | bytes 940036
  27.4 2.6 %copy-start.4 = (bf16[3,3,256,256]{3,2,1,0:T(8,128)(2,1)S(1)}, bf16[3,3,256,256]{3,2,1,0:T(8,128)(2,1)}, u32[]{:S(2)}) copy-start(bf16[3,3,256,256]{3,2,1,0:T(8,128)(2,1)} %param.13) | copy-start | bytes 3538948
  31.6 0.9 %copy-start.2 = (pred[20,36,256]{2,1,0:T(8,128)(4,1)S(1)}, pred[20,36,256]{2,1,0:T(8,128)(4,1)}, u32[]{:S(2)}) copy-start(pred[20,36,256]{2,1,0:T(8,128)(4,1)} %broadcast_compare_fusion) | copy-start | bytes 552964
  31.6 0.9 %copy-start.9 = (f32[256]{0:T(256)S(1)}, f32[256]{0:T(256)}, u32[]{:S(2)}) copy-start(f32[256]{0:T(256)} %param.14) | copy-start | bytes 3076
  34.3 1.3 %copy-start.5 = (bf16[3,3,256,256]{3,2,1,0:T(8,128)(2,1)S(1)}, bf16[3,3,256,256]{3,2,1,0:T(8,128)(2,1)}, u32[]{:S(2)}) copy-start(bf16[3,3,256,256]{3,2,1,0:T(8,128)(2,1)} %param.15) | copy-start | bytes 3538948
  36.7 1.1 %copy-start.6 = (bf16[224,1280]{1,0:T(8,128)(2,1)S(1)}, bf16[224,1280]{1,0:T(8,128)(2,1)}, u32[]{:S(2)}) copy-start(bf16[224,1280]{1,0:T(8,128)(2,1)} %constant_dynamic-update-slice_fusion.6) | copy-start | bytes 1720324
  37.0 2.6 %copy-start.8 = (bf16[32,1280]{1,0:T(8,128)(2,1)S(1)}, bf16[32,1280]{1,0:T(8,128)(2,1)}, u32[]{:S(2)}) copy-start(bf16[32,1280]{1,0:T(8,128)(2,1)} %param.19) | copy-start | bytes 245764
  40.6 9.7 %collective-permute-start.7 = (bf16[128,1280]{1,0:T(8,128)(2,1)S(1)}, bf16[128,1280]{1,0:T(8,128)(2,1)S(1)}, u32[]{:S(2)}, u32[]{:S(2)}) collective-permute-start(bf16[128,1280]{1,0:T(8,128)(2,1)S(1)} %constant_dynamic-slice_fusion), channel_id=1, source_target_pairs={{0,8},{4,12},{8,0},{12,4},{1,9},{5,13},{9,1},{13,5},{2,10},{6,14},... | collective-permute-start | bytes 983048 | tf_op jit(solution)/shard_map/ppermute | solution.py:19
  42.3 8.1 %copy-start.10 = (f32[256]{0:T(256)S(1)}, f32[256]{0:T(256)}, u32[]{:S(2)}) copy-start(f32[256]{0:T(256)} %param.16) | copy-start | bytes 3076
  50.3 2.2 %collective-permute-start.8 = (bf16[256,1280]{1,0:T(8,128)(2,1)S(1)}, bf16[256,1280]{1,0:T(8,128)(2,1)S(1)}, u32[]{:S(2)}, u32[]{:S(2)}) collective-permute-start(bf16[256,1280]{1,0:T(8,128)(2,1)S(1)} %pad_maximum_fusion.1), channel_id=1, source_target_pairs={{0,4},{4,0},{8,12},{12,8},{1,5},{5,1},{9,13},{13,9},{2,6},{6,2},{1... | collective-permute-start | bytes 1966088 | tf_op jit(solution)/shard_map/ppermute | solution.py:19
  57.6 5.7 %collective-permute-start.11 = (bf16[272,128]{1,0:T(8,128)(2,1)S(1)}, bf16[272,128]{1,0:T(8,128)(2,1)S(1)}, u32[]{:S(2)}, u32[]{:S(2)}) collective-permute-start(bf16[272,128]{1,0:T(8,128)(2,1)S(1)} %concatenate.33), channel_id=1, source_target_pairs={{0,3},{1,0},{2,1},{3,2},{4,7},{5,4},{6,5},{7,6},{8,11},{9,8},{10,9... | collective-permute-start | bytes 208904 | tf_op jit(solution)/shard_map/ppermute | solution.py:14
  58.1 8.3 %collective-permute-start.10 = (bf16[272,128]{1,0:T(8,128)(2,1)S(1)}, bf16[272,128]{1,0:T(8,128)(2,1)S(1)}, u32[]{:S(2)}, u32[]{:S(2)}) collective-permute-start(bf16[272,128]{1,0:T(8,128)(2,1)S(1)} %concatenate.32), channel_id=1, source_target_pairs={{0,2},{1,3},{2,0},{3,1},{4,6},{5,7},{6,4},{7,5},{8,10},{9,11},{10,... | collective-permute-start | bytes 208904 | tf_op jit(solution)/shard_map/ppermute | solution.py:14
  58.4 8.0 %collective-permute-start.9 = (bf16[272,128]{1,0:T(8,128)(2,1)S(1)}, bf16[272,128]{1,0:T(8,128)(2,1)S(1)}, u32[]{:S(2)}, u32[]{:S(2)}) collective-permute-start(bf16[272,128]{1,0:T(8,128)(2,1)S(1)} %concatenate.31), channel_id=1, source_target_pairs={{0,1},{1,2},{2,3},{3,0},{4,5},{5,6},{6,7},{7,4},{8,9},{9,10},{10,1... | collective-permute-start | bytes 208904 | tf_op jit(solution)/shard_map/ppermute | solution.py:14
  63.3 9.6 %copy-start.7 = (bf16[256,1280]{1,0:T(8,128)(2,1)S(1)}, bf16[256,1280]{1,0:T(8,128)(2,1)}, u32[]{:S(2)}) copy-start(bf16[256,1280]{1,0:T(8,128)(2,1)} %param.18) | copy-start | bytes 1966084
  66.9 4.4 %collective-permute-start.12 = (bf16[272,128]{1,0:T(8,128)(2,1)S(1)}, bf16[272,128]{1,0:T(8,128)(2,1)S(1)}, u32[]{:S(2)}, u32[]{:S(2)}) collective-permute-start(bf16[272,128]{1,0:T(8,128)(2,1)S(1)} %concatenate.34), channel_id=1, source_target_pairs={{0,8},{4,12},{8,0},{12,4},{1,9},{5,13},{9,1},{13,5},{2,10},{6,14},... | collective-permute-start | bytes 208904 | tf_op jit(solution)/shard_map/ppermute | solution.py:19
  71.5 1.3 %collective-permute-start.13 = (bf16[272,128]{1,0:T(8,128)(2,1)S(1)}, bf16[272,128]{1,0:T(8,128)(2,1)S(1)}, u32[]{:S(2)}, u32[]{:S(2)}) collective-permute-start(bf16[272,128]{1,0:T(8,128)(2,1)S(1)} %concatenate.35), channel_id=1, source_target_pairs={{0,4},{4,0},{8,12},{12,8},{1,5},{5,1},{9,13},{13,9},{2,6},{6,2},{1... | collective-permute-start | bytes 208904 | tf_op jit(solution)/shard_map/ppermute | solution.py:19

commit v2 on v1

--- a/solution.py
+++ b/solution.py
@@ -1,12 +1,17 @@
+import functools
 import math
 
 import jax
 import jax.numpy as jnp
 from jax import lax
+from jax.experimental import pallas as pl
+from jax.experimental.pallas import tpu as pltpu
 from jax.sharding import PartitionSpec as P
 
 HALO = 2
 FAR = float("inf")
+EDGE = 8
+LEAD = 16
 
 
 def shifted(array, axis, step):
@@ -104,22 +109,10 @@
     return pooled, top, total
 
 
-def shards(
-    features,
-    tissue,
-    conv_first,
-    bias_first,
-    conv_second,
-    bias_second,
-    key_weight,
-    value_weight,
-    latent_queries,
-    out_weight,
-):
+def plain_attend(features, tissue, marked, latent_queries, weights):
+    conv_first, bias_first, conv_second, bias_second, key_weight = weights
     height, breadth, channels = features.shape
     rows = lax.axis_size("row")
-    marked = jnp.where(tissue[:, :, None] > 0, features, jnp.asarray(FAR, features.dtype))
-    marked = with_halo(with_halo(marked, "row", 0), "col", 1)
     queries = gathered_queries(latent_queries)
     alive = marked < FAR
     inputs = jnp.where(alive, marked, jnp.zeros_like(marked))
@@ -140,11 +133,11 @@
     )
     scores = jnp.where(tissue.reshape(-1, 1) > 0, scores, -1e30)
     shift = jnp.max(scores, axis=0, keepdims=True)
-    weights = jnp.exp(scores - shift)
-    total = jnp.sum(weights, axis=0, keepdims=True)
+    chosen = jnp.exp(scores - shift)
+    total = jnp.sum(chosen, axis=0, keepdims=True)
     pooled = lax.dot_general(
         flattened,
-        weights.astype(jnp.bfloat16),
+        chosen.astype(jnp.bfloat16),
         (((0,), (0,)), ((), ())),
         preferred_element_type=jnp.float32,
     )
@@ -165,6 +158,297 @@
         partial = merged([partial, unpacked(other, channels)])
         bit //= 2
     normalized = (partial[0] / partial[2]).astype(jnp.bfloat16)
+    return normalized
+
+
+def gelu(value):
+    return 0.5 * value * (1.0 + lax.erf(value * math.sqrt(0.5)))
+
+
+def conv_kernel(
+    marked, top, bottom, left, right, first, bias_first, second, bias_second, key_weight,
+    out, keys, cells, mid, taps,
+):
+    height, breadth, channels = marked.shape
+    slot = (cells.shape[0] - 2 * EDGE - LEAD) // (height + 2 * HALO)
+    flat = cells.shape[0] - 2 * EDGE
+    row, col = lax.axis_index("row"), lax.axis_index("col")
+    first_row, last_row = row == 0, row == lax.axis_size("row") - 1
+    first_col, last_col = col == 0, col == lax.axis_size("col") - 1
+
+    def put(line, place, values, outside):
+        start = EDGE + LEAD + line * slot + place
+        values = values.astype(jnp.float32)
+        if outside is not None:
+            values = jnp.where(outside, FAR, values)
+        cells[start : start + values.shape[0], :] = values
+
+    cells[...] = jnp.full(cells.shape, FAR, jnp.float32)
+    for line in range(height):
+        put(line + HALO, 0, marked[line], None)
+    for line in range(HALO):
+        put(line, 0, top[line], first_row)
+        put(height + HALO + line, 0, bottom[line], last_row)
+    for line in range(height + 2 * HALO):
+        beyond_left, beyond_right = first_col, last_col
+        if line < HALO:
+            beyond_left, beyond_right = first_col | first_row, last_col | first_row
+        if line >= height + HALO:
+            beyond_left, beyond_right = first_col | last_row, last_col | last_row
+        put(line, -HALO, left[line], beyond_left)
+        put(line, breadth, right[line], beyond_right)
+
+    for shift in range(3):
+        values = cells[EDGE - 1 + shift : EDGE - 1 + shift + flat, :]
+        taps[:, shift * channels : (shift + 1) * channels] = jnp.where(
+            values < FAR, values, 0.0
+        ).astype(jnp.bfloat16)
+
+    count = flat - 2 * slot
+    summed = jnp.dot(taps[0:count, :], first[0], preferred_element_type=jnp.float32)
+    for line in range(1, 3):
+        summed = summed + jnp.dot(
+            taps[line * slot : line * slot + count, :], first[line],
+            preferred_element_type=jnp.float32,
+        )
+    alive = cells[EDGE + slot : EDGE + slot + count, :] < FAR
+    edge = jnp.zeros((EDGE, channels), jnp.float32)
+    mid[0:EDGE, :] = edge
+    mid[EDGE + count : 2 * EDGE + count, :] = edge
+    mid[EDGE : EDGE + count, :] = jnp.where(alive, gelu(summed + bias_first[...]), 0.0)
+
+    for shift in range(3):
+        taps[0:count, shift * channels : (shift + 1) * channels] = mid[
+            EDGE - 1 + shift : EDGE - 1 + shift + count, :
+        ].astype(jnp.bfloat16)
+    inner = height * slot
+    summed = jnp.dot(taps[LEAD : LEAD + inner, :], second[0], preferred_element_type=jnp.float32)
+    for line in range(1, 3):
+        summed = summed + jnp.dot(
+            taps[LEAD + line * slot : LEAD + line * slot + inner, :], second[line],
+            preferred_element_type=jnp.float32,
+        )
+    summed = summed.reshape(height, slot, channels)[:, :breadth].reshape(height * breadth, channels)
+    alive = marked[...].reshape(height * breadth, channels) < FAR
+    out[...] = jnp.where(alive, gelu(summed + bias_second[...]), 0.0).astype(jnp.bfloat16)
+    keys[...] = jnp.dot(out[...], key_weight[...], preferred_element_type=jnp.float32).astype(
+        jnp.bfloat16
+    )
+
+
+def write_parts(block, values, top, total):
+    channels = values.shape[0]
+    parts = []
+    for source, count in ((top, 3), (total, 2)):
+        rest = source
+        for _ in range(count):
+            part = rest.astype(jnp.bfloat16).astype(jnp.float32)
+            parts.append(part)
+            rest = rest - part
+    parts.append(jnp.zeros((block.shape[0] - channels - 5, values.shape[1]), jnp.float32))
+    block[0:channels, :] = values.astype(jnp.bfloat16)
+    block[channels:, :] = jnp.concatenate(parts, axis=0).astype(jnp.bfloat16)
+
+
+def read_parts(block):
+    channels = block.shape[0] - 16
+    tail = block[channels:, :].astype(jnp.float32)
+    row = lambda k: tail[k : k + 1]
+    return (
+        block[0:channels, :].astype(jnp.float32),
+        row(0) + row(1) + row(2),
+        row(3) + row(4),
+    )
+
+
+def read_whole(block):
+    channels = block.shape[0] - 8
+    tail = block[channels:, :]
+    return block[0:channels, :], tail[0:1], tail[1:2]
+
+
+def write_whole(block, values, top, total):
+    channels = values.shape[0]
+    block[0:channels, :] = values
+    block[channels:, :] = jnp.concatenate(
+        [top, total, jnp.zeros((6, values.shape[1]), jnp.float32)], axis=0
+    )
+
+
+def score_blocks(cells, keys, marked, queries, scale):
+    scores = lax.dot_general(
+        keys[...], queries, (((1,), (1,)), ((), ())), preferred_element_type=jnp.float32
+    )
+    alive = marked[...] < FAR
+    if alive.shape != scores.shape:
+        alive = jnp.broadcast_to(alive[:, :1], scores.shape)
+    scores = jnp.where(alive, scores * scale, -1e30)
+    top = jnp.max(scores, axis=0, keepdims=True)
+    chosen = jnp.exp(scores - top)
+    total = jnp.sum(chosen, axis=0, keepdims=True)
+    pooled = lax.dot_general(
+        cells[...], chosen.astype(jnp.bfloat16), (((0,), (0,)), ((), ())),
+        preferred_element_type=jnp.float32,
+    )
+    return pooled, top, total
+
+
+def score_kernel(cells, keys, marked, *refs):
+    *queries, out, held = refs
+    size = queries[0].shape[0]
+    for place, part in enumerate(queries):
+        held[place * size : (place + 1) * size, :] = part[...]
+    pooled, top, total = score_blocks(
+        cells, keys, marked, held[...], 1.0 / math.sqrt(held.shape[1])
+    )
+    for place in range(len(queries)):
+        cut = slice(place * size, (place + 1) * size)
+        write_whole(out.at[place], pooled[:, cut], top[:, cut], total[:, cut])
+
+
+def spread_kernel(count, size, *refs):
+    held, own, sends, all_blocks = refs[:-count - 1], refs[-count - 1], refs[-count : -1], refs[-1]
+    done = 0
+    for part in held:
+        all_blocks[done : done + part.shape[0]] = part[...]
+        done += part.shape[0]
+    row, col = lax.axis_index("row"), lax.axis_index("col")
+    for step in range(count):
+        block = all_blocks[lax.rem(row + step, count) ^ col]
+        block = pltpu.roll(block, lax.rem(row + 1, count) * size, 1)
+        channels = block.shape[0] - 8
+        if step == 0:
+            own[...] = block
+        else:
+            write_parts(
+                sends[step - 1],
+                block[:channels],
+                block[channels : channels + 1],
+                block[channels + 1 : channels + 2],
+            )
+
+
+def merge_kernel(own, *refs):
+    *arrived, whole, packed_out = refs
+    values, top, total = merged([read_whole(own)] + [read_parts(block) for block in arrived])
+    write_whole(whole, values, top, total)
+    write_parts(packed_out, values, top, total)
+
+
+def finish_kernel(own, arrived, value_weight, out_weight, out):
+    values, _, total = merged([read_whole(own), read_parts(arrived)])
+    normalized = (values / total).astype(jnp.bfloat16)
+    attended = lax.dot_general(
+        normalized, value_weight[...], (((0,), (0,)), ((), ())),
+        preferred_element_type=jnp.float32,
+    ).astype(jnp.bfloat16)
+    out[...] = jnp.dot(
+        attended, out_weight[...], preferred_element_type=jnp.float32
+    ).astype(out.dtype)
+
+
+def shape_of(*dims, dtype=jnp.bfloat16):
+    return jax.ShapeDtypeStruct(dims, dtype)
+
+
+def kernel_path(
+    features, tissue, conv_first, bias_first, conv_second, bias_second, key_weight,
+    value_weight, latent_queries, out_weight,
+):
+    height, breadth, channels = features.shape
+    rows, cols = lax.axis_size("row"), lax.axis_size("col")
+    width = latent_queries.shape[1]
+    cells = height * breadth
+    slot = -(-(breadth + 2 * HALO) // 16) * 16
+    flat = LEAD + (height + 2 * HALO) * slot
+
+    with jax.named_scope("query_rows"):
+        turned = [shifted(latent_queries, "row", k) for k in range(1, rows)]
+    marked = jnp.where(tissue[:, :, None] > 0, features, jnp.asarray(FAR, features.dtype))
+    with jax.named_scope("halo_rows"):
+        top = shifted(marked[height - HALO :], "row", 1)
+        bottom = shifted(marked[:HALO], "row", -1)
+    edge = lambda cut: jnp.concatenate([top[:, cut], marked[:, cut], bottom[:, cut]], axis=0)
+    with jax.named_scope("halo_cols"):
+        left = shifted(edge(slice(breadth - HALO, breadth)), "col", 1)
+        right = shifted(edge(slice(0, HALO)), "col", -1)
+
+    own_column = jnp.concatenate(turned[::-1] + [latent_queries], axis=0)
+    block = own_column.shape[0]
+    blocks = [own_column]
+    bit = cols // 2
+    pairs = []
+    with jax.named_scope("query_cols"):
+        across = flipped(own_column, "col", 2)
+        beside = flipped(own_column, "col", 1)
+        diagonal = flipped(across, "col", 1)
+
+    second, keys = pl.pallas_call(
+        conv_kernel,
+        out_shape=(shape_of(cells, channels), shape_of(cells, width)),
+        scratch_shapes=[
+            pltpu.VMEM((flat + 2 * EDGE, channels), jnp.float32),
+            pltpu.VMEM((flat - 2 * slot + 2 * EDGE, channels), jnp.float32),
+            pltpu.VMEM((flat, 3 * channels), jnp.bfloat16),
+        ],
+        name="convolve",
+    )(
+        marked, top, bottom, left, right,
+        conv_first.reshape(3, 3 * channels, channels), bias_first.reshape(1, channels),
+        conv_second.reshape(3, 3 * channels, channels), bias_second.reshape(1, channels),
+        key_weight,
+    )
+    alive = marked.reshape(cells, channels)
+    score = lambda *queries: pl.pallas_call(
+        score_kernel,
+        out_shape=shape_of(len(queries), channels + 8, block, dtype=jnp.float32),
+        scratch_shapes=[pltpu.VMEM((len(queries) * block, width), jnp.bfloat16)],
+        name="score",
+    )(second, keys, alive, *queries)
+    near, far = score(own_column, beside), score(across, diagonal)
+    own, *sends = pl.pallas_call(
+        functools.partial(spread_kernel, cols, latent_queries.shape[0]),
+        out_shape=[shape_of(channels + 8, block, dtype=jnp.float32)]
+        + [shape_of(channels + 16, block)] * (rows - 1),
+        scratch_shapes=[pltpu.VMEM((cols, channels + 8, block), jnp.float32)],
+        name="spread",
+    )(near, far)
+    with jax.named_scope("pool_rows"):
+        arrived = [shifted(part, "row", k + 1) for k, part in enumerate(sends)]
+    merge = lambda *parts: pl.pallas_call(
+        merge_kernel,
+        out_shape=[shape_of(channels + 8, block, dtype=jnp.float32), shape_of(channels + 16, block)],
+        name="merge",
+    )(*parts)
+    own, packed_own = merge(own, *arrived)
+    with jax.named_scope("pool_across"):
+        arrived = flipped(packed_own, "col", 2)
+    own, packed_own = merge(own, arrived)
+    with jax.named_scope("pool_beside"):
+        arrived = flipped(packed_own, "col", 1)
+    return pl.pallas_call(
+        finish_kernel,
+        out_shape=shape_of(block, out_weight.shape[1]),
+        name="finish",
+    )(own, arrived, value_weight, out_weight)
+
+
+def shards(
+    features, tissue, conv_first, bias_first, conv_second, bias_second, key_weight,
+    value_weight, latent_queries, out_weight,
+):
+    rows, cols = lax.axis_size("row"), lax.axis_size("col")
+    if rows == cols == 4 and (rows * latent_queries.shape[0]) % 128 == 0:
+        return kernel_path(
+            features, tissue, conv_first, bias_first, conv_second, bias_second, key_weight,
+            value_weight, latent_queries, out_weight,
+        )
+    marked = jnp.where(tissue[:, :, None] > 0, features, jnp.asarray(FAR, features.dtype))
+    marked = with_halo(with_halo(marked, "row", 0), "col", 1)
+    normalized = plain_attend(
+        features, tissue, marked, latent_queries,
+        (conv_first, bias_first, conv_second, bias_second, key_weight),
+    )
     attended = lax.dot_general(
         normalized, value_weight, (((0,), (0,)), ((), ())), preferred_element_type=jnp.float32
     ).astype(jnp.bfloat16)

time: 74.8 us -> 69.6 us (0.930)
  Pallas kernels: 0 us -> 22.2 us
  matrix products: 11.3 us -> 0 us
  local copies, waits for them, and re-layouts: 15.2 us -> 6.97 us
  waiting for transfers between devices: 25.7 us -> 18.4 us
  other arithmetic: 7.76 us -> 1.85 us
  starting transfers between devices: 13.7 us -> 19.6 us
    pallas_call x0 -> x7, Pallas kernels: none -> 22.2 us  [the longest x1 7.58 us: kernel_path(): pl.pallas_call(conv_kernel, out_shape=(shape_of(cells, channels), shape_o...]
    dot_general x21 -> x0, matrix products: 11.3 us -> none  [the longest x18 6.33 us: convolve_valid(): jnp.dot(window.reshape(height * breadth, channels), weight[offset_row, of...]
    reshape x10 -> x0, local copies, waits for them, and re-layouts: 5.01 us -> none  [the longest x9 4.93 us: convolve_valid(): window.reshape(height * breadth, channels)]
    ppermute x10, waiting for transfers between devices: 12.6 us -> 8.09 us  [shifted(): lax.ppermute(array, axis, [(i, (i + step) % count) for i in range(count)])]
    ppermute x10, starting transfers between devices: 11.7 us -> 16.1 us  [shifted(): lax.ppermute(array, axis, [(i, (i + step) % count) for i in range(count)])]
    convert_element_type x16 -> x0, other arithmetic: 4.25 us -> none  [the longest x1 1.99 us: shards(): jnp.where(alive[HALO:-HALO, HALO:-HALO], second, 0.0).astype(jnp.bfloat16)]
    ppermute x4 -> x5, waiting for transfers between devices: 13.1 us -> 10.3 us  [flipped(): return lax.ppermute(array, axis, [(i, i ^ bit) for i in range(count)])]
    concatenate x6 -> x1, local copies, waits for them, and re-layouts: 1.71 us -> 0.01 us  [kernel_path(): own_column = jnp.concatenate(turned[::-1] + [latent_queries], axis=0)]
  transfers between devices with their start and end apart: 14 -> 15, of which waited for: 10 -> 8; matrix products, arithmetic and copies ran while one was open for 31% -> 5% of each run, Pallas kernels for 0% -> 16%
where the time goes in v2:
time: 69.6 us; the launch traced here: 69.2 us
  Pallas kernels  22.2 us (32%)
  starting transfers between devices  19.6 us (28%)
  waiting for transfers between devices  18.4 us (26%)
  local copies, waits for them, and re-layouts  6.97 us (10%)
  other arithmetic  1.85 us (3%)
    ppermute x10, starting transfers between devices, shifted(): lax.ppermute(array, axis, [(i, (i + step) % count) for i in range(count)])  16.1 us
    ppermute x5, waiting for transfers between devices, flipped(): return lax.ppermute(array, axis, [(i, i ^ bit) for i in range(count)])  10.3 us
    ppermute x10, waiting for transfers between devices, shifted(): lax.ppermute(array, axis, [(i, (i + step) % count) for i in range(count)])  8.09 us
    pallas_call x1, Pallas kernels, kernel_path(): pl.pallas_call(conv_kernel, out_shape=(shape_of(cells, channels), shape_o...  7.58 us
    pallas_call x2, Pallas kernels, kernel_path(): pl.pallas_call(score_kernel, out_shape=shape_of(len(queries), channels +...  6.55 us
    unnamed x36, local copies, waits for them, and re-layouts  5.28 us
    ppermute x5, starting transfers between devices, flipped(): return lax.ppermute(array, axis, [(i, i ^ bit) for i in range(count)])  3.52 us
    pallas_call x2, Pallas kernels, kernel_path(): pl.pallas_call(merge_kernel, out_shape=[shape_of(channels + 8, block, dty...  3.44 us
  transfers between devices with their start and end apart: 15, of which 8 were waited for; matrix products, arithmetic and copies ran while one was open for 5% of the time, Pallas kernels for 16%

profile of v2, /device:TPU:0, one launch (start us, length us, event | category | flops | bytes accessed | tf_op | source)
XLA Modules:
  0.0 69.2 jit_solution(11453918551740456494)
XLA Ops:
  0.0 5.1 %collective-permute-start.4 = (bf16[32,1280]{1,0:T(8,128)(2,1)}, bf16[32,1280]{1,0:T(8,128)(2,1)S(1)}, u32[]{:S(2)}, u32[]{:S(2)}) collective-permute-start(bf16[32,1280]{1,0:T(8,128)(2,1)} %param.18), channel_id=1, source_target_pairs={{0,3},{1,0},{2,1},{3,2},{4,7},{5,4},{6,5},{7,6},{8,11},{9,8},{10,9... | collective-permute-start | bytes 245768 | tf_op jit(solution)/shard_map/query_rows/ppermute | solution.py:19
  5.1 1.0 %collective-permute-start.6 = (bf16[32,1280]{1,0:T(8,128)(2,1)}, bf16[32,1280]{1,0:T(8,128)(2,1)S(1)}, u32[]{:S(2)}, u32[]{:S(2)}) collective-permute-start(bf16[32,1280]{1,0:T(8,128)(2,1)} %param.18), channel_id=1, source_target_pairs={{0,1},{1,2},{2,3},{3,0},{4,5},{5,6},{6,7},{7,4},{8,9},{9,10},{10,1... | collective-permute-start | bytes 245768 | tf_op jit(solution)/shard_map/query_rows/ppermute | solution.py:19
  6.1 0.7 %broadcast_compare_fusion = pred[16,32]{1,0:T(8,128)(4,1)S(1)} fusion(s32[16,32]{1,0:T(8,128)} %param.11), kind=kLoop, calls=%fused_computation.7 | loop fusion | flops 512 | bytes 2560 | tf_op jit(solution)/shard_map/gt | solution.py:367
  6.8 1.1 %broadcast_select_fusion.marked = bf16[16,32,256]{2,1,0:T(8,128)(2,1)S(1)} fusion(bf16[16,32,256]{2,1,0:T(8,128)(2,1)} %param.10, pred[16,32]{1,0:T(8,128)(4,1)S(1)} %broadcast_compare_fusion), kind=kLoop, calls=%fused_computation | loop fusion | flops 131072 | bytes 524800 | tf_op jit(solution)/shard_map/jit(_where)/select_n | solution.py:367
  7.9 2.5 %collective-permute-start = (bf16[2,32,256]{2,1,0:T(8,128)(2,1)S(1)}, bf16[2,32,256]{2,1,0:T(8,128)(2,1)S(1)}, u32[]{:S(2)}, u32[]{:S(2)}) collective-permute-start(bf16[2,32,256]{2,1,0:T(8,128)(2,1)S(1)} %get-tuple-element.28), channel_id=1, source_target_pairs={{0,1},{1,2},{2,3},{3,0},{4,5},{5,6},{6,7},{7,4},{8,9},{9,10},{10,1... | collective-permute-start | bytes 98312 | tf_op jit(solution)/shard_map/halo_rows/ppermute | solution.py:19
  10.4 1.3 %collective-permute-start.1 = (bf16[2,32,256]{2,1,0:T(8,128)(2,1)S(1)}, bf16[2,32,256]{2,1,0:T(8,128)(2,1)S(1)}, u32[]{:S(2)}, u32[]{:S(2)}) collective-permute-start(bf16[2,32,256]{2,1,0:T(8,128)(2,1)S(1)} %get-tuple-element.27), channel_id=1, source_target_pairs={{0,3},{1,0},{2,1},{3,2},{4,7},{5,4},{6,5},{7,6},{8,11},{9,8},{10,9... | collective-permute-start | bytes 98312 | tf_op jit(solution)/shard_map/halo_rows/ppermute | solution.py:19
  11.8 2.1 %collective-permute-done.5 = bf16[32,1280]{1,0:T(8,128)(2,1)S(1)} collective-permute-done((bf16[32,1280]{1,0:T(8,128)(2,1)}, bf16[32,1280]{1,0:T(8,128)(2,1)S(1)}, u32[]{:S(2)}, u32[]{:S(2)}) %collective-permute-start.5) | collective-permute-done | bytes 81952 | tf_op jit(solution)/shard_map/query_rows/ppermute | solution.py:19
  13.9 1.6 %collective-permute-start.8 = (bf16[128,1280]{1,0:T(8,128)(2,1)S(1)}, bf16[128,1280]{1,0:T(8,128)(2,1)S(1)}, u32[]{:S(2)}, u32[]{:S(2)}) collective-permute-start(bf16[128,1280]{1,0:T(8,128)(2,1)S(1)} %constant_dynamic-update-slice_fusion.refs_0_), channel_id=1, source_target_pairs={{0,8},{4,12},{8,0},{12,4},{1,9},{5,13},{9,1},{13,5},{2,10},{6,14},... | collective-permute-start | bytes 983048 | tf_op jit(solution)/shard_map/query_cols/ppermute | solution.py:24
  15.6 7.1 %collective-permute-done.8.refs_0_ = bf16[128,1280]{1,0:T(8,128)(2,1)S(1)} collective-permute-done((bf16[128,1280]{1,0:T(8,128)(2,1)S(1)}, bf16[128,1280]{1,0:T(8,128)(2,1)S(1)}, u32[]{:S(2)}, u32[]{:S(2)}) %collective-permute-start.8) | collective-permute-done | bytes 327712 | tf_op jit(solution)/shard_map/query_cols/ppermute | solution.py:24
  22.8 0.5 collective-permute-start.2
  23.3 1.3 %collective-permute-start.3 = (bf16[20,2,256]{2,1,0:T(2,128)(2,1)S(1)}, bf16[20,2,256]{2,1,0:T(2,128)(2,1)S(1)}, u32[]{:S(2)}, u32[]{:S(2)}) collective-permute-start(bf16[20,2,256]{2,1,0:T(2,128)(2,1)S(1)} %pad_maximum_fusion.1), channel_id=1, source_target_pairs={{0,12},{4,0},{8,4},{12,8},{1,13},{5,1},{9,5},{13,9},{2,14},{6,2},{... | collective-permute-start | bytes 61448 | tf_op jit(solution)/shard_map/halo_cols/ppermute | solution.py:19
  24.7 1.4 %collective-permute-done.2.left = bf16[20,2,256]{2,1,0:T(2,128)(2,1)S(1)} collective-permute-done((bf16[20,2,256]{2,1,0:T(2,128)(2,1)S(1)}, bf16[20,2,256]{2,1,0:T(2,128)(2,1)S(1)}, u32[]{:S(2)}, u32[]{:S(2)}) %collective-permute-start.2) | collective-permute-done | bytes 20512 | tf_op jit(solution)/shard_map/halo_cols/ppermute | solution.py:19
  26.7 7.6 %convolve.1 = (bf16[512,256]{1,0:T(8,128)(2,1)}, bf16[512,1280]{1,0:T(8,128)(2,1)}) custom-call(bf16[16,32,256]{2,1,0:T(8,128)(2,1)} %copy-done, bf16[2,32,256]{2,1,0:T(8,128)(2,1)} %copy-done.12, bf16[2,32,256]{2,1,0:T(8,128)(2,1)} %copy-done.13, bf16[20,2,256]{2,1,0:T(2,128)(2,1)} %copy-done.14, bf16[20,2,256]{2,1,0:T(2,128)(2,1)} %copy-done.15, ...), custom_call_target="tpu_custom_call" | custom-call | tf_op jit(solution)/shard_map/convolve/pallas_call | solution.py:386
  34.3 0.7 %copy-done.4 = bf16[128,1280]{1,0:T(8,128)(2,1)} copy-done((bf16[128,1280]{1,0:T(8,128)(2,1)}, bf16[128,1280]{1,0:T(8,128)(2,1)S(1)}, u32[]{:S(2)}) %copy-start.4) | copy-done | bytes 327704
  35.1 3.3 %score.2.refs_0_ = f32[2,264,128]{2,1,0:T(8,128)} custom-call(bf16[512,256]{1,0:T(8,128)(2,1)} %get-tuple-element.15.cells, bf16[512,1280]{1,0:T(8,128)(2,1)} %get-tuple-element.16.keys, bf16[512,256]{1,0:T(8,128)(2,1)} %bitcast.5, bf16[128,1280]{1,0:T(8,128)(2,1)} %copy-done.2, bf16[128,1280]{1,0:T(8,128)(2,1)} %copy-done.4), custom_call_target="tpu_custom_call" | custom-call | tf_op jit(solution)/shard_map/score/pallas_call | solution.py:402
  38.4 0.7 %copy-done.5 = bf16[128,1280]{1,0:T(8,128)(2,1)} copy-done((bf16[128,1280]{1,0:T(8,128)(2,1)}, bf16[128,1280]{1,0:T(8,128)(2,1)S(1)}, u32[]{:S(2)}) %copy-start.5) | copy-done | bytes 327704
  39.1 3.3 %score.3.refs_1_ = f32[2,264,128]{2,1,0:T(8,128)} custom-call(bf16[512,256]{1,0:T(8,128)(2,1)} %get-tuple-element.15.cells, bf16[512,1280]{1,0:T(8,128)(2,1)} %get-tuple-element.16.keys, bf16[512,256]{1,0:T(8,128)(2,1)} %bitcast.6, bf16[128,1280]{1,0:T(8,128)(2,1)} %copy-done.3, bf16[128,1280]{1,0:T(8,128)(2,1)} %copy-done.5), custom_call_target="tpu_custom_call" | custom-call | tf_op jit(solution)/shard_map/score/pallas_call | solution.py:402
  42.4 2.0 %spread.1 = (f32[264,128]{1,0:T(8,128)}, bf16[272,128]{1,0:T(8,128)(2,1)}, bf16[272,128]{1,0:T(8,128)(2,1)}, bf16[272,128]{1,0:T(8,128)(2,1)}) custom-call(f32[2,264,128]{2,1,0:T(8,128)} %score.2.refs_0_, f32[2,264,128]{2,1,0:T(8,128)} %score.3.refs_1_), custom_call_target="tpu_custom_call" | custom-call | tf_op jit(solution)/shard_map/spread/pallas_call | solution.py:409
  44.3 1.3 %collective-permute-start.11 = (bf16[272,128]{1,0:T(8,128)(2,1)}, bf16[272,128]{1,0:T(8,128)(2,1)S(1)}, u32[]{:S(2)}, u32[]{:S(2)}) collective-permute-start(bf16[272,128]{1,0:T(8,128)(2,1)} %get-tuple-element.19), channel_id=1, source_target_pairs={{0,2},{1,3},{2,0},{3,1},{4,6},{5,7},{6,4},{7,5},{8,10},{9,11},{10,... | collective-permute-start | bytes 208904 | tf_op jit(solution)/shard_map/pool_rows/ppermute | solution.py:19
  45.6 2.9 %collective-permute-start.12 = (bf16[272,128]{1,0:T(8,128)(2,1)}, bf16[272,128]{1,0:T(8,128)(2,1)S(1)}, u32[]{:S(2)}, u32[]{:S(2)}) collective-permute-start(bf16[272,128]{1,0:T(8,128)(2,1)} %get-tuple-element.20), channel_id=1, source_target_pairs={{0,3},{1,0},{2,1},{3,2},{4,7},{5,4},{6,5},{7,6},{8,11},{9,8},{10,9... | collective-permute-start | bytes 208904 | tf_op jit(solution)/shard_map/pool_rows/ppermute | solution.py:19
  48.6 2.3 %collective-permute-done.10.refs_0_ = bf16[272,128]{1,0:T(8,128)(2,1)S(1)} collective-permute-done((bf16[272,128]{1,0:T(8,128)(2,1)}, bf16[272,128]{1,0:T(8,128)(2,1)S(1)}, u32[]{:S(2)}, u32[]{:S(2)}) %collective-permute-start.10) | collective-permute-done | bytes 69664 | tf_op jit(solution)/shard_map/pool_rows/ppermute | solution.py:19
  50.9 2.2 %collective-permute-done.12.refs_2_ = bf16[272,128]{1,0:T(8,128)(2,1)S(1)} collective-permute-done((bf16[272,128]{1,0:T(8,128)(2,1)}, bf16[272,128]{1,0:T(8,128)(2,1)S(1)}, u32[]{:S(2)}, u32[]{:S(2)}) %collective-permute-start.12) | collective-permute-done | bytes 69664 | tf_op jit(solution)/shard_map/pool_rows/ppermute | solution.py:19
  53.1 0.6 copy-done.9
  53.7 1.8 %merge.2 = (f32[264,128]{1,0:T(8,128)}, bf16[272,128]{1,0:T(8,128)(2,1)}) custom-call(f32[264,128]{1,0:T(8,128)} %get-tuple-element.17.own, bf16[272,128]{1,0:T(8,128)(2,1)} %copy-done.7, bf16[272,128]{1,0:T(8,128)(2,1)} %copy-done.8, bf16[272,128]{1,0:T(8,128)(2,1)} %copy-done.9), custom_call_target="tpu_custom_call" | custom-call | tf_op jit(solution)/shard_map/merge/pallas_call | solution.py:418
  55.5 1.9 %collective-permute-start.13 = (bf16[272,128]{1,0:T(8,128)(2,1)}, bf16[272,128]{1,0:T(8,128)(2,1)S(1)}, u32[]{:S(2)}, u32[]{:S(2)}) collective-permute-start(bf16[272,128]{1,0:T(8,128)(2,1)} %get-tuple-element.22), channel_id=1, source_target_pairs={{0,8},{4,12},{8,0},{12,4},{1,9},{5,13},{9,1},{13,5},{2,10},{6,14},... | collective-permute-start | bytes 208904 | tf_op jit(solution)/shard_map/pool_across/ppermute | solution.py:24
  57.4 3.1 %collective-permute-done.13.refs_0_ = bf16[272,128]{1,0:T(8,128)(2,1)S(1)} collective-permute-done((bf16[272,128]{1,0:T(8,128)(2,1)}, bf16[272,128]{1,0:T(8,128)(2,1)S(1)}, u32[]{:S(2)}, u32[]{:S(2)}) %collective-permute-start.13) | collective-permute-done | bytes 69664 | tf_op jit(solution)/shard_map/pool_across/ppermute | solution.py:24
  60.5 0.6 copy-done.10
  61.1 1.7 %merge.3 = (f32[264,128]{1,0:T(8,128)}, bf16[272,128]{1,0:T(8,128)(2,1)}) custom-call(f32[264,128]{1,0:T(8,128)} %get-tuple-element.21.own, bf16[272,128]{1,0:T(8,128)(2,1)} %copy-done.10), custom_call_target="tpu_custom_call" | custom-call | tf_op jit(solution)/shard_map/merge/pallas_call | solution.py:418
  62.8 1.3 %copy.11.out_weight = bf16[1280,320]{1,0:T(8,128)(2,1)} copy(bf16[1280,320]{0,1:T(8,128)(2,1)S(1)} %copy-done.1) | data formatting | bytes 1638400 | tf_op args[9]
  64.3 0.6 copy-done.11
  64.9 2.7 %finish.1 = bf16[128,320]{1,0:T(8,128)(2,1)} custom-call(f32[264,128]{1,0:T(8,128)} %get-tuple-element.23.own, bf16[272,128]{1,0:T(8,128)(2,1)} %copy-done.11, bf16[256,1280]{1,0:T(8,128)(2,1)} %value_weight.1, bf16[1280,320]{1,0:T(8,128)(2,1)} %copy.11.out_weight), custom_call_target="tpu_custom_call" | custom-call | tf_op jit(solution)/shard_map/finish/pallas_call | solution.py:429
  67.6 1.6 %copy.12 = bf16[128,320]{0,1:T(8,128)(2,1)} copy(bf16[128,320]{1,0:T(8,128)(2,1)} %finish.1) | data formatting | bytes 163840 | tf_op jit(solution)/shard_map/finish/pallas_call | solution.py:429
  (51 shorter events, 1.2 us)
Async XLA Ops:
  0.0 13.9 %copy-start.6 = (bf16[32,1280]{1,0:T(8,128)(2,1)S(1)}, bf16[32,1280]{1,0:T(8,128)(2,1)}, u32[]{:S(2)}) copy-start(bf16[32,1280]{1,0:T(8,128)(2,1)} %param.18) | copy-start | bytes 245764
  0.0 11.8 %collective-permute-start.4 = (bf16[32,1280]{1,0:T(8,128)(2,1)}, bf16[32,1280]{1,0:T(8,128)(2,1)S(1)}, u32[]{:S(2)}, u32[]{:S(2)}) collective-permute-start(bf16[32,1280]{1,0:T(8,128)(2,1)} %param.18), channel_id=1, source_target_pairs={{0,3},{1,0},{2,1},{3,2},{4,7},{5,4},{6,5},{7,6},{8,11},{9,8},{10,9... | collective-permute-start | bytes 245768 | tf_op jit(solution)/shard_map/query_rows/ppermute | solution.py:19
  5.1 8.8 %collective-permute-start.5 = (bf16[32,1280]{1,0:T(8,128)(2,1)}, bf16[32,1280]{1,0:T(8,128)(2,1)S(1)}, u32[]{:S(2)}, u32[]{:S(2)}) collective-permute-start(bf16[32,1280]{1,0:T(8,128)(2,1)} %param.18), channel_id=1, source_target_pairs={{0,2},{1,3},{2,0},{3,1},{4,6},{5,7},{6,4},{7,5},{8,10},{9,11},{10,... | collective-permute-start | bytes 245768 | tf_op jit(solution)/shard_map/query_rows/ppermute | solution.py:19
  5.1 8.8 %collective-permute-start.6 = (bf16[32,1280]{1,0:T(8,128)(2,1)}, bf16[32,1280]{1,0:T(8,128)(2,1)S(1)}, u32[]{:S(2)}, u32[]{:S(2)}) collective-permute-start(bf16[32,1280]{1,0:T(8,128)(2,1)} %param.18), channel_id=1, source_target_pairs={{0,1},{1,2},{2,3},{3,0},{4,5},{5,6},{6,7},{7,4},{8,9},{9,10},{10,1... | collective-permute-start | bytes 245768 | tf_op jit(solution)/shard_map/query_rows/ppermute | solution.py:19
  7.9 18.3 %copy-start = (bf16[16,32,256]{2,1,0:T(8,128)(2,1)}, bf16[16,32,256]{2,1,0:T(8,128)(2,1)S(1)}, u32[]{:S(2)}) copy-start(bf16[16,32,256]{2,1,0:T(8,128)(2,1)S(1)} %broadcast_select_fusion.marked) | copy-start | bytes 786436
  7.9 14.8 %collective-permute-start = (bf16[2,32,256]{2,1,0:T(8,128)(2,1)S(1)}, bf16[2,32,256]{2,1,0:T(8,128)(2,1)S(1)}, u32[]{:S(2)}, u32[]{:S(2)}) collective-permute-start(bf16[2,32,256]{2,1,0:T(8,128)(2,1)S(1)} %get-tuple-element.28), channel_id=1, source_target_pairs={{0,1},{1,2},{2,3},{3,0},{4,5},{5,6},{6,7},{7,4},{8,9},{9,10},{10,1... | collective-permute-start | bytes 98312 | tf_op jit(solution)/shard_map/halo_rows/ppermute | solution.py:19
  10.4 5.1 %collective-permute-start.1 = (bf16[2,32,256]{2,1,0:T(8,128)(2,1)S(1)}, bf16[2,32,256]{2,1,0:T(8,128)(2,1)S(1)}, u32[]{:S(2)}, u32[]{:S(2)}) collective-permute-start(bf16[2,32,256]{2,1,0:T(8,128)(2,1)S(1)} %get-tuple-element.27), channel_id=1, source_target_pairs={{0,3},{1,0},{2,1},{3,2},{4,7},{5,4},{6,5},{7,6},{8,11},{9,8},{10,9... | collective-permute-start | bytes 98312 | tf_op jit(solution)/shard_map/halo_rows/ppermute | solution.py:19
  13.9 20.4 %copy-start.2 = (bf16[128,1280]{1,0:T(8,128)(2,1)}, bf16[128,1280]{1,0:T(8,128)(2,1)S(1)}, u32[]{:S(2)}) copy-start(bf16[128,1280]{1,0:T(8,128)(2,1)S(1)} %constant_dynamic-update-slice_fusion.refs_0_) | copy-start | bytes 983044
  13.9 8.8 %collective-permute-start.8 = (bf16[128,1280]{1,0:T(8,128)(2,1)S(1)}, bf16[128,1280]{1,0:T(8,128)(2,1)S(1)}, u32[]{:S(2)}, u32[]{:S(2)}) collective-permute-start(bf16[128,1280]{1,0:T(8,128)(2,1)S(1)} %constant_dynamic-update-slice_fusion.refs_0_), channel_id=1, source_target_pairs={{0,8},{4,12},{8,0},{12,4},{1,9},{5,13},{9,1},{13,5},{2,10},{6,14},... | collective-permute-start | bytes 983048 | tf_op jit(solution)/shard_map/query_cols/ppermute | solution.py:24
  15.5 10.6 %copy-start.13 = (bf16[2,32,256]{2,1,0:T(8,128)(2,1)}, bf16[2,32,256]{2,1,0:T(8,128)(2,1)S(1)}, u32[]{:S(2)}) copy-start(bf16[2,32,256]{2,1,0:T(8,128)(2,1)S(1)} %collective-permute-done.1.bottom) | copy-start | bytes 98308
  15.6 18.8 %collective-permute-start.7 = (bf16[128,1280]{1,0:T(8,128)(2,1)S(1)}, bf16[128,1280]{1,0:T(8,128)(2,1)S(1)}, u32[]{:S(2)}, u32[]{:S(2)}) collective-permute-start(bf16[128,1280]{1,0:T(8,128)(2,1)S(1)} %constant_dynamic-update-slice_fusion.refs_0_), channel_id=1, source_target_pairs={{0,4},{4,0},{8,12},{12,8},{1,5},{5,1},{9,13},{13,9},{2,6},{6,2},{1... | collective-permute-start | bytes 983048 | tf_op jit(solution)/shard_map/query_cols/ppermute | solution.py:24
  22.7 11.6 %copy-start.3 = (bf16[128,1280]{1,0:T(8,128)(2,1)}, bf16[128,1280]{1,0:T(8,128)(2,1)S(1)}, u32[]{:S(2)}) copy-start(bf16[128,1280]{1,0:T(8,128)(2,1)S(1)} %collective-permute-done.8.refs_0_) | copy-start | bytes 983044
  22.7 15.7 %collective-permute-start.9 = (bf16[128,1280]{1,0:T(8,128)(2,1)S(1)}, bf16[128,1280]{1,0:T(8,128)(2,1)S(1)}, u32[]{:S(2)}, u32[]{:S(2)}) collective-permute-start(bf16[128,1280]{1,0:T(8,128)(2,1)S(1)} %collective-permute-done.8.refs_0_), channel_id=1, source_target_pairs={{0,4},{4,0},{8,12},{12,8},{1,5},{5,1},{9,13},{13,9},{2,6},{6,2},{1... | collective-permute-start | bytes 983048 | tf_op jit(solution)/shard_map/query_cols/ppermute | solution.py:24
  22.7 3.4 %copy-start.12 = (bf16[2,32,256]{2,1,0:T(8,128)(2,1)}, bf16[2,32,256]{2,1,0:T(8,128)(2,1)S(1)}, u32[]{:S(2)}) copy-start(bf16[2,32,256]{2,1,0:T(8,128)(2,1)S(1)} %collective-permute-done.top) | copy-start | bytes 98308
  22.8 3.3 %collective-permute-start.2 = (bf16[20,2,256]{2,1,0:T(2,128)(2,1)S(1)}, bf16[20,2,256]{2,1,0:T(2,128)(2,1)S(1)}, u32[]{:S(2)}, u32[]{:S(2)}) collective-permute-start(bf16[20,2,256]{2,1,0:T(2,128)(2,1)S(1)} %pad_maximum_fusion), channel_id=1, source_target_pairs={{0,4},{4,8},{8,12},{12,0},{1,5},{5,9},{9,13},{13,1},{2,6},{6,10},{... | collective-permute-start | bytes 61448 | tf_op jit(solution)/shard_map/halo_cols/ppermute | solution.py:19
  23.3 2.8 %collective-permute-start.3 = (bf16[20,2,256]{2,1,0:T(2,128)(2,1)S(1)}, bf16[20,2,256]{2,1,0:T(2,128)(2,1)S(1)}, u32[]{:S(2)}, u32[]{:S(2)}) collective-permute-start(bf16[20,2,256]{2,1,0:T(2,128)(2,1)S(1)} %pad_maximum_fusion.1), channel_id=1, source_target_pairs={{0,12},{4,0},{8,4},{12,8},{1,13},{5,1},{9,5},{13,9},{2,14},{6,2},{... | collective-permute-start | bytes 61448 | tf_op jit(solution)/shard_map/halo_cols/ppermute | solution.py:19
  26.0 0.6 copy-start.14
  26.1 0.6 copy-start.15
  34.3 0.7 %copy-start.4 = (bf16[128,1280]{1,0:T(8,128)(2,1)}, bf16[128,1280]{1,0:T(8,128)(2,1)S(1)}, u32[]{:S(2)}) copy-start(bf16[128,1280]{1,0:T(8,128)(2,1)S(1)} %collective-permute-done.7.refs_1_) | copy-start | bytes 983044
  38.4 0.7 %copy-start.5 = (bf16[128,1280]{1,0:T(8,128)(2,1)}, bf16[128,1280]{1,0:T(8,128)(2,1)S(1)}, u32[]{:S(2)}) copy-start(bf16[128,1280]{1,0:T(8,128)(2,1)S(1)} %collective-permute-done.9.refs_1_) | copy-start | bytes 983044
  42.4 20.5 %copy-start.1 = (bf16[1280,320]{0,1:T(8,128)(2,1)S(1)}, bf16[1280,320]{0,1:T(8,128)(2,1)}, u32[]{:S(2)}) copy-start(bf16[1280,320]{0,1:T(8,128)(2,1)} %param.19) | copy-start | bytes 2457604
  44.3 6.6 %collective-permute-start.10 = (bf16[272,128]{1,0:T(8,128)(2,1)}, bf16[272,128]{1,0:T(8,128)(2,1)S(1)}, u32[]{:S(2)}, u32[]{:S(2)}) collective-permute-start(bf16[272,128]{1,0:T(8,128)(2,1)} %get-tuple-element.18), channel_id=1, source_target_pairs={{0,1},{1,2},{2,3},{3,0},{4,5},{5,6},{6,7},{7,4},{8,9},{9,10},{10,1... | collective-permute-start | bytes 208904 | tf_op jit(solution)/shard_map/pool_rows/ppermute | solution.py:19
  44.3 6.6 %collective-permute-start.11 = (bf16[272,128]{1,0:T(8,128)(2,1)}, bf16[272,128]{1,0:T(8,128)(2,1)S(1)}, u32[]{:S(2)}, u32[]{:S(2)}) collective-permute-start(bf16[272,128]{1,0:T(8,128)(2,1)} %get-tuple-element.19), channel_id=1, source_target_pairs={{0,2},{1,3},{2,0},{3,1},{4,6},{5,7},{6,4},{7,5},{8,10},{9,11},{10,... | collective-permute-start | bytes 208904 | tf_op jit(solution)/shard_map/pool_rows/ppermute | solution.py:19
  45.6 7.5 %collective-permute-start.12 = (bf16[272,128]{1,0:T(8,128)(2,1)}, bf16[272,128]{1,0:T(8,128)(2,1)S(1)}, u32[]{:S(2)}, u32[]{:S(2)}) collective-permute-start(bf16[272,128]{1,0:T(8,128)(2,1)} %get-tuple-element.20), channel_id=1, source_target_pairs={{0,3},{1,0},{2,1},{3,2},{4,7},{5,4},{6,5},{7,6},{8,11},{9,8},{10,9... | collective-permute-start | bytes 208904 | tf_op jit(solution)/shard_map/pool_rows/ppermute | solution.py:19
  50.9 2.2 %copy-start.7 = (bf16[272,128]{1,0:T(8,128)(2,1)}, bf16[272,128]{1,0:T(8,128)(2,1)S(1)}, u32[]{:S(2)}) copy-start(bf16[272,128]{1,0:T(8,128)(2,1)S(1)} %collective-permute-done.10.refs_0_) | copy-start | bytes 208900
  50.9 2.2 %copy-start.8 = (bf16[272,128]{1,0:T(8,128)(2,1)}, bf16[272,128]{1,0:T(8,128)(2,1)S(1)}, u32[]{:S(2)}) copy-start(bf16[272,128]{1,0:T(8,128)(2,1)S(1)} %collective-permute-done.11.refs_1_) | copy-start | bytes 208900
  53.1 0.6 copy-start.9
  55.5 5.0 %collective-permute-start.13 = (bf16[272,128]{1,0:T(8,128)(2,1)}, bf16[272,128]{1,0:T(8,128)(2,1)S(1)}, u32[]{:S(2)}, u32[]{:S(2)}) collective-permute-start(bf16[272,128]{1,0:T(8,128)(2,1)} %get-tuple-element.22), channel_id=1, source_target_pairs={{0,8},{4,12},{8,0},{12,4},{1,9},{5,13},{9,1},{13,5},{2,10},{6,14},... | collective-permute-start | bytes 208904 | tf_op jit(solution)/shard_map/pool_across/ppermute | solution.py:24
  60.5 0.6 copy-start.10
  62.8 1.5 %collective-permute-start.14 = (bf16[272,128]{1,0:T(8,128)(2,1)}, bf16[272,128]{1,0:T(8,128)(2,1)S(1)}, u32[]{:S(2)}, u32[]{:S(2)}) collective-permute-start(bf16[272,128]{1,0:T(8,128)(2,1)} %get-tuple-element.24), channel_id=1, source_target_pairs={{0,4},{4,0},{8,12},{12,8},{1,5},{5,1},{9,13},{13,9},{2,6},{6,2},{1... | collective-permute-start | bytes 208904 | tf_op jit(solution)/shard_map/pool_beside/ppermute | solution.py:24
  64.3 0.6 copy-start.11

commit v3 on v2

--- a/solution.py
+++ b/solution.py
@@ -1,4 +1,3 @@
-import functools
 import math
 
 import jax
@@ -7,6 +6,7 @@
 from jax.experimental import pallas as pl
 from jax.experimental.pallas import tpu as pltpu
 from jax.sharding import PartitionSpec as P
+
 
 HALO = 2
 FAR = float("inf")
@@ -167,8 +167,14 @@
 
 def conv_kernel(
     marked, top, bottom, left, right, first, bias_first, second, bias_second, key_weight,
-    out, keys, cells, mid, taps,
+    out, keys, cells, mid, taps, second_held, key_held, done,
 ):
+    later = [
+        pltpu.make_async_copy(second, second_held, done.at[0]),
+        pltpu.make_async_copy(key_weight, key_held, done.at[1]),
+    ]
+    for copy in later:
+        copy.start()
     height, breadth, channels = marked.shape
     slot = (cells.shape[0] - 2 * EDGE - LEAD) // (height + 2 * HALO)
     flat = cells.shape[0] - 2 * EDGE
@@ -222,16 +228,20 @@
             EDGE - 1 + shift : EDGE - 1 + shift + count, :
         ].astype(jnp.bfloat16)
     inner = height * slot
-    summed = jnp.dot(taps[LEAD : LEAD + inner, :], second[0], preferred_element_type=jnp.float32)
+    later[0].wait()
+    summed = jnp.dot(
+        taps[LEAD : LEAD + inner, :], second_held[0], preferred_element_type=jnp.float32
+    )
     for line in range(1, 3):
         summed = summed + jnp.dot(
-            taps[LEAD + line * slot : LEAD + line * slot + inner, :], second[line],
+            taps[LEAD + line * slot : LEAD + line * slot + inner, :], second_held[line],
             preferred_element_type=jnp.float32,
         )
     summed = summed.reshape(height, slot, channels)[:, :breadth].reshape(height * breadth, channels)
     alive = marked[...].reshape(height * breadth, channels) < FAR
     out[...] = jnp.where(alive, gelu(summed + bias_second[...]), 0.0).astype(jnp.bfloat16)
-    keys[...] = jnp.dot(out[...], key_weight[...], preferred_element_type=jnp.float32).astype(
+    later[1].wait()
+    keys[...] = jnp.dot(out[...], key_held[...], preferred_element_type=jnp.float32).astype(
         jnp.bfloat16
     )
 
@@ -306,16 +316,20 @@
         write_whole(out.at[place], pooled[:, cut], top[:, cut], total[:, cut])
 
 
-def spread_kernel(count, size, *refs):
-    held, own, sends, all_blocks = refs[:-count - 1], refs[-count - 1], refs[-count : -1], refs[-1]
+def last_score_kernel(rows, size, held, cells, keys, marked, queries, *refs):
+    own, *sends, blocks = refs
     done = 0
     for part in held:
-        all_blocks[done : done + part.shape[0]] = part[...]
+        blocks[done : done + part.shape[0]] = part[...]
         done += part.shape[0]
+    pooled, top, total = score_blocks(
+        cells, keys, marked, queries[...], 1.0 / math.sqrt(queries.shape[1])
+    )
+    write_whole(blocks.at[done], pooled, top, total)
     row, col = lax.axis_index("row"), lax.axis_index("col")
-    for step in range(count):
-        block = all_blocks[lax.rem(row + step, count) ^ col]
-        block = pltpu.roll(block, lax.rem(row + 1, count) * size, 1)
+    for step in range(rows):
+        block = blocks[lax.rem(row + step, rows) ^ col]
+        block = pltpu.roll(block, lax.rem(row + 1, rows) * size, 1)
         channels = block.shape[0] - 8
         if step == 0:
             own[...] = block
@@ -342,13 +356,33 @@
         normalized, value_weight[...], (((0,), (0,)), ((), ())),
         preferred_element_type=jnp.float32,
     ).astype(jnp.bfloat16)
-    out[...] = jnp.dot(
-        attended, out_weight[...], preferred_element_type=jnp.float32
+    out[...] = lax.dot_general(
+        out_weight[...], attended, (((1,), (1,)), ((), ())), preferred_element_type=jnp.float32
     ).astype(out.dtype)
 
 
-def shape_of(*dims, dtype=jnp.bfloat16):
-    return jax.ShapeDtypeStruct(dims, dtype)
+MIB = 1 << 20
+
+
+def call(kernel, outs, args, scratch=(), limit=4, flops=0, far=()):
+    held = pl.BlockSpec(memory_space=pltpu.VMEM)
+    outside = pl.BlockSpec(memory_space=pltpu.HBM)
+    return pl.pallas_call(
+        kernel,
+        out_shape=[pltpu.VMEM(shape, dtype) for shape, dtype in outs],
+        in_specs=[outside if k in far else held for k in range(len(args))],
+        out_specs=[held] * len(outs),
+        scratch_shapes=[
+            pltpu.VMEM(*kind) if isinstance(kind, tuple) else kind for kind in scratch
+        ],
+        compiler_params=pltpu.CompilerParams(vmem_limit_bytes=limit * MIB),
+        cost_estimate=pl.CostEstimate(flops=flops, bytes_accessed=0, transcendentals=0),
+    )(
+        *[
+            pltpu.with_memory_space_constraint(arg, pltpu.HBM if k in far else pltpu.VMEM)
+            for k, arg in enumerate(args)
+        ]
+    )
 
 
 def kernel_path(
@@ -361,76 +395,79 @@
     cells = height * breadth
     slot = -(-(breadth + 2 * HALO) // 16) * 16
     flat = LEAD + (height + 2 * HALO) * slot
-
-    with jax.named_scope("query_rows"):
-        turned = [shifted(latent_queries, "row", k) for k in range(1, rows)]
+    wide, half = jnp.float32, jnp.bfloat16
+    block = rows * latent_queries.shape[0]
+    whole_block, sent_block = (channels + 8, block), (channels + 16, block)
+
+    turned = [shifted(latent_queries, "row", k) for k in range(1, rows)]
     marked = jnp.where(tissue[:, :, None] > 0, features, jnp.asarray(FAR, features.dtype))
-    with jax.named_scope("halo_rows"):
-        top = shifted(marked[height - HALO :], "row", 1)
-        bottom = shifted(marked[:HALO], "row", -1)
+    top = shifted(marked[height - HALO :], "row", 1)
+    bottom = shifted(marked[:HALO], "row", -1)
     edge = lambda cut: jnp.concatenate([top[:, cut], marked[:, cut], bottom[:, cut]], axis=0)
-    with jax.named_scope("halo_cols"):
-        left = shifted(edge(slice(breadth - HALO, breadth)), "col", 1)
-        right = shifted(edge(slice(0, HALO)), "col", -1)
+    left = shifted(edge(slice(breadth - HALO, breadth)), "col", 1)
+    right = shifted(edge(slice(0, HALO)), "col", -1)
 
     own_column = jnp.concatenate(turned[::-1] + [latent_queries], axis=0)
-    block = own_column.shape[0]
-    blocks = [own_column]
-    bit = cols // 2
-    pairs = []
-    with jax.named_scope("query_cols"):
-        across = flipped(own_column, "col", 2)
-        beside = flipped(own_column, "col", 1)
-        diagonal = flipped(across, "col", 1)
-
-    second, keys = pl.pallas_call(
-        conv_kernel,
-        out_shape=(shape_of(cells, channels), shape_of(cells, width)),
-        scratch_shapes=[
-            pltpu.VMEM((flat + 2 * EDGE, channels), jnp.float32),
-            pltpu.VMEM((flat - 2 * slot + 2 * EDGE, channels), jnp.float32),
-            pltpu.VMEM((flat, 3 * channels), jnp.bfloat16),
+    across = flipped(own_column, "col", 2)
+    beside = flipped(own_column, "col", 1)
+    diagonal = flipped(across, "col", 1)
+
+    second, keys = call(
+        conv_kernel, [((cells, channels), half), ((cells, width), half)],
+        [
+            marked, top, bottom, left, right,
+            conv_first.reshape(3, 3 * channels, channels), bias_first.reshape(1, channels),
+            conv_second.reshape(3, 3 * channels, channels), bias_second.reshape(1, channels),
+            key_weight,
         ],
-        name="convolve",
-    )(
-        marked, top, bottom, left, right,
-        conv_first.reshape(3, 3 * channels, channels), bias_first.reshape(1, channels),
-        conv_second.reshape(3, 3 * channels, channels), bias_second.reshape(1, channels),
-        key_weight,
-    )
-    alive = marked.reshape(cells, channels)
-    score = lambda *queries: pl.pallas_call(
-        score_kernel,
-        out_shape=shape_of(len(queries), channels + 8, block, dtype=jnp.float32),
-        scratch_shapes=[pltpu.VMEM((len(queries) * block, width), jnp.bfloat16)],
-        name="score",
-    )(second, keys, alive, *queries)
-    near, far = score(own_column, beside), score(across, diagonal)
-    own, *sends = pl.pallas_call(
-        functools.partial(spread_kernel, cols, latent_queries.shape[0]),
-        out_shape=[shape_of(channels + 8, block, dtype=jnp.float32)]
-        + [shape_of(channels + 16, block)] * (rows - 1),
-        scratch_shapes=[pltpu.VMEM((cols, channels + 8, block), jnp.float32)],
-        name="spread",
-    )(near, far)
-    with jax.named_scope("pool_rows"):
-        arrived = [shifted(part, "row", k + 1) for k, part in enumerate(sends)]
-    merge = lambda *parts: pl.pallas_call(
-        merge_kernel,
-        out_shape=[shape_of(channels + 8, block, dtype=jnp.float32), shape_of(channels + 16, block)],
-        name="merge",
-    )(*parts)
-    own, packed_own = merge(own, *arrived)
-    with jax.named_scope("pool_across"):
-        arrived = flipped(packed_own, "col", 2)
-    own, packed_own = merge(own, arrived)
-    with jax.named_scope("pool_beside"):
-        arrived = flipped(packed_own, "col", 1)
+        [
+            ((flat + 2 * EDGE, channels), wide),
+            ((flat - 2 * slot + 2 * EDGE, channels), wide),
+            ((flat, 3 * channels), half),
+            ((3, 3 * channels, channels), half),
+            ((channels, width), half),
+            pltpu.SemaphoreType.DMA((2,)),
+        ],
+        limit=16, far=(7, 9), flops=2 * cells * channels * (21 * channels + width),
+    )
+    marked = marked.reshape(cells, channels)
+
+    def score(*queries):
+        return call(
+            score_kernel, [((len(queries),) + whole_block, wide)],
+            [second, keys, marked, *queries],
+            [((len(queries) * block, width), half)],
+            limit=8, flops=2 * cells * block * len(queries) * (width + channels),
+        )[0]
+
+    near = score(own_column, beside)
+    far = score(across)
+
+    def last(near, far, *rest):
+        last_score_kernel(rows, latent_queries.shape[0], (near, far), *rest)
+
+    own, *sends = call(
+        last, [(whole_block, wide)] + [(sent_block, half)] * (rows - 1),
+        [near, far, second, keys, marked, diagonal],
+        [((cols,) + whole_block, wide)],
+        limit=8, flops=2 * cells * block * (width + channels),
+    )
+    arrived = [shifted(part, "row", k + 1) for k, part in enumerate(sends)]
+    merge = lambda *parts: call(merge_kernel, [(whole_block, wide), (sent_block, half)], parts)
+    own, sent = merge(own, *arrived)
+    arrived = flipped(sent, "col", 2)
+    own, sent = merge(own, arrived)
+    arrived = flipped(sent, "col", 1)
+    held = pl.BlockSpec(memory_space=pltpu.VMEM)
+    keep = lambda array: pltpu.with_memory_space_constraint(array, pltpu.VMEM)
     return pl.pallas_call(
         finish_kernel,
-        out_shape=shape_of(block, out_weight.shape[1]),
+        out_shape=jax.ShapeDtypeStruct((out_weight.shape[1], block), half),
+        in_specs=[held] * 4,
+        out_specs=held,
+        compiler_params=pltpu.CompilerParams(vmem_limit_bytes=6 * MIB),
         name="finish",
-    )(own, arrived, value_weight, out_weight)
+    )(keep(own), keep(arrived), keep(value_weight), keep(out_weight.T)).T
 
 
 def shards(

time: 69.6 us -> 52.1 us (0.75)
  Pallas kernels: 22.2 us -> 9.34 us
  local copies, waits for them, and re-layouts: 6.97 us -> 0.11 us
  waiting for transfers between devices: 18.4 us -> 22.4 us
  starting transfers between devices: 19.6 us -> 18.1 us
    pallas_call x7, Pallas kernels: 22.2 us -> 9.34 us  [the longest x6 8.05 us: call(): pl.pallas_call(kernel, out_shape=[pltpu.VMEM(shape, dtype) for shape, dty...]
    unnamed x36 -> x15, local copies, waits for them, and re-layouts: 5.28 us -> 0.05 us
    ppermute x5, waiting for transfers between devices: 10.3 us -> 12.7 us  [flipped(): return lax.ppermute(array, axis, [(i, i ^ bit) for i in range(count)])]
    pallas_call x1 -> x0, local copies, waits for them, and re-layouts: 1.63 us -> none  [kernel_path(): pl.pallas_call(finish_kernel, out_shape=shape_of(block, out_weight.shape[...]
    ppermute x10, waiting for transfers between devices: 8.09 us -> 9.69 us  [shifted(): lax.ppermute(array, axis, [(i, (i + step) % count) for i in range(count)])]
    ppermute x5, starting transfers between devices: 3.52 us -> 1.97 us  [flipped(): return lax.ppermute(array, axis, [(i, i ^ bit) for i in range(count)])]
  transfers between devices with their start and end apart: 15 -> 15, of which waited for: 8 -> 7; matrix products, arithmetic and copies ran while one was open for 5% -> 4% of each run, Pallas kernels for 16% -> 13%
where the time goes in v3:
time: 52.1 us; the launch traced here: 51.9 us
  waiting for transfers between devices  22.4 us (43%)
  starting transfers between devices  18.1 us (35%)
  Pallas kernels  9.34 us (18%)
  other arithmetic  1.85 us (4%)
    ppermute x10, starting transfers between devices, shifted(): lax.ppermute(array, axis, [(i, (i + step) % count) for i in range(count)])  16.1 us
    ppermute x5, waiting for transfers between devices, flipped(): return lax.ppermute(array, axis, [(i, i ^ bit) for i in range(count)])  12.7 us
    ppermute x10, waiting for transfers between devices, shifted(): lax.ppermute(array, axis, [(i, (i + step) % count) for i in range(count)])  9.69 us
    pallas_call x6, Pallas kernels, call(): pl.pallas_call(kernel, out_shape=[pltpu.VMEM(shape, dtype) for shape, dty...  8.05 us
    ppermute x5, starting transfers between devices, flipped(): return lax.ppermute(array, axis, [(i, i ^ bit) for i in range(count)])  1.97 us
    pallas_call x1, Pallas kernels, kernel_path(): pl.pallas_call(finish_kernel, out_shape=jax.ShapeDtypeStruct((out_weight....  1.29 us
    select_n x1, other arithmetic, kernel_path(): jnp.where(tissue[:, :, None] > 0, features, jnp.asarray(FAR, features.dty...  1.08 us
  transfers between devices with their start and end apart: 15, of which 7 were waited for; matrix products, arithmetic and copies ran while one was open for 4% of the time, Pallas kernels for 13%

profile of v3, /device:TPU:0, one launch (start us, length us, event | category | flops | bytes accessed | tf_op | source)
XLA Modules:
  0.0 51.9 jit_solution(12002291618327194348)
XLA Ops:
  0.0 5.1 %collective-permute-start.4 = (bf16[32,1280]{1,0:T(8,128)(2,1)}, bf16[32,1280]{1,0:T(8,128)(2,1)S(1)}, u32[]{:S(2)}, u32[]{:S(2)}) collective-permute-start(bf16[32,1280]{1,0:T(8,128)(2,1)} %param.18), channel_id=1, source_target_pairs={{0,3},{1,0},{2,1},{3,2},{4,7},{5,4},{6,5},{7,6},{8,11},{9,8},{10,9... | collective-permute-start | bytes 245768 | tf_op jit(solution)/shard_map/ppermute | solution.py:19
  5.2 0.0 collective-permute-start.5
  5.2 1.0 %collective-permute-start.6 = (bf16[32,1280]{1,0:T(8,128)(2,1)}, bf16[32,1280]{1,0:T(8,128)(2,1)S(1)}, u32[]{:S(2)}, u32[]{:S(2)}) collective-permute-start(bf16[32,1280]{1,0:T(8,128)(2,1)} %param.18), channel_id=1, source_target_pairs={{0,1},{1,2},{2,3},{3,0},{4,5},{5,6},{6,7},{7,4},{8,9},{9,10},{10,1... | collective-permute-start | bytes 245768 | tf_op jit(solution)/shard_map/ppermute | solution.py:19
  6.2 0.7 %broadcast_compare_fusion = pred[16,32]{1,0:T(8,128)(4,1)S(1)} fusion(s32[16,32]{1,0:T(8,128)} %param.11), kind=kLoop, calls=%fused_computation.7 | loop fusion | flops 512 | bytes 2560 | tf_op jit(solution)/shard_map/gt | solution.py:403
  6.9 1.1 %broadcast_select_fusion.marked = bf16[16,32,256]{2,1,0:T(8,128)(2,1)S(1)} fusion(bf16[16,32,256]{2,1,0:T(8,128)(2,1)} %param.10, pred[16,32]{1,0:T(8,128)(4,1)S(1)} %broadcast_compare_fusion), kind=kLoop, calls=%fused_computation | loop fusion | flops 131072 | bytes 524800 | tf_op jit(solution)/shard_map/jit(_where)/select_n | solution.py:403
  8.0 2.5 %collective-permute-start = (bf16[2,32,256]{2,1,0:T(8,128)(2,1)S(1)}, bf16[2,32,256]{2,1,0:T(8,128)(2,1)S(1)}, u32[]{:S(2)}, u32[]{:S(2)}) collective-permute-start(bf16[2,32,256]{2,1,0:T(8,128)(2,1)S(1)} %get-tuple-element.28), channel_id=1, source_target_pairs={{0,1},{1,2},{2,3},{3,0},{4,5},{5,6},{6,7},{7,4},{8,9},{9,10},{10,1... | collective-permute-start | bytes 98312 | tf_op jit(solution)/shard_map/ppermute | solution.py:19
  10.5 1.3 %collective-permute-start.1 = (bf16[2,32,256]{2,1,0:T(8,128)(2,1)S(1)}, bf16[2,32,256]{2,1,0:T(8,128)(2,1)S(1)}, u32[]{:S(2)}, u32[]{:S(2)}) collective-permute-start(bf16[2,32,256]{2,1,0:T(8,128)(2,1)S(1)} %get-tuple-element.27), channel_id=1, source_target_pairs={{0,3},{1,0},{2,1},{3,2},{4,7},{5,4},{6,5},{7,6},{8,11},{9,8},{10,9... | collective-permute-start | bytes 98312 | tf_op jit(solution)/shard_map/ppermute | solution.py:19
  11.9 2.5 %collective-permute-done.1.bottom = bf16[2,32,256]{2,1,0:T(8,128)(2,1)S(1)} collective-permute-done((bf16[2,32,256]{2,1,0:T(8,128)(2,1)S(1)}, bf16[2,32,256]{2,1,0:T(8,128)(2,1)S(1)}, u32[]{:S(2)}, u32[]{:S(2)}) %collective-permute-start.1) | collective-permute-done | bytes 32800 | tf_op jit(solution)/shard_map/ppermute | solution.py:19
  14.5 1.6 %collective-permute-start.8 = (bf16[128,1280]{1,0:T(8,128)(2,1)S(1)}, bf16[128,1280]{1,0:T(8,128)(2,1)S(1)}, u32[]{:S(2)}, u32[]{:S(2)}) collective-permute-start(bf16[128,1280]{1,0:T(8,128)(2,1)S(1)} %constant_dynamic-update-slice_fusion.refs_0_), channel_id=1, source_target_pairs={{0,8},{4,12},{8,0},{12,4},{1,9},{5,13},{9,1},{13,5},{2,10},{6,14},... | collective-permute-start | bytes 983048 | tf_op jit(solution)/shard_map/ppermute | solution.py:24
  16.1 0.1 collective-permute-start.7
  16.2 0.5 %collective-permute-start.2 = (bf16[20,2,256]{2,1,0:T(2,128)(2,1)S(1)}, bf16[20,2,256]{2,1,0:T(2,128)(2,1)S(1)}, u32[]{:S(2)}, u32[]{:S(2)}) collective-permute-start(bf16[20,2,256]{2,1,0:T(2,128)(2,1)S(1)} %pad_maximum_fusion), channel_id=1, source_target_pairs={{0,4},{4,8},{8,12},{12,0},{1,5},{5,9},{9,13},{13,1},{2,6},{6,10},{... | collective-permute-start | bytes 61448 | tf_op jit(solution)/shard_map/ppermute | solution.py:19
  16.8 7.3 %collective-permute-done.8.refs_0_ = bf16[128,1280]{1,0:T(8,128)(2,1)S(1)} collective-permute-done((bf16[128,1280]{1,0:T(8,128)(2,1)S(1)}, bf16[128,1280]{1,0:T(8,128)(2,1)S(1)}, u32[]{:S(2)}, u32[]{:S(2)}) %collective-permute-start.8) | collective-permute-done | bytes 327712 | tf_op jit(solution)/shard_map/ppermute | solution.py:24
  24.1 1.7 %collective-permute-start.3 = (bf16[20,2,256]{2,1,0:T(2,128)(2,1)S(1)}, bf16[20,2,256]{2,1,0:T(2,128)(2,1)S(1)}, u32[]{:S(2)}, u32[]{:S(2)}) collective-permute-start(bf16[20,2,256]{2,1,0:T(2,128)(2,1)S(1)} %pad_maximum_fusion.1), channel_id=1, source_target_pairs={{0,12},{4,0},{8,4},{12,8},{1,13},{5,1},{9,5},{13,9},{2,14},{6,2},{... | collective-permute-start | bytes 61448 | tf_op jit(solution)/shard_map/ppermute | solution.py:19
  25.8 1.5 %collective-permute-done.3.right = bf16[20,2,256]{2,1,0:T(2,128)(2,1)S(1)} collective-permute-done((bf16[20,2,256]{2,1,0:T(2,128)(2,1)S(1)}, bf16[20,2,256]{2,1,0:T(2,128)(2,1)S(1)}, u32[]{:S(2)}, u32[]{:S(2)}) %collective-permute-start.3) | collective-permute-done | bytes 20512 | tf_op jit(solution)/shard_map/ppermute | solution.py:19
  27.2 5.1 %shard_map.100 = (bf16[512,256]{1,0:T(8,128)(2,1)S(1)}, bf16[512,1280]{1,0:T(8,128)(2,1)S(1)}) custom-call(bf16[16,32,256]{2,1,0:T(8,128)(2,1)S(1)} %broadcast_select_fusion.marked, bf16[2,32,256]{2,1,0:T(8,128)(2,1)S(1)} %collective-permute-done.top, bf16[2,32,256]{2,1,0:T(8,128)(2,1)S(1)} %collective-permute-done.1.bottom, ...), custom_call_target="tpu_custom_call" | custom-call | flops 1744830464 | tf_op jit(solution)/shard_map/pallas_call | solution.py:370
  32.4 0.9 %shard_map.102.far = f32[1,264,128]{2,1,0:T(8,128)S(1)} custom-call(bf16[512,256]{1,0:T(8,128)(2,1)S(1)} %get-tuple-element.15.cells.rest_0_, bf16[512,1280]{1,0:T(8,128)(2,1)S(1)} %get-tuple-element.16.keys.rest_1_, bf16[512,256]{1,0:T(8,128)(2,1)S(1)} %bitcast.7, bf16[128,1280]{1,0:T(8,128)(2,1)S(1)} %collective-permute-done.8.refs_0_), custom_call_target="tpu_custom_call" | custom-call | flops 201326592 | tf_op jit(solution)/shard_map/pallas_call | solution.py:370
  33.2 0.0 collective-permute-done.7.refs_1_
  33.2 0.9 %shard_map.101.near = f32[2,264,128]{2,1,0:T(8,128)S(1)} custom-call(bf16[512,256]{1,0:T(8,128)(2,1)S(1)} %get-tuple-element.15.cells.rest_0_, bf16[512,1280]{1,0:T(8,128)(2,1)S(1)} %get-tuple-element.16.keys.rest_1_, bf16[512,256]{1,0:T(8,128)(2,1)S(1)} %bitcast.8, bf16[128,1280]{1,0:T(8,128)(2,1)S(1)} %constant_dynamic-update-slice_fusion.refs_0_, ...), custom_call_target="tpu_custom_call" | custom-call | flops 402653184 | tf_op jit(solution)/shard_map/pallas_call | solution.py:370
  34.2 0.0 copy-start
  34.2 0.0 copy-start.1
  34.2 1.0 %shard_map.103 = (f32[264,128]{1,0:T(8,128)S(1)}, bf16[272,128]{1,0:T(8,128)(2,1)S(1)}, bf16[272,128]{1,0:T(8,128)(2,1)S(1)}, bf16[272,128]{1,0:T(8,128)(2,1)S(1)}) custom-call(f32[2,264,128]{2,1,0:T(8,128)S(1)} %shard_map.101.near, f32[1,264,128]{2,1,0:T(8,128)S(1)} %shard_map.102.far, bf16[512,256]{1,0:T(8,128)(2,1)S(1)} %get-tuple-element.15.cells.rest_0_, ...), custom_call_target="tpu_custom_call" | custom-call | flops 201326592 | tf_op jit(solution)/shard_map/pallas_call | solution.py:370
  35.3 0.6 %collective-permute-start.10 = (bf16[272,128]{1,0:T(8,128)(2,1)S(1)}, bf16[272,128]{1,0:T(8,128)(2,1)S(1)}, u32[]{:S(2)}, u32[]{:S(2)}) collective-permute-start(bf16[272,128]{1,0:T(8,128)(2,1)S(1)} %get-tuple-element.18), channel_id=1, source_target_pairs={{0,1},{1,2},{2,3},{3,0},{4,5},{5,6},{6,7},{7,4},{8,9},{9,10},{10,1... | collective-permute-start | bytes 208904 | tf_op jit(solution)/shard_map/ppermute | solution.py:19
  35.9 1.5 %collective-permute-start.11 = (bf16[272,128]{1,0:T(8,128)(2,1)S(1)}, bf16[272,128]{1,0:T(8,128)(2,1)S(1)}, u32[]{:S(2)}, u32[]{:S(2)}) collective-permute-start(bf16[272,128]{1,0:T(8,128)(2,1)S(1)} %get-tuple-element.19), channel_id=1, source_target_pairs={{0,2},{1,3},{2,0},{3,1},{4,6},{5,7},{6,4},{7,5},{8,10},{9,11},{10,... | collective-permute-start | bytes 208904 | tf_op jit(solution)/shard_map/ppermute | solution.py:19
  37.3 1.8 %collective-permute-start.12 = (bf16[272,128]{1,0:T(8,128)(2,1)S(1)}, bf16[272,128]{1,0:T(8,128)(2,1)S(1)}, u32[]{:S(2)}, u32[]{:S(2)}) collective-permute-start(bf16[272,128]{1,0:T(8,128)(2,1)S(1)} %get-tuple-element.20), channel_id=1, source_target_pairs={{0,3},{1,0},{2,1},{3,2},{4,7},{5,4},{6,5},{7,6},{8,11},{9,8},{10,9... | collective-permute-start | bytes 208904 | tf_op jit(solution)/shard_map/ppermute | solution.py:19
  39.1 3.1 %collective-permute-done.10.refs_0_ = bf16[272,128]{1,0:T(8,128)(2,1)S(1)} collective-permute-done((bf16[272,128]{1,0:T(8,128)(2,1)S(1)}, bf16[272,128]{1,0:T(8,128)(2,1)S(1)}, u32[]{:S(2)}, u32[]{:S(2)}) %collective-permute-start.10) | collective-permute-done | bytes 69664 | tf_op jit(solution)/shard_map/ppermute | solution.py:19
  42.3 2.5 %collective-permute-done.11.refs_1_ = bf16[272,128]{1,0:T(8,128)(2,1)S(1)} collective-permute-done((bf16[272,128]{1,0:T(8,128)(2,1)S(1)}, bf16[272,128]{1,0:T(8,128)(2,1)S(1)}, u32[]{:S(2)}, u32[]{:S(2)}) %collective-permute-start.11) | collective-permute-done | bytes 69664 | tf_op jit(solution)/shard_map/ppermute | solution.py:19
  44.8 0.1 shard_map.104
  44.9 0.3 collective-permute-start.13
  45.2 4.1 %collective-permute-done.13.refs_0_ = bf16[272,128]{1,0:T(8,128)(2,1)S(1)} collective-permute-done((bf16[272,128]{1,0:T(8,128)(2,1)S(1)}, bf16[272,128]{1,0:T(8,128)(2,1)S(1)}, u32[]{:S(2)}, u32[]{:S(2)}) %collective-permute-start.13) | collective-permute-done | bytes 69664 | tf_op jit(solution)/shard_map/ppermute | solution.py:24
  49.3 0.1 collective-permute-start.14
  49.4 1.2 %collective-permute-done.14.arrived = bf16[272,128]{1,0:T(8,128)(2,1)S(1)} collective-permute-done((bf16[272,128]{1,0:T(8,128)(2,1)S(1)}, bf16[272,128]{1,0:T(8,128)(2,1)S(1)}, u32[]{:S(2)}, u32[]{:S(2)}) %collective-permute-start.14) | collective-permute-done | bytes 69664 | tf_op jit(solution)/shard_map/ppermute | solution.py:24
  50.6 1.3 %finish.1 = bf16[320,128]{1,0:T(8,128)(2,1)} custom-call(f32[264,128]{1,0:T(8,128)S(1)} %get-tuple-element.23.own, bf16[272,128]{1,0:T(8,128)(2,1)S(1)} %collective-permute-done.14.arrived, bf16[256,1280]{1,0:T(8,128)(2,1)S(1)} %copy-done.1, bf16[320,1280]{1,0:T(8,128)(2,1)S(1)} %bitcast.10), custom_call_target="tpu_custom_call" | custom-call | tf_op jit(solution)/shard_map/finish/pallas_call | solution.py:463
  (29 shorter events, 0.2 us)
Async XLA Ops:
  0.0 14.5 %copy-start.5 = (bf16[32,1280]{1,0:T(8,128)(2,1)S(1)}, bf16[32,1280]{1,0:T(8,128)(2,1)}, u32[]{:S(2)}) copy-start(bf16[32,1280]{1,0:T(8,128)(2,1)} %param.18) | copy-start | bytes 245764
  0.0 27.2 %copy-start.2 = (bf16[3,3,256,256]{3,2,1,0:T(8,128)(2,1)S(1)}, bf16[3,3,256,256]{3,2,1,0:T(8,128)(2,1)}, u32[]{:S(2)}) copy-start(bf16[3,3,256,256]{3,2,1,0:T(8,128)(2,1)} %param.12) | copy-start | bytes 3538948
  0.0 27.2 %copy-start.3 = (f32[256]{0:T(256)S(1)}, f32[256]{0:T(256)}, u32[]{:S(2)}) copy-start(f32[256]{0:T(256)} %param.13) | copy-start | bytes 3076
  0.0 27.2 %copy-start.4 = (f32[256]{0:T(256)S(1)}, f32[256]{0:T(256)}, u32[]{:S(2)}) copy-start(f32[256]{0:T(256)} %param.15) | copy-start | bytes 3076
  0.0 14.4 %collective-permute-start.4 = (bf16[32,1280]{1,0:T(8,128)(2,1)}, bf16[32,1280]{1,0:T(8,128)(2,1)S(1)}, u32[]{:S(2)}, u32[]{:S(2)}) collective-permute-start(bf16[32,1280]{1,0:T(8,128)(2,1)} %param.18), channel_id=1, source_target_pairs={{0,3},{1,0},{2,1},{3,2},{4,7},{5,4},{6,5},{7,6},{8,11},{9,8},{10,9... | collective-permute-start | bytes 245768 | tf_op jit(solution)/shard_map/ppermute | solution.py:19
  5.2 9.3 %collective-permute-start.5 = (bf16[32,1280]{1,0:T(8,128)(2,1)}, bf16[32,1280]{1,0:T(8,128)(2,1)S(1)}, u32[]{:S(2)}, u32[]{:S(2)}) collective-permute-start(bf16[32,1280]{1,0:T(8,128)(2,1)} %param.18), channel_id=1, source_target_pairs={{0,2},{1,3},{2,0},{3,1},{4,6},{5,7},{6,4},{7,5},{8,10},{9,11},{10,... | collective-permute-start | bytes 245768 | tf_op jit(solution)/shard_map/ppermute | solution.py:19
  5.2 9.3 %collective-permute-start.6 = (bf16[32,1280]{1,0:T(8,128)(2,1)}, bf16[32,1280]{1,0:T(8,128)(2,1)S(1)}, u32[]{:S(2)}, u32[]{:S(2)}) collective-permute-start(bf16[32,1280]{1,0:T(8,128)(2,1)} %param.18), channel_id=1, source_target_pairs={{0,1},{1,2},{2,3},{3,0},{4,5},{5,6},{6,7},{7,4},{8,9},{9,10},{10,1... | collective-permute-start | bytes 245768 | tf_op jit(solution)/shard_map/ppermute | solution.py:19
  8.0 8.1 %collective-permute-start = (bf16[2,32,256]{2,1,0:T(8,128)(2,1)S(1)}, bf16[2,32,256]{2,1,0:T(8,128)(2,1)S(1)}, u32[]{:S(2)}, u32[]{:S(2)}) collective-permute-start(bf16[2,32,256]{2,1,0:T(8,128)(2,1)S(1)} %get-tuple-element.28), channel_id=1, source_target_pairs={{0,1},{1,2},{2,3},{3,0},{4,5},{5,6},{6,7},{7,4},{8,9},{9,10},{10,1... | collective-permute-start | bytes 98312 | tf_op jit(solution)/shard_map/ppermute | solution.py:19
  10.5 3.9 %collective-permute-start.1 = (bf16[2,32,256]{2,1,0:T(8,128)(2,1)S(1)}, bf16[2,32,256]{2,1,0:T(8,128)(2,1)S(1)}, u32[]{:S(2)}, u32[]{:S(2)}) collective-permute-start(bf16[2,32,256]{2,1,0:T(8,128)(2,1)S(1)} %get-tuple-element.27), channel_id=1, source_target_pairs={{0,3},{1,0},{2,1},{3,2},{4,7},{5,4},{6,5},{7,6},{8,11},{9,8},{10,9... | collective-permute-start | bytes 98312 | tf_op jit(solution)/shard_map/ppermute | solution.py:19
  14.5 9.5 %collective-permute-start.8 = (bf16[128,1280]{1,0:T(8,128)(2,1)S(1)}, bf16[128,1280]{1,0:T(8,128)(2,1)S(1)}, u32[]{:S(2)}, u32[]{:S(2)}) collective-permute-start(bf16[128,1280]{1,0:T(8,128)(2,1)S(1)} %constant_dynamic-update-slice_fusion.refs_0_), channel_id=1, source_target_pairs={{0,8},{4,12},{8,0},{12,4},{1,9},{5,13},{9,1},{13,5},{2,10},{6,14},... | collective-permute-start | bytes 983048 | tf_op jit(solution)/shard_map/ppermute | solution.py:24
  16.1 17.1 %collective-permute-start.7 = (bf16[128,1280]{1,0:T(8,128)(2,1)S(1)}, bf16[128,1280]{1,0:T(8,128)(2,1)S(1)}, u32[]{:S(2)}, u32[]{:S(2)}) collective-permute-start(bf16[128,1280]{1,0:T(8,128)(2,1)S(1)} %constant_dynamic-update-slice_fusion.refs_0_), channel_id=1, source_target_pairs={{0,4},{4,0},{8,12},{12,8},{1,5},{5,1},{9,13},{13,9},{2,6},{6,2},{1... | collective-permute-start | bytes 983048 | tf_op jit(solution)/shard_map/ppermute | solution.py:24
  16.2 9.5 %collective-permute-start.2 = (bf16[20,2,256]{2,1,0:T(2,128)(2,1)S(1)}, bf16[20,2,256]{2,1,0:T(2,128)(2,1)S(1)}, u32[]{:S(2)}, u32[]{:S(2)}) collective-permute-start(bf16[20,2,256]{2,1,0:T(2,128)(2,1)S(1)} %pad_maximum_fusion), channel_id=1, source_target_pairs={{0,4},{4,8},{8,12},{12,0},{1,5},{5,9},{9,13},{13,1},{2,6},{6,10},{... | collective-permute-start | bytes 61448 | tf_op jit(solution)/shard_map/ppermute | solution.py:19
  24.1 10.2 %collective-permute-start.9 = (bf16[128,1280]{1,0:T(8,128)(2,1)S(1)}, bf16[128,1280]{1,0:T(8,128)(2,1)S(1)}, u32[]{:S(2)}, u32[]{:S(2)}) collective-permute-start(bf16[128,1280]{1,0:T(8,128)(2,1)S(1)} %collective-permute-done.8.refs_0_), channel_id=1, source_target_pairs={{0,4},{4,0},{8,12},{12,8},{1,5},{5,1},{9,13},{13,9},{2,6},{6,2},{1... | collective-permute-start | bytes 983048 | tf_op jit(solution)/shard_map/ppermute | solution.py:24
  24.1 3.1 %collective-permute-start.3 = (bf16[20,2,256]{2,1,0:T(2,128)(2,1)S(1)}, bf16[20,2,256]{2,1,0:T(2,128)(2,1)S(1)}, u32[]{:S(2)}, u32[]{:S(2)}) collective-permute-start(bf16[20,2,256]{2,1,0:T(2,128)(2,1)S(1)} %pad_maximum_fusion.1), channel_id=1, source_target_pairs={{0,12},{4,0},{8,4},{12,8},{1,13},{5,1},{9,5},{13,9},{2,14},{6,2},{... | collective-permute-start | bytes 61448 | tf_op jit(solution)/shard_map/ppermute | solution.py:19
  34.2 16.4 %copy-start = (bf16[1280,320]{0,1:T(8,128)(2,1)S(1)}, bf16[1280,320]{0,1:T(8,128)(2,1)}, u32[]{:S(2)}) copy-start(bf16[1280,320]{0,1:T(8,128)(2,1)} %param.19) | copy-start | bytes 2457604
  34.2 16.4 %copy-start.1 = (bf16[256,1280]{1,0:T(8,128)(2,1)S(1)}, bf16[256,1280]{1,0:T(8,128)(2,1)}, u32[]{:S(2)}) copy-start(bf16[256,1280]{1,0:T(8,128)(2,1)} %value_weight.1) | copy-start | bytes 1966084
  35.3 7.0 %collective-permute-start.10 = (bf16[272,128]{1,0:T(8,128)(2,1)S(1)}, bf16[272,128]{1,0:T(8,128)(2,1)S(1)}, u32[]{:S(2)}, u32[]{:S(2)}) collective-permute-start(bf16[272,128]{1,0:T(8,128)(2,1)S(1)} %get-tuple-element.18), channel_id=1, source_target_pairs={{0,1},{1,2},{2,3},{3,0},{4,5},{5,6},{6,7},{7,4},{8,9},{9,10},{10,1... | collective-permute-start | bytes 208904 | tf_op jit(solution)/shard_map/ppermute | solution.py:19
  35.9 8.9 %collective-permute-start.11 = (bf16[272,128]{1,0:T(8,128)(2,1)S(1)}, bf16[272,128]{1,0:T(8,128)(2,1)S(1)}, u32[]{:S(2)}, u32[]{:S(2)}) collective-permute-start(bf16[272,128]{1,0:T(8,128)(2,1)S(1)} %get-tuple-element.19), channel_id=1, source_target_pairs={{0,2},{1,3},{2,0},{3,1},{4,6},{5,7},{6,4},{7,5},{8,10},{9,11},{10,... | collective-permute-start | bytes 208904 | tf_op jit(solution)/shard_map/ppermute | solution.py:19
  37.3 7.5 %collective-permute-start.12 = (bf16[272,128]{1,0:T(8,128)(2,1)S(1)}, bf16[272,128]{1,0:T(8,128)(2,1)S(1)}, u32[]{:S(2)}, u32[]{:S(2)}) collective-permute-start(bf16[272,128]{1,0:T(8,128)(2,1)S(1)} %get-tuple-element.20), channel_id=1, source_target_pairs={{0,3},{1,0},{2,1},{3,2},{4,7},{5,4},{6,5},{7,6},{8,11},{9,8},{10,9... | collective-permute-start | bytes 208904 | tf_op jit(solution)/shard_map/ppermute | solution.py:19
  44.9 4.4 %collective-permute-start.13 = (bf16[272,128]{1,0:T(8,128)(2,1)S(1)}, bf16[272,128]{1,0:T(8,128)(2,1)S(1)}, u32[]{:S(2)}, u32[]{:S(2)}) collective-permute-start(bf16[272,128]{1,0:T(8,128)(2,1)S(1)} %get-tuple-element.22), channel_id=1, source_target_pairs={{0,8},{4,12},{8,0},{12,4},{1,9},{5,13},{9,1},{13,5},{2,10},{6,14},... | collective-permute-start | bytes 208904 | tf_op jit(solution)/shard_map/ppermute | solution.py:24
  49.3 1.3 %collective-permute-start.14 = (bf16[272,128]{1,0:T(8,128)(2,1)S(1)}, bf16[272,128]{1,0:T(8,128)(2,1)S(1)}, u32[]{:S(2)}, u32[]{:S(2)}) collective-permute-start(bf16[272,128]{1,0:T(8,128)(2,1)S(1)} %get-tuple-element.24), channel_id=1, source_target_pairs={{0,4},{4,0},{8,12},{12,8},{1,5},{5,1},{9,13},{13,9},{2,6},{6,2},{1... | collective-permute-start | bytes 208904 | tf_op jit(solution)/shard_map/ppermute | solution.py:24

commit v4 on v3

--- a/solution.py
+++ b/solution.py
@@ -165,22 +165,57 @@
     return 0.5 * value * (1.0 + lax.erf(value * math.sqrt(0.5)))
 
 
+def mark_kernel(features, tissue, queries, out, queries_out, features_held, tissue_held, done):
+    copies = [
+        pltpu.make_async_copy(tissue, tissue_held, done.at[0]),
+        pltpu.make_async_copy(features, features_held, done.at[1]),
+        pltpu.make_async_copy(queries, queries_out, done.at[2]),
+    ]
+    for copy in copies:
+        copy.start()
+    height, breadth, channels = features.shape
+    copies[0].wait()
+    line = lax.broadcasted_iota(jnp.int32, (breadth, breadth), 0)
+    place = lax.broadcasted_iota(jnp.int32, (breadth, breadth), 1)
+    flags = tissue_held[...].astype(jnp.float32)
+    spread = [
+        jnp.where(line == place, jnp.broadcast_to(flags[k : k + 1], line.shape), 0.0)
+        for k in range(height)
+    ]
+    keep = jnp.dot(
+        jnp.concatenate(spread, axis=0).astype(jnp.bfloat16),
+        jnp.ones((breadth, channels), jnp.bfloat16),
+        preferred_element_type=jnp.float32,
+    )
+    copies[1].wait()
+    for k in range(height):
+        out[k] = jnp.where(
+            keep[k * breadth : (k + 1) * breadth] > 0.0, features_held[k].astype(jnp.float32), FAR
+        ).astype(jnp.bfloat16)
+    copies[2].wait()
+
+
+def halve_kernel(own, other, out):
+    half = own.shape[0] // 2
+    core = lax.rem(lax.axis_index("col"), 2)
+    start = pl.multiple_of(core * half, half)
+    out[pl.ds(start, half), :] = own[pl.ds(start, half), :]
+    out[pl.ds(pl.multiple_of((1 - core) * half, half), half), :] = other[pl.ds(start, half), :]
+
+
 def conv_kernel(
-    marked, top, bottom, left, right, first, bias_first, second, bias_second, key_weight,
-    out, keys, cells, mid, taps, second_held, key_held, done,
+    marked, top, bottom, paired, crossed, first, bias_first, second, bias_second,
+    out, sent, cells, mid, taps, second_held, done,
 ):
-    later = [
-        pltpu.make_async_copy(second, second_held, done.at[0]),
-        pltpu.make_async_copy(key_weight, key_held, done.at[1]),
-    ]
-    for copy in later:
-        copy.start()
+    later = pltpu.make_async_copy(second, second_held, done)
+    later.start()
     height, breadth, channels = marked.shape
     slot = (cells.shape[0] - 2 * EDGE - LEAD) // (height + 2 * HALO)
     flat = cells.shape[0] - 2 * EDGE
     row, col = lax.axis_index("row"), lax.axis_index("col")
     first_row, last_row = row == 0, row == lax.axis_size("row") - 1
     first_col, last_col = col == 0, col == lax.axis_size("col") - 1
+    even = lax.rem(col, 2) == 0
 
     def put(line, place, values, outside):
         start = EDGE + LEAD + line * slot + place
@@ -201,8 +236,9 @@
             beyond_left, beyond_right = first_col | first_row, last_col | first_row
         if line >= height + HALO:
             beyond_left, beyond_right = first_col | last_row, last_col | last_row
-        put(line, -HALO, left[line], beyond_left)
-        put(line, breadth, right[line], beyond_right)
+        one, two = paired[line].astype(jnp.float32), crossed[line].astype(jnp.float32)
+        put(line, -HALO, jnp.where(even, two, one), beyond_left)
+        put(line, breadth, jnp.where(even, one, two), beyond_right)
 
     for shift in range(3):
         values = cells[EDGE - 1 + shift : EDGE - 1 + shift + flat, :]
@@ -228,7 +264,7 @@
             EDGE - 1 + shift : EDGE - 1 + shift + count, :
         ].astype(jnp.bfloat16)
     inner = height * slot
-    later[0].wait()
+    later.wait()
     summed = jnp.dot(
         taps[LEAD : LEAD + inner, :], second_held[0], preferred_element_type=jnp.float32
     )
@@ -239,9 +275,13 @@
         )
     summed = summed.reshape(height, slot, channels)[:, :breadth].reshape(height * breadth, channels)
     alive = marked[...].reshape(height * breadth, channels) < FAR
-    out[...] = jnp.where(alive, gelu(summed + bias_second[...]), 0.0).astype(jnp.bfloat16)
-    later[1].wait()
-    keys[...] = jnp.dot(out[...], key_held[...], preferred_element_type=jnp.float32).astype(
+    value = gelu(summed + bias_second[...])
+    out[...] = jnp.where(alive, value, 0.0).astype(jnp.bfloat16)
+    sent[...] = jnp.where(alive, value, FAR).astype(jnp.bfloat16)
+
+
+def key_kernel(cells, weight, keys):
+    keys[...] = jnp.dot(cells[...], weight[...], preferred_element_type=jnp.float32).astype(
         jnp.bfloat16
     )
 
@@ -285,61 +325,72 @@
     )
 
 
-def score_blocks(cells, keys, marked, queries, scale):
-    scores = lax.dot_general(
-        keys[...], queries, (((1,), (1,)), ((), ())), preferred_element_type=jnp.float32
-    )
-    alive = marked[...] < FAR
-    if alive.shape != scores.shape:
-        alive = jnp.broadcast_to(alive[:, :1], scores.shape)
-    scores = jnp.where(alive, scores * scale, -1e30)
-    top = jnp.max(scores, axis=0, keepdims=True)
-    chosen = jnp.exp(scores - top)
-    total = jnp.sum(chosen, axis=0, keepdims=True)
-    pooled = lax.dot_general(
-        cells[...], chosen.astype(jnp.bfloat16), (((0,), (0,)), ((), ())),
-        preferred_element_type=jnp.float32,
-    )
-    return pooled, top, total
-
-
-def score_kernel(cells, keys, marked, *refs):
-    *queries, out, held = refs
-    size = queries[0].shape[0]
-    for place, part in enumerate(queries):
-        held[place * size : (place + 1) * size, :] = part[...]
-    pooled, top, total = score_blocks(
-        cells, keys, marked, held[...], 1.0 / math.sqrt(held.shape[1])
-    )
-    for place in range(len(queries)):
-        cut = slice(place * size, (place + 1) * size)
-        write_whole(out.at[place], pooled[:, cut], top[:, cut], total[:, cut])
-
-
-def last_score_kernel(rows, size, held, cells, keys, marked, queries, *refs):
-    own, *sends, blocks = refs
-    done = 0
-    for part in held:
-        blocks[done : done + part.shape[0]] = part[...]
-        done += part.shape[0]
-    pooled, top, total = score_blocks(
-        cells, keys, marked, queries[...], 1.0 / math.sqrt(queries.shape[1])
-    )
-    write_whole(blocks.at[done], pooled, top, total)
-    row, col = lax.axis_index("row"), lax.axis_index("col")
-    for step in range(rows):
-        block = blocks[lax.rem(row + step, rows) ^ col]
-        block = pltpu.roll(block, lax.rem(row + 1, rows) * size, 1)
-        channels = block.shape[0] - 8
-        if step == 0:
-            own[...] = block
-        else:
-            write_parts(
-                sends[step - 1],
-                block[:channels],
-                block[channels : channels + 1],
-                block[channels + 1 : channels + 2],
-            )
+def score_blocks(held, queries, sides):
+    half = queries.shape[0] // 8
+    row = lax.axis_index("row")
+    for place in range(4):
+        for parity in range(2):
+            source = (2 * place + parity) * half
+            target = pl.multiple_of(parity * 4 * half + (row ^ place) * half, half)
+            held[pl.ds(target, half), :] = queries[source : source + half, :]
+    scale = 1.0 / math.sqrt(held.shape[1])
+    scores = []
+    for _, marked, keys in sides:
+        raw = lax.dot_general(
+            keys[...], held[...], (((1,), (1,)), ((), ())), preferred_element_type=jnp.float32
+        )
+        alive = marked[:, : raw.shape[1]] < FAR
+        scores.append(jnp.where(alive, raw * scale, -1e30))
+    top = jnp.maximum(*[jnp.max(part, axis=0, keepdims=True) for part in scores])
+    pooled = total = 0.0
+    for part, (cells, _, _) in zip(scores, sides):
+        chosen = jnp.exp(part - top)
+        total = total + jnp.sum(chosen, axis=0, keepdims=True)
+        pooled = pooled + lax.dot_general(
+            cells[...], chosen.astype(jnp.bfloat16), (((0,), (0,)), ((), ())),
+            preferred_element_type=jnp.float32,
+        )
+    channels, lanes = pooled.shape[0] // 2, pooled.shape[1]
+    turn = lambda array: pltpu.roll(array, lanes // 2, 1)
+    lower = lambda rows: lax.broadcasted_iota(jnp.int32, (rows, lanes), 1) < lanes // 2
+    tall, flat = lower(channels), lower(1)
+    turned, turned_top, turned_total = turn(pooled), turn(top), turn(total)
+    return (
+        (
+            jnp.where(tall, pooled[:channels], turned[channels:]),
+            jnp.where(flat, top, turned_top),
+            jnp.where(flat, total, turned_total),
+        ),
+        (
+            jnp.where(tall, turned[:channels], pooled[channels:]),
+            jnp.where(flat, turned_top, top),
+            jnp.where(flat, turned_total, total),
+        ),
+    )
+
+
+def near_kernel(own, own_sent, own_keys, other_sent, weight, queries, out, other, keys, held):
+    values = other_sent[...].astype(jnp.float32)
+    other[...] = jnp.where(values < FAR, values, 0.0).astype(jnp.bfloat16)
+    key_kernel(other, weight, keys)
+    sides = ((own, own_sent, own_keys), (other, other_sent, keys))
+    for parity, block in enumerate(score_blocks(held, queries, sides)):
+        write_whole(out.at[parity], *block)
+
+
+def far_kernel(
+    near, own, own_sent, own_keys, other, other_sent, other_keys, queries,
+    kept, send_1, send_2, send_3, held, blocks,
+):
+    row, across = lax.axis_index("row"), lax.axis_index("col") // 2
+    sides = ((own, own_sent, own_keys), (other, other_sent, other_keys))
+    for parity in range(2):
+        blocks[2 * across + parity] = near[parity]
+    for parity, block in enumerate(score_blocks(held, queries, sides)):
+        write_whole(blocks.at[2 * (1 - across) + parity], *block)
+    kept[...] = blocks[row]
+    for step, send in ((1, send_1), (2, send_2), (3, send_3)):
+        write_parts(send, *read_whole(blocks.at[row ^ step]))
 
 
 def merge_kernel(own, *refs):
@@ -349,15 +400,37 @@
     write_parts(packed_out, values, top, total)
 
 
-def finish_kernel(own, arrived, value_weight, out_weight, out):
+def normalize_kernel(own, arrived, out):
     values, _, total = merged([read_whole(own), read_parts(arrived)])
-    normalized = (values / total).astype(jnp.bfloat16)
-    attended = lax.dot_general(
+    out[...] = (values / total).astype(jnp.bfloat16)
+
+
+def finish_kernel(own, arrived, value_weight, out_weight, out, attended):
+    lanes = own.shape[1]
+    half = lanes // 2
+    first_core = lax.rem(lax.axis_index("col"), 2) == 0
+    mine, other = own[...].astype(jnp.float32), arrived[...].astype(jnp.float32)
+    even, odd = jnp.where(first_core, mine, other), jnp.where(first_core, other, mine)
+    lower = lax.broadcasted_iota(jnp.int32, mine.shape, 1) < half
+    normalized = jnp.concatenate(
+        [
+            jnp.where(lower, even, pltpu.roll(odd, half, 1)),
+            jnp.where(lower, pltpu.roll(even, half, 1), odd),
+        ],
+        axis=0,
+    ).astype(jnp.bfloat16)
+    product = lax.dot_general(
         normalized, value_weight[...], (((0,), (0,)), ((), ())),
         preferred_element_type=jnp.float32,
     ).astype(jnp.bfloat16)
+    piece = half // 4
+    for core in range(2):
+        for place in range(4):
+            source, target = core * half + place * piece, (2 * place + core) * piece
+            attended[target : target + piece, :] = product[source : source + piece]
     out[...] = lax.dot_general(
-        out_weight[...], attended, (((1,), (1,)), ((), ())), preferred_element_type=jnp.float32
+        out_weight[...], attended[...], (((1,), (1,)), ((), ())),
+        preferred_element_type=jnp.float32,
     ).astype(out.dtype)
 
 
@@ -390,74 +463,76 @@
     value_weight, latent_queries, out_weight,
 ):
     height, breadth, channels = features.shape
-    rows, cols = lax.axis_size("row"), lax.axis_size("col")
-    width = latent_queries.shape[1]
+    col, cols = lax.axis_index("col"), lax.axis_size("col")
+    size, width = latent_queries.shape
     cells = height * breadth
     slot = -(-(breadth + 2 * HALO) // 16) * 16
     flat = LEAD + (height + 2 * HALO) * slot
     wide, half = jnp.float32, jnp.bfloat16
-    block = rows * latent_queries.shape[0]
-    whole_block, sent_block = (channels + 8, block), (channels + 16, block)
-
-    turned = [shifted(latent_queries, "row", k) for k in range(1, rows)]
-    marked = jnp.where(tissue[:, :, None] > 0, features, jnp.asarray(FAR, features.dtype))
+    block = 4 * size
+    whole_block, sent_block = (channels // 2 + 8, block), (channels // 2 + 16, block)
+    score_flops = 4 * cells * block * (width + channels)
+
+    beside = flipped(latent_queries, "col", 1)
+    marked, queries = call(
+        mark_kernel, [(features.shape, half), ((size, width), half)],
+        [features, tissue, latent_queries],
+        [(features.shape, half), (tissue.shape, jnp.int32), pltpu.SemaphoreType.DMA((3,))],
+        far=(0, 1, 2), flops=1 << 20,
+    )
+    (queries,) = call(halve_kernel, [((size, width), half)], [queries, beside])
+    turned = [flipped(queries, "row", k) for k in range(1, 4)]
     top = shifted(marked[height - HALO :], "row", 1)
     bottom = shifted(marked[:HALO], "row", -1)
     edge = lambda cut: jnp.concatenate([top[:, cut], marked[:, cut], bottom[:, cut]], axis=0)
-    left = shifted(edge(slice(breadth - HALO, breadth)), "col", 1)
-    right = shifted(edge(slice(0, HALO)), "col", -1)
-
-    own_column = jnp.concatenate(turned[::-1] + [latent_queries], axis=0)
-    across = flipped(own_column, "col", 2)
-    beside = flipped(own_column, "col", 1)
-    diagonal = flipped(across, "col", 1)
-
-    second, keys = call(
-        conv_kernel, [((cells, channels), half), ((cells, width), half)],
+    even = lax.rem(col, 2) == 0
+    ends = edge(slice(breadth - HALO, breadth)), edge(slice(0, HALO))
+    paired = flipped(jnp.where(even, *ends), "col", 1)
+    rounds = [(k, (k + 1 if k % 2 else k - 1) % cols) for k in range(cols)]
+    crossed = lax.ppermute(jnp.where(even, *ends[::-1]), "col", rounds)
+
+    near_queries = jnp.concatenate([queries] + turned, axis=0)
+    far_queries = flipped(near_queries, "col", 2)
+
+    own, own_sent = call(
+        conv_kernel, [((cells, channels), half)] * 2,
         [
-            marked, top, bottom, left, right,
+            marked, top, bottom, paired, crossed,
             conv_first.reshape(3, 3 * channels, channels), bias_first.reshape(1, channels),
             conv_second.reshape(3, 3 * channels, channels), bias_second.reshape(1, channels),
-            key_weight,
         ],
         [
             ((flat + 2 * EDGE, channels), wide),
             ((flat - 2 * slot + 2 * EDGE, channels), wide),
             ((flat, 3 * channels), half),
             ((3, 3 * channels, channels), half),
-            ((channels, width), half),
-            pltpu.SemaphoreType.DMA((2,)),
+            pltpu.SemaphoreType.DMA,
         ],
-        limit=16, far=(7, 9), flops=2 * cells * channels * (21 * channels + width),
-    )
-    marked = marked.reshape(cells, channels)
-
-    def score(*queries):
-        return call(
-            score_kernel, [((len(queries),) + whole_block, wide)],
-            [second, keys, marked, *queries],
-            [((len(queries) * block, width), half)],
-            limit=8, flops=2 * cells * block * len(queries) * (width + channels),
-        )[0]
-
-    near = score(own_column, beside)
-    far = score(across)
-
-    def last(near, far, *rest):
-        last_score_kernel(rows, latent_queries.shape[0], (near, far), *rest)
-
-    own, *sends = call(
-        last, [(whole_block, wide)] + [(sent_block, half)] * (rows - 1),
-        [near, far, second, keys, marked, diagonal],
-        [((cols,) + whole_block, wide)],
-        limit=8, flops=2 * cells * block * (width + channels),
-    )
-    arrived = [shifted(part, "row", k + 1) for k, part in enumerate(sends)]
-    merge = lambda *parts: call(merge_kernel, [(whole_block, wide), (sent_block, half)], parts)
-    own, sent = merge(own, *arrived)
+        limit=16, far=(7,), flops=42 * cells * channels * channels,
+    )
+    other_sent = flipped(own_sent, "col", 1)
+    (own_keys,) = call(
+        key_kernel, [((cells, width), half)], [own, key_weight],
+        limit=6, flops=2 * cells * channels * width,
+    )
+    near, other, other_keys = call(
+        near_kernel,
+        [((2,) + whole_block, wide), ((cells, channels), half), ((cells, width), half)],
+        [own, own_sent, own_keys, other_sent, key_weight, near_queries],
+        [((block, width), half)],
+        limit=8, flops=score_flops + 2 * cells * channels * width,
+    )
+    kept, *sends = call(
+        far_kernel, [(whole_block, wide)] + [(sent_block, half)] * 3,
+        [near, own, own_sent, own_keys, other, other_sent, other_keys, far_queries],
+        [((block, width), half), ((4,) + whole_block, wide)],
+        limit=8, flops=score_flops,
+    )
+    arrived = [flipped(part, "row", k + 1) for k, part in enumerate(sends)]
+    kept, sent = call(merge_kernel, [(whole_block, wide), (sent_block, half)], [kept, *arrived])
     arrived = flipped(sent, "col", 2)
-    own, sent = merge(own, arrived)
-    arrived = flipped(sent, "col", 1)
+    (normalized,) = call(normalize_kernel, [((channels // 2, block), half)], [kept, arrived])
+    arrived = flipped(normalized, "col", 1)
     held = pl.BlockSpec(memory_space=pltpu.VMEM)
     keep = lambda array: pltpu.with_memory_space_constraint(array, pltpu.VMEM)
     return pl.pallas_call(
@@ -465,9 +540,10 @@
         out_shape=jax.ShapeDtypeStruct((out_weight.shape[1], block), half),
         in_specs=[held] * 4,
         out_specs=held,
+        scratch_shapes=[pltpu.VMEM((block, width), half)],
         compiler_params=pltpu.CompilerParams(vmem_limit_bytes=6 * MIB),
         name="finish",
-    )(keep(own), keep(arrived), keep(value_weight), keep(out_weight.T)).T
+    )(keep(normalized), keep(arrived), keep(value_weight), keep(out_weight.T)).T
 
 
 def shards(
@@ -475,7 +551,7 @@
     value_weight, latent_queries, out_weight,
 ):
     rows, cols = lax.axis_size("row"), lax.axis_size("col")
-    if rows == cols == 4 and (rows * latent_queries.shape[0]) % 128 == 0:
+    if rows == cols == 4 and rows * latent_queries.shape[0] == 128:
         return kernel_path(
             features, tissue, conv_first, bias_first, conv_second, bias_second, key_weight,
             value_weight, latent_queries, out_weight,

time: 52.1 us -> 50.6 us (0.971)
  local copies, waits for them, and re-layouts: 0.11 us -> 2.69 us
  waiting for transfers between devices: 22.4 us -> 19.9 us
  other arithmetic: 1.85 us -> 0.09 us
  Pallas kernels: 9.34 us -> 10.6 us
  starting transfers between devices: 18.1 us -> 17.1 us
    ppermute x10 -> x2, starting transfers between devices: 16.1 us -> 4.64 us  [shifted(): lax.ppermute(array, axis, [(i, (i + step) % count) for i in range(count)])]
    ppermute x5 -> x12, starting transfers between devices: 1.97 us -> 12.2 us  [flipped(): return lax.ppermute(array, axis, [(i, i ^ bit) for i in range(count)])]
    ppermute x10 -> x2, waiting for transfers between devices: 9.69 us -> 5.66 us  [shifted(): lax.ppermute(array, axis, [(i, (i + step) % count) for i in range(count)])]
    unnamed x15 -> x12, local copies, waits for them, and re-layouts: 0.05 us -> 2.64 us
    ppermute x5 -> x12, waiting for transfers between devices: 12.7 us -> 14.2 us  [flipped(): return lax.ppermute(array, axis, [(i, i ^ bit) for i in range(count)])]
    pallas_call x6 -> x8, Pallas kernels: 8.05 us -> 9.23 us  [call(): pl.pallas_call(kernel, out_shape=[pltpu.VMEM(shape, dtype) for shape, dty...]
    select_n x1, other arithmetic: 1.08 us -> 0.07 us  [kernel_path(): crossed = lax.ppermute(jnp.where(even, *ends[::-1]), 'col', rounds)]
    gt x1 -> x0, other arithmetic: 0.7 us -> none  [kernel_path(): tissue[:, :, None] > 0]
  transfers between devices with their start and end apart: 15 -> 15, of which waited for: 7 -> 8; matrix products, arithmetic and copies ran while one was open for 4% -> 0% of each run, Pallas kernels for 13% -> 16%
where the time goes in v4:
time: 50.6 us; the launch traced here: 50.4 us
  waiting for transfers between devices  19.9 us (39%)
  starting transfers between devices  17.1 us (34%)
  Pallas kernels  10.6 us (21%)
  local copies, waits for them, and re-layouts  2.69 us (5%)
    ppermute x12, waiting for transfers between devices, flipped(): return lax.ppermute(array, axis, [(i, i ^ bit) for i in range(count)])  14.2 us
    ppermute x12, starting transfers between devices, flipped(): return lax.ppermute(array, axis, [(i, i ^ bit) for i in range(count)])  12.2 us
    pallas_call x8, Pallas kernels, call(): pl.pallas_call(kernel, out_shape=[pltpu.VMEM(shape, dtype) for shape, dty...  9.23 us
    ppermute x2, waiting for transfers between devices, shifted(): lax.ppermute(array, axis, [(i, (i + step) % count) for i in range(count)])  5.66 us
    ppermute x2, starting transfers between devices, shifted(): lax.ppermute(array, axis, [(i, (i + step) % count) for i in range(count)])  4.64 us
    unnamed x12, local copies, waits for them, and re-layouts  2.64 us
    pallas_call x1, Pallas kernels, kernel_path(): pl.pallas_call(finish_kernel, out_shape=jax.ShapeDtypeStruct((out_weight....  1.34 us
  transfers between devices with their start and end apart: 15, of which 8 were waited for; matrix products, arithmetic and copies ran while one was open for 0% of the time, Pallas kernels for 16%

profile of v4, /device:TPU:0, one launch (start us, length us, event | category | flops | bytes accessed | tf_op | source)
XLA Modules:
  0.0 50.4 jit_solution(18285197212681325730)
XLA Ops:
  0.0 0.5 collective-permute-start.5
  0.5 1.1 %shard_map.100 = (bf16[16,32,256]{2,1,0:T(8,128)(2,1)S(1)}, bf16[32,1280]{1,0:T(8,128)(2,1)S(1)}) custom-call(bf16[16,32,256]{2,1,0:T(8,128)(2,1)} %features.1, s32[16,32]{1,0:T(8,128)} %tissue.1, bf16[32,1280]{1,0:T(8,128)(2,1)} %queries.1), custom_call_target="tpu_custom_call" | custom-call | flops 1048576 | tf_op jit(solution)/shard_map/pallas_call | solution.py:443
  1.6 4.6 %collective-permute-start.1 = (bf16[2,32,256]{2,1,0:T(8,128)(2,1)S(1)}, bf16[2,32,256]{2,1,0:T(8,128)(2,1)S(1)}, u32[]{:S(2)}, u32[]{:S(2)}) collective-permute-start(bf16[2,32,256]{2,1,0:T(8,128)(2,1)S(1)} %get-tuple-element.33), channel_id=1, source_target_pairs={{0,3},{1,0},{2,1},{3,2},{4,7},{5,4},{6,5},{7,6},{8,11},{9,8},{10,9... | collective-permute-start | bytes 98312 | tf_op jit(solution)/shard_map/ppermute | solution.py:19
  6.3 1.6 %collective-permute-done.1.bottom = bf16[2,32,256]{2,1,0:T(8,128)(2,1)S(1)} collective-permute-done((bf16[2,32,256]{2,1,0:T(8,128)(2,1)S(1)}, bf16[2,32,256]{2,1,0:T(8,128)(2,1)S(1)}, u32[]{:S(2)}, u32[]{:S(2)}) %collective-permute-start.1) | collective-permute-done | bytes 32800 | tf_op jit(solution)/shard_map/ppermute | solution.py:19
  7.9 4.0 %collective-permute-done.top = bf16[2,32,256]{2,1,0:T(8,128)(2,1)S(1)} collective-permute-done((bf16[2,32,256]{2,1,0:T(8,128)(2,1)S(1)}, bf16[2,32,256]{2,1,0:T(8,128)(2,1)S(1)}, u32[]{:S(2)}, u32[]{:S(2)}) %collective-permute-start) | collective-permute-done | bytes 32800 | tf_op jit(solution)/shard_map/ppermute | solution.py:19
  11.9 0.1 broadcast_select_fusion
  12.0 0.2 collective-permute-start.3
  12.2 1.4 %collective-permute-start.2 = (bf16[20,2,256]{2,1,0:T(2,128)(2,1)S(1)}, bf16[20,2,256]{2,1,0:T(2,128)(2,1)S(1)}, u32[]{:S(2)}, u32[]{:S(2)}) collective-permute-start(bf16[20,2,256]{2,1,0:T(2,128)(2,1)S(1)} %get-tuple-element.36), channel_id=1, source_target_pairs={{0,4},{4,0},{8,12},{12,8},{1,5},{5,1},{9,13},{13,9},{2,6},{6,2},{1... | collective-permute-start | bytes 61448 | tf_op jit(solution)/shard_map/ppermute | solution.py:24
  13.7 0.3 collective-permute-start.8
  14.0 4.1 %collective-permute-start.6 = (bf16[32,1280]{1,0:T(8,128)(2,1)S(1)}, bf16[32,1280]{1,0:T(8,128)(2,1)S(1)}, u32[]{:S(2)}, u32[]{:S(2)}) collective-permute-start(bf16[32,1280]{1,0:T(8,128)(2,1)S(1)} %shard_map.103), channel_id=1, source_target_pairs={{0,1},{1,0},{2,3},{3,2},{4,5},{5,4},{6,7},{7,6},{8,9},{9,8},{10,11... | collective-permute-start | bytes 245768 | tf_op jit(solution)/shard_map/ppermute | solution.py:24
  18.2 1.3 %copy-done.3 = bf16[3,3,256,256]{3,2,1,0:T(8,128)(2,1)S(1)} copy-done((bf16[3,3,256,256]{3,2,1,0:T(8,128)(2,1)S(1)}, bf16[3,3,256,256]{3,2,1,0:T(8,128)(2,1)}, u32[]{:S(2)}) %copy-start.3) | copy-done | bytes 1179672
  19.4 0.7 %copy-done.4 = f32[256]{0:T(256)S(1)} copy-done((f32[256]{0:T(256)S(1)}, f32[256]{0:T(256)}, u32[]{:S(2)}) %copy-start.4) | copy-done | bytes 1048
  20.1 0.7 %copy-done.5 = f32[256]{0:T(256)S(1)} copy-done((f32[256]{0:T(256)S(1)}, f32[256]{0:T(256)}, u32[]{:S(2)}) %copy-start.5) | copy-done | bytes 1048
  20.8 4.5 %shard_map.101 = (bf16[512,256]{1,0:T(8,128)(2,1)S(1)}, bf16[512,256]{1,0:T(8,128)(2,1)S(1)}) custom-call(bf16[16,32,256]{2,1,0:T(8,128)(2,1)S(1)} %get-tuple-element.18.marked, bf16[2,32,256]{2,1,0:T(8,128)(2,1)S(1)} %collective-permute-done.top, bf16[2,32,256]{2,1,0:T(8,128)(2,1)S(1)} %collective-permute-done.1.bottom, ...), custom_call_target="tpu_custom_call" | custom-call | flops 1409286144 | tf_op jit(solution)/shard_map/pallas_call | solution.py:443
  25.3 0.1 collective-permute-start.4
  25.4 0.6 %collective-permute-start.9 = (bf16[128,1280]{1,0:T(8,128)(2,1)S(1)}, bf16[128,1280]{1,0:T(8,128)(2,1)S(1)}, u32[]{:S(2)}, u32[]{:S(2)}) collective-permute-start(bf16[128,1280]{1,0:T(8,128)(2,1)S(1)} %pad_maximum_fusion.queries), channel_id=1, source_target_pairs={{0,8},{4,12},{8,0},{12,4},{1,9},{5,13},{9,1},{13,5},{2,10},{6,14},... | collective-permute-start | bytes 983048 | tf_op jit(solution)/shard_map/ppermute | solution.py:24
  26.0 0.5 shard_map.102.own_keys
  26.5 0.3 collective-permute-done.4.other_sent
  26.9 1.8 %shard_map.104 = (f32[2,136,128]{2,1,0:T(8,128)S(1)}, bf16[512,256]{1,0:T(8,128)(2,1)S(1)}, bf16[512,1280]{1,0:T(8,128)(2,1)S(1)}) custom-call(bf16[512,256]{1,0:T(8,128)(2,1)S(1)} %get-tuple-element.19.cells.own, bf16[512,256]{1,0:T(8,128)(2,1)S(1)} %get-tuple-element.20.own_sent, bf16[512,1280]{1,0:T(8,128)(2,1)S(1)} %shard_map.102.own_keys, ...), custom_call_target="tpu_custom_call" | custom-call | flops 738197504 | tf_op jit(solution)/shard_map/pallas_call | solution.py:443
  28.7 6.9 %collective-permute-done.9.queries = bf16[128,1280]{1,0:T(8,128)(2,1)S(1)} collective-permute-done((bf16[128,1280]{1,0:T(8,128)(2,1)S(1)}, bf16[128,1280]{1,0:T(8,128)(2,1)S(1)}, u32[]{:S(2)}, u32[]{:S(2)}) %collective-permute-start.9) | collective-permute-done | bytes 327712 | tf_op jit(solution)/shard_map/ppermute | solution.py:24
  35.6 1.3 %shard_map.105 = (f32[136,128]{1,0:T(8,128)S(1)}, bf16[144,128]{1,0:T(8,128)(2,1)S(1)}, bf16[144,128]{1,0:T(8,128)(2,1)S(1)}, bf16[144,128]{1,0:T(8,128)(2,1)S(1)}) custom-call(f32[2,136,128]{2,1,0:T(8,128)S(1)} %get-tuple-element.22.near, bf16[512,256]{1,0:T(8,128)(2,1)S(1)} %get-tuple-element.19.cells.own, ...), custom_call_target="tpu_custom_call" | custom-call | flops 402653184 | tf_op jit(solution)/shard_map/pallas_call | solution.py:443
  36.9 0.1 collective-permute-start.10
  37.0 0.8 %collective-permute-start.11 = (bf16[144,128]{1,0:T(8,128)(2,1)S(1)}, bf16[144,128]{1,0:T(8,128)(2,1)S(1)}, u32[]{:S(2)}, u32[]{:S(2)}) collective-permute-start(bf16[144,128]{1,0:T(8,128)(2,1)S(1)} %get-tuple-element.27), channel_id=1, source_target_pairs={{0,2},{1,3},{2,0},{3,1},{4,6},{5,7},{6,4},{7,5},{8,10},{9,11},{10,... | collective-permute-start | bytes 110600 | tf_op jit(solution)/shard_map/ppermute | solution.py:24
  37.8 3.5 %collective-permute-start.12 = (bf16[144,128]{1,0:T(8,128)(2,1)S(1)}, bf16[144,128]{1,0:T(8,128)(2,1)S(1)}, u32[]{:S(2)}, u32[]{:S(2)}) collective-permute-start(bf16[144,128]{1,0:T(8,128)(2,1)S(1)} %get-tuple-element.28), channel_id=1, source_target_pairs={{0,3},{1,2},{2,1},{3,0},{4,7},{5,6},{6,5},{7,4},{8,11},{9,10},{10,... | collective-permute-start | bytes 110600 | tf_op jit(solution)/shard_map/ppermute | solution.py:24
  41.4 1.1 %collective-permute-done.11.refs_1_ = bf16[144,128]{1,0:T(8,128)(2,1)S(1)} collective-permute-done((bf16[144,128]{1,0:T(8,128)(2,1)S(1)}, bf16[144,128]{1,0:T(8,128)(2,1)S(1)}, u32[]{:S(2)}, u32[]{:S(2)}) %collective-permute-start.11) | collective-permute-done | bytes 36896 | tf_op jit(solution)/shard_map/ppermute | solution.py:24
  42.5 1.2 %collective-permute-done.12.refs_2_ = bf16[144,128]{1,0:T(8,128)(2,1)S(1)} collective-permute-done((bf16[144,128]{1,0:T(8,128)(2,1)S(1)}, bf16[144,128]{1,0:T(8,128)(2,1)S(1)}, u32[]{:S(2)}, u32[]{:S(2)}) %collective-permute-start.12) | collective-permute-done | bytes 36896 | tf_op jit(solution)/shard_map/ppermute | solution.py:24
  43.7 0.1 shard_map.106
  43.7 0.6 %collective-permute-start.13 = (bf16[144,128]{1,0:T(8,128)(2,1)S(1)}, bf16[144,128]{1,0:T(8,128)(2,1)S(1)}, u32[]{:S(2)}, u32[]{:S(2)}) collective-permute-start(bf16[144,128]{1,0:T(8,128)(2,1)S(1)} %get-tuple-element.30), channel_id=1, source_target_pairs={{0,8},{4,12},{8,0},{12,4},{1,9},{5,13},{9,1},{13,5},{2,10},{6,14},... | collective-permute-start | bytes 110600 | tf_op jit(solution)/shard_map/ppermute | solution.py:24
  44.4 3.4 %collective-permute-done.13.arrived = bf16[144,128]{1,0:T(8,128)(2,1)S(1)} collective-permute-done((bf16[144,128]{1,0:T(8,128)(2,1)S(1)}, bf16[144,128]{1,0:T(8,128)(2,1)S(1)}, u32[]{:S(2)}, u32[]{:S(2)}) %collective-permute-start.13) | collective-permute-done | bytes 36896 | tf_op jit(solution)/shard_map/ppermute | solution.py:24
  47.8 0.1 collective-permute-start.14
  47.9 1.2 %collective-permute-done.14.arrived = bf16[128,128]{1,0:T(8,128)(2,1)S(1)} collective-permute-done((bf16[128,128]{1,0:T(8,128)(2,1)S(1)}, bf16[128,128]{1,0:T(8,128)(2,1)S(1)}, u32[]{:S(2)}, u32[]{:S(2)}) %collective-permute-start.14) | collective-permute-done | bytes 32800 | tf_op jit(solution)/shard_map/ppermute | solution.py:24
  49.1 1.3 %finish.1 = bf16[320,128]{1,0:T(8,128)(2,1)} custom-call(bf16[128,128]{1,0:T(8,128)(2,1)S(1)} %shard_map.107.own, bf16[128,128]{1,0:T(8,128)(2,1)S(1)} %collective-permute-done.14.arrived, bf16[256,1280]{1,0:T(8,128)(2,1)S(1)} %copy-done.2, bf16[320,1280]{1,0:T(8,128)(2,1)S(1)} %bitcast.6), custom_call_target="tpu_custom_call" | custom-call | tf_op jit(solution)/shard_map/finish/pallas_call | solution.py:538
  (25 shorter events, 0.1 us)
Async XLA Ops:
  0.0 13.7 %collective-permute-start.5 = (bf16[32,1280]{1,0:T(8,128)(2,1)}, bf16[32,1280]{1,0:T(8,128)(2,1)S(1)}, u32[]{:S(2)}, u32[]{:S(2)}) collective-permute-start(bf16[32,1280]{1,0:T(8,128)(2,1)} %queries.1), channel_id=1, source_target_pairs={{0,4},{4,0},{8,12},{12,8},{1,5},{5,1},{9,13},{13,9},{2,6},{6,2},{1... | collective-permute-start | bytes 245768 | tf_op jit(solution)/shard_map/ppermute | solution.py:24
  1.6 6.3 %collective-permute-start.1 = (bf16[2,32,256]{2,1,0:T(8,128)(2,1)S(1)}, bf16[2,32,256]{2,1,0:T(8,128)(2,1)S(1)}, u32[]{:S(2)}, u32[]{:S(2)}) collective-permute-start(bf16[2,32,256]{2,1,0:T(8,128)(2,1)S(1)} %get-tuple-element.33), channel_id=1, source_target_pairs={{0,3},{1,0},{2,1},{3,2},{4,7},{5,4},{6,5},{7,6},{8,11},{9,8},{10,9... | collective-permute-start | bytes 98312 | tf_op jit(solution)/shard_map/ppermute | solution.py:19
  6.2 5.7 %collective-permute-start = (bf16[2,32,256]{2,1,0:T(8,128)(2,1)S(1)}, bf16[2,32,256]{2,1,0:T(8,128)(2,1)S(1)}, u32[]{:S(2)}, u32[]{:S(2)}) collective-permute-start(bf16[2,32,256]{2,1,0:T(8,128)(2,1)S(1)} %get-tuple-element.34), channel_id=1, source_target_pairs={{0,1},{1,2},{2,3},{3,0},{4,5},{5,6},{6,7},{7,4},{8,9},{9,10},{10,1... | collective-permute-start | bytes 98312 | tf_op jit(solution)/shard_map/ppermute | solution.py:19
  12.0 6.1 %collective-permute-start.3 = (bf16[20,2,256]{2,1,0:T(2,128)(2,1)S(1)}, bf16[20,2,256]{2,1,0:T(2,128)(2,1)S(1)}, u32[]{:S(2)}, u32[]{:S(2)}) collective-permute-start(bf16[20,2,256]{2,1,0:T(2,128)(2,1)S(1)} %get-tuple-element.35), channel_id=1, source_target_pairs={{0,12},{4,8},{8,4},{12,0},{1,13},{5,9},{9,5},{13,1},{2,14},{6,10},... | collective-permute-start | bytes 61448 | tf_op jit(solution)/shard_map/ppermute | solution.py:492
  12.2 5.9 %collective-permute-start.2 = (bf16[20,2,256]{2,1,0:T(2,128)(2,1)S(1)}, bf16[20,2,256]{2,1,0:T(2,128)(2,1)S(1)}, u32[]{:S(2)}, u32[]{:S(2)}) collective-permute-start(bf16[20,2,256]{2,1,0:T(2,128)(2,1)S(1)} %get-tuple-element.36), channel_id=1, source_target_pairs={{0,4},{4,0},{8,12},{12,8},{1,5},{5,1},{9,13},{13,9},{2,6},{6,2},{1... | collective-permute-start | bytes 61448 | tf_op jit(solution)/shard_map/ppermute | solution.py:24
  13.7 11.6 %collective-permute-start.8 = (bf16[32,1280]{1,0:T(8,128)(2,1)S(1)}, bf16[32,1280]{1,0:T(8,128)(2,1)S(1)}, u32[]{:S(2)}, u32[]{:S(2)}) collective-permute-start(bf16[32,1280]{1,0:T(8,128)(2,1)S(1)} %shard_map.103), channel_id=1, source_target_pairs={{0,3},{1,2},{2,1},{3,0},{4,7},{5,6},{6,5},{7,4},{8,11},{9,10},{10,... | collective-permute-start | bytes 245768 | tf_op jit(solution)/shard_map/ppermute | solution.py:24
  14.0 11.3 %collective-permute-start.7 = (bf16[32,1280]{1,0:T(8,128)(2,1)S(1)}, bf16[32,1280]{1,0:T(8,128)(2,1)S(1)}, u32[]{:S(2)}, u32[]{:S(2)}) collective-permute-start(bf16[32,1280]{1,0:T(8,128)(2,1)S(1)} %shard_map.103), channel_id=1, source_target_pairs={{0,2},{1,3},{2,0},{3,1},{4,6},{5,7},{6,4},{7,5},{8,10},{9,11},{10,... | collective-permute-start | bytes 245768 | tf_op jit(solution)/shard_map/ppermute | solution.py:24
  14.0 11.3 %collective-permute-start.6 = (bf16[32,1280]{1,0:T(8,128)(2,1)S(1)}, bf16[32,1280]{1,0:T(8,128)(2,1)S(1)}, u32[]{:S(2)}, u32[]{:S(2)}) collective-permute-start(bf16[32,1280]{1,0:T(8,128)(2,1)S(1)} %shard_map.103), channel_id=1, source_target_pairs={{0,1},{1,0},{2,3},{3,2},{4,5},{5,4},{6,7},{7,6},{8,9},{9,8},{10,11... | collective-permute-start | bytes 245768 | tf_op jit(solution)/shard_map/ppermute | solution.py:24
  18.2 1.3 %copy-start.3 = (bf16[3,3,256,256]{3,2,1,0:T(8,128)(2,1)S(1)}, bf16[3,3,256,256]{3,2,1,0:T(8,128)(2,1)}, u32[]{:S(2)}) copy-start(bf16[3,3,256,256]{3,2,1,0:T(8,128)(2,1)} %param.12) | copy-start | bytes 3538948
  19.4 0.7 %copy-start.4 = (f32[256]{0:T(256)S(1)}, f32[256]{0:T(256)}, u32[]{:S(2)}) copy-start(f32[256]{0:T(256)} %param.13) | copy-start | bytes 3076
  20.1 0.7 %copy-start.5 = (f32[256]{0:T(256)S(1)}, f32[256]{0:T(256)}, u32[]{:S(2)}) copy-start(f32[256]{0:T(256)} %param.15) | copy-start | bytes 3076
  20.8 5.2 %copy-start = (bf16[256,1280]{1,0:T(8,128)(2,1)S(1)}, bf16[256,1280]{1,0:T(8,128)(2,1)}, u32[]{:S(2)}) copy-start(bf16[256,1280]{1,0:T(8,128)(2,1)} %weight.3) | copy-start | bytes 1966084
  25.3 1.6 %collective-permute-start.4 = (bf16[512,256]{1,0:T(8,128)(2,1)S(1)}, bf16[512,256]{1,0:T(8,128)(2,1)S(1)}, u32[]{:S(2)}, u32[]{:S(2)}) collective-permute-start(bf16[512,256]{1,0:T(8,128)(2,1)S(1)} %get-tuple-element.20.own_sent), channel_id=1, source_target_pairs={{0,4},{4,0},{8,12},{12,8},{1,5},{5,1},{9,13},{13,9},{2,6},{6,2},{1... | collective-permute-start | bytes 786440 | tf_op jit(solution)/shard_map/ppermute | solution.py:24
  25.4 10.2 %collective-permute-start.9 = (bf16[128,1280]{1,0:T(8,128)(2,1)S(1)}, bf16[128,1280]{1,0:T(8,128)(2,1)S(1)}, u32[]{:S(2)}, u32[]{:S(2)}) collective-permute-start(bf16[128,1280]{1,0:T(8,128)(2,1)S(1)} %pad_maximum_fusion.queries), channel_id=1, source_target_pairs={{0,8},{4,12},{8,0},{12,4},{1,9},{5,13},{9,1},{13,5},{2,10},{6,14},... | collective-permute-start | bytes 983048 | tf_op jit(solution)/shard_map/ppermute | solution.py:24
  35.6 13.5 %copy-start.1 = (bf16[1280,320]{0,1:T(8,128)(2,1)S(1)}, bf16[1280,320]{0,1:T(8,128)(2,1)}, u32[]{:S(2)}) copy-start(bf16[1280,320]{0,1:T(8,128)(2,1)} %param.19) | copy-start | bytes 2457604
  35.6 13.5 %copy-start.2 = (bf16[256,1280]{1,0:T(8,128)(2,1)S(1)}, bf16[256,1280]{1,0:T(8,128)(2,1)}, u32[]{:S(2)}) copy-start(bf16[256,1280]{1,0:T(8,128)(2,1)} %value_weight.1) | copy-start | bytes 1966084
  36.9 4.5 %collective-permute-start.10 = (bf16[144,128]{1,0:T(8,128)(2,1)S(1)}, bf16[144,128]{1,0:T(8,128)(2,1)S(1)}, u32[]{:S(2)}, u32[]{:S(2)}) collective-permute-start(bf16[144,128]{1,0:T(8,128)(2,1)S(1)} %get-tuple-element.26), channel_id=1, source_target_pairs={{0,1},{1,0},{2,3},{3,2},{4,5},{5,4},{6,7},{7,6},{8,9},{9,8},{10,11... | collective-permute-start | bytes 110600 | tf_op jit(solution)/shard_map/ppermute | solution.py:24
  37.0 5.5 %collective-permute-start.11 = (bf16[144,128]{1,0:T(8,128)(2,1)S(1)}, bf16[144,128]{1,0:T(8,128)(2,1)S(1)}, u32[]{:S(2)}, u32[]{:S(2)}) collective-permute-start(bf16[144,128]{1,0:T(8,128)(2,1)S(1)} %get-tuple-element.27), channel_id=1, source_target_pairs={{0,2},{1,3},{2,0},{3,1},{4,6},{5,7},{6,4},{7,5},{8,10},{9,11},{10,... | collective-permute-start | bytes 110600 | tf_op jit(solution)/shard_map/ppermute | solution.py:24
  37.8 5.9 %collective-permute-start.12 = (bf16[144,128]{1,0:T(8,128)(2,1)S(1)}, bf16[144,128]{1,0:T(8,128)(2,1)S(1)}, u32[]{:S(2)}, u32[]{:S(2)}) collective-permute-start(bf16[144,128]{1,0:T(8,128)(2,1)S(1)} %get-tuple-element.28), channel_id=1, source_target_pairs={{0,3},{1,2},{2,1},{3,0},{4,7},{5,6},{6,5},{7,4},{8,11},{9,10},{10,... | collective-permute-start | bytes 110600 | tf_op jit(solution)/shard_map/ppermute | solution.py:24
  43.7 4.0 %collective-permute-start.13 = (bf16[144,128]{1,0:T(8,128)(2,1)S(1)}, bf16[144,128]{1,0:T(8,128)(2,1)S(1)}, u32[]{:S(2)}, u32[]{:S(2)}) collective-permute-start(bf16[144,128]{1,0:T(8,128)(2,1)S(1)} %get-tuple-element.30), channel_id=1, source_target_pairs={{0,8},{4,12},{8,0},{12,4},{1,9},{5,13},{9,1},{13,5},{2,10},{6,14},... | collective-permute-start | bytes 110600 | tf_op jit(solution)/shard_map/ppermute | solution.py:24
  47.8 1.3 %collective-permute-start.14 = (bf16[128,128]{1,0:T(8,128)(2,1)S(1)}, bf16[128,128]{1,0:T(8,128)(2,1)S(1)}, u32[]{:S(2)}, u32[]{:S(2)}) collective-permute-start(bf16[128,128]{1,0:T(8,128)(2,1)S(1)} %shard_map.107.own), channel_id=1, source_target_pairs={{0,4},{4,0},{8,12},{12,8},{1,5},{5,1},{9,13},{13,9},{2,6},{6,2},{1... | collective-permute-start | bytes 98312 | tf_op jit(solution)/shard_map/ppermute | solution.py:24

commit v5 on v4

--- a/solution.py
+++ b/solution.py
@@ -204,8 +204,8 @@
 
 
 def conv_kernel(
-    marked, top, bottom, paired, crossed, first, bias_first, second, bias_second,
-    out, sent, cells, mid, taps, second_held, done,
+    marked, top, bottom, paired, crossed, first, bias_first, second,
+    mid, second_held, cells, taps, done,
 ):
     later = pltpu.make_async_copy(second, second_held, done)
     later.start()
@@ -258,19 +258,22 @@
     mid[0:EDGE, :] = edge
     mid[EDGE + count : 2 * EDGE + count, :] = edge
     mid[EDGE : EDGE + count, :] = jnp.where(alive, gelu(summed + bias_first[...]), 0.0)
-
+    later.wait()
+
+
+def second_conv_kernel(marked, mid, second, bias_second, out, sent, taps):
+    height, breadth, channels = marked.shape
+    count = mid.shape[0] - 2 * EDGE
+    slot = (count - LEAD) // (height + 2)
     for shift in range(3):
         taps[0:count, shift * channels : (shift + 1) * channels] = mid[
             EDGE - 1 + shift : EDGE - 1 + shift + count, :
         ].astype(jnp.bfloat16)
     inner = height * slot
-    later.wait()
-    summed = jnp.dot(
-        taps[LEAD : LEAD + inner, :], second_held[0], preferred_element_type=jnp.float32
-    )
+    summed = jnp.dot(taps[LEAD : LEAD + inner, :], second[0], preferred_element_type=jnp.float32)
     for line in range(1, 3):
         summed = summed + jnp.dot(
-            taps[LEAD + line * slot : LEAD + line * slot + inner, :], second_held[line],
+            taps[LEAD + line * slot : LEAD + line * slot + inner, :], second[line],
             preferred_element_type=jnp.float32,
         )
     summed = summed.reshape(height, slot, channels)[:, :breadth].reshape(height * breadth, channels)
@@ -325,25 +328,32 @@
     )
 
 
-def score_blocks(held, queries, sides):
-    half = queries.shape[0] // 8
+PLACES = (0, 2, 1, 3)
+
+
+def hold_queries(held, parts):
+    half = held.shape[0] // 8
     row = lax.axis_index("row")
-    for place in range(4):
+    for number, place in enumerate(PLACES):
+        part = parts[number // 2]
         for parity in range(2):
-            source = (2 * place + parity) * half
+            source = (2 * (number % 2) + parity) * half
             target = pl.multiple_of(parity * 4 * half + (row ^ place) * half, half)
-            held[pl.ds(target, half), :] = queries[source : source + half, :]
-    scale = 1.0 / math.sqrt(held.shape[1])
-    scores = []
-    for _, marked, keys in sides:
-        raw = lax.dot_general(
-            keys[...], held[...], (((1,), (1,)), ((), ())), preferred_element_type=jnp.float32
-        )
-        alive = marked[:, : raw.shape[1]] < FAR
-        scores.append(jnp.where(alive, raw * scale, -1e30))
+            held[pl.ds(target, half), :] = part[source : source + half, :]
+
+
+def masked_scores(queries, marked, keys):
+    scale = 1.0 / math.sqrt(queries.shape[1])
+    raw = lax.dot_general(
+        keys[...], queries[...], (((1,), (1,)), ((), ())), preferred_element_type=jnp.float32
+    )
+    return jnp.where(marked[:, : raw.shape[1]] < FAR, raw * scale, -1e30)
+
+
+def score_blocks(scores, sides):
     top = jnp.maximum(*[jnp.max(part, axis=0, keepdims=True) for part in scores])
     pooled = total = 0.0
-    for part, (cells, _, _) in zip(scores, sides):
+    for part, cells in zip(scores, sides):
         chosen = jnp.exp(part - top)
         total = total + jnp.sum(chosen, axis=0, keepdims=True)
         pooled = pooled + lax.dot_general(
@@ -369,24 +379,33 @@
     )
 
 
-def near_kernel(own, own_sent, own_keys, other_sent, weight, queries, out, other, keys, held):
+def own_kernel(own, own_sent, weight, first_queries, last_queries, keys, scores, held):
+    key_kernel(own, weight, keys)
+    hold_queries(held, (first_queries, last_queries))
+    scores[...] = masked_scores(held, own_sent, keys)
+
+
+def near_kernel(own, own_scores, other_sent, weight, held, out, other, keys):
     values = other_sent[...].astype(jnp.float32)
     other[...] = jnp.where(values < FAR, values, 0.0).astype(jnp.bfloat16)
     key_kernel(other, weight, keys)
-    sides = ((own, own_sent, own_keys), (other, other_sent, keys))
-    for parity, block in enumerate(score_blocks(held, queries, sides)):
+    scores = (own_scores[...], masked_scores(held, other_sent, keys))
+    for parity, block in enumerate(score_blocks(scores, (own, other))):
         write_whole(out.at[parity], *block)
 
 
 def far_kernel(
-    near, own, own_sent, own_keys, other, other_sent, other_keys, queries,
+    near, own, own_sent, own_keys, other, other_sent, other_keys, first_queries, last_queries,
     kept, send_1, send_2, send_3, held, blocks,
 ):
     row, across = lax.axis_index("row"), lax.axis_index("col") // 2
-    sides = ((own, own_sent, own_keys), (other, other_sent, other_keys))
     for parity in range(2):
         blocks[2 * across + parity] = near[parity]
-    for parity, block in enumerate(score_blocks(held, queries, sides)):
+    hold_queries(held, (first_queries, last_queries))
+    scores = (
+        masked_scores(held, own_sent, own_keys), masked_scores(held, other_sent, other_keys)
+    )
+    for parity, block in enumerate(score_blocks(scores, (own, other))):
         write_whole(blocks.at[2 * (1 - across) + parity], *block)
     kept[...] = blocks[row]
     for step, send in ((1, send_1), (2, send_2), (3, send_3)):
@@ -405,29 +424,25 @@
     out[...] = (values / total).astype(jnp.bfloat16)
 
 
-def finish_kernel(own, arrived, value_weight, out_weight, out, attended):
-    lanes = own.shape[1]
-    half = lanes // 2
-    first_core = lax.rem(lax.axis_index("col"), 2) == 0
-    mine, other = own[...].astype(jnp.float32), arrived[...].astype(jnp.float32)
-    even, odd = jnp.where(first_core, mine, other), jnp.where(first_core, other, mine)
-    lower = lax.broadcasted_iota(jnp.int32, mine.shape, 1) < half
-    normalized = jnp.concatenate(
-        [
-            jnp.where(lower, even, pltpu.roll(odd, half, 1)),
-            jnp.where(lower, pltpu.roll(even, half, 1), odd),
-        ],
-        axis=0,
-    ).astype(jnp.bfloat16)
-    product = lax.dot_general(
-        normalized, value_weight[...], (((0,), (0,)), ((), ())),
-        preferred_element_type=jnp.float32,
-    ).astype(jnp.bfloat16)
-    piece = half // 4
-    for core in range(2):
-        for place in range(4):
-            source, target = core * half + place * piece, (2 * place + core) * piece
-            attended[target : target + piece, :] = product[source : source + piece]
+def attend_kernel(normalized, value_weight, attended):
+    lanes = normalized.shape[1] // 2
+    values = normalized[...].astype(jnp.float32)
+    tall = jnp.concatenate([values, pltpu.roll(values, lanes, 1)], axis=0).astype(jnp.bfloat16)
+    attended[...] = lax.dot_general(
+        tall, value_weight[...], (((0,), (0,)), ((), ())), preferred_element_type=jnp.float32
+    )[:lanes].astype(jnp.bfloat16)
+
+
+def finish_kernel(mine, arrived, value_weight, out_weight, out, other, attended):
+    attend_kernel(arrived, value_weight, other)
+    core = lax.rem(lax.axis_index("col"), 2)
+    piece = mine.shape[0] // 4
+    for place in range(4):
+        source = slice(place * piece, (place + 1) * piece)
+        first = pl.multiple_of((2 * place + core) * piece, piece)
+        last = pl.multiple_of((2 * place + 1 - core) * piece, piece)
+        attended[pl.ds(first, piece), :] = mine[source]
+        attended[pl.ds(last, piece), :] = other[source]
     out[...] = lax.dot_general(
         out_weight[...], attended[...], (((1,), (1,)), ((), ())),
         preferred_element_type=jnp.float32,
@@ -481,7 +496,7 @@
         far=(0, 1, 2), flops=1 << 20,
     )
     (queries,) = call(halve_kernel, [((size, width), half)], [queries, beside])
-    turned = [flipped(queries, "row", k) for k in range(1, 4)]
+    two = flipped(queries, "row", 2)
     top = shifted(marked[height - HALO :], "row", 1)
     bottom = shifted(marked[:HALO], "row", -1)
     edge = lambda cut: jnp.concatenate([top[:, cut], marked[:, cut], bottom[:, cut]], axis=0)
@@ -491,40 +506,52 @@
     rounds = [(k, (k + 1 if k % 2 else k - 1) % cols) for k in range(cols)]
     crossed = lax.ppermute(jnp.where(even, *ends[::-1]), "col", rounds)
 
-    near_queries = jnp.concatenate([queries] + turned, axis=0)
-    far_queries = flipped(near_queries, "col", 2)
-
-    own, own_sent = call(
-        conv_kernel, [((cells, channels), half)] * 2,
+    pair = jnp.concatenate([queries, two], axis=0)
+    far_pair = flipped(pair, "col", 2)
+    next_pair = flipped(pair, "row", 1)
+    last_pair = flipped(next_pair, "col", 2)
+
+    count = flat - 2 * slot
+    mid, weight = call(
+        conv_kernel,
+        [((count + 2 * EDGE, channels), wide), ((3, 3 * channels, channels), half)],
         [
             marked, top, bottom, paired, crossed,
             conv_first.reshape(3, 3 * channels, channels), bias_first.reshape(1, channels),
-            conv_second.reshape(3, 3 * channels, channels), bias_second.reshape(1, channels),
+            conv_second.reshape(3, 3 * channels, channels),
         ],
         [
             ((flat + 2 * EDGE, channels), wide),
-            ((flat - 2 * slot + 2 * EDGE, channels), wide),
             ((flat, 3 * channels), half),
-            ((3, 3 * channels, channels), half),
             pltpu.SemaphoreType.DMA,
         ],
-        limit=16, far=(7,), flops=42 * cells * channels * channels,
+        limit=12, far=(7,), flops=21 * cells * channels * channels,
+    )
+    own, own_sent = call(
+        second_conv_kernel, [((cells, channels), half)] * 2,
+        [marked, mid, weight, bias_second.reshape(1, channels)],
+        [((count, 3 * channels), half)],
+        limit=10, flops=18 * cells * channels * channels,
     )
     other_sent = flipped(own_sent, "col", 1)
-    (own_keys,) = call(
-        key_kernel, [((cells, width), half)], [own, key_weight],
-        limit=6, flops=2 * cells * channels * width,
+    own_keys, own_scores, held_queries = call(
+        own_kernel,
+        [((cells, width), half), ((cells, block), wide), ((block, width), half)],
+        [own, own_sent, key_weight, pair, next_pair],
+        limit=6, flops=2 * cells * width * (channels + block),
     )
     near, other, other_keys = call(
         near_kernel,
         [((2,) + whole_block, wide), ((cells, channels), half), ((cells, width), half)],
-        [own, own_sent, own_keys, other_sent, key_weight, near_queries],
-        [((block, width), half)],
-        limit=8, flops=score_flops + 2 * cells * channels * width,
+        [own, own_scores, other_sent, key_weight, held_queries],
+        limit=8, flops=score_flops,
     )
     kept, *sends = call(
         far_kernel, [(whole_block, wide)] + [(sent_block, half)] * 3,
-        [near, own, own_sent, own_keys, other, other_sent, other_keys, far_queries],
+        [
+            near, own, own_sent, own_keys, other, other_sent, other_keys,
+            far_pair, last_pair,
+        ],
         [((block, width), half), ((4,) + whole_block, wide)],
         limit=8, flops=score_flops,
     )
@@ -533,6 +560,10 @@
     arrived = flipped(sent, "col", 2)
     (normalized,) = call(normalize_kernel, [((channels // 2, block), half)], [kept, arrived])
     arrived = flipped(normalized, "col", 1)
+    (attended,) = call(
+        attend_kernel, [((2 * size, width), half)], [normalized, value_weight],
+        flops=8 * size * channels * width,
+    )
     held = pl.BlockSpec(memory_space=pltpu.VMEM)
     keep = lambda array: pltpu.with_memory_space_constraint(array, pltpu.VMEM)
     return pl.pallas_call(
@@ -540,10 +571,10 @@
         out_shape=jax.ShapeDtypeStruct((out_weight.shape[1], block), half),
         in_specs=[held] * 4,
         out_specs=held,
-        scratch_shapes=[pltpu.VMEM((block, width), half)],
+        scratch_shapes=[pltpu.VMEM((2 * size, width), half), pltpu.VMEM((block, width), half)],
         compiler_params=pltpu.CompilerParams(vmem_limit_bytes=6 * MIB),
         name="finish",
-    )(keep(normalized), keep(arrived), keep(value_weight), keep(out_weight.T)).T
+    )(keep(attended), keep(arrived), keep(value_weight), keep(out_weight.T)).T
 
 
 def shards(

time: 50.6 us -> 47.8 us (0.945)
  starting transfers between devices: 17.1 us -> 13.8 us
  waiting for transfers between devices: 19.9 us -> 22.1 us
  Pallas kernels: 10.6 us -> 9.33 us
  local copies, waits for them, and re-layouts: 2.69 us -> 2.02 us
    ppermute x12, starting transfers between devices: 12.2 us -> 8.94 us  [flipped(): return lax.ppermute(array, axis, [(i, i ^ bit) for i in range(count)])]
    ppermute x1, waiting for transfers between devices: 0.01 us -> 1.68 us  [kernel_path(): crossed = lax.ppermute(jnp.where(even, *ends[::-1]), 'col', rounds)]
    pallas_call x8 -> x10, Pallas kernels: 9.23 us -> 7.96 us  [call(): pl.pallas_call(kernel, out_shape=[pltpu.VMEM(shape, dtype) for shape, dty...]
    unnamed x12, local copies, waits for them, and re-layouts: 2.64 us -> 1.97 us
    ppermute x12, waiting for transfers between devices: 14.2 us -> 14.8 us  [flipped(): return lax.ppermute(array, axis, [(i, i ^ bit) for i in range(count)])]
  transfers between devices with their start and end apart: 15 -> 15, of which waited for: 8 -> 10; matrix products, arithmetic and copies ran while one was open for 0% -> 0% of each run, Pallas kernels for 16% -> 14%
where the time goes in v5:
time: 47.8 us; the launch traced here: 47.6 us
  waiting for transfers between devices  22.1 us (46%)
  starting transfers between devices  13.8 us (29%)
  Pallas kernels  9.33 us (20%)
  local copies, waits for them, and re-layouts  2.02 us (4%)
    ppermute x12, waiting for transfers between devices, flipped(): return lax.ppermute(array, axis, [(i, i ^ bit) for i in range(count)])  14.8 us
    ppermute x12, starting transfers between devices, flipped(): return lax.ppermute(array, axis, [(i, i ^ bit) for i in range(count)])  8.94 us
    pallas_call x10, Pallas kernels, call(): pl.pallas_call(kernel, out_shape=[pltpu.VMEM(shape, dtype) for shape, dty...  7.96 us
    ppermute x2, waiting for transfers between devices, shifted(): lax.ppermute(array, axis, [(i, (i + step) % count) for i in range(count)])  5.66 us
    ppermute x2, starting transfers between devices, shifted(): lax.ppermute(array, axis, [(i, (i + step) % count) for i in range(count)])  4.64 us
    unnamed x12, local copies, waits for them, and re-layouts  1.97 us
    ppermute x1, waiting for transfers between devices, kernel_path(): crossed = lax.ppermute(jnp.where(even, *ends[::-1]), 'col', rounds)  1.68 us
    pallas_call x1, Pallas kernels, kernel_path(): pl.pallas_call(finish_kernel, out_shape=jax.ShapeDtypeStruct((out_weight....  1.37 us
  transfers between devices with their start and end apart: 15, of which 10 were waited for; matrix products, arithmetic and copies ran while one was open for 0% of the time, Pallas kernels for 14%

profile of v5, /device:TPU:0, one launch (start us, length us, event | category | flops | bytes accessed | tf_op | source)
XLA Modules:
  0.0 47.6 jit_solution(9949782423030004869)
XLA Ops:
  0.0 0.5 %collective-permute-start.4 = (bf16[32,1280]{1,0:T(8,128)(2,1)}, bf16[32,1280]{1,0:T(8,128)(2,1)S(1)}, u32[]{:S(2)}, u32[]{:S(2)}) collective-permute-start(bf16[32,1280]{1,0:T(8,128)(2,1)} %queries.1), channel_id=1, source_target_pairs={{0,4},{4,0},{8,12},{12,8},{1,5},{5,1},{9,13},{13,9},{2,6},{6,2},{1... | collective-permute-start | bytes 245768 | tf_op jit(solution)/shard_map/ppermute | solution.py:24
  0.5 1.1 %shard_map.100 = (bf16[16,32,256]{2,1,0:T(8,128)(2,1)S(1)}, bf16[32,1280]{1,0:T(8,128)(2,1)S(1)}) custom-call(bf16[16,32,256]{2,1,0:T(8,128)(2,1)} %features.1, s32[16,32]{1,0:T(8,128)} %tissue.1, bf16[32,1280]{1,0:T(8,128)(2,1)} %queries.1), custom_call_target="tpu_custom_call" | custom-call | flops 1048576 | tf_op jit(solution)/shard_map/pallas_call | solution.py:458
  1.6 4.6 %collective-permute-start.1 = (bf16[2,32,256]{2,1,0:T(8,128)(2,1)S(1)}, bf16[2,32,256]{2,1,0:T(8,128)(2,1)S(1)}, u32[]{:S(2)}, u32[]{:S(2)}) collective-permute-start(bf16[2,32,256]{2,1,0:T(8,128)(2,1)S(1)} %get-tuple-element.43), channel_id=1, source_target_pairs={{0,3},{1,0},{2,1},{3,2},{4,7},{5,4},{6,5},{7,6},{8,11},{9,8},{10,9... | collective-permute-start | bytes 98312 | tf_op jit(solution)/shard_map/ppermute | solution.py:19
  6.3 1.6 %collective-permute-done.1.bottom = bf16[2,32,256]{2,1,0:T(8,128)(2,1)S(1)} collective-permute-done((bf16[2,32,256]{2,1,0:T(8,128)(2,1)S(1)}, bf16[2,32,256]{2,1,0:T(8,128)(2,1)S(1)}, u32[]{:S(2)}, u32[]{:S(2)}) %collective-permute-start.1) | collective-permute-done | bytes 32800 | tf_op jit(solution)/shard_map/ppermute | solution.py:19
  7.9 4.0 %collective-permute-done.top = bf16[2,32,256]{2,1,0:T(8,128)(2,1)S(1)} collective-permute-done((bf16[2,32,256]{2,1,0:T(8,128)(2,1)S(1)}, bf16[2,32,256]{2,1,0:T(8,128)(2,1)S(1)}, u32[]{:S(2)}, u32[]{:S(2)}) %collective-permute-start) | collective-permute-done | bytes 32800 | tf_op jit(solution)/shard_map/ppermute | solution.py:19
  12.0 0.2 collective-permute-start.3
  12.2 1.4 %collective-permute-start.2 = (bf16[20,2,256]{2,1,0:T(2,128)(2,1)S(1)}, bf16[20,2,256]{2,1,0:T(2,128)(2,1)S(1)}, u32[]{:S(2)}, u32[]{:S(2)}) collective-permute-start(bf16[20,2,256]{2,1,0:T(2,128)(2,1)S(1)} %get-tuple-element.46), channel_id=1, source_target_pairs={{0,4},{4,0},{8,12},{12,8},{1,5},{5,1},{9,13},{13,9},{2,6},{6,2},{1... | collective-permute-start | bytes 61448 | tf_op jit(solution)/shard_map/ppermute | solution.py:24
  13.8 1.7 %collective-permute-done.3.crossed = bf16[20,2,256]{2,1,0:T(2,128)(2,1)S(1)} collective-permute-done((bf16[20,2,256]{2,1,0:T(2,128)(2,1)S(1)}, bf16[20,2,256]{2,1,0:T(2,128)(2,1)S(1)}, u32[]{:S(2)}, u32[]{:S(2)}) %collective-permute-start.3) | collective-permute-done | bytes 20512 | tf_op jit(solution)/shard_map/ppermute | solution.py:507
  15.5 1.3 %copy-done.1 = bf16[3,3,256,256]{3,2,1,0:T(8,128)(2,1)S(1)} copy-done((bf16[3,3,256,256]{3,2,1,0:T(8,128)(2,1)S(1)}, bf16[3,3,256,256]{3,2,1,0:T(8,128)(2,1)}, u32[]{:S(2)}) %copy-start.1) | copy-done | bytes 1179672
  16.7 0.7 %copy-done.4 = f32[256]{0:T(256)S(1)} copy-done((f32[256]{0:T(256)S(1)}, f32[256]{0:T(256)}, u32[]{:S(2)}) %copy-start.4) | copy-done | bytes 1048
  17.4 1.5 %shard_map.101 = (f32[896,256]{1,0:T(8,128)S(1)}, bf16[3,768,256]{2,1,0:T(8,128)(2,1)S(1)}) custom-call(bf16[16,32,256]{2,1,0:T(8,128)(2,1)S(1)} %get-tuple-element.23.marked, bf16[2,32,256]{2,1,0:T(8,128)(2,1)S(1)} %collective-permute-done.top, bf16[2,32,256]{2,1,0:T(8,128)(2,1)S(1)} %collective-permute-done.1.bottom, ...), custom_call_target="tpu_custom_call" | custom-call | flops 704643072 | tf_op jit(solution)/shard_map/pallas_call | solution.py:458
  18.9 0.2 collective-permute-done.5
  19.1 0.1 collective-permute-start.6
  19.2 1.1 %shard_map.102 = (bf16[512,256]{1,0:T(8,128)(2,1)S(1)}, bf16[512,256]{1,0:T(8,128)(2,1)S(1)}) custom-call(bf16[16,32,256]{2,1,0:T(8,128)(2,1)S(1)} %get-tuple-element.23.marked, f32[896,256]{1,0:T(8,128)S(1)} %get-tuple-element.24.mid, bf16[3,768,256]{2,1,0:T(8,128)(2,1)S(1)} %get-tuple-element.25.second, f32[1,256]{1,0:T(1,128)S(1)} %bitcast.9), custom_call_target="tpu_custom_call" | custom-call | flops 603979776 | tf_op jit(solution)/shard_map/pallas_call | solution.py:458
  20.4 0.1 collective-permute-start.7
  20.4 1.2 %collective-permute-start.8 = (bf16[64,1280]{1,0:T(8,128)(2,1)S(1)}, bf16[64,1280]{1,0:T(8,128)(2,1)S(1)}, u32[]{:S(2)}, u32[]{:S(2)}) collective-permute-start(bf16[64,1280]{1,0:T(8,128)(2,1)S(1)} %pad_maximum_fusion.first_queries), channel_id=1, source_target_pairs={{0,8},{4,12},{8,0},{12,4},{1,9},{5,13},{9,1},{13,5},{2,10},{6,14},... | collective-permute-start | bytes 491528 | tf_op jit(solution)/shard_map/ppermute | solution.py:24
  21.7 3.6 %collective-permute-done.6.last_queries = bf16[64,1280]{1,0:T(8,128)(2,1)S(1)} collective-permute-done((bf16[64,1280]{1,0:T(8,128)(2,1)S(1)}, bf16[64,1280]{1,0:T(8,128)(2,1)S(1)}, u32[]{:S(2)}, u32[]{:S(2)}) %collective-permute-start.6) | collective-permute-done | bytes 163872 | tf_op jit(solution)/shard_map/ppermute | solution.py:24
  25.2 0.4 collective-permute-start.9
  25.7 1.0 %shard_map.104 = (bf16[512,1280]{1,0:T(8,128)(2,1)S(1)}, f32[512,128]{1,0:T(8,128)S(1)}, bf16[128,1280]{1,0:T(8,128)(2,1)S(1)}) custom-call(bf16[512,256]{1,0:T(8,128)(2,1)S(1)} %get-tuple-element.26.own, bf16[512,256]{1,0:T(8,128)(2,1)S(1)} %get-tuple-element.27.own_sent, bf16[256,1280]{1,0:T(8,128)(2,1)S(1)} %copy-done.3, ...), custom_call_target="tpu_custom_call" | custom-call | flops 503316480 | tf_op jit(solution)/shard_map/pallas_call | solution.py:458
  26.6 1.5 %shard_map.105 = (f32[2,136,128]{2,1,0:T(8,128)S(1)}, bf16[512,256]{1,0:T(8,128)(2,1)S(1)}, bf16[512,1280]{1,0:T(8,128)(2,1)S(1)}) custom-call(bf16[512,256]{1,0:T(8,128)(2,1)S(1)} %get-tuple-element.26.own, f32[512,128]{1,0:T(8,128)S(1)} %get-tuple-element.29.own_scores, bf16[512,256]{1,0:T(8,128)(2,1)S(1)} %collective-permute-done.7.other_sent, ...), custom_call_target="tpu_custom_call" | custom-call | flops 402653184 | tf_op jit(solution)/shard_map/pallas_call | solution.py:458
  28.2 2.4 %collective-permute-done.9.last_queries = bf16[64,1280]{1,0:T(8,128)(2,1)S(1)} collective-permute-done((bf16[64,1280]{1,0:T(8,128)(2,1)S(1)}, bf16[64,1280]{1,0:T(8,128)(2,1)S(1)}, u32[]{:S(2)}, u32[]{:S(2)}) %collective-permute-start.9) | collective-permute-done | bytes 163872 | tf_op jit(solution)/shard_map/ppermute | solution.py:24
  30.6 1.3 %shard_map.106 = (f32[136,128]{1,0:T(8,128)S(1)}, bf16[144,128]{1,0:T(8,128)(2,1)S(1)}, bf16[144,128]{1,0:T(8,128)(2,1)S(1)}, bf16[144,128]{1,0:T(8,128)(2,1)S(1)}) custom-call(f32[2,136,128]{2,1,0:T(8,128)S(1)} %get-tuple-element.31.near, bf16[512,256]{1,0:T(8,128)(2,1)S(1)} %get-tuple-element.26.own, bf16[512,256]{1,0:T(8,128)(2,1)S(1)} %get-tuple-element.27.own_sent, ...), custom_call_target="tpu_custom_call" | custom-call | flops 402653184 | tf_op jit(solution)/shard_map/pallas_call | solution.py:458
  31.9 2.0 %collective-permute-start.10 = (bf16[144,128]{1,0:T(8,128)(2,1)S(1)}, bf16[144,128]{1,0:T(8,128)(2,1)S(1)}, u32[]{:S(2)}, u32[]{:S(2)}) collective-permute-start(bf16[144,128]{1,0:T(8,128)(2,1)S(1)} %get-tuple-element.36), channel_id=1, source_target_pairs={{0,1},{1,0},{2,3},{3,2},{4,5},{5,4},{6,7},{7,6},{8,9},{9,8},{10,11... | collective-permute-start | bytes 110600 | tf_op jit(solution)/shard_map/ppermute | solution.py:24
  34.0 1.1 %collective-permute-start.11 = (bf16[144,128]{1,0:T(8,128)(2,1)S(1)}, bf16[144,128]{1,0:T(8,128)(2,1)S(1)}, u32[]{:S(2)}, u32[]{:S(2)}) collective-permute-start(bf16[144,128]{1,0:T(8,128)(2,1)S(1)} %get-tuple-element.37), channel_id=1, source_target_pairs={{0,2},{1,3},{2,0},{3,1},{4,6},{5,7},{6,4},{7,5},{8,10},{9,11},{10,... | collective-permute-start | bytes 110600 | tf_op jit(solution)/shard_map/ppermute | solution.py:24
  35.1 1.3 %collective-permute-start.12 = (bf16[144,128]{1,0:T(8,128)(2,1)S(1)}, bf16[144,128]{1,0:T(8,128)(2,1)S(1)}, u32[]{:S(2)}, u32[]{:S(2)}) collective-permute-start(bf16[144,128]{1,0:T(8,128)(2,1)S(1)} %get-tuple-element.38), channel_id=1, source_target_pairs={{0,3},{1,2},{2,1},{3,0},{4,7},{5,6},{6,5},{7,4},{8,11},{9,10},{10,... | collective-permute-start | bytes 110600 | tf_op jit(solution)/shard_map/ppermute | solution.py:24
  36.4 2.8 %collective-permute-done.11.refs_1_ = bf16[144,128]{1,0:T(8,128)(2,1)S(1)} collective-permute-done((bf16[144,128]{1,0:T(8,128)(2,1)S(1)}, bf16[144,128]{1,0:T(8,128)(2,1)S(1)}, u32[]{:S(2)}, u32[]{:S(2)}) %collective-permute-start.11) | collective-permute-done | bytes 36896 | tf_op jit(solution)/shard_map/ppermute | solution.py:24
  39.2 1.6 %collective-permute-done.12.refs_2_ = bf16[144,128]{1,0:T(8,128)(2,1)S(1)} collective-permute-done((bf16[144,128]{1,0:T(8,128)(2,1)S(1)}, bf16[144,128]{1,0:T(8,128)(2,1)S(1)}, u32[]{:S(2)}, u32[]{:S(2)}) %collective-permute-start.12) | collective-permute-done | bytes 36896 | tf_op jit(solution)/shard_map/ppermute | solution.py:24
  40.9 0.6 %collective-permute-start.13 = (bf16[144,128]{1,0:T(8,128)(2,1)S(1)}, bf16[144,128]{1,0:T(8,128)(2,1)S(1)}, u32[]{:S(2)}, u32[]{:S(2)}) collective-permute-start(bf16[144,128]{1,0:T(8,128)(2,1)S(1)} %get-tuple-element.40), channel_id=1, source_target_pairs={{0,8},{4,12},{8,0},{12,4},{1,9},{5,13},{9,1},{13,5},{2,10},{6,14},... | collective-permute-start | bytes 110600 | tf_op jit(solution)/shard_map/ppermute | solution.py:24
  41.5 3.4 %collective-permute-done.13.arrived = bf16[144,128]{1,0:T(8,128)(2,1)S(1)} collective-permute-done((bf16[144,128]{1,0:T(8,128)(2,1)S(1)}, bf16[144,128]{1,0:T(8,128)(2,1)S(1)}, u32[]{:S(2)}, u32[]{:S(2)}) %collective-permute-start.13) | collective-permute-done | bytes 36896 | tf_op jit(solution)/shard_map/ppermute | solution.py:24
  45.0 0.3 shard_map.109.mine
  45.4 0.8 %collective-permute-done.14.arrived = bf16[128,128]{1,0:T(8,128)(2,1)S(1)} collective-permute-done((bf16[128,128]{1,0:T(8,128)(2,1)S(1)}, bf16[128,128]{1,0:T(8,128)(2,1)S(1)}, u32[]{:S(2)}, u32[]{:S(2)}) %collective-permute-start.14) | collective-permute-done | bytes 32800 | tf_op jit(solution)/shard_map/ppermute | solution.py:24
  46.2 1.4 %finish.1 = bf16[320,128]{1,0:T(8,128)(2,1)} custom-call(bf16[64,1280]{1,0:T(8,128)(2,1)S(1)} %shard_map.109.mine, bf16[128,128]{1,0:T(8,128)(2,1)S(1)} %collective-permute-done.14.arrived, bf16[256,1280]{1,0:T(8,128)(2,1)S(1)} %copy-done, bf16[320,1280]{1,0:T(8,128)(2,1)S(1)} %bitcast.7), custom_call_target="tpu_custom_call" | custom-call | tf_op jit(solution)/shard_map/finish/pallas_call | solution.py:569
  (27 shorter events, 0.4 us)
Async XLA Ops:
  0.0 13.7 %collective-permute-start.4 = (bf16[32,1280]{1,0:T(8,128)(2,1)}, bf16[32,1280]{1,0:T(8,128)(2,1)S(1)}, u32[]{:S(2)}, u32[]{:S(2)}) collective-permute-start(bf16[32,1280]{1,0:T(8,128)(2,1)} %queries.1), channel_id=1, source_target_pairs={{0,4},{4,0},{8,12},{12,8},{1,5},{5,1},{9,13},{13,9},{2,6},{6,2},{1... | collective-permute-start | bytes 245768 | tf_op jit(solution)/shard_map/ppermute | solution.py:24
  1.6 6.3 %collective-permute-start.1 = (bf16[2,32,256]{2,1,0:T(8,128)(2,1)S(1)}, bf16[2,32,256]{2,1,0:T(8,128)(2,1)S(1)}, u32[]{:S(2)}, u32[]{:S(2)}) collective-permute-start(bf16[2,32,256]{2,1,0:T(8,128)(2,1)S(1)} %get-tuple-element.43), channel_id=1, source_target_pairs={{0,3},{1,0},{2,1},{3,2},{4,7},{5,4},{6,5},{7,6},{8,11},{9,8},{10,9... | collective-permute-start | bytes 98312 | tf_op jit(solution)/shard_map/ppermute | solution.py:19
  6.2 5.7 %collective-permute-start = (bf16[2,32,256]{2,1,0:T(8,128)(2,1)S(1)}, bf16[2,32,256]{2,1,0:T(8,128)(2,1)S(1)}, u32[]{:S(2)}, u32[]{:S(2)}) collective-permute-start(bf16[2,32,256]{2,1,0:T(8,128)(2,1)S(1)} %get-tuple-element.44), channel_id=1, source_target_pairs={{0,1},{1,2},{2,3},{3,0},{4,5},{5,6},{6,7},{7,4},{8,9},{9,10},{10,1... | collective-permute-start | bytes 98312 | tf_op jit(solution)/shard_map/ppermute | solution.py:19
  12.0 3.4 %collective-permute-start.3 = (bf16[20,2,256]{2,1,0:T(2,128)(2,1)S(1)}, bf16[20,2,256]{2,1,0:T(2,128)(2,1)S(1)}, u32[]{:S(2)}, u32[]{:S(2)}) collective-permute-start(bf16[20,2,256]{2,1,0:T(2,128)(2,1)S(1)} %get-tuple-element.45), channel_id=1, source_target_pairs={{0,12},{4,8},{8,4},{12,0},{1,13},{5,9},{9,5},{13,1},{2,14},{6,10},... | collective-permute-start | bytes 61448 | tf_op jit(solution)/shard_map/ppermute | solution.py:507
  12.2 3.2 %collective-permute-start.2 = (bf16[20,2,256]{2,1,0:T(2,128)(2,1)S(1)}, bf16[20,2,256]{2,1,0:T(2,128)(2,1)S(1)}, u32[]{:S(2)}, u32[]{:S(2)}) collective-permute-start(bf16[20,2,256]{2,1,0:T(2,128)(2,1)S(1)} %get-tuple-element.46), channel_id=1, source_target_pairs={{0,4},{4,0},{8,12},{12,8},{1,5},{5,1},{9,13},{13,9},{2,6},{6,2},{1... | collective-permute-start | bytes 61448 | tf_op jit(solution)/shard_map/ppermute | solution.py:24
  13.7 5.4 %collective-permute-start.5 = (bf16[32,1280]{1,0:T(8,128)(2,1)S(1)}, bf16[32,1280]{1,0:T(8,128)(2,1)S(1)}, u32[]{:S(2)}, u32[]{:S(2)}) collective-permute-start(bf16[32,1280]{1,0:T(8,128)(2,1)S(1)} %shard_map.103), channel_id=1, source_target_pairs={{0,2},{1,3},{2,0},{3,1},{4,6},{5,7},{6,4},{7,5},{8,10},{9,11},{10,... | collective-permute-start | bytes 245768 | tf_op jit(solution)/shard_map/ppermute | solution.py:24
  15.5 1.3 %copy-start.1 = (bf16[3,3,256,256]{3,2,1,0:T(8,128)(2,1)S(1)}, bf16[3,3,256,256]{3,2,1,0:T(8,128)(2,1)}, u32[]{:S(2)}) copy-start(bf16[3,3,256,256]{3,2,1,0:T(8,128)(2,1)} %param.12) | copy-start | bytes 3538948
  16.7 0.7 %copy-start.4 = (f32[256]{0:T(256)S(1)}, f32[256]{0:T(256)}, u32[]{:S(2)}) copy-start(f32[256]{0:T(256)} %param.13) | copy-start | bytes 3076
  17.4 1.8 %copy-start.5 = (f32[256]{0:T(256)S(1)}, f32[256]{0:T(256)}, u32[]{:S(2)}) copy-start(f32[256]{0:T(256)} %param.15) | copy-start | bytes 3076
  19.1 6.1 %collective-permute-start.6 = (bf16[64,1280]{1,0:T(8,128)(2,1)S(1)}, bf16[64,1280]{1,0:T(8,128)(2,1)S(1)}, u32[]{:S(2)}, u32[]{:S(2)}) collective-permute-start(bf16[64,1280]{1,0:T(8,128)(2,1)S(1)} %pad_maximum_fusion.first_queries), channel_id=1, source_target_pairs={{0,1},{1,0},{2,3},{3,2},{4,5},{5,4},{6,7},{7,6},{8,9},{9,8},{10,11... | collective-permute-start | bytes 491528 | tf_op jit(solution)/shard_map/ppermute | solution.py:24
  19.2 6.5 %copy-start.3 = (bf16[256,1280]{1,0:T(8,128)(2,1)S(1)}, bf16[256,1280]{1,0:T(8,128)(2,1)}, u32[]{:S(2)}) copy-start(bf16[256,1280]{1,0:T(8,128)(2,1)} %weight.3) | copy-start | bytes 1966084
  20.4 6.3 %collective-permute-start.7 = (bf16[512,256]{1,0:T(8,128)(2,1)S(1)}, bf16[512,256]{1,0:T(8,128)(2,1)S(1)}, u32[]{:S(2)}, u32[]{:S(2)}) collective-permute-start(bf16[512,256]{1,0:T(8,128)(2,1)S(1)} %get-tuple-element.27.own_sent), channel_id=1, source_target_pairs={{0,4},{4,0},{8,12},{12,8},{1,5},{5,1},{9,13},{13,9},{2,6},{6,2},{1... | collective-permute-start | bytes 786440 | tf_op jit(solution)/shard_map/ppermute | solution.py:24
  20.4 7.7 %collective-permute-start.8 = (bf16[64,1280]{1,0:T(8,128)(2,1)S(1)}, bf16[64,1280]{1,0:T(8,128)(2,1)S(1)}, u32[]{:S(2)}, u32[]{:S(2)}) collective-permute-start(bf16[64,1280]{1,0:T(8,128)(2,1)S(1)} %pad_maximum_fusion.first_queries), channel_id=1, source_target_pairs={{0,8},{4,12},{8,0},{12,4},{1,9},{5,13},{9,1},{13,5},{2,10},{6,14},... | collective-permute-start | bytes 491528 | tf_op jit(solution)/shard_map/ppermute | solution.py:24
  25.2 5.3 %collective-permute-start.9 = (bf16[64,1280]{1,0:T(8,128)(2,1)S(1)}, bf16[64,1280]{1,0:T(8,128)(2,1)S(1)}, u32[]{:S(2)}, u32[]{:S(2)}) collective-permute-start(bf16[64,1280]{1,0:T(8,128)(2,1)S(1)} %collective-permute-done.6.last_queries), channel_id=1, source_target_pairs={{0,8},{4,12},{8,0},{12,4},{1,9},{5,13},{9,1},{13,5},{2,10},{6,14},... | collective-permute-start | bytes 491528 | tf_op jit(solution)/shard_map/ppermute | solution.py:24
  30.6 14.4 %copy-start = (bf16[256,1280]{1,0:T(8,128)(2,1)S(1)}, bf16[256,1280]{1,0:T(8,128)(2,1)}, u32[]{:S(2)}) copy-start(bf16[256,1280]{1,0:T(8,128)(2,1)} %value_weight.3) | copy-start | bytes 1966084
  31.9 14.3 %copy-start.2 = (bf16[1280,320]{0,1:T(8,128)(2,1)S(1)}, bf16[1280,320]{0,1:T(8,128)(2,1)}, u32[]{:S(2)}) copy-start(bf16[1280,320]{0,1:T(8,128)(2,1)} %param.19) | copy-start | bytes 2457604
  31.9 4.5 %collective-permute-start.10 = (bf16[144,128]{1,0:T(8,128)(2,1)S(1)}, bf16[144,128]{1,0:T(8,128)(2,1)S(1)}, u32[]{:S(2)}, u32[]{:S(2)}) collective-permute-start(bf16[144,128]{1,0:T(8,128)(2,1)S(1)} %get-tuple-element.36), channel_id=1, source_target_pairs={{0,1},{1,0},{2,3},{3,2},{4,5},{5,4},{6,7},{7,6},{8,9},{9,8},{10,11... | collective-permute-start | bytes 110600 | tf_op jit(solution)/shard_map/ppermute | solution.py:24
  34.0 5.3 %collective-permute-start.11 = (bf16[144,128]{1,0:T(8,128)(2,1)S(1)}, bf16[144,128]{1,0:T(8,128)(2,1)S(1)}, u32[]{:S(2)}, u32[]{:S(2)}) collective-permute-start(bf16[144,128]{1,0:T(8,128)(2,1)S(1)} %get-tuple-element.37), channel_id=1, source_target_pairs={{0,2},{1,3},{2,0},{3,1},{4,6},{5,7},{6,4},{7,5},{8,10},{9,11},{10,... | collective-permute-start | bytes 110600 | tf_op jit(solution)/shard_map/ppermute | solution.py:24
  35.1 5.8 %collective-permute-start.12 = (bf16[144,128]{1,0:T(8,128)(2,1)S(1)}, bf16[144,128]{1,0:T(8,128)(2,1)S(1)}, u32[]{:S(2)}, u32[]{:S(2)}) collective-permute-start(bf16[144,128]{1,0:T(8,128)(2,1)S(1)} %get-tuple-element.38), channel_id=1, source_target_pairs={{0,3},{1,2},{2,1},{3,0},{4,7},{5,6},{6,5},{7,4},{8,11},{9,10},{10,... | collective-permute-start | bytes 110600 | tf_op jit(solution)/shard_map/ppermute | solution.py:24
  40.9 4.0 %collective-permute-start.13 = (bf16[144,128]{1,0:T(8,128)(2,1)S(1)}, bf16[144,128]{1,0:T(8,128)(2,1)S(1)}, u32[]{:S(2)}, u32[]{:S(2)}) collective-permute-start(bf16[144,128]{1,0:T(8,128)(2,1)S(1)} %get-tuple-element.40), channel_id=1, source_target_pairs={{0,8},{4,12},{8,0},{12,4},{1,9},{5,13},{9,1},{13,5},{2,10},{6,14},... | collective-permute-start | bytes 110600 | tf_op jit(solution)/shard_map/ppermute | solution.py:24
  44.9 1.3 %collective-permute-start.14 = (bf16[128,128]{1,0:T(8,128)(2,1)S(1)}, bf16[128,128]{1,0:T(8,128)(2,1)S(1)}, u32[]{:S(2)}, u32[]{:S(2)}) collective-permute-start(bf16[128,128]{1,0:T(8,128)(2,1)S(1)} %shard_map.108.normalized), channel_id=1, source_target_pairs={{0,4},{4,0},{8,12},{12,8},{1,5},{5,1},{9,13},{13,9},{2,6},{6,2},{1... | collective-permute-start | bytes 98312 | tf_op jit(solution)/shard_map/ppermute | solution.py:24

commit v6 on v5

--- a/solution.py
+++ b/solution.py
@@ -334,10 +334,10 @@
 def hold_queries(held, parts):
     half = held.shape[0] // 8
     row = lax.axis_index("row")
-    for number, place in enumerate(PLACES):
-        part = parts[number // 2]
+    blocks = [(part, 2 * k * half) for part in parts for k in range(part.shape[0] // (2 * half))]
+    for (part, start), place in zip(blocks, PLACES):
         for parity in range(2):
-            source = (2 * (number % 2) + parity) * half
+            source = start + parity * half
             target = pl.multiple_of(parity * 4 * half + (row ^ place) * half, half)
             held[pl.ds(target, half), :] = part[source : source + half, :]
 
@@ -497,6 +497,7 @@
     )
     (queries,) = call(halve_kernel, [((size, width), half)], [queries, beside])
     two = flipped(queries, "row", 2)
+    one = flipped(queries, "row", 1)
     top = shifted(marked[height - HALO :], "row", 1)
     bottom = shifted(marked[:HALO], "row", -1)
     edge = lambda cut: jnp.concatenate([top[:, cut], marked[:, cut], bottom[:, cut]], axis=0)
@@ -506,10 +507,10 @@
     rounds = [(k, (k + 1 if k % 2 else k - 1) % cols) for k in range(cols)]
     crossed = lax.ppermute(jnp.where(even, *ends[::-1]), "col", rounds)
 
-    pair = jnp.concatenate([queries, two], axis=0)
-    far_pair = flipped(pair, "col", 2)
-    next_pair = flipped(pair, "row", 1)
-    last_pair = flipped(next_pair, "col", 2)
+    trio = jnp.concatenate([queries, two, one], axis=0)
+    far_trio = flipped(trio, "col", 2)
+    three = flipped(two, "row", 1)
+    far_three = flipped(three, "col", 2)
 
     count = flat - 2 * slot
     mid, weight = call(
@@ -537,7 +538,7 @@
     own_keys, own_scores, held_queries = call(
         own_kernel,
         [((cells, width), half), ((cells, block), wide), ((block, width), half)],
-        [own, own_sent, key_weight, pair, next_pair],
+        [own, own_sent, key_weight, trio, three],
         limit=6, flops=2 * cells * width * (channels + block),
     )
     near, other, other_keys = call(
@@ -550,7 +551,7 @@
         far_kernel, [(whole_block, wide)] + [(sent_block, half)] * 3,
         [
             near, own, own_sent, own_keys, other, other_sent, other_keys,
-            far_pair, last_pair,
+            far_trio, far_three,
         ],
         [((block, width), half), ((4,) + whole_block, wide)],
         limit=8, flops=score_flops,

time: 47.8 us -> 47.8 us (level)
  starting transfers between devices: 13.8 us -> 15.5 us
  waiting for transfers between devices: 22.1 us -> 20.5 us
    ppermute x12 -> x13, starting transfers between devices: 8.94 us -> 10.6 us  [flipped(): return lax.ppermute(array, axis, [(i, i ^ bit) for i in range(count)])]
    ppermute x12 -> x13, waiting for transfers between devices: 14.8 us -> 14 us  [flipped(): return lax.ppermute(array, axis, [(i, i ^ bit) for i in range(count)])]
    ppermute x1, waiting for transfers between devices: 1.68 us -> 0.86 us  [kernel_path(): crossed = lax.ppermute(jnp.where(even, *ends[::-1]), 'col', rounds)]
  transfers between devices with their start and end apart: 15 -> 16, of which waited for: 10 -> 10; matrix products, arithmetic and copies ran while one was open for 0% -> 0% of each run, Pallas kernels for 14% -> 14%
where the time goes in v6:
time: 47.8 us; the launch traced here: 47.6 us
  waiting for transfers between devices  20.5 us (43%)
  starting transfers between devices  15.5 us (32%)
  Pallas kernels  9.33 us (20%)
  local copies, waits for them, and re-layouts  2.02 us (4%)
    ppermute x13, waiting for transfers between devices, flipped(): return lax.ppermute(array, axis, [(i, i ^ bit) for i in range(count)])  14 us
    ppermute x13, starting transfers between devices, flipped(): return lax.ppermute(array, axis, [(i, i ^ bit) for i in range(count)])  10.6 us
    pallas_call x10, Pallas kernels, call(): pl.pallas_call(kernel, out_shape=[pltpu.VMEM(shape, dtype) for shape, dty...  7.96 us
    ppermute x2, waiting for transfers between devices, shifted(): lax.ppermute(array, axis, [(i, (i + step) % count) for i in range(count)])  5.66 us
    ppermute x2, starting transfers between devices, shifted(): lax.ppermute(array, axis, [(i, (i + step) % count) for i in range(count)])  4.64 us
    unnamed x12, local copies, waits for them, and re-layouts  1.97 us
    pallas_call x1, Pallas kernels, kernel_path(): pl.pallas_call(finish_kernel, out_shape=jax.ShapeDtypeStruct((out_weight....  1.37 us
  transfers between devices with their start and end apart: 16, of which 10 were waited for; matrix products, arithmetic and copies ran while one was open for 0% of the time, Pallas kernels for 14%

profile of v6, /device:TPU:0, one launch (start us, length us, event | category | flops | bytes accessed | tf_op | source)
XLA Modules:
  0.0 47.6 jit_solution(3181563187732292099)
XLA Ops:
  0.0 0.5 %collective-permute-start.4 = (bf16[32,1280]{1,0:T(8,128)(2,1)}, bf16[32,1280]{1,0:T(8,128)(2,1)S(1)}, u32[]{:S(2)}, u32[]{:S(2)}) collective-permute-start(bf16[32,1280]{1,0:T(8,128)(2,1)} %queries.1), channel_id=1, source_target_pairs={{0,4},{4,0},{8,12},{12,8},{1,5},{5,1},{9,13},{13,9},{2,6},{6,2},{1... | collective-permute-start | bytes 245768 | tf_op jit(solution)/shard_map/ppermute | solution.py:24
  0.5 1.1 %shard_map.100 = (bf16[16,32,256]{2,1,0:T(8,128)(2,1)S(1)}, bf16[32,1280]{1,0:T(8,128)(2,1)S(1)}) custom-call(bf16[16,32,256]{2,1,0:T(8,128)(2,1)} %features.1, s32[16,32]{1,0:T(8,128)} %tissue.1, bf16[32,1280]{1,0:T(8,128)(2,1)} %queries.1), custom_call_target="tpu_custom_call" | custom-call | flops 1048576 | tf_op jit(solution)/shard_map/pallas_call | solution.py:458
  1.6 4.6 %collective-permute-start.1 = (bf16[2,32,256]{2,1,0:T(8,128)(2,1)S(1)}, bf16[2,32,256]{2,1,0:T(8,128)(2,1)S(1)}, u32[]{:S(2)}, u32[]{:S(2)}) collective-permute-start(bf16[2,32,256]{2,1,0:T(8,128)(2,1)S(1)} %get-tuple-element.43), channel_id=1, source_target_pairs={{0,3},{1,0},{2,1},{3,2},{4,7},{5,4},{6,5},{7,6},{8,11},{9,8},{10,9... | collective-permute-start | bytes 98312 | tf_op jit(solution)/shard_map/ppermute | solution.py:19
  6.3 1.6 %collective-permute-done.1.bottom = bf16[2,32,256]{2,1,0:T(8,128)(2,1)S(1)} collective-permute-done((bf16[2,32,256]{2,1,0:T(8,128)(2,1)S(1)}, bf16[2,32,256]{2,1,0:T(8,128)(2,1)S(1)}, u32[]{:S(2)}, u32[]{:S(2)}) %collective-permute-start.1) | collective-permute-done | bytes 32800 | tf_op jit(solution)/shard_map/ppermute | solution.py:19
  7.9 4.0 %collective-permute-done.top = bf16[2,32,256]{2,1,0:T(8,128)(2,1)S(1)} collective-permute-done((bf16[2,32,256]{2,1,0:T(8,128)(2,1)S(1)}, bf16[2,32,256]{2,1,0:T(8,128)(2,1)S(1)}, u32[]{:S(2)}, u32[]{:S(2)}) %collective-permute-start) | collective-permute-done | bytes 32800 | tf_op jit(solution)/shard_map/ppermute | solution.py:19
  12.0 0.2 collective-permute-start.3
  12.2 1.4 %collective-permute-start.2 = (bf16[20,2,256]{2,1,0:T(2,128)(2,1)S(1)}, bf16[20,2,256]{2,1,0:T(2,128)(2,1)S(1)}, u32[]{:S(2)}, u32[]{:S(2)}) collective-permute-start(bf16[20,2,256]{2,1,0:T(2,128)(2,1)S(1)} %get-tuple-element.46), channel_id=1, source_target_pairs={{0,4},{4,0},{8,12},{12,8},{1,5},{5,1},{9,13},{13,9},{2,6},{6,2},{1... | collective-permute-start | bytes 61448 | tf_op jit(solution)/shard_map/ppermute | solution.py:24
  13.8 0.8 %collective-permute-start.5 = (bf16[32,1280]{1,0:T(8,128)(2,1)S(1)}, bf16[32,1280]{1,0:T(8,128)(2,1)S(1)}, u32[]{:S(2)}, u32[]{:S(2)}) collective-permute-start(bf16[32,1280]{1,0:T(8,128)(2,1)S(1)} %shard_map.103), channel_id=1, source_target_pairs={{0,2},{1,3},{2,0},{3,1},{4,6},{5,7},{6,4},{7,5},{8,10},{9,11},{10,... | collective-permute-start | bytes 245768 | tf_op jit(solution)/shard_map/ppermute | solution.py:24
  14.6 0.9 %collective-permute-done.3.crossed = bf16[20,2,256]{2,1,0:T(2,128)(2,1)S(1)} collective-permute-done((bf16[20,2,256]{2,1,0:T(2,128)(2,1)S(1)}, bf16[20,2,256]{2,1,0:T(2,128)(2,1)S(1)}, u32[]{:S(2)}, u32[]{:S(2)}) %collective-permute-start.3) | collective-permute-done | bytes 20512 | tf_op jit(solution)/shard_map/ppermute | solution.py:508
  15.5 1.3 %copy-done.1 = bf16[3,3,256,256]{3,2,1,0:T(8,128)(2,1)S(1)} copy-done((bf16[3,3,256,256]{3,2,1,0:T(8,128)(2,1)S(1)}, bf16[3,3,256,256]{3,2,1,0:T(8,128)(2,1)}, u32[]{:S(2)}) %copy-start.1) | copy-done | bytes 1179672
  16.7 0.7 %copy-done.4 = f32[256]{0:T(256)S(1)} copy-done((f32[256]{0:T(256)S(1)}, f32[256]{0:T(256)}, u32[]{:S(2)}) %copy-start.4) | copy-done | bytes 1048
  17.4 1.5 %shard_map.101 = (f32[896,256]{1,0:T(8,128)S(1)}, bf16[3,768,256]{2,1,0:T(8,128)(2,1)S(1)}) custom-call(bf16[16,32,256]{2,1,0:T(8,128)(2,1)S(1)} %get-tuple-element.23.marked, bf16[2,32,256]{2,1,0:T(8,128)(2,1)S(1)} %collective-permute-done.top, bf16[2,32,256]{2,1,0:T(8,128)(2,1)S(1)} %collective-permute-done.1.bottom, ...), custom_call_target="tpu_custom_call" | custom-call | flops 704643072 | tf_op jit(solution)/shard_map/pallas_call | solution.py:458
  19.0 1.1 %shard_map.102 = (bf16[512,256]{1,0:T(8,128)(2,1)S(1)}, bf16[512,256]{1,0:T(8,128)(2,1)S(1)}) custom-call(bf16[16,32,256]{2,1,0:T(8,128)(2,1)S(1)} %get-tuple-element.23.marked, f32[896,256]{1,0:T(8,128)S(1)} %get-tuple-element.24.mid, bf16[3,768,256]{2,1,0:T(8,128)(2,1)S(1)} %get-tuple-element.25.second, f32[1,256]{1,0:T(1,128)S(1)} %bitcast.9), custom_call_target="tpu_custom_call" | custom-call | flops 603979776 | tf_op jit(solution)/shard_map/pallas_call | solution.py:458
  20.1 0.2 collective-permute-start.8
  20.3 0.7 %collective-permute-done.5 = bf16[32,1280]{1,0:T(8,128)(2,1)S(1)} collective-permute-done((bf16[32,1280]{1,0:T(8,128)(2,1)S(1)}, bf16[32,1280]{1,0:T(8,128)(2,1)S(1)}, u32[]{:S(2)}, u32[]{:S(2)}) %collective-permute-start.5) | collective-permute-done | bytes 81952 | tf_op jit(solution)/shard_map/ppermute | solution.py:24
  21.0 0.7 %collective-permute-start.9 = (bf16[96,1280]{1,0:T(8,128)(2,1)S(1)}, bf16[96,1280]{1,0:T(8,128)(2,1)S(1)}, u32[]{:S(2)}, u32[]{:S(2)}) collective-permute-start(bf16[96,1280]{1,0:T(8,128)(2,1)S(1)} %pad_maximum_fusion.first_queries), channel_id=1, source_target_pairs={{0,8},{4,12},{8,0},{12,4},{1,9},{5,13},{9,1},{13,5},{2,10},{6,14},... | collective-permute-start | bytes 737288 | tf_op jit(solution)/shard_map/ppermute | solution.py:24
  21.8 4.4 %collective-permute-done.7.last_queries = bf16[32,1280]{1,0:T(8,128)(2,1)S(1)} collective-permute-done((bf16[32,1280]{1,0:T(8,128)(2,1)S(1)}, bf16[32,1280]{1,0:T(8,128)(2,1)S(1)}, u32[]{:S(2)}, u32[]{:S(2)}) %collective-permute-start.7) | collective-permute-done | bytes 81952 | tf_op jit(solution)/shard_map/ppermute | solution.py:24
  26.2 1.3 %collective-permute-start.10 = (bf16[32,1280]{1,0:T(8,128)(2,1)S(1)}, bf16[32,1280]{1,0:T(8,128)(2,1)S(1)}, u32[]{:S(2)}, u32[]{:S(2)}) collective-permute-start(bf16[32,1280]{1,0:T(8,128)(2,1)S(1)} %collective-permute-done.7.last_queries), channel_id=1, source_target_pairs={{0,8},{4,12},{8,0},{12,4},{1,9},{5,13},{9,1},{13,5},{2,10},{6,14},... | collective-permute-start | bytes 245768 | tf_op jit(solution)/shard_map/ppermute | solution.py:24
  27.5 1.0 %shard_map.104 = (bf16[512,1280]{1,0:T(8,128)(2,1)S(1)}, f32[512,128]{1,0:T(8,128)S(1)}, bf16[128,1280]{1,0:T(8,128)(2,1)S(1)}) custom-call(bf16[512,256]{1,0:T(8,128)(2,1)S(1)} %get-tuple-element.26.own, bf16[512,256]{1,0:T(8,128)(2,1)S(1)} %get-tuple-element.27.own_sent, bf16[256,1280]{1,0:T(8,128)(2,1)S(1)} %copy-done.3, ...), custom_call_target="tpu_custom_call" | custom-call | flops 503316480 | tf_op jit(solution)/shard_map/pallas_call | solution.py:458
  28.5 1.5 %shard_map.105 = (f32[2,136,128]{2,1,0:T(8,128)S(1)}, bf16[512,256]{1,0:T(8,128)(2,1)S(1)}, bf16[512,1280]{1,0:T(8,128)(2,1)S(1)}) custom-call(bf16[512,256]{1,0:T(8,128)(2,1)S(1)} %get-tuple-element.26.own, f32[512,128]{1,0:T(8,128)S(1)} %get-tuple-element.29.own_scores, bf16[512,256]{1,0:T(8,128)(2,1)S(1)} %collective-permute-done.8.other_sent, ...), custom_call_target="tpu_custom_call" | custom-call | flops 402653184 | tf_op jit(solution)/shard_map/pallas_call | solution.py:458
  30.0 0.6 %collective-permute-done.10.last_queries = bf16[32,1280]{1,0:T(8,128)(2,1)S(1)} collective-permute-done((bf16[32,1280]{1,0:T(8,128)(2,1)S(1)}, bf16[32,1280]{1,0:T(8,128)(2,1)S(1)}, u32[]{:S(2)}, u32[]{:S(2)}) %collective-permute-start.10) | collective-permute-done | bytes 81952 | tf_op jit(solution)/shard_map/ppermute | solution.py:24
  30.6 1.3 %shard_map.106 = (f32[136,128]{1,0:T(8,128)S(1)}, bf16[144,128]{1,0:T(8,128)(2,1)S(1)}, bf16[144,128]{1,0:T(8,128)(2,1)S(1)}, bf16[144,128]{1,0:T(8,128)(2,1)S(1)}) custom-call(f32[2,136,128]{2,1,0:T(8,128)S(1)} %get-tuple-element.31.near, bf16[512,256]{1,0:T(8,128)(2,1)S(1)} %get-tuple-element.26.own, bf16[512,256]{1,0:T(8,128)(2,1)S(1)} %get-tuple-element.27.own_sent, ...), custom_call_target="tpu_custom_call" | custom-call | flops 402653184 | tf_op jit(solution)/shard_map/pallas_call | solution.py:458
  32.0 0.4 collective-permute-start.11
  32.3 2.8 %collective-permute-start.12 = (bf16[144,128]{1,0:T(8,128)(2,1)S(1)}, bf16[144,128]{1,0:T(8,128)(2,1)S(1)}, u32[]{:S(2)}, u32[]{:S(2)}) collective-permute-start(bf16[144,128]{1,0:T(8,128)(2,1)S(1)} %get-tuple-element.37), channel_id=1, source_target_pairs={{0,2},{1,3},{2,0},{3,1},{4,6},{5,7},{6,4},{7,5},{8,10},{9,11},{10,... | collective-permute-start | bytes 110600 | tf_op jit(solution)/shard_map/ppermute | solution.py:24
  35.1 1.3 %collective-permute-start.13 = (bf16[144,128]{1,0:T(8,128)(2,1)S(1)}, bf16[144,128]{1,0:T(8,128)(2,1)S(1)}, u32[]{:S(2)}, u32[]{:S(2)}) collective-permute-start(bf16[144,128]{1,0:T(8,128)(2,1)S(1)} %get-tuple-element.38), channel_id=1, source_target_pairs={{0,3},{1,2},{2,1},{3,0},{4,7},{5,6},{6,5},{7,4},{8,11},{9,10},{10,... | collective-permute-start | bytes 110600 | tf_op jit(solution)/shard_map/ppermute | solution.py:24
  36.4 0.9 %collective-permute-done.12.refs_1_ = bf16[144,128]{1,0:T(8,128)(2,1)S(1)} collective-permute-done((bf16[144,128]{1,0:T(8,128)(2,1)S(1)}, bf16[144,128]{1,0:T(8,128)(2,1)S(1)}, u32[]{:S(2)}, u32[]{:S(2)}) %collective-permute-start.12) | collective-permute-done | bytes 36896 | tf_op jit(solution)/shard_map/ppermute | solution.py:24
  37.3 3.5 %collective-permute-done.13.refs_2_ = bf16[144,128]{1,0:T(8,128)(2,1)S(1)} collective-permute-done((bf16[144,128]{1,0:T(8,128)(2,1)S(1)}, bf16[144,128]{1,0:T(8,128)(2,1)S(1)}, u32[]{:S(2)}, u32[]{:S(2)}) %collective-permute-start.13) | collective-permute-done | bytes 36896 | tf_op jit(solution)/shard_map/ppermute | solution.py:24
  40.9 1.0 %collective-permute-start.14 = (bf16[144,128]{1,0:T(8,128)(2,1)S(1)}, bf16[144,128]{1,0:T(8,128)(2,1)S(1)}, u32[]{:S(2)}, u32[]{:S(2)}) collective-permute-start(bf16[144,128]{1,0:T(8,128)(2,1)S(1)} %get-tuple-element.40), channel_id=1, source_target_pairs={{0,8},{4,12},{8,0},{12,4},{1,9},{5,13},{9,1},{13,5},{2,10},{6,14},... | collective-permute-start | bytes 110600 | tf_op jit(solution)/shard_map/ppermute | solution.py:24
  41.9 3.0 %collective-permute-done.14.arrived = bf16[144,128]{1,0:T(8,128)(2,1)S(1)} collective-permute-done((bf16[144,128]{1,0:T(8,128)(2,1)S(1)}, bf16[144,128]{1,0:T(8,128)(2,1)S(1)}, u32[]{:S(2)}, u32[]{:S(2)}) %collective-permute-start.14) | collective-permute-done | bytes 36896 | tf_op jit(solution)/shard_map/ppermute | solution.py:24
  45.0 0.3 shard_map.109.mine
  45.4 0.8 %collective-permute-done.15.arrived = bf16[128,128]{1,0:T(8,128)(2,1)S(1)} collective-permute-done((bf16[128,128]{1,0:T(8,128)(2,1)S(1)}, bf16[128,128]{1,0:T(8,128)(2,1)S(1)}, u32[]{:S(2)}, u32[]{:S(2)}) %collective-permute-start.15) | collective-permute-done | bytes 32800 | tf_op jit(solution)/shard_map/ppermute | solution.py:24
  46.2 1.4 %finish.1 = bf16[320,128]{1,0:T(8,128)(2,1)} custom-call(bf16[64,1280]{1,0:T(8,128)(2,1)S(1)} %shard_map.109.mine, bf16[128,128]{1,0:T(8,128)(2,1)S(1)} %collective-permute-done.15.arrived, bf16[256,1280]{1,0:T(8,128)(2,1)S(1)} %copy-done, bf16[320,1280]{1,0:T(8,128)(2,1)S(1)} %bitcast.7), custom_call_target="tpu_custom_call" | custom-call | tf_op jit(solution)/shard_map/finish/pallas_call | solution.py:570
  (29 shorter events, 0.5 us)
Async XLA Ops:
  0.0 13.7 %collective-permute-start.4 = (bf16[32,1280]{1,0:T(8,128)(2,1)}, bf16[32,1280]{1,0:T(8,128)(2,1)S(1)}, u32[]{:S(2)}, u32[]{:S(2)}) collective-permute-start(bf16[32,1280]{1,0:T(8,128)(2,1)} %queries.1), channel_id=1, source_target_pairs={{0,4},{4,0},{8,12},{12,8},{1,5},{5,1},{9,13},{13,9},{2,6},{6,2},{1... | collective-permute-start | bytes 245768 | tf_op jit(solution)/shard_map/ppermute | solution.py:24
  1.6 6.3 %collective-permute-start.1 = (bf16[2,32,256]{2,1,0:T(8,128)(2,1)S(1)}, bf16[2,32,256]{2,1,0:T(8,128)(2,1)S(1)}, u32[]{:S(2)}, u32[]{:S(2)}) collective-permute-start(bf16[2,32,256]{2,1,0:T(8,128)(2,1)S(1)} %get-tuple-element.43), channel_id=1, source_target_pairs={{0,3},{1,0},{2,1},{3,2},{4,7},{5,4},{6,5},{7,6},{8,11},{9,8},{10,9... | collective-permute-start | bytes 98312 | tf_op jit(solution)/shard_map/ppermute | solution.py:19
  6.2 5.7 %collective-permute-start = (bf16[2,32,256]{2,1,0:T(8,128)(2,1)S(1)}, bf16[2,32,256]{2,1,0:T(8,128)(2,1)S(1)}, u32[]{:S(2)}, u32[]{:S(2)}) collective-permute-start(bf16[2,32,256]{2,1,0:T(8,128)(2,1)S(1)} %get-tuple-element.44), channel_id=1, source_target_pairs={{0,1},{1,2},{2,3},{3,0},{4,5},{5,6},{6,7},{7,4},{8,9},{9,10},{10,1... | collective-permute-start | bytes 98312 | tf_op jit(solution)/shard_map/ppermute | solution.py:19
  12.0 3.4 %collective-permute-start.3 = (bf16[20,2,256]{2,1,0:T(2,128)(2,1)S(1)}, bf16[20,2,256]{2,1,0:T(2,128)(2,1)S(1)}, u32[]{:S(2)}, u32[]{:S(2)}) collective-permute-start(bf16[20,2,256]{2,1,0:T(2,128)(2,1)S(1)} %get-tuple-element.45), channel_id=1, source_target_pairs={{0,12},{4,8},{8,4},{12,0},{1,13},{5,9},{9,5},{13,1},{2,14},{6,10},... | collective-permute-start | bytes 61448 | tf_op jit(solution)/shard_map/ppermute | solution.py:508
  12.2 3.2 %collective-permute-start.2 = (bf16[20,2,256]{2,1,0:T(2,128)(2,1)S(1)}, bf16[20,2,256]{2,1,0:T(2,128)(2,1)S(1)}, u32[]{:S(2)}, u32[]{:S(2)}) collective-permute-start(bf16[20,2,256]{2,1,0:T(2,128)(2,1)S(1)} %get-tuple-element.46), channel_id=1, source_target_pairs={{0,4},{4,0},{8,12},{12,8},{1,5},{5,1},{9,13},{13,9},{2,6},{6,2},{1... | collective-permute-start | bytes 61448 | tf_op jit(solution)/shard_map/ppermute | solution.py:24
  13.7 6.6 %collective-permute-start.6 = (bf16[32,1280]{1,0:T(8,128)(2,1)S(1)}, bf16[32,1280]{1,0:T(8,128)(2,1)S(1)}, u32[]{:S(2)}, u32[]{:S(2)}) collective-permute-start(bf16[32,1280]{1,0:T(8,128)(2,1)S(1)} %shard_map.103), channel_id=1, source_target_pairs={{0,1},{1,0},{2,3},{3,2},{4,5},{5,4},{6,7},{7,6},{8,9},{9,8},{10,11... | collective-permute-start | bytes 245768 | tf_op jit(solution)/shard_map/ppermute | solution.py:24
  13.8 7.2 %collective-permute-start.5 = (bf16[32,1280]{1,0:T(8,128)(2,1)S(1)}, bf16[32,1280]{1,0:T(8,128)(2,1)S(1)}, u32[]{:S(2)}, u32[]{:S(2)}) collective-permute-start(bf16[32,1280]{1,0:T(8,128)(2,1)S(1)} %shard_map.103), channel_id=1, source_target_pairs={{0,2},{1,3},{2,0},{3,1},{4,6},{5,7},{6,4},{7,5},{8,10},{9,11},{10,... | collective-permute-start | bytes 245768 | tf_op jit(solution)/shard_map/ppermute | solution.py:24
  15.5 1.3 %copy-start.1 = (bf16[3,3,256,256]{3,2,1,0:T(8,128)(2,1)S(1)}, bf16[3,3,256,256]{3,2,1,0:T(8,128)(2,1)}, u32[]{:S(2)}) copy-start(bf16[3,3,256,256]{3,2,1,0:T(8,128)(2,1)} %param.12) | copy-start | bytes 3538948
  16.7 0.7 %copy-start.4 = (f32[256]{0:T(256)S(1)}, f32[256]{0:T(256)}, u32[]{:S(2)}) copy-start(f32[256]{0:T(256)} %param.13) | copy-start | bytes 3076
  17.4 1.5 %copy-start.5 = (f32[256]{0:T(256)S(1)}, f32[256]{0:T(256)}, u32[]{:S(2)}) copy-start(f32[256]{0:T(256)} %param.15) | copy-start | bytes 3076
  18.9 8.5 %copy-start.3 = (bf16[256,1280]{1,0:T(8,128)(2,1)S(1)}, bf16[256,1280]{1,0:T(8,128)(2,1)}, u32[]{:S(2)}) copy-start(bf16[256,1280]{1,0:T(8,128)(2,1)} %weight.3) | copy-start | bytes 1966084
  20.1 8.4 %collective-permute-start.8 = (bf16[512,256]{1,0:T(8,128)(2,1)S(1)}, bf16[512,256]{1,0:T(8,128)(2,1)S(1)}, u32[]{:S(2)}, u32[]{:S(2)}) collective-permute-start(bf16[512,256]{1,0:T(8,128)(2,1)S(1)} %get-tuple-element.27.own_sent), channel_id=1, source_target_pairs={{0,4},{4,0},{8,12},{12,8},{1,5},{5,1},{9,13},{13,9},{2,6},{6,2},{1... | collective-permute-start | bytes 786440 | tf_op jit(solution)/shard_map/ppermute | solution.py:24
  21.0 9.7 %collective-permute-start.9 = (bf16[96,1280]{1,0:T(8,128)(2,1)S(1)}, bf16[96,1280]{1,0:T(8,128)(2,1)S(1)}, u32[]{:S(2)}, u32[]{:S(2)}) collective-permute-start(bf16[96,1280]{1,0:T(8,128)(2,1)S(1)} %pad_maximum_fusion.first_queries), channel_id=1, source_target_pairs={{0,8},{4,12},{8,0},{12,4},{1,9},{5,13},{9,1},{13,5},{2,10},{6,14},... | collective-permute-start | bytes 737288 | tf_op jit(solution)/shard_map/ppermute | solution.py:24
  21.6 4.5 %collective-permute-start.7 = (bf16[32,1280]{1,0:T(8,128)(2,1)S(1)}, bf16[32,1280]{1,0:T(8,128)(2,1)S(1)}, u32[]{:S(2)}, u32[]{:S(2)}) collective-permute-start(bf16[32,1280]{1,0:T(8,128)(2,1)S(1)} %collective-permute-done.5), channel_id=1, source_target_pairs={{0,1},{1,0},{2,3},{3,2},{4,5},{5,4},{6,7},{7,6},{8,9},{9,8},{10,11... | collective-permute-start | bytes 245768 | tf_op jit(solution)/shard_map/ppermute | solution.py:24
  26.2 4.4 %collective-permute-start.10 = (bf16[32,1280]{1,0:T(8,128)(2,1)S(1)}, bf16[32,1280]{1,0:T(8,128)(2,1)S(1)}, u32[]{:S(2)}, u32[]{:S(2)}) collective-permute-start(bf16[32,1280]{1,0:T(8,128)(2,1)S(1)} %collective-permute-done.7.last_queries), channel_id=1, source_target_pairs={{0,8},{4,12},{8,0},{12,4},{1,9},{5,13},{9,1},{13,5},{2,10},{6,14},... | collective-permute-start | bytes 245768 | tf_op jit(solution)/shard_map/ppermute | solution.py:24
  30.6 14.4 %copy-start = (bf16[256,1280]{1,0:T(8,128)(2,1)S(1)}, bf16[256,1280]{1,0:T(8,128)(2,1)}, u32[]{:S(2)}) copy-start(bf16[256,1280]{1,0:T(8,128)(2,1)} %value_weight.3) | copy-start | bytes 1966084
  32.0 14.3 %copy-start.2 = (bf16[1280,320]{0,1:T(8,128)(2,1)S(1)}, bf16[1280,320]{0,1:T(8,128)(2,1)}, u32[]{:S(2)}) copy-start(bf16[1280,320]{0,1:T(8,128)(2,1)} %param.19) | copy-start | bytes 2457604
  32.0 4.5 %collective-permute-start.11 = (bf16[144,128]{1,0:T(8,128)(2,1)S(1)}, bf16[144,128]{1,0:T(8,128)(2,1)S(1)}, u32[]{:S(2)}, u32[]{:S(2)}) collective-permute-start(bf16[144,128]{1,0:T(8,128)(2,1)S(1)} %get-tuple-element.36), channel_id=1, source_target_pairs={{0,1},{1,0},{2,3},{3,2},{4,5},{5,4},{6,7},{7,6},{8,9},{9,8},{10,11... | collective-permute-start | bytes 110600 | tf_op jit(solution)/shard_map/ppermute | solution.py:24
  32.3 5.0 %collective-permute-start.12 = (bf16[144,128]{1,0:T(8,128)(2,1)S(1)}, bf16[144,128]{1,0:T(8,128)(2,1)S(1)}, u32[]{:S(2)}, u32[]{:S(2)}) collective-permute-start(bf16[144,128]{1,0:T(8,128)(2,1)S(1)} %get-tuple-element.37), channel_id=1, source_target_pairs={{0,2},{1,3},{2,0},{3,1},{4,6},{5,7},{6,4},{7,5},{8,10},{9,11},{10,... | collective-permute-start | bytes 110600 | tf_op jit(solution)/shard_map/ppermute | solution.py:24
  35.1 5.8 %collective-permute-start.13 = (bf16[144,128]{1,0:T(8,128)(2,1)S(1)}, bf16[144,128]{1,0:T(8,128)(2,1)S(1)}, u32[]{:S(2)}, u32[]{:S(2)}) collective-permute-start(bf16[144,128]{1,0:T(8,128)(2,1)S(1)} %get-tuple-element.38), channel_id=1, source_target_pairs={{0,3},{1,2},{2,1},{3,0},{4,7},{5,6},{6,5},{7,4},{8,11},{9,10},{10,... | collective-permute-start | bytes 110600 | tf_op jit(solution)/shard_map/ppermute | solution.py:24
  40.9 4.0 %collective-permute-start.14 = (bf16[144,128]{1,0:T(8,128)(2,1)S(1)}, bf16[144,128]{1,0:T(8,128)(2,1)S(1)}, u32[]{:S(2)}, u32[]{:S(2)}) collective-permute-start(bf16[144,128]{1,0:T(8,128)(2,1)S(1)} %get-tuple-element.40), channel_id=1, source_target_pairs={{0,8},{4,12},{8,0},{12,4},{1,9},{5,13},{9,1},{13,5},{2,10},{6,14},... | collective-permute-start | bytes 110600 | tf_op jit(solution)/shard_map/ppermute | solution.py:24
  45.0 1.3 %collective-permute-start.15 = (bf16[128,128]{1,0:T(8,128)(2,1)S(1)}, bf16[128,128]{1,0:T(8,128)(2,1)S(1)}, u32[]{:S(2)}, u32[]{:S(2)}) collective-permute-start(bf16[128,128]{1,0:T(8,128)(2,1)S(1)} %shard_map.108.normalized), channel_id=1, source_target_pairs={{0,4},{4,0},{8,12},{12,8},{1,5},{5,1},{9,13},{13,9},{2,6},{6,2},{1... | collective-permute-start | bytes 98312 | tf_op jit(solution)/shard_map/ppermute | solution.py:24

commit v7 on v6

--- a/solution.py
+++ b/solution.py
@@ -379,9 +379,10 @@
     )
 
 
-def own_kernel(own, own_sent, weight, first_queries, last_queries, keys, scores, held):
+def own_kernel(own, own_sent, weight, *refs):
+    *queries, keys, scores, held = refs
     key_kernel(own, weight, keys)
-    hold_queries(held, (first_queries, last_queries))
+    hold_queries(held, queries)
     scores[...] = masked_scores(held, own_sent, keys)
 
 
@@ -395,13 +396,13 @@
 
 
 def far_kernel(
-    near, own, own_sent, own_keys, other, other_sent, other_keys, first_queries, last_queries,
-    kept, send_1, send_2, send_3, held, blocks,
+    near, own, own_sent, own_keys, other, other_sent, other_keys, *refs
 ):
+    *queries, kept, send_1, send_2, send_3, held, blocks = refs
     row, across = lax.axis_index("row"), lax.axis_index("col") // 2
     for parity in range(2):
         blocks[2 * across + parity] = near[parity]
-    hold_queries(held, (first_queries, last_queries))
+    hold_queries(held, queries)
     scores = (
         masked_scores(held, own_sent, own_keys), masked_scores(held, other_sent, other_keys)
     )
@@ -496,6 +497,7 @@
         far=(0, 1, 2), flops=1 << 20,
     )
     (queries,) = call(halve_kernel, [((size, width), half)], [queries, beside])
+    far_queries = flipped(queries, "col", 2)
     two = flipped(queries, "row", 2)
     one = flipped(queries, "row", 1)
     top = shifted(marked[height - HALO :], "row", 1)
@@ -507,8 +509,8 @@
     rounds = [(k, (k + 1 if k % 2 else k - 1) % cols) for k in range(cols)]
     crossed = lax.ppermute(jnp.where(even, *ends[::-1]), "col", rounds)
 
-    trio = jnp.concatenate([queries, two, one], axis=0)
-    far_trio = flipped(trio, "col", 2)
+    pair = jnp.concatenate([two, one], axis=0)
+    far_pair = flipped(pair, "col", 2)
     three = flipped(two, "row", 1)
     far_three = flipped(three, "col", 2)
 
@@ -538,7 +540,7 @@
     own_keys, own_scores, held_queries = call(
         own_kernel,
         [((cells, width), half), ((cells, block), wide), ((block, width), half)],
-        [own, own_sent, key_weight, trio, three],
+        [own, own_sent, key_weight, queries, pair, three],
         limit=6, flops=2 * cells * width * (channels + block),
     )
     near, other, other_keys = call(
@@ -551,7 +553,7 @@
         far_kernel, [(whole_block, wide)] + [(sent_block, half)] * 3,
         [
             near, own, own_sent, own_keys, other, other_sent, other_keys,
-            far_trio, far_three,
+            far_queries, far_pair, far_three,
         ],
         [((block, width), half), ((4,) + whole_block, wide)],
         limit=8, flops=score_flops,

time: 47.8 us -> 50.2 us (1.050)
  starting transfers between devices: 15.5 us -> 17.5 us
    ppermute x13 -> x14, starting transfers between devices: 10.6 us -> 12.6 us  [flipped(): return lax.ppermute(array, axis, [(i, i ^ bit) for i in range(count)])]
    ppermute x1, waiting for transfers between devices: 0.86 us -> 1.68 us  [kernel_path(): crossed = lax.ppermute(jnp.where(even, *ends[::-1]), 'col', rounds)]
    ppermute x13 -> x14, waiting for transfers between devices: 14 us -> 13.6 us  [flipped(): return lax.ppermute(array, axis, [(i, i ^ bit) for i in range(count)])]
    unnamed x12 -> x13, local copies, waits for them, and re-layouts: 1.97 us -> 1.98 us
  transfers between devices with their start and end apart: 16 -> 17, of which waited for: 10 -> 10; matrix products, arithmetic and copies ran while one was open for 0% -> 0% of each run, Pallas kernels for 14% -> 13%
where the time goes in v7:
time: 50.2 us; the launch traced here: 50 us
  waiting for transfers between devices  20.9 us (42%)
  starting transfers between devices  17.5 us (35%)
  Pallas kernels  9.32 us (19%)
  local copies, waits for them, and re-layouts  2.03 us (4%)
    ppermute x14, waiting for transfers between devices, flipped(): return lax.ppermute(array, axis, [(i, i ^ bit) for i in range(count)])  13.6 us
    ppermute x14, starting transfers between devices, flipped(): return lax.ppermute(array, axis, [(i, i ^ bit) for i in range(count)])  12.6 us
    pallas_call x10, Pallas kernels, call(): pl.pallas_call(kernel, out_shape=[pltpu.VMEM(shape, dtype) for shape, dty...  7.95 us
    ppermute x2, waiting for transfers between devices, shifted(): lax.ppermute(array, axis, [(i, (i + step) % count) for i in range(count)])  5.66 us
    ppermute x2, starting transfers between devices, shifted(): lax.ppermute(array, axis, [(i, (i + step) % count) for i in range(count)])  4.64 us
    unnamed x13, local copies, waits for them, and re-layouts  1.98 us
    ppermute x1, waiting for transfers between devices, kernel_path(): crossed = lax.ppermute(jnp.where(even, *ends[::-1]), 'col', rounds)  1.68 us
    pallas_call x1, Pallas kernels, kernel_path(): pl.pallas_call(finish_kernel, out_shape=jax.ShapeDtypeStruct((out_weight....  1.37 us
  transfers between devices with their start and end apart: 17, of which 10 were waited for; matrix products, arithmetic and copies ran while one was open for 0% of the time, Pallas kernels for 13%

profile of v7, /device:TPU:0, one launch (start us, length us, event | category | flops | bytes accessed | tf_op | source)
XLA Modules:
  0.0 50.0 jit_solution(15463521603447196276)
XLA Ops:
  0.0 0.5 collective-permute-start.4
  0.5 1.1 %shard_map.100 = (bf16[16,32,256]{2,1,0:T(8,128)(2,1)S(1)}, bf16[32,1280]{1,0:T(8,128)(2,1)S(1)}) custom-call(bf16[16,32,256]{2,1,0:T(8,128)(2,1)} %features.1, s32[16,32]{1,0:T(8,128)} %tissue.1, bf16[32,1280]{1,0:T(8,128)(2,1)} %queries.1), custom_call_target="tpu_custom_call" | custom-call | flops 1048576 | tf_op jit(solution)/shard_map/pallas_call | solution.py:459
  1.6 4.6 %collective-permute-start.1 = (bf16[2,32,256]{2,1,0:T(8,128)(2,1)S(1)}, bf16[2,32,256]{2,1,0:T(8,128)(2,1)S(1)}, u32[]{:S(2)}, u32[]{:S(2)}) collective-permute-start(bf16[2,32,256]{2,1,0:T(8,128)(2,1)S(1)} %get-tuple-element.43), channel_id=1, source_target_pairs={{0,3},{1,0},{2,1},{3,2},{4,7},{5,4},{6,5},{7,6},{8,11},{9,8},{10,9... | collective-permute-start | bytes 98312 | tf_op jit(solution)/shard_map/ppermute | solution.py:19
  6.3 1.6 %collective-permute-done.1.bottom = bf16[2,32,256]{2,1,0:T(8,128)(2,1)S(1)} collective-permute-done((bf16[2,32,256]{2,1,0:T(8,128)(2,1)S(1)}, bf16[2,32,256]{2,1,0:T(8,128)(2,1)S(1)}, u32[]{:S(2)}, u32[]{:S(2)}) %collective-permute-start.1) | collective-permute-done | bytes 32800 | tf_op jit(solution)/shard_map/ppermute | solution.py:19
  7.9 4.0 %collective-permute-done.top = bf16[2,32,256]{2,1,0:T(8,128)(2,1)S(1)} collective-permute-done((bf16[2,32,256]{2,1,0:T(8,128)(2,1)S(1)}, bf16[2,32,256]{2,1,0:T(8,128)(2,1)S(1)}, u32[]{:S(2)}, u32[]{:S(2)}) %collective-permute-start) | collective-permute-done | bytes 32800 | tf_op jit(solution)/shard_map/ppermute | solution.py:19
  12.0 0.2 collective-permute-start.3
  12.2 1.4 %collective-permute-start.2 = (bf16[20,2,256]{2,1,0:T(2,128)(2,1)S(1)}, bf16[20,2,256]{2,1,0:T(2,128)(2,1)S(1)}, u32[]{:S(2)}, u32[]{:S(2)}) collective-permute-start(bf16[20,2,256]{2,1,0:T(2,128)(2,1)S(1)} %get-tuple-element.46), channel_id=1, source_target_pairs={{0,4},{4,0},{8,12},{12,8},{1,5},{5,1},{9,13},{13,9},{2,6},{6,2},{1... | collective-permute-start | bytes 61448 | tf_op jit(solution)/shard_map/ppermute | solution.py:24
  13.8 1.7 %collective-permute-done.3.crossed = bf16[20,2,256]{2,1,0:T(2,128)(2,1)S(1)} collective-permute-done((bf16[20,2,256]{2,1,0:T(2,128)(2,1)S(1)}, bf16[20,2,256]{2,1,0:T(2,128)(2,1)S(1)}, u32[]{:S(2)}, u32[]{:S(2)}) %collective-permute-start.3) | collective-permute-done | bytes 20512 | tf_op jit(solution)/shard_map/ppermute | solution.py:510
  15.5 1.3 %copy-done.1 = bf16[3,3,256,256]{3,2,1,0:T(8,128)(2,1)S(1)} copy-done((bf16[3,3,256,256]{3,2,1,0:T(8,128)(2,1)S(1)}, bf16[3,3,256,256]{3,2,1,0:T(8,128)(2,1)}, u32[]{:S(2)}) %copy-start.1) | copy-done | bytes 1179672
  16.7 0.7 %copy-done.4 = f32[256]{0:T(256)S(1)} copy-done((f32[256]{0:T(256)S(1)}, f32[256]{0:T(256)}, u32[]{:S(2)}) %copy-start.4) | copy-done | bytes 1048
  17.4 1.5 %shard_map.101 = (f32[896,256]{1,0:T(8,128)S(1)}, bf16[3,768,256]{2,1,0:T(8,128)(2,1)S(1)}) custom-call(bf16[16,32,256]{2,1,0:T(8,128)(2,1)S(1)} %get-tuple-element.23.marked, bf16[2,32,256]{2,1,0:T(8,128)(2,1)S(1)} %collective-permute-done.top, bf16[2,32,256]{2,1,0:T(8,128)(2,1)S(1)} %collective-permute-done.1.bottom, ...), custom_call_target="tpu_custom_call" | custom-call | flops 704643072 | tf_op jit(solution)/shard_map/pallas_call | solution.py:459
  19.0 1.1 %shard_map.102 = (bf16[512,256]{1,0:T(8,128)(2,1)S(1)}, bf16[512,256]{1,0:T(8,128)(2,1)S(1)}) custom-call(bf16[16,32,256]{2,1,0:T(8,128)(2,1)S(1)} %get-tuple-element.23.marked, f32[896,256]{1,0:T(8,128)S(1)} %get-tuple-element.24.mid, bf16[3,768,256]{2,1,0:T(8,128)(2,1)S(1)} %get-tuple-element.25.second, f32[1,256]{1,0:T(1,128)S(1)} %bitcast.9), custom_call_target="tpu_custom_call" | custom-call | flops 603979776 | tf_op jit(solution)/shard_map/pallas_call | solution.py:459
  20.3 2.0 %collective-permute-start.7 = (bf16[32,1280]{1,0:T(8,128)(2,1)S(1)}, bf16[32,1280]{1,0:T(8,128)(2,1)S(1)}, u32[]{:S(2)}, u32[]{:S(2)}) collective-permute-start(bf16[32,1280]{1,0:T(8,128)(2,1)S(1)} %collective-permute-done.5), channel_id=1, source_target_pairs={{0,1},{1,0},{2,3},{3,2},{4,5},{5,4},{6,7},{7,6},{8,9},{9,8},{10,11... | collective-permute-start | bytes 245768 | tf_op jit(solution)/shard_map/ppermute | solution.py:24
  22.3 3.3 %collective-permute-done.6 = bf16[32,1280]{1,0:T(8,128)(2,1)S(1)} collective-permute-done((bf16[32,1280]{1,0:T(8,128)(2,1)S(1)}, bf16[32,1280]{1,0:T(8,128)(2,1)S(1)}, u32[]{:S(2)}, u32[]{:S(2)}) %collective-permute-start.6) | collective-permute-done | bytes 81952 | tf_op jit(solution)/shard_map/ppermute | solution.py:24
  25.6 1.3 %collective-permute-start.10 = (bf16[64,1280]{1,0:T(8,128)(2,1)S(1)}, bf16[64,1280]{1,0:T(8,128)(2,1)S(1)}, u32[]{:S(2)}, u32[]{:S(2)}) collective-permute-start(bf16[64,1280]{1,0:T(8,128)(2,1)S(1)} %constant_dynamic-update-slice_fusion.refs_1_), channel_id=1, source_target_pairs={{0,8},{4,12},{8,0},{12,4},{1,9},{5,13},{9,1},{13,5},{2,10},{6,14},... | collective-permute-start | bytes 491528 | tf_op jit(solution)/shard_map/ppermute | solution.py:24
  26.9 0.7 %collective-permute-start.9 = (bf16[32,1280]{1,0:T(8,128)(2,1)S(1)}, bf16[32,1280]{1,0:T(8,128)(2,1)S(1)}, u32[]{:S(2)}, u32[]{:S(2)}) collective-permute-start(bf16[32,1280]{1,0:T(8,128)(2,1)S(1)} %shard_map.103.refs_0_), channel_id=1, source_target_pairs={{0,8},{4,12},{8,0},{12,4},{1,9},{5,13},{9,1},{13,5},{2,10},{6,14},... | collective-permute-start | bytes 245768 | tf_op jit(solution)/shard_map/ppermute | solution.py:24
  27.6 1.3 %collective-permute-start.11 = (bf16[32,1280]{1,0:T(8,128)(2,1)S(1)}, bf16[32,1280]{1,0:T(8,128)(2,1)S(1)}, u32[]{:S(2)}, u32[]{:S(2)}) collective-permute-start(bf16[32,1280]{1,0:T(8,128)(2,1)S(1)} %collective-permute-done.7.refs_2_), channel_id=1, source_target_pairs={{0,8},{4,12},{8,0},{12,4},{1,9},{5,13},{9,1},{13,5},{2,10},{6,14},... | collective-permute-start | bytes 245768 | tf_op jit(solution)/shard_map/ppermute | solution.py:24
  28.9 1.0 %shard_map.104 = (bf16[512,1280]{1,0:T(8,128)(2,1)S(1)}, f32[512,128]{1,0:T(8,128)S(1)}, bf16[128,1280]{1,0:T(8,128)(2,1)S(1)}) custom-call(bf16[512,256]{1,0:T(8,128)(2,1)S(1)} %get-tuple-element.26.own, bf16[512,256]{1,0:T(8,128)(2,1)S(1)} %get-tuple-element.27.own_sent, bf16[256,1280]{1,0:T(8,128)(2,1)S(1)} %copy-done.3, ...), custom_call_target="tpu_custom_call" | custom-call | flops 503316480 | tf_op jit(solution)/shard_map/pallas_call | solution.py:459
  29.9 1.5 %shard_map.105 = (f32[2,136,128]{2,1,0:T(8,128)S(1)}, bf16[512,256]{1,0:T(8,128)(2,1)S(1)}, bf16[512,1280]{1,0:T(8,128)(2,1)S(1)}) custom-call(bf16[512,256]{1,0:T(8,128)(2,1)S(1)} %get-tuple-element.26.own, f32[512,128]{1,0:T(8,128)S(1)} %get-tuple-element.29.own_scores, bf16[512,256]{1,0:T(8,128)(2,1)S(1)} %collective-permute-done.8.other_sent, ...), custom_call_target="tpu_custom_call" | custom-call | flops 402653184 | tf_op jit(solution)/shard_map/pallas_call | solution.py:459
  31.4 1.9 %collective-permute-done.9.refs_0_ = bf16[32,1280]{1,0:T(8,128)(2,1)S(1)} collective-permute-done((bf16[32,1280]{1,0:T(8,128)(2,1)S(1)}, bf16[32,1280]{1,0:T(8,128)(2,1)S(1)}, u32[]{:S(2)}, u32[]{:S(2)}) %collective-permute-start.9) | collective-permute-done | bytes 81952 | tf_op jit(solution)/shard_map/ppermute | solution.py:24
  33.3 0.9 %collective-permute-done.11.refs_2_ = bf16[32,1280]{1,0:T(8,128)(2,1)S(1)} collective-permute-done((bf16[32,1280]{1,0:T(8,128)(2,1)S(1)}, bf16[32,1280]{1,0:T(8,128)(2,1)S(1)}, u32[]{:S(2)}, u32[]{:S(2)}) %collective-permute-start.11) | collective-permute-done | bytes 81952 | tf_op jit(solution)/shard_map/ppermute | solution.py:24
  34.2 1.3 %shard_map.106 = (f32[136,128]{1,0:T(8,128)S(1)}, bf16[144,128]{1,0:T(8,128)(2,1)S(1)}, bf16[144,128]{1,0:T(8,128)(2,1)S(1)}, bf16[144,128]{1,0:T(8,128)(2,1)S(1)}) custom-call(f32[2,136,128]{2,1,0:T(8,128)S(1)} %get-tuple-element.31.near, bf16[512,256]{1,0:T(8,128)(2,1)S(1)} %get-tuple-element.26.own, bf16[512,256]{1,0:T(8,128)(2,1)S(1)} %get-tuple-element.27.own_sent, ...), custom_call_target="tpu_custom_call" | custom-call | flops 402653184 | tf_op jit(solution)/shard_map/pallas_call | solution.py:459
  35.5 0.6 %collective-permute-start.12 = (bf16[144,128]{1,0:T(8,128)(2,1)S(1)}, bf16[144,128]{1,0:T(8,128)(2,1)S(1)}, u32[]{:S(2)}, u32[]{:S(2)}) collective-permute-start(bf16[144,128]{1,0:T(8,128)(2,1)S(1)} %get-tuple-element.36), channel_id=1, source_target_pairs={{0,1},{1,0},{2,3},{3,2},{4,5},{5,4},{6,7},{7,6},{8,9},{9,8},{10,11... | collective-permute-start | bytes 110600 | tf_op jit(solution)/shard_map/ppermute | solution.py:24
  36.2 1.3 %collective-permute-start.13 = (bf16[144,128]{1,0:T(8,128)(2,1)S(1)}, bf16[144,128]{1,0:T(8,128)(2,1)S(1)}, u32[]{:S(2)}, u32[]{:S(2)}) collective-permute-start(bf16[144,128]{1,0:T(8,128)(2,1)S(1)} %get-tuple-element.37), channel_id=1, source_target_pairs={{0,2},{1,3},{2,0},{3,1},{4,6},{5,7},{6,4},{7,5},{8,10},{9,11},{10,... | collective-permute-start | bytes 110600 | tf_op jit(solution)/shard_map/ppermute | solution.py:24
  37.4 2.6 %collective-permute-start.14 = (bf16[144,128]{1,0:T(8,128)(2,1)S(1)}, bf16[144,128]{1,0:T(8,128)(2,1)S(1)}, u32[]{:S(2)}, u32[]{:S(2)}) collective-permute-start(bf16[144,128]{1,0:T(8,128)(2,1)S(1)} %get-tuple-element.38), channel_id=1, source_target_pairs={{0,3},{1,2},{2,1},{3,0},{4,7},{5,6},{6,5},{7,4},{8,11},{9,10},{10,... | collective-permute-start | bytes 110600 | tf_op jit(solution)/shard_map/ppermute | solution.py:24
  40.0 1.1 %collective-permute-done.13.refs_1_ = bf16[144,128]{1,0:T(8,128)(2,1)S(1)} collective-permute-done((bf16[144,128]{1,0:T(8,128)(2,1)S(1)}, bf16[144,128]{1,0:T(8,128)(2,1)S(1)}, u32[]{:S(2)}, u32[]{:S(2)}) %collective-permute-start.13) | collective-permute-done | bytes 36896 | tf_op jit(solution)/shard_map/ppermute | solution.py:24
  41.1 2.1 %collective-permute-done.14.refs_2_ = bf16[144,128]{1,0:T(8,128)(2,1)S(1)} collective-permute-done((bf16[144,128]{1,0:T(8,128)(2,1)S(1)}, bf16[144,128]{1,0:T(8,128)(2,1)S(1)}, u32[]{:S(2)}, u32[]{:S(2)}) %collective-permute-start.14) | collective-permute-done | bytes 36896 | tf_op jit(solution)/shard_map/ppermute | solution.py:24
  43.3 0.5 %collective-permute-start.15 = (bf16[144,128]{1,0:T(8,128)(2,1)S(1)}, bf16[144,128]{1,0:T(8,128)(2,1)S(1)}, u32[]{:S(2)}, u32[]{:S(2)}) collective-permute-start(bf16[144,128]{1,0:T(8,128)(2,1)S(1)} %get-tuple-element.40), channel_id=1, source_target_pairs={{0,8},{4,12},{8,0},{12,4},{1,9},{5,13},{9,1},{13,5},{2,10},{6,14},... | collective-permute-start | bytes 110600 | tf_op jit(solution)/shard_map/ppermute | solution.py:24
  43.8 3.5 %collective-permute-done.15.arrived = bf16[144,128]{1,0:T(8,128)(2,1)S(1)} collective-permute-done((bf16[144,128]{1,0:T(8,128)(2,1)S(1)}, bf16[144,128]{1,0:T(8,128)(2,1)S(1)}, u32[]{:S(2)}, u32[]{:S(2)}) %collective-permute-start.15) | collective-permute-done | bytes 36896 | tf_op jit(solution)/shard_map/ppermute | solution.py:24
  47.4 0.3 shard_map.109.mine
  47.8 0.8 %collective-permute-done.16.arrived = bf16[128,128]{1,0:T(8,128)(2,1)S(1)} collective-permute-done((bf16[128,128]{1,0:T(8,128)(2,1)S(1)}, bf16[128,128]{1,0:T(8,128)(2,1)S(1)}, u32[]{:S(2)}, u32[]{:S(2)}) %collective-permute-start.16) | collective-permute-done | bytes 32800 | tf_op jit(solution)/shard_map/ppermute | solution.py:24
  48.6 1.4 %finish.1 = bf16[320,128]{1,0:T(8,128)(2,1)} custom-call(bf16[64,1280]{1,0:T(8,128)(2,1)S(1)} %shard_map.109.mine, bf16[128,128]{1,0:T(8,128)(2,1)S(1)} %collective-permute-done.16.arrived, bf16[256,1280]{1,0:T(8,128)(2,1)S(1)} %copy-done, bf16[320,1280]{1,0:T(8,128)(2,1)S(1)} %bitcast.7), custom_call_target="tpu_custom_call" | custom-call | tf_op jit(solution)/shard_map/finish/pallas_call | solution.py:572
  (32 shorter events, 0.6 us)
Async XLA Ops:
  0.0 13.7 %collective-permute-start.4 = (bf16[32,1280]{1,0:T(8,128)(2,1)}, bf16[32,1280]{1,0:T(8,128)(2,1)S(1)}, u32[]{:S(2)}, u32[]{:S(2)}) collective-permute-start(bf16[32,1280]{1,0:T(8,128)(2,1)} %queries.1), channel_id=1, source_target_pairs={{0,4},{4,0},{8,12},{12,8},{1,5},{5,1},{9,13},{13,9},{2,6},{6,2},{1... | collective-permute-start | bytes 245768 | tf_op jit(solution)/shard_map/ppermute | solution.py:24
  1.6 6.3 %collective-permute-start.1 = (bf16[2,32,256]{2,1,0:T(8,128)(2,1)S(1)}, bf16[2,32,256]{2,1,0:T(8,128)(2,1)S(1)}, u32[]{:S(2)}, u32[]{:S(2)}) collective-permute-start(bf16[2,32,256]{2,1,0:T(8,128)(2,1)S(1)} %get-tuple-element.43), channel_id=1, source_target_pairs={{0,3},{1,0},{2,1},{3,2},{4,7},{5,4},{6,5},{7,6},{8,11},{9,8},{10,9... | collective-permute-start | bytes 98312 | tf_op jit(solution)/shard_map/ppermute | solution.py:19
  6.2 5.7 %collective-permute-start = (bf16[2,32,256]{2,1,0:T(8,128)(2,1)S(1)}, bf16[2,32,256]{2,1,0:T(8,128)(2,1)S(1)}, u32[]{:S(2)}, u32[]{:S(2)}) collective-permute-start(bf16[2,32,256]{2,1,0:T(8,128)(2,1)S(1)} %get-tuple-element.44), channel_id=1, source_target_pairs={{0,1},{1,2},{2,3},{3,0},{4,5},{5,6},{6,7},{7,4},{8,9},{9,10},{10,1... | collective-permute-start | bytes 98312 | tf_op jit(solution)/shard_map/ppermute | solution.py:19
  12.0 3.4 %collective-permute-start.3 = (bf16[20,2,256]{2,1,0:T(2,128)(2,1)S(1)}, bf16[20,2,256]{2,1,0:T(2,128)(2,1)S(1)}, u32[]{:S(2)}, u32[]{:S(2)}) collective-permute-start(bf16[20,2,256]{2,1,0:T(2,128)(2,1)S(1)} %get-tuple-element.45), channel_id=1, source_target_pairs={{0,12},{4,8},{8,4},{12,0},{1,13},{5,9},{9,5},{13,1},{2,14},{6,10},... | collective-permute-start | bytes 61448 | tf_op jit(solution)/shard_map/ppermute | solution.py:510
  12.2 3.2 %collective-permute-start.2 = (bf16[20,2,256]{2,1,0:T(2,128)(2,1)S(1)}, bf16[20,2,256]{2,1,0:T(2,128)(2,1)S(1)}, u32[]{:S(2)}, u32[]{:S(2)}) collective-permute-start(bf16[20,2,256]{2,1,0:T(2,128)(2,1)S(1)} %get-tuple-element.46), channel_id=1, source_target_pairs={{0,4},{4,0},{8,12},{12,8},{1,5},{5,1},{9,13},{13,9},{2,6},{6,2},{1... | collective-permute-start | bytes 61448 | tf_op jit(solution)/shard_map/ppermute | solution.py:24
  13.7 6.6 %collective-permute-start.5 = (bf16[32,1280]{1,0:T(8,128)(2,1)S(1)}, bf16[32,1280]{1,0:T(8,128)(2,1)S(1)}, u32[]{:S(2)}, u32[]{:S(2)}) collective-permute-start(bf16[32,1280]{1,0:T(8,128)(2,1)S(1)} %shard_map.103.refs_0_), channel_id=1, source_target_pairs={{0,2},{1,3},{2,0},{3,1},{4,6},{5,7},{6,4},{7,5},{8,10},{9,11},{10,... | collective-permute-start | bytes 245768 | tf_op jit(solution)/shard_map/ppermute | solution.py:24
  15.5 1.3 %copy-start.1 = (bf16[3,3,256,256]{3,2,1,0:T(8,128)(2,1)S(1)}, bf16[3,3,256,256]{3,2,1,0:T(8,128)(2,1)}, u32[]{:S(2)}) copy-start(bf16[3,3,256,256]{3,2,1,0:T(8,128)(2,1)} %param.12) | copy-start | bytes 3538948
  16.7 0.7 %copy-start.4 = (f32[256]{0:T(256)S(1)}, f32[256]{0:T(256)}, u32[]{:S(2)}) copy-start(f32[256]{0:T(256)} %param.13) | copy-start | bytes 3076
  17.4 1.5 %copy-start.5 = (f32[256]{0:T(256)S(1)}, f32[256]{0:T(256)}, u32[]{:S(2)}) copy-start(f32[256]{0:T(256)} %param.15) | copy-start | bytes 3076
  18.9 10.0 %copy-start.3 = (bf16[256,1280]{1,0:T(8,128)(2,1)S(1)}, bf16[256,1280]{1,0:T(8,128)(2,1)}, u32[]{:S(2)}) copy-start(bf16[256,1280]{1,0:T(8,128)(2,1)} %weight.3) | copy-start | bytes 1966084
  20.1 9.8 %collective-permute-start.8 = (bf16[512,256]{1,0:T(8,128)(2,1)S(1)}, bf16[512,256]{1,0:T(8,128)(2,1)S(1)}, u32[]{:S(2)}, u32[]{:S(2)}) collective-permute-start(bf16[512,256]{1,0:T(8,128)(2,1)S(1)} %get-tuple-element.27.own_sent), channel_id=1, source_target_pairs={{0,4},{4,0},{8,12},{12,8},{1,5},{5,1},{9,13},{13,9},{2,6},{6,2},{1... | collective-permute-start | bytes 786440 | tf_op jit(solution)/shard_map/ppermute | solution.py:24
  20.3 5.3 %collective-permute-start.6 = (bf16[32,1280]{1,0:T(8,128)(2,1)S(1)}, bf16[32,1280]{1,0:T(8,128)(2,1)S(1)}, u32[]{:S(2)}, u32[]{:S(2)}) collective-permute-start(bf16[32,1280]{1,0:T(8,128)(2,1)S(1)} %shard_map.103.refs_0_), channel_id=1, source_target_pairs={{0,1},{1,0},{2,3},{3,2},{4,5},{5,4},{6,7},{7,6},{8,9},{9,8},{10,11... | collective-permute-start | bytes 245768 | tf_op jit(solution)/shard_map/ppermute | solution.py:24
  20.3 7.3 %collective-permute-start.7 = (bf16[32,1280]{1,0:T(8,128)(2,1)S(1)}, bf16[32,1280]{1,0:T(8,128)(2,1)S(1)}, u32[]{:S(2)}, u32[]{:S(2)}) collective-permute-start(bf16[32,1280]{1,0:T(8,128)(2,1)S(1)} %collective-permute-done.5), channel_id=1, source_target_pairs={{0,1},{1,0},{2,3},{3,2},{4,5},{5,4},{6,7},{7,6},{8,9},{9,8},{10,11... | collective-permute-start | bytes 245768 | tf_op jit(solution)/shard_map/ppermute | solution.py:24
  25.6 8.6 %collective-permute-start.10 = (bf16[64,1280]{1,0:T(8,128)(2,1)S(1)}, bf16[64,1280]{1,0:T(8,128)(2,1)S(1)}, u32[]{:S(2)}, u32[]{:S(2)}) collective-permute-start(bf16[64,1280]{1,0:T(8,128)(2,1)S(1)} %constant_dynamic-update-slice_fusion.refs_1_), channel_id=1, source_target_pairs={{0,8},{4,12},{8,0},{12,4},{1,9},{5,13},{9,1},{13,5},{2,10},{6,14},... | collective-permute-start | bytes 491528 | tf_op jit(solution)/shard_map/ppermute | solution.py:24
  26.9 6.4 %collective-permute-start.9 = (bf16[32,1280]{1,0:T(8,128)(2,1)S(1)}, bf16[32,1280]{1,0:T(8,128)(2,1)S(1)}, u32[]{:S(2)}, u32[]{:S(2)}) collective-permute-start(bf16[32,1280]{1,0:T(8,128)(2,1)S(1)} %shard_map.103.refs_0_), channel_id=1, source_target_pairs={{0,8},{4,12},{8,0},{12,4},{1,9},{5,13},{9,1},{13,5},{2,10},{6,14},... | collective-permute-start | bytes 245768 | tf_op jit(solution)/shard_map/ppermute | solution.py:24
  27.6 6.5 %collective-permute-start.11 = (bf16[32,1280]{1,0:T(8,128)(2,1)S(1)}, bf16[32,1280]{1,0:T(8,128)(2,1)S(1)}, u32[]{:S(2)}, u32[]{:S(2)}) collective-permute-start(bf16[32,1280]{1,0:T(8,128)(2,1)S(1)} %collective-permute-done.7.refs_2_), channel_id=1, source_target_pairs={{0,8},{4,12},{8,0},{12,4},{1,9},{5,13},{9,1},{13,5},{2,10},{6,14},... | collective-permute-start | bytes 245768 | tf_op jit(solution)/shard_map/ppermute | solution.py:24
  34.2 13.2 %copy-start = (bf16[256,1280]{1,0:T(8,128)(2,1)S(1)}, bf16[256,1280]{1,0:T(8,128)(2,1)}, u32[]{:S(2)}) copy-start(bf16[256,1280]{1,0:T(8,128)(2,1)} %value_weight.3) | copy-start | bytes 1966084
  35.5 13.1 %copy-start.2 = (bf16[1280,320]{0,1:T(8,128)(2,1)S(1)}, bf16[1280,320]{0,1:T(8,128)(2,1)}, u32[]{:S(2)}) copy-start(bf16[1280,320]{0,1:T(8,128)(2,1)} %param.19) | copy-start | bytes 2457604
  35.5 4.5 %collective-permute-start.12 = (bf16[144,128]{1,0:T(8,128)(2,1)S(1)}, bf16[144,128]{1,0:T(8,128)(2,1)S(1)}, u32[]{:S(2)}, u32[]{:S(2)}) collective-permute-start(bf16[144,128]{1,0:T(8,128)(2,1)S(1)} %get-tuple-element.36), channel_id=1, source_target_pairs={{0,1},{1,0},{2,3},{3,2},{4,5},{5,4},{6,7},{7,6},{8,9},{9,8},{10,11... | collective-permute-start | bytes 110600 | tf_op jit(solution)/shard_map/ppermute | solution.py:24
  36.2 4.9 %collective-permute-start.13 = (bf16[144,128]{1,0:T(8,128)(2,1)S(1)}, bf16[144,128]{1,0:T(8,128)(2,1)S(1)}, u32[]{:S(2)}, u32[]{:S(2)}) collective-permute-start(bf16[144,128]{1,0:T(8,128)(2,1)S(1)} %get-tuple-element.37), channel_id=1, source_target_pairs={{0,2},{1,3},{2,0},{3,1},{4,6},{5,7},{6,4},{7,5},{8,10},{9,11},{10,... | collective-permute-start | bytes 110600 | tf_op jit(solution)/shard_map/ppermute | solution.py:24
  37.4 5.8 %collective-permute-start.14 = (bf16[144,128]{1,0:T(8,128)(2,1)S(1)}, bf16[144,128]{1,0:T(8,128)(2,1)S(1)}, u32[]{:S(2)}, u32[]{:S(2)}) collective-permute-start(bf16[144,128]{1,0:T(8,128)(2,1)S(1)} %get-tuple-element.38), channel_id=1, source_target_pairs={{0,3},{1,2},{2,1},{3,0},{4,7},{5,6},{6,5},{7,4},{8,11},{9,10},{10,... | collective-permute-start | bytes 110600 | tf_op jit(solution)/shard_map/ppermute | solution.py:24
  43.3 4.0 %collective-permute-start.15 = (bf16[144,128]{1,0:T(8,128)(2,1)S(1)}, bf16[144,128]{1,0:T(8,128)(2,1)S(1)}, u32[]{:S(2)}, u32[]{:S(2)}) collective-permute-start(bf16[144,128]{1,0:T(8,128)(2,1)S(1)} %get-tuple-element.40), channel_id=1, source_target_pairs={{0,8},{4,12},{8,0},{12,4},{1,9},{5,13},{9,1},{13,5},{2,10},{6,14},... | collective-permute-start | bytes 110600 | tf_op jit(solution)/shard_map/ppermute | solution.py:24
  47.3 1.3 %collective-permute-start.16 = (bf16[128,128]{1,0:T(8,128)(2,1)S(1)}, bf16[128,128]{1,0:T(8,128)(2,1)S(1)}, u32[]{:S(2)}, u32[]{:S(2)}) collective-permute-start(bf16[128,128]{1,0:T(8,128)(2,1)S(1)} %shard_map.108.normalized), channel_id=1, source_target_pairs={{0,4},{4,0},{8,12},{12,8},{1,5},{5,1},{9,13},{13,9},{2,6},{6,2},{1... | collective-permute-start | bytes 98312 | tf_op jit(solution)/shard_map/ppermute | solution.py:24

commit v8 on v7

--- a/solution.py
+++ b/solution.py
@@ -331,15 +331,19 @@
 PLACES = (0, 2, 1, 3)
 
 
-def hold_queries(held, parts):
+def hold_queries(held, near, far, use_near):
     half = held.shape[0] // 8
     row = lax.axis_index("row")
-    blocks = [(part, 2 * k * half) for part in parts for k in range(part.shape[0] // (2 * half))]
-    for (part, start), place in zip(blocks, PLACES):
+    blocks = [
+        (one, other, 2 * k * half)
+        for one, other in zip(near, far)
+        for k in range(one.shape[0] // (2 * half))
+    ]
+    for (one, other, start), place in zip(blocks, PLACES):
         for parity in range(2):
-            source = start + parity * half
+            source = slice(start + parity * half, start + (parity + 1) * half)
             target = pl.multiple_of(parity * 4 * half + (row ^ place) * half, half)
-            held[pl.ds(target, half), :] = part[source : source + half, :]
+            held[pl.ds(target, half), :] = jnp.where(use_near, one[source, :], other[source, :])
 
 
 def masked_scores(queries, marked, keys):
@@ -379,38 +383,31 @@
     )
 
 
-def own_kernel(own, own_sent, weight, *refs):
-    *queries, keys, scores, held = refs
-    key_kernel(own, weight, keys)
-    hold_queries(held, queries)
-    scores[...] = masked_scores(held, own_sent, keys)
-
-
-def near_kernel(own, own_scores, other_sent, weight, held, out, other, keys):
+def first_score_kernel(own, own_sent, own_keys, other_sent, weight, *refs):
+    *queries, send_2, send_3, other, keys, held, blocks = refs
+    row, across = lax.axis_index("row"), lax.axis_index("col") // 2
+    hold_queries(held, queries[:3], queries[3:], row // 2 != across)
     values = other_sent[...].astype(jnp.float32)
     other[...] = jnp.where(values < FAR, values, 0.0).astype(jnp.bfloat16)
     key_kernel(other, weight, keys)
-    scores = (own_scores[...], masked_scores(held, other_sent, keys))
+    scores = masked_scores(held, own_sent, own_keys), masked_scores(held, other_sent, keys)
     for parity, block in enumerate(score_blocks(scores, (own, other))):
-        write_whole(out.at[parity], *block)
-
-
-def far_kernel(
-    near, own, own_sent, own_keys, other, other_sent, other_keys, *refs
-):
-    *queries, kept, send_1, send_2, send_3, held, blocks = refs
+        write_whole(blocks.at[parity], *block)
+    odd = lax.rem(row, 2)
+    write_parts(send_2, *read_whole(blocks.at[odd]))
+    write_parts(send_3, *read_whole(blocks.at[1 - odd]))
+
+
+def last_score_kernel(own, own_sent, own_keys, other, other_sent, other_keys, *refs):
+    *queries, kept, send_1, held, blocks = refs
     row, across = lax.axis_index("row"), lax.axis_index("col") // 2
-    for parity in range(2):
-        blocks[2 * across + parity] = near[parity]
-    hold_queries(held, queries)
-    scores = (
-        masked_scores(held, own_sent, own_keys), masked_scores(held, other_sent, other_keys)
-    )
+    hold_queries(held, queries[:3], queries[3:], row // 2 == across)
+    scores = masked_scores(held, own_sent, own_keys), masked_scores(held, other_sent, other_keys)
     for parity, block in enumerate(score_blocks(scores, (own, other))):
-        write_whole(blocks.at[2 * (1 - across) + parity], *block)
-    kept[...] = blocks[row]
-    for step, send in ((1, send_1), (2, send_2), (3, send_3)):
-        write_parts(send, *read_whole(blocks.at[row ^ step]))
+        write_whole(blocks.at[parity], *block)
+    odd = lax.rem(row, 2)
+    kept[...] = blocks[odd]
+    write_parts(send_1, *read_whole(blocks.at[1 - odd]))
 
 
 def merge_kernel(own, *refs):
@@ -461,9 +458,7 @@
         out_shape=[pltpu.VMEM(shape, dtype) for shape, dtype in outs],
         in_specs=[outside if k in far else held for k in range(len(args))],
         out_specs=[held] * len(outs),
-        scratch_shapes=[
-            pltpu.VMEM(*kind) if isinstance(kind, tuple) else kind for kind in scratch
-        ],
+        scratch_shapes=[pltpu.VMEM(*kind) if isinstance(kind, tuple) else kind for kind in scratch],
         compiler_params=pltpu.CompilerParams(vmem_limit_bytes=limit * MIB),
         cost_estimate=pl.CostEstimate(flops=flops, bytes_accessed=0, transcendentals=0),
     )(
@@ -484,6 +479,7 @@
     cells = height * breadth
     slot = -(-(breadth + 2 * HALO) // 16) * 16
     flat = LEAD + (height + 2 * HALO) * slot
+    count = flat - 2 * slot
     wide, half = jnp.float32, jnp.bfloat16
     block = 4 * size
     whole_block, sent_block = (channels // 2 + 8, block), (channels // 2 + 16, block)
@@ -497,11 +493,13 @@
         far=(0, 1, 2), flops=1 << 20,
     )
     (queries,) = call(halve_kernel, [((size, width), half)], [queries, beside])
-    far_queries = flipped(queries, "col", 2)
     two = flipped(queries, "row", 2)
-    one = flipped(queries, "row", 1)
     top = shifted(marked[height - HALO :], "row", 1)
     bottom = shifted(marked[:HALO], "row", -1)
+    one = flipped(queries, "row", 1)
+    three = flipped(queries, "row", 3)
+    far_queries = flipped(queries, "col", 2)
+
     edge = lambda cut: jnp.concatenate([top[:, cut], marked[:, cut], bottom[:, cut]], axis=0)
     even = lax.rem(col, 2) == 0
     ends = edge(slice(breadth - HALO, breadth)), edge(slice(0, HALO))
@@ -511,10 +509,8 @@
 
     pair = jnp.concatenate([two, one], axis=0)
     far_pair = flipped(pair, "col", 2)
-    three = flipped(two, "row", 1)
     far_three = flipped(three, "col", 2)
 
-    count = flat - 2 * slot
     mid, weight = call(
         conv_kernel,
         [((count + 2 * EDGE, channels), wide), ((3, 3 * channels, channels), half)],
@@ -537,29 +533,29 @@
         limit=10, flops=18 * cells * channels * channels,
     )
     other_sent = flipped(own_sent, "col", 1)
-    own_keys, own_scores, held_queries = call(
-        own_kernel,
-        [((cells, width), half), ((cells, block), wide), ((block, width), half)],
-        [own, own_sent, key_weight, queries, pair, three],
-        limit=6, flops=2 * cells * width * (channels + block),
-    )
-    near, other, other_keys = call(
-        near_kernel,
-        [((2,) + whole_block, wide), ((cells, channels), half), ((cells, width), half)],
-        [own, own_scores, other_sent, key_weight, held_queries],
-        limit=8, flops=score_flops,
-    )
-    kept, *sends = call(
-        far_kernel, [(whole_block, wide)] + [(sent_block, half)] * 3,
-        [
-            near, own, own_sent, own_keys, other, other_sent, other_keys,
-            far_queries, far_pair, far_three,
-        ],
-        [((block, width), half), ((4,) + whole_block, wide)],
-        limit=8, flops=score_flops,
-    )
-    arrived = [flipped(part, "row", k + 1) for k, part in enumerate(sends)]
-    kept, sent = call(merge_kernel, [(whole_block, wide), (sent_block, half)], [kept, *arrived])
+    (own_keys,) = call(
+        key_kernel, [((cells, width), half)], [own, key_weight],
+        limit=4, flops=2 * cells * width * channels,
+    )
+    all_queries = [queries, pair, three, far_queries, far_pair, far_three]
+    score_scratch = [((block, width), half), ((2,) + whole_block, wide)]
+    send_2, send_3, other, other_keys = call(
+        first_score_kernel,
+        [(sent_block, half)] * 2 + [((cells, channels), half), ((cells, width), half)],
+        [own, own_sent, own_keys, other_sent, key_weight, *all_queries],
+        score_scratch, limit=8, flops=score_flops + 2 * cells * channels * width,
+    )
+    arrived_2, arrived_3 = flipped(send_2, "row", 2), flipped(send_3, "row", 3)
+    kept, send_1 = call(
+        last_score_kernel, [(whole_block, wide), (sent_block, half)],
+        [own, own_sent, own_keys, other, other_sent, other_keys, *all_queries],
+        score_scratch, limit=8, flops=score_flops,
+    )
+    arrived_1 = flipped(send_1, "row", 1)
+    kept, sent = call(
+        merge_kernel, [(whole_block, wide), (sent_block, half)],
+        [kept, arrived_1, arrived_2, arrived_3],
+    )
     arrived = flipped(sent, "col", 2)
     (normalized,) = call(normalize_kernel, [((channels // 2, block), half)], [kept, arrived])
     arrived = flipped(normalized, "col", 1)
@@ -576,7 +572,7 @@
         out_specs=held,
         scratch_shapes=[pltpu.VMEM((2 * size, width), half), pltpu.VMEM((block, width), half)],
         compiler_params=pltpu.CompilerParams(vmem_limit_bytes=6 * MIB),
-        name="finish",
+        name="fn",
     )(keep(attended), keep(arrived), keep(value_weight), keep(out_weight.T)).T
 
 

time: 50.2 us -> 54.8 us (1.092)
  waiting for transfers between devices: 20.9 us -> 23.6 us
  starting transfers between devices: 17.5 us -> 19.6 us
    ppermute x14, waiting for transfers between devices: 13.6 us -> 16.3 us  [flipped(): return lax.ppermute(array, axis, [(i, i ^ bit) for i in range(count)])]
    ppermute x14, starting transfers between devices: 12.6 us -> 14.7 us  [flipped(): return lax.ppermute(array, axis, [(i, i ^ bit) for i in range(count)])]
  transfers between devices with their start and end apart: 17 -> 17, of which waited for: 10 -> 11; matrix products, arithmetic and copies ran while one was open for 0% -> 0% of each run, Pallas kernels for 13% -> 8%
where the time goes in v8:
time: 54.8 us; the launch traced here: 54.6 us
  waiting for transfers between devices  23.6 us (43%)
  starting transfers between devices  19.6 us (36%)
  Pallas kernels  9.2 us (17%)
  local copies, waits for them, and re-layouts  2.03 us (4%)
    ppermute x14, waiting for transfers between devices, flipped(): return lax.ppermute(array, axis, [(i, i ^ bit) for i in range(count)])  16.3 us
    ppermute x14, starting transfers between devices, flipped(): return lax.ppermute(array, axis, [(i, i ^ bit) for i in range(count)])  14.7 us
    pallas_call x10, Pallas kernels, call(): pl.pallas_call(kernel, out_shape=[pltpu.VMEM(shape, dtype) for shape, dty...  7.84 us
    ppermute x2, waiting for transfers between devices, shifted(): lax.ppermute(array, axis, [(i, (i + step) % count) for i in range(count)])  5.66 us
    ppermute x2, starting transfers between devices, shifted(): lax.ppermute(array, axis, [(i, (i + step) % count) for i in range(count)])  4.64 us
    unnamed x13, local copies, waits for them, and re-layouts  1.97 us
    ppermute x1, waiting for transfers between devices, kernel_path(): crossed = lax.ppermute(jnp.where(even, *ends[::-1]), 'col', rounds)  1.68 us
    pallas_call x1, Pallas kernels, kernel_path(): pl.pallas_call(finish_kernel, out_shape=jax.ShapeDtypeStruct((out_weight....  1.37 us
  transfers between devices with their start and end apart: 17, of which 11 were waited for; matrix products, arithmetic and copies ran while one was open for 0% of the time, Pallas kernels for 8%

profile of v8, /device:TPU:0, one launch (start us, length us, event | category | flops | bytes accessed | tf_op | source)
XLA Modules:
  0.0 54.6 jit_solution(12888338991304844100)
XLA Ops:
  0.0 0.5 collective-permute-start.5
  0.5 1.1 %shard_map.100 = (bf16[16,32,256]{2,1,0:T(8,128)(2,1)S(1)}, bf16[32,1280]{1,0:T(8,128)(2,1)S(1)}) custom-call(bf16[16,32,256]{2,1,0:T(8,128)(2,1)} %features.1, s32[16,32]{1,0:T(8,128)} %tissue.1, bf16[32,1280]{1,0:T(8,128)(2,1)} %queries.1), custom_call_target="tpu_custom_call" | custom-call | flops 1048576 | tf_op jit(solution)/shard_map/pallas_call | solution.py:456
  1.6 4.6 %collective-permute-start.1 = (bf16[2,32,256]{2,1,0:T(8,128)(2,1)S(1)}, bf16[2,32,256]{2,1,0:T(8,128)(2,1)S(1)}, u32[]{:S(2)}, u32[]{:S(2)}) collective-permute-start(bf16[2,32,256]{2,1,0:T(8,128)(2,1)S(1)} %get-tuple-element.35), channel_id=1, source_target_pairs={{0,3},{1,0},{2,1},{3,2},{4,7},{5,4},{6,5},{7,6},{8,11},{9,8},{10,9... | collective-permute-start | bytes 98312 | tf_op jit(solution)/shard_map/ppermute | solution.py:19
  6.3 1.6 %collective-permute-done.1.bottom = bf16[2,32,256]{2,1,0:T(8,128)(2,1)S(1)} collective-permute-done((bf16[2,32,256]{2,1,0:T(8,128)(2,1)S(1)}, bf16[2,32,256]{2,1,0:T(8,128)(2,1)S(1)}, u32[]{:S(2)}, u32[]{:S(2)}) %collective-permute-start.1) | collective-permute-done | bytes 32800 | tf_op jit(solution)/shard_map/ppermute | solution.py:19
  7.9 4.0 %collective-permute-done.top = bf16[2,32,256]{2,1,0:T(8,128)(2,1)S(1)} collective-permute-done((bf16[2,32,256]{2,1,0:T(8,128)(2,1)S(1)}, bf16[2,32,256]{2,1,0:T(8,128)(2,1)S(1)}, u32[]{:S(2)}, u32[]{:S(2)}) %collective-permute-start) | collective-permute-done | bytes 32800 | tf_op jit(solution)/shard_map/ppermute | solution.py:19
  12.2 1.4 %collective-permute-start.2 = (bf16[20,2,256]{2,1,0:T(2,128)(2,1)S(1)}, bf16[20,2,256]{2,1,0:T(2,128)(2,1)S(1)}, u32[]{:S(2)}, u32[]{:S(2)}) collective-permute-start(bf16[20,2,256]{2,1,0:T(2,128)(2,1)S(1)} %get-tuple-element.38), channel_id=1, source_target_pairs={{0,4},{4,0},{8,12},{12,8},{1,5},{5,1},{9,13},{13,9},{2,6},{6,2},{1... | collective-permute-start | bytes 61448 | tf_op jit(solution)/shard_map/ppermute | solution.py:24
  13.8 1.7 %collective-permute-done.3.crossed = bf16[20,2,256]{2,1,0:T(2,128)(2,1)S(1)} collective-permute-done((bf16[20,2,256]{2,1,0:T(2,128)(2,1)S(1)}, bf16[20,2,256]{2,1,0:T(2,128)(2,1)S(1)}, u32[]{:S(2)}, u32[]{:S(2)}) %collective-permute-start.3) | collective-permute-done | bytes 20512 | tf_op jit(solution)/shard_map/ppermute | solution.py:508
  15.5 1.3 %copy-done.2 = bf16[3,3,256,256]{3,2,1,0:T(8,128)(2,1)S(1)} copy-done((bf16[3,3,256,256]{3,2,1,0:T(8,128)(2,1)S(1)}, bf16[3,3,256,256]{3,2,1,0:T(8,128)(2,1)}, u32[]{:S(2)}) %copy-start.2) | copy-done | bytes 1179672
  16.7 0.7 %copy-done.4 = f32[256]{0:T(256)S(1)} copy-done((f32[256]{0:T(256)S(1)}, f32[256]{0:T(256)}, u32[]{:S(2)}) %copy-start.4) | copy-done | bytes 1048
  17.4 1.5 %shard_map.101 = (f32[896,256]{1,0:T(8,128)S(1)}, bf16[3,768,256]{2,1,0:T(8,128)(2,1)S(1)}) custom-call(bf16[16,32,256]{2,1,0:T(8,128)(2,1)S(1)} %get-tuple-element.19.marked, bf16[2,32,256]{2,1,0:T(8,128)(2,1)S(1)} %collective-permute-done.top, bf16[2,32,256]{2,1,0:T(8,128)(2,1)S(1)} %collective-permute-done.1.bottom, ...), custom_call_target="tpu_custom_call" | custom-call | flops 704643072 | tf_op jit(solution)/shard_map/pallas_call | solution.py:456
  19.0 1.1 %shard_map.102 = (bf16[512,256]{1,0:T(8,128)(2,1)S(1)}, bf16[512,256]{1,0:T(8,128)(2,1)S(1)}) custom-call(bf16[16,32,256]{2,1,0:T(8,128)(2,1)S(1)} %get-tuple-element.19.marked, f32[896,256]{1,0:T(8,128)S(1)} %get-tuple-element.20.mid, bf16[3,768,256]{2,1,0:T(8,128)(2,1)S(1)} %get-tuple-element.21.second, f32[1,256]{1,0:T(1,128)S(1)} %bitcast.9), custom_call_target="tpu_custom_call" | custom-call | flops 603979776 | tf_op jit(solution)/shard_map/pallas_call | solution.py:456
  20.5 1.5 %collective-permute-start.7 = (bf16[32,1280]{1,0:T(8,128)(2,1)S(1)}, bf16[32,1280]{1,0:T(8,128)(2,1)S(1)}, u32[]{:S(2)}, u32[]{:S(2)}) collective-permute-start(bf16[32,1280]{1,0:T(8,128)(2,1)S(1)} %shard_map.104.refs_0_), channel_id=1, source_target_pairs={{0,1},{1,0},{2,3},{3,2},{4,5},{5,4},{6,7},{7,6},{8,9},{9,8},{10,11... | collective-permute-start | bytes 245768 | tf_op jit(solution)/shard_map/ppermute | solution.py:24
  22.1 3.0 %collective-permute-done.7 = bf16[32,1280]{1,0:T(8,128)(2,1)S(1)} collective-permute-done((bf16[32,1280]{1,0:T(8,128)(2,1)S(1)}, bf16[32,1280]{1,0:T(8,128)(2,1)S(1)}, u32[]{:S(2)}, u32[]{:S(2)}) %collective-permute-start.7) | collective-permute-done | bytes 81952 | tf_op jit(solution)/shard_map/ppermute | solution.py:24
  25.0 1.3 %collective-permute-start.10 = (bf16[64,1280]{1,0:T(8,128)(2,1)S(1)}, bf16[64,1280]{1,0:T(8,128)(2,1)S(1)}, u32[]{:S(2)}, u32[]{:S(2)}) collective-permute-start(bf16[64,1280]{1,0:T(8,128)(2,1)S(1)} %constant_dynamic-update-slice_fusion.refs_1_), channel_id=1, source_target_pairs={{0,8},{4,12},{8,0},{12,4},{1,9},{5,13},{9,1},{13,5},{2,10},{6,14},... | collective-permute-start | bytes 491528 | tf_op jit(solution)/shard_map/ppermute | solution.py:24
  26.4 0.7 %collective-permute-start.9 = (bf16[32,1280]{1,0:T(8,128)(2,1)S(1)}, bf16[32,1280]{1,0:T(8,128)(2,1)S(1)}, u32[]{:S(2)}, u32[]{:S(2)}) collective-permute-start(bf16[32,1280]{1,0:T(8,128)(2,1)S(1)} %shard_map.104.refs_0_), channel_id=1, source_target_pairs={{0,8},{4,12},{8,0},{12,4},{1,9},{5,13},{9,1},{13,5},{2,10},{6,14},... | collective-permute-start | bytes 245768 | tf_op jit(solution)/shard_map/ppermute | solution.py:24
  27.1 0.3 collective-permute-done.8.refs_2_
  27.4 1.3 %collective-permute-start.11 = (bf16[32,1280]{1,0:T(8,128)(2,1)S(1)}, bf16[32,1280]{1,0:T(8,128)(2,1)S(1)}, u32[]{:S(2)}, u32[]{:S(2)}) collective-permute-start(bf16[32,1280]{1,0:T(8,128)(2,1)S(1)} %collective-permute-done.8.refs_2_), channel_id=1, source_target_pairs={{0,8},{4,12},{8,0},{12,4},{1,9},{5,13},{9,1},{13,5},{2,10},{6,14},... | collective-permute-start | bytes 245768 | tf_op jit(solution)/shard_map/ppermute | solution.py:24
  28.7 0.5 shard_map.103.own_keys
  29.2 3.9 %collective-permute-done.9.refs_3_ = bf16[32,1280]{1,0:T(8,128)(2,1)S(1)} collective-permute-done((bf16[32,1280]{1,0:T(8,128)(2,1)S(1)}, bf16[32,1280]{1,0:T(8,128)(2,1)S(1)}, u32[]{:S(2)}, u32[]{:S(2)}) %collective-permute-start.9) | collective-permute-done | bytes 81952 | tf_op jit(solution)/shard_map/ppermute | solution.py:24
  33.0 0.9 %collective-permute-done.11.refs_5_ = bf16[32,1280]{1,0:T(8,128)(2,1)S(1)} collective-permute-done((bf16[32,1280]{1,0:T(8,128)(2,1)S(1)}, bf16[32,1280]{1,0:T(8,128)(2,1)S(1)}, u32[]{:S(2)}, u32[]{:S(2)}) %collective-permute-start.11) | collective-permute-done | bytes 81952 | tf_op jit(solution)/shard_map/ppermute | solution.py:24
  33.9 1.8 %shard_map.105 = (bf16[144,128]{1,0:T(8,128)(2,1)S(1)}, bf16[144,128]{1,0:T(8,128)(2,1)S(1)}, bf16[512,256]{1,0:T(8,128)(2,1)S(1)}, bf16[512,1280]{1,0:T(8,128)(2,1)S(1)}) custom-call(bf16[512,256]{1,0:T(8,128)(2,1)S(1)} %get-tuple-element.22.cells.own, bf16[512,256]{1,0:T(8,128)(2,1)S(1)} %get-tuple-element.23.own_sent, ...), custom_call_target="tpu_custom_call" | custom-call | flops 738197504 | tf_op jit(solution)/shard_map/pallas_call | solution.py:456
  35.8 1.4 %shard_map.106 = (f32[136,128]{1,0:T(8,128)S(1)}, bf16[144,128]{1,0:T(8,128)(2,1)S(1)}) custom-call(bf16[512,256]{1,0:T(8,128)(2,1)S(1)} %get-tuple-element.22.cells.own, bf16[512,256]{1,0:T(8,128)(2,1)S(1)} %get-tuple-element.23.own_sent, bf16[512,1280]{1,0:T(8,128)(2,1)S(1)} %shard_map.103.own_keys, bf16[512,256]{1,0:T(8,128)(2,1)S(1)} %get-tuple-element.25.other, ...), custom_call_target="tpu_custom_call" | custom-call | flops 402653184 | tf_op jit(solution)/shard_map/pallas_call | solution.py:456
  37.1 2.4 %collective-permute-start.12 = (bf16[144,128]{1,0:T(8,128)(2,1)S(1)}, bf16[144,128]{1,0:T(8,128)(2,1)S(1)}, u32[]{:S(2)}, u32[]{:S(2)}) collective-permute-start(bf16[144,128]{1,0:T(8,128)(2,1)S(1)} %get-tuple-element.28), channel_id=1, source_target_pairs={{0,1},{1,0},{2,3},{3,2},{4,5},{5,4},{6,7},{7,6},{8,9},{9,8},{10,11... | collective-permute-start | bytes 110600 | tf_op jit(solution)/shard_map/ppermute | solution.py:24
  39.6 2.5 %collective-permute-start.13 = (bf16[144,128]{1,0:T(8,128)(2,1)S(1)}, bf16[144,128]{1,0:T(8,128)(2,1)S(1)}, u32[]{:S(2)}, u32[]{:S(2)}) collective-permute-start(bf16[144,128]{1,0:T(8,128)(2,1)S(1)} %get-tuple-element.29), channel_id=1, source_target_pairs={{0,2},{1,3},{2,0},{3,1},{4,6},{5,7},{6,4},{7,5},{8,10},{9,11},{10,... | collective-permute-start | bytes 110600 | tf_op jit(solution)/shard_map/ppermute | solution.py:24
  42.1 1.0 %collective-permute-start.14 = (bf16[144,128]{1,0:T(8,128)(2,1)S(1)}, bf16[144,128]{1,0:T(8,128)(2,1)S(1)}, u32[]{:S(2)}, u32[]{:S(2)}) collective-permute-start(bf16[144,128]{1,0:T(8,128)(2,1)S(1)} %get-tuple-element.30), channel_id=1, source_target_pairs={{0,3},{1,2},{2,1},{3,0},{4,7},{5,6},{6,5},{7,4},{8,11},{9,10},{10,... | collective-permute-start | bytes 110600 | tf_op jit(solution)/shard_map/ppermute | solution.py:24
  43.1 1.5 %collective-permute-done.13.refs_1_ = bf16[144,128]{1,0:T(8,128)(2,1)S(1)} collective-permute-done((bf16[144,128]{1,0:T(8,128)(2,1)S(1)}, bf16[144,128]{1,0:T(8,128)(2,1)S(1)}, u32[]{:S(2)}, u32[]{:S(2)}) %collective-permute-start.13) | collective-permute-done | bytes 36896 | tf_op jit(solution)/shard_map/ppermute | solution.py:24
  44.6 3.3 %collective-permute-done.14.refs_2_ = bf16[144,128]{1,0:T(8,128)(2,1)S(1)} collective-permute-done((bf16[144,128]{1,0:T(8,128)(2,1)S(1)}, bf16[144,128]{1,0:T(8,128)(2,1)S(1)}, u32[]{:S(2)}, u32[]{:S(2)}) %collective-permute-start.14) | collective-permute-done | bytes 36896 | tf_op jit(solution)/shard_map/ppermute | solution.py:24
  47.9 1.5 %collective-permute-start.15 = (bf16[144,128]{1,0:T(8,128)(2,1)S(1)}, bf16[144,128]{1,0:T(8,128)(2,1)S(1)}, u32[]{:S(2)}, u32[]{:S(2)}) collective-permute-start(bf16[144,128]{1,0:T(8,128)(2,1)S(1)} %get-tuple-element.32), channel_id=1, source_target_pairs={{0,8},{4,12},{8,0},{12,4},{1,9},{5,13},{9,1},{13,5},{2,10},{6,14},... | collective-permute-start | bytes 110600 | tf_op jit(solution)/shard_map/ppermute | solution.py:24
  49.4 2.6 %collective-permute-done.15.arrived = bf16[144,128]{1,0:T(8,128)(2,1)S(1)} collective-permute-done((bf16[144,128]{1,0:T(8,128)(2,1)S(1)}, bf16[144,128]{1,0:T(8,128)(2,1)S(1)}, u32[]{:S(2)}, u32[]{:S(2)}) %collective-permute-start.15) | collective-permute-done | bytes 36896 | tf_op jit(solution)/shard_map/ppermute | solution.py:24
  52.1 0.3 shard_map.109.mine
  52.4 0.8 %collective-permute-done.16.arrived = bf16[128,128]{1,0:T(8,128)(2,1)S(1)} collective-permute-done((bf16[128,128]{1,0:T(8,128)(2,1)S(1)}, bf16[128,128]{1,0:T(8,128)(2,1)S(1)}, u32[]{:S(2)}, u32[]{:S(2)}) %collective-permute-start.16) | collective-permute-done | bytes 32800 | tf_op jit(solution)/shard_map/ppermute | solution.py:24
  53.3 1.4 %fn.1 = bf16[320,128]{1,0:T(8,128)(2,1)} custom-call(bf16[64,1280]{1,0:T(8,128)(2,1)S(1)} %shard_map.109.mine, bf16[128,128]{1,0:T(8,128)(2,1)S(1)} %collective-permute-done.16.arrived, bf16[256,1280]{1,0:T(8,128)(2,1)S(1)} %copy-done, bf16[320,1280]{1,0:T(8,128)(2,1)S(1)} %bitcast.7), custom_call_target="tpu_custom_call" | custom-call | tf_op jit(solution)/shard_map/fn/pallas_call | solution.py:568
  (32 shorter events, 1.1 us)
Async XLA Ops:
  0.0 13.7 %collective-permute-start.5 = (bf16[32,1280]{1,0:T(8,128)(2,1)}, bf16[32,1280]{1,0:T(8,128)(2,1)S(1)}, u32[]{:S(2)}, u32[]{:S(2)}) collective-permute-start(bf16[32,1280]{1,0:T(8,128)(2,1)} %queries.1), channel_id=1, source_target_pairs={{0,4},{4,0},{8,12},{12,8},{1,5},{5,1},{9,13},{13,9},{2,6},{6,2},{1... | collective-permute-start | bytes 245768 | tf_op jit(solution)/shard_map/ppermute | solution.py:24
  1.6 6.3 %collective-permute-start.1 = (bf16[2,32,256]{2,1,0:T(8,128)(2,1)S(1)}, bf16[2,32,256]{2,1,0:T(8,128)(2,1)S(1)}, u32[]{:S(2)}, u32[]{:S(2)}) collective-permute-start(bf16[2,32,256]{2,1,0:T(8,128)(2,1)S(1)} %get-tuple-element.35), channel_id=1, source_target_pairs={{0,3},{1,0},{2,1},{3,2},{4,7},{5,4},{6,5},{7,6},{8,11},{9,8},{10,9... | collective-permute-start | bytes 98312 | tf_op jit(solution)/shard_map/ppermute | solution.py:19
  6.2 5.7 %collective-permute-start = (bf16[2,32,256]{2,1,0:T(8,128)(2,1)S(1)}, bf16[2,32,256]{2,1,0:T(8,128)(2,1)S(1)}, u32[]{:S(2)}, u32[]{:S(2)}) collective-permute-start(bf16[2,32,256]{2,1,0:T(8,128)(2,1)S(1)} %get-tuple-element.36), channel_id=1, source_target_pairs={{0,1},{1,2},{2,3},{3,0},{4,5},{5,6},{6,7},{7,4},{8,9},{9,10},{10,1... | collective-permute-start | bytes 98312 | tf_op jit(solution)/shard_map/ppermute | solution.py:19
  12.0 3.4 %collective-permute-start.3 = (bf16[20,2,256]{2,1,0:T(2,128)(2,1)S(1)}, bf16[20,2,256]{2,1,0:T(2,128)(2,1)S(1)}, u32[]{:S(2)}, u32[]{:S(2)}) collective-permute-start(bf16[20,2,256]{2,1,0:T(2,128)(2,1)S(1)} %get-tuple-element.37), channel_id=1, source_target_pairs={{0,12},{4,8},{8,4},{12,0},{1,13},{5,9},{9,5},{13,1},{2,14},{6,10},... | collective-permute-start | bytes 61448 | tf_op jit(solution)/shard_map/ppermute | solution.py:508
  12.2 3.2 %collective-permute-start.2 = (bf16[20,2,256]{2,1,0:T(2,128)(2,1)S(1)}, bf16[20,2,256]{2,1,0:T(2,128)(2,1)S(1)}, u32[]{:S(2)}, u32[]{:S(2)}) collective-permute-start(bf16[20,2,256]{2,1,0:T(2,128)(2,1)S(1)} %get-tuple-element.38), channel_id=1, source_target_pairs={{0,4},{4,0},{8,12},{12,8},{1,5},{5,1},{9,13},{13,9},{2,6},{6,2},{1... | collective-permute-start | bytes 61448 | tf_op jit(solution)/shard_map/ppermute | solution.py:24
  13.7 8.4 %collective-permute-start.6 = (bf16[32,1280]{1,0:T(8,128)(2,1)S(1)}, bf16[32,1280]{1,0:T(8,128)(2,1)S(1)}, u32[]{:S(2)}, u32[]{:S(2)}) collective-permute-start(bf16[32,1280]{1,0:T(8,128)(2,1)S(1)} %shard_map.104.refs_0_), channel_id=1, source_target_pairs={{0,2},{1,3},{2,0},{3,1},{4,6},{5,7},{6,4},{7,5},{8,10},{9,11},{10,... | collective-permute-start | bytes 245768 | tf_op jit(solution)/shard_map/ppermute | solution.py:24
  15.5 1.3 %copy-start.2 = (bf16[3,3,256,256]{3,2,1,0:T(8,128)(2,1)S(1)}, bf16[3,3,256,256]{3,2,1,0:T(8,128)(2,1)}, u32[]{:S(2)}) copy-start(bf16[3,3,256,256]{3,2,1,0:T(8,128)(2,1)} %param.12) | copy-start | bytes 3538948
  16.7 0.7 %copy-start.4 = (f32[256]{0:T(256)S(1)}, f32[256]{0:T(256)}, u32[]{:S(2)}) copy-start(f32[256]{0:T(256)} %param.13) | copy-start | bytes 3076
  17.4 1.5 %copy-start.5 = (f32[256]{0:T(256)S(1)}, f32[256]{0:T(256)}, u32[]{:S(2)}) copy-start(f32[256]{0:T(256)} %param.15) | copy-start | bytes 3076
  18.9 9.7 %copy-start.1 = (bf16[256,1280]{1,0:T(8,128)(2,1)S(1)}, bf16[256,1280]{1,0:T(8,128)(2,1)}, u32[]{:S(2)}) copy-start(bf16[256,1280]{1,0:T(8,128)(2,1)} %weight.3) | copy-start | bytes 1966084
  20.1 13.8 %collective-permute-start.4 = (bf16[512,256]{1,0:T(8,128)(2,1)S(1)}, bf16[512,256]{1,0:T(8,128)(2,1)S(1)}, u32[]{:S(2)}, u32[]{:S(2)}) collective-permute-start(bf16[512,256]{1,0:T(8,128)(2,1)S(1)} %get-tuple-element.23.own_sent), channel_id=1, source_target_pairs={{0,4},{4,0},{8,12},{12,8},{1,5},{5,1},{9,13},{13,9},{2,6},{6,2},{1... | collective-permute-start | bytes 786440 | tf_op jit(solution)/shard_map/ppermute | solution.py:24
  20.3 7.1 %collective-permute-start.8 = (bf16[32,1280]{1,0:T(8,128)(2,1)S(1)}, bf16[32,1280]{1,0:T(8,128)(2,1)S(1)}, u32[]{:S(2)}, u32[]{:S(2)}) collective-permute-start(bf16[32,1280]{1,0:T(8,128)(2,1)S(1)} %shard_map.104.refs_0_), channel_id=1, source_target_pairs={{0,3},{1,2},{2,1},{3,0},{4,7},{5,6},{6,5},{7,4},{8,11},{9,10},{10,... | collective-permute-start | bytes 245768 | tf_op jit(solution)/shard_map/ppermute | solution.py:24
  20.5 4.5 %collective-permute-start.7 = (bf16[32,1280]{1,0:T(8,128)(2,1)S(1)}, bf16[32,1280]{1,0:T(8,128)(2,1)S(1)}, u32[]{:S(2)}, u32[]{:S(2)}) collective-permute-start(bf16[32,1280]{1,0:T(8,128)(2,1)S(1)} %shard_map.104.refs_0_), channel_id=1, source_target_pairs={{0,1},{1,0},{2,3},{3,2},{4,5},{5,4},{6,7},{7,6},{8,9},{9,8},{10,11... | collective-permute-start | bytes 245768 | tf_op jit(solution)/shard_map/ppermute | solution.py:24
  25.0 8.9 %collective-permute-start.10 = (bf16[64,1280]{1,0:T(8,128)(2,1)S(1)}, bf16[64,1280]{1,0:T(8,128)(2,1)S(1)}, u32[]{:S(2)}, u32[]{:S(2)}) collective-permute-start(bf16[64,1280]{1,0:T(8,128)(2,1)S(1)} %constant_dynamic-update-slice_fusion.refs_1_), channel_id=1, source_target_pairs={{0,8},{4,12},{8,0},{12,4},{1,9},{5,13},{9,1},{13,5},{2,10},{6,14},... | collective-permute-start | bytes 491528 | tf_op jit(solution)/shard_map/ppermute | solution.py:24
  26.4 6.7 %collective-permute-start.9 = (bf16[32,1280]{1,0:T(8,128)(2,1)S(1)}, bf16[32,1280]{1,0:T(8,128)(2,1)S(1)}, u32[]{:S(2)}, u32[]{:S(2)}) collective-permute-start(bf16[32,1280]{1,0:T(8,128)(2,1)S(1)} %shard_map.104.refs_0_), channel_id=1, source_target_pairs={{0,8},{4,12},{8,0},{12,4},{1,9},{5,13},{9,1},{13,5},{2,10},{6,14},... | collective-permute-start | bytes 245768 | tf_op jit(solution)/shard_map/ppermute | solution.py:24
  27.4 6.5 %collective-permute-start.11 = (bf16[32,1280]{1,0:T(8,128)(2,1)S(1)}, bf16[32,1280]{1,0:T(8,128)(2,1)S(1)}, u32[]{:S(2)}, u32[]{:S(2)}) collective-permute-start(bf16[32,1280]{1,0:T(8,128)(2,1)S(1)} %collective-permute-done.8.refs_2_), channel_id=1, source_target_pairs={{0,8},{4,12},{8,0},{12,4},{1,9},{5,13},{9,1},{13,5},{2,10},{6,14},... | collective-permute-start | bytes 245768 | tf_op jit(solution)/shard_map/ppermute | solution.py:24
  35.8 16.3 %copy-start = (bf16[256,1280]{1,0:T(8,128)(2,1)S(1)}, bf16[256,1280]{1,0:T(8,128)(2,1)}, u32[]{:S(2)}) copy-start(bf16[256,1280]{1,0:T(8,128)(2,1)} %value_weight.3) | copy-start | bytes 1966084
  37.1 16.1 %copy-start.3 = (bf16[1280,320]{0,1:T(8,128)(2,1)S(1)}, bf16[1280,320]{0,1:T(8,128)(2,1)}, u32[]{:S(2)}) copy-start(bf16[1280,320]{0,1:T(8,128)(2,1)} %param.19) | copy-start | bytes 2457604
  37.1 5.9 %collective-permute-start.12 = (bf16[144,128]{1,0:T(8,128)(2,1)S(1)}, bf16[144,128]{1,0:T(8,128)(2,1)S(1)}, u32[]{:S(2)}, u32[]{:S(2)}) collective-permute-start(bf16[144,128]{1,0:T(8,128)(2,1)S(1)} %get-tuple-element.28), channel_id=1, source_target_pairs={{0,1},{1,0},{2,3},{3,2},{4,5},{5,4},{6,7},{7,6},{8,9},{9,8},{10,11... | collective-permute-start | bytes 110600 | tf_op jit(solution)/shard_map/ppermute | solution.py:24
  39.6 5.0 %collective-permute-start.13 = (bf16[144,128]{1,0:T(8,128)(2,1)S(1)}, bf16[144,128]{1,0:T(8,128)(2,1)S(1)}, u32[]{:S(2)}, u32[]{:S(2)}) collective-permute-start(bf16[144,128]{1,0:T(8,128)(2,1)S(1)} %get-tuple-element.29), channel_id=1, source_target_pairs={{0,2},{1,3},{2,0},{3,1},{4,6},{5,7},{6,4},{7,5},{8,10},{9,11},{10,... | collective-permute-start | bytes 110600 | tf_op jit(solution)/shard_map/ppermute | solution.py:24
  42.1 5.8 %collective-permute-start.14 = (bf16[144,128]{1,0:T(8,128)(2,1)S(1)}, bf16[144,128]{1,0:T(8,128)(2,1)S(1)}, u32[]{:S(2)}, u32[]{:S(2)}) collective-permute-start(bf16[144,128]{1,0:T(8,128)(2,1)S(1)} %get-tuple-element.30), channel_id=1, source_target_pairs={{0,3},{1,2},{2,1},{3,0},{4,7},{5,6},{6,5},{7,4},{8,11},{9,10},{10,... | collective-permute-start | bytes 110600 | tf_op jit(solution)/shard_map/ppermute | solution.py:24
  47.9 4.0 %collective-permute-start.15 = (bf16[144,128]{1,0:T(8,128)(2,1)S(1)}, bf16[144,128]{1,0:T(8,128)(2,1)S(1)}, u32[]{:S(2)}, u32[]{:S(2)}) collective-permute-start(bf16[144,128]{1,0:T(8,128)(2,1)S(1)} %get-tuple-element.32), channel_id=1, source_target_pairs={{0,8},{4,12},{8,0},{12,4},{1,9},{5,13},{9,1},{13,5},{2,10},{6,14},... | collective-permute-start | bytes 110600 | tf_op jit(solution)/shard_map/ppermute | solution.py:24
  52.0 1.3 %collective-permute-start.16 = (bf16[128,128]{1,0:T(8,128)(2,1)S(1)}, bf16[128,128]{1,0:T(8,128)(2,1)S(1)}, u32[]{:S(2)}, u32[]{:S(2)}) collective-permute-start(bf16[128,128]{1,0:T(8,128)(2,1)S(1)} %shard_map.108.normalized), channel_id=1, source_target_pairs={{0,4},{4,0},{8,12},{12,8},{1,5},{5,1},{9,13},{13,9},{2,6},{6,2},{1... | collective-permute-start | bytes 98312 | tf_op jit(solution)/shard_map/ppermute | solution.py:24

commit v9 on v8

--- a/solution.py
+++ b/solution.py
@@ -383,14 +383,17 @@
     )
 
 
-def first_score_kernel(own, own_sent, own_keys, other_sent, weight, *refs):
-    *queries, send_2, send_3, other, keys, held, blocks = refs
-    row, across = lax.axis_index("row"), lax.axis_index("col") // 2
-    hold_queries(held, queries[:3], queries[3:], row // 2 != across)
+def other_kernel(other_sent, weight, other, keys):
     values = other_sent[...].astype(jnp.float32)
     other[...] = jnp.where(values < FAR, values, 0.0).astype(jnp.bfloat16)
     key_kernel(other, weight, keys)
-    scores = masked_scores(held, own_sent, own_keys), masked_scores(held, other_sent, keys)
+
+
+def first_score_kernel(own, own_sent, own_keys, other, other_sent, other_keys, *refs):
+    *queries, send_2, send_3, held, blocks = refs
+    row, across = lax.axis_index("row"), lax.axis_index("col") // 2
+    hold_queries(held, queries[:2], queries[2:], row // 2 != across)
+    scores = masked_scores(held, own_sent, own_keys), masked_scores(held, other_sent, other_keys)
     for parity, block in enumerate(score_blocks(scores, (own, other))):
         write_whole(blocks.at[parity], *block)
     odd = lax.rem(row, 2)
@@ -401,7 +404,7 @@
 def last_score_kernel(own, own_sent, own_keys, other, other_sent, other_keys, *refs):
     *queries, kept, send_1, held, blocks = refs
     row, across = lax.axis_index("row"), lax.axis_index("col") // 2
-    hold_queries(held, queries[:3], queries[3:], row // 2 == across)
+    hold_queries(held, queries[:2], queries[2:], row // 2 == across)
     scores = masked_scores(held, own_sent, own_keys), masked_scores(held, other_sent, other_keys)
     for parity, block in enumerate(score_blocks(scores, (own, other))):
         write_whole(blocks.at[parity], *block)
@@ -498,7 +501,6 @@
     bottom = shifted(marked[:HALO], "row", -1)
     one = flipped(queries, "row", 1)
     three = flipped(queries, "row", 3)
-    far_queries = flipped(queries, "col", 2)
 
     edge = lambda cut: jnp.concatenate([top[:, cut], marked[:, cut], bottom[:, cut]], axis=0)
     even = lax.rem(col, 2) == 0
@@ -507,8 +509,8 @@
     rounds = [(k, (k + 1 if k % 2 else k - 1) % cols) for k in range(cols)]
     crossed = lax.ppermute(jnp.where(even, *ends[::-1]), "col", rounds)
 
-    pair = jnp.concatenate([two, one], axis=0)
-    far_pair = flipped(pair, "col", 2)
+    trio = jnp.concatenate([queries, two, one], axis=0)
+    far_trio = flipped(trio, "col", 2)
     far_three = flipped(three, "col", 2)
 
     mid, weight = call(
@@ -537,13 +539,16 @@
         key_kernel, [((cells, width), half)], [own, key_weight],
         limit=4, flops=2 * cells * width * channels,
     )
-    all_queries = [queries, pair, three, far_queries, far_pair, far_three]
+    all_queries = [trio, three, far_trio, far_three]
     score_scratch = [((block, width), half), ((2,) + whole_block, wide)]
-    send_2, send_3, other, other_keys = call(
-        first_score_kernel,
-        [(sent_block, half)] * 2 + [((cells, channels), half), ((cells, width), half)],
-        [own, own_sent, own_keys, other_sent, key_weight, *all_queries],
-        score_scratch, limit=8, flops=score_flops + 2 * cells * channels * width,
+    other, other_keys = call(
+        other_kernel, [((cells, channels), half), ((cells, width), half)],
+        [other_sent, key_weight], limit=4, flops=2 * cells * channels * width,
+    )
+    send_2, send_3 = call(
+        first_score_kernel, [(sent_block, half)] * 2,
+        [own, own_sent, own_keys, other, other_sent, other_keys, *all_queries],
+        score_scratch, limit=8, flops=score_flops,
     )
     arrived_2, arrived_3 = flipped(send_2, "row", 2), flipped(send_3, "row", 3)
     kept, send_1 = call(

time: 54.8 us -> 46.9 us (0.86)
  waiting for transfers between devices: 23.6 us -> 15 us
    ppermute x14 -> x13, waiting for transfers between devices: 16.3 us -> 12.7 us  [flipped(): return lax.ppermute(array, axis, [(i, i ^ bit) for i in range(count)])]
    ppermute x2, waiting for transfers between devices: 5.66 us -> 2.3 us  [shifted(): lax.ppermute(array, axis, [(i, (i + step) % count) for i in range(count)])]
    ppermute x1, waiting for transfers between devices: 1.68 us -> 0.01 us  [kernel_path(): crossed = lax.ppermute(jnp.where(even, *ends[::-1]), 'col', rounds)]
    ppermute x1, starting transfers between devices: 0.24 us -> 1.59 us  [kernel_path(): crossed = lax.ppermute(jnp.where(even, *ends[::-1]), 'col', rounds)]
    ppermute x14 -> x13, starting transfers between devices: 14.7 us -> 13.7 us  [flipped(): return lax.ppermute(array, axis, [(i, i ^ bit) for i in range(count)])]
    pallas_call x10 -> x11, Pallas kernels: 7.84 us -> 7.92 us  [call(): pl.pallas_call(kernel, out_shape=[pltpu.VMEM(shape, dtype) for shape, dty...]
    unnamed x13 -> x12, local copies, waits for them, and re-layouts: 1.97 us -> 1.97 us
  transfers between devices with their start and end apart: 17 -> 16, of which waited for: 11 -> 8; matrix products, arithmetic and copies ran while one was open for 0% -> 0% of each run, Pallas kernels for 8% -> 14%
where the time goes in v9:
time: 46.9 us; the launch traced here: 46.7 us
  starting transfers between devices  20 us (43%)
  waiting for transfers between devices  15 us (32%)
  Pallas kernels  9.29 us (20%)
  local copies, waits for them, and re-layouts  2.02 us (4%)
    ppermute x13, starting transfers between devices, flipped(): return lax.ppermute(array, axis, [(i, i ^ bit) for i in range(count)])  13.7 us
    ppermute x13, waiting for transfers between devices, flipped(): return lax.ppermute(array, axis, [(i, i ^ bit) for i in range(count)])  12.7 us
    pallas_call x11, Pallas kernels, call(): pl.pallas_call(kernel, out_shape=[pltpu.VMEM(shape, dtype) for shape, dty...  7.92 us
    ppermute x2, starting transfers between devices, shifted(): lax.ppermute(array, axis, [(i, (i + step) % count) for i in range(count)])  4.71 us
    ppermute x2, waiting for transfers between devices, shifted(): lax.ppermute(array, axis, [(i, (i + step) % count) for i in range(count)])  2.3 us
    unnamed x12, local copies, waits for them, and re-layouts  1.97 us
    ppermute x1, starting transfers between devices, kernel_path(): crossed = lax.ppermute(jnp.where(even, *ends[::-1]), 'col', rounds)  1.59 us
    pallas_call x1, Pallas kernels, kernel_path(): pl.pallas_call(finish_kernel, out_shape=jax.ShapeDtypeStruct((out_weight....  1.37 us
  transfers between devices with their start and end apart: 16, of which 8 were waited for; matrix products, arithmetic and copies ran while one was open for 0% of the time, Pallas kernels for 14%

profile of v9, /device:TPU:0, one launch (start us, length us, event | category | flops | bytes accessed | tf_op | source)
XLA Modules:
  0.0 46.7 jit_solution(7044037583130538405)
XLA Ops:
  0.0 0.5 %collective-permute-start.5 = (bf16[32,1280]{1,0:T(8,128)(2,1)}, bf16[32,1280]{1,0:T(8,128)(2,1)S(1)}, u32[]{:S(2)}, u32[]{:S(2)}) collective-permute-start(bf16[32,1280]{1,0:T(8,128)(2,1)} %queries.1), channel_id=1, source_target_pairs={{0,4},{4,0},{8,12},{12,8},{1,5},{5,1},{9,13},{13,9},{2,6},{6,2},{1... | collective-permute-start | bytes 245768 | tf_op jit(solution)/shard_map/ppermute | solution.py:24
  0.5 1.1 %shard_map.100 = (bf16[16,32,256]{2,1,0:T(8,128)(2,1)S(1)}, bf16[32,1280]{1,0:T(8,128)(2,1)S(1)}) custom-call(bf16[16,32,256]{2,1,0:T(8,128)(2,1)} %features.1, s32[16,32]{1,0:T(8,128)} %tissue.1, bf16[32,1280]{1,0:T(8,128)(2,1)} %queries.1), custom_call_target="tpu_custom_call" | custom-call | flops 1048576 | tf_op jit(solution)/shard_map/pallas_call | solution.py:459
  1.6 2.6 %collective-permute-start = (bf16[2,32,256]{2,1,0:T(8,128)(2,1)S(1)}, bf16[2,32,256]{2,1,0:T(8,128)(2,1)S(1)}, u32[]{:S(2)}, u32[]{:S(2)}) collective-permute-start(bf16[2,32,256]{2,1,0:T(8,128)(2,1)S(1)} %get-tuple-element.36), channel_id=1, source_target_pairs={{0,1},{1,2},{2,3},{3,0},{4,5},{5,6},{6,7},{7,4},{8,9},{9,10},{10,1... | collective-permute-start | bytes 98312 | tf_op jit(solution)/shard_map/ppermute | solution.py:19
  4.2 2.1 %collective-permute-start.1 = (bf16[2,32,256]{2,1,0:T(8,128)(2,1)S(1)}, bf16[2,32,256]{2,1,0:T(8,128)(2,1)S(1)}, u32[]{:S(2)}, u32[]{:S(2)}) collective-permute-start(bf16[2,32,256]{2,1,0:T(8,128)(2,1)S(1)} %get-tuple-element.35), channel_id=1, source_target_pairs={{0,3},{1,0},{2,1},{3,2},{4,7},{5,4},{6,5},{7,6},{8,11},{9,8},{10,9... | collective-permute-start | bytes 98312 | tf_op jit(solution)/shard_map/ppermute | solution.py:19
  6.3 2.0 %collective-permute-done.top = bf16[2,32,256]{2,1,0:T(8,128)(2,1)S(1)} collective-permute-done((bf16[2,32,256]{2,1,0:T(8,128)(2,1)S(1)}, bf16[2,32,256]{2,1,0:T(8,128)(2,1)S(1)}, u32[]{:S(2)}, u32[]{:S(2)}) %collective-permute-start) | collective-permute-done | bytes 32800 | tf_op jit(solution)/shard_map/ppermute | solution.py:19
  8.3 0.3 collective-permute-done.1.bottom
  8.7 0.1 collective-permute-start.2
  8.8 1.6 %collective-permute-start.3 = (bf16[20,2,256]{2,1,0:T(2,128)(2,1)S(1)}, bf16[20,2,256]{2,1,0:T(2,128)(2,1)S(1)}, u32[]{:S(2)}, u32[]{:S(2)}) collective-permute-start(bf16[20,2,256]{2,1,0:T(2,128)(2,1)S(1)} %get-tuple-element.37), channel_id=1, source_target_pairs={{0,12},{4,8},{8,4},{12,0},{1,13},{5,9},{9,5},{13,1},{2,14},{6,10},... | collective-permute-start | bytes 61448 | tf_op jit(solution)/shard_map/ppermute | solution.py:510
  10.4 2.1 %collective-permute-start.6 = (bf16[32,1280]{1,0:T(8,128)(2,1)S(1)}, bf16[32,1280]{1,0:T(8,128)(2,1)S(1)}, u32[]{:S(2)}, u32[]{:S(2)}) collective-permute-start(bf16[32,1280]{1,0:T(8,128)(2,1)S(1)} %shard_map.105), channel_id=1, source_target_pairs={{0,2},{1,3},{2,0},{3,1},{4,6},{5,7},{6,4},{7,5},{8,10},{9,11},{10,... | collective-permute-start | bytes 245768 | tf_op jit(solution)/shard_map/ppermute | solution.py:24
  12.5 2.0 %collective-permute-start.7 = (bf16[32,1280]{1,0:T(8,128)(2,1)S(1)}, bf16[32,1280]{1,0:T(8,128)(2,1)S(1)}, u32[]{:S(2)}, u32[]{:S(2)}) collective-permute-start(bf16[32,1280]{1,0:T(8,128)(2,1)S(1)} %shard_map.105), channel_id=1, source_target_pairs={{0,1},{1,0},{2,3},{3,2},{4,5},{5,4},{6,7},{7,6},{8,9},{9,8},{10,11... | collective-permute-start | bytes 245768 | tf_op jit(solution)/shard_map/ppermute | solution.py:24
  14.6 1.3 %copy-done.1 = bf16[3,3,256,256]{3,2,1,0:T(8,128)(2,1)S(1)} copy-done((bf16[3,3,256,256]{3,2,1,0:T(8,128)(2,1)S(1)}, bf16[3,3,256,256]{3,2,1,0:T(8,128)(2,1)}, u32[]{:S(2)}) %copy-start.1) | copy-done | bytes 1179672
  15.8 0.7 %copy-done.4 = f32[256]{0:T(256)S(1)} copy-done((f32[256]{0:T(256)S(1)}, f32[256]{0:T(256)}, u32[]{:S(2)}) %copy-start.4) | copy-done | bytes 1048
  16.5 1.5 %shard_map.101 = (f32[896,256]{1,0:T(8,128)S(1)}, bf16[3,768,256]{2,1,0:T(8,128)(2,1)S(1)}) custom-call(bf16[16,32,256]{2,1,0:T(8,128)(2,1)S(1)} %get-tuple-element.19.marked, bf16[2,32,256]{2,1,0:T(8,128)(2,1)S(1)} %collective-permute-done.top, bf16[2,32,256]{2,1,0:T(8,128)(2,1)S(1)} %collective-permute-done.1.bottom, ...), custom_call_target="tpu_custom_call" | custom-call | flops 704643072 | tf_op jit(solution)/shard_map/pallas_call | solution.py:459
  18.1 1.1 %shard_map.102 = (bf16[512,256]{1,0:T(8,128)(2,1)S(1)}, bf16[512,256]{1,0:T(8,128)(2,1)S(1)}) custom-call(bf16[16,32,256]{2,1,0:T(8,128)(2,1)S(1)} %get-tuple-element.19.marked, f32[896,256]{1,0:T(8,128)S(1)} %get-tuple-element.20.mid, bf16[3,768,256]{2,1,0:T(8,128)(2,1)S(1)} %get-tuple-element.21.second, f32[1,256]{1,0:T(1,128)S(1)} %bitcast.9), custom_call_target="tpu_custom_call" | custom-call | flops 603979776 | tf_op jit(solution)/shard_map/pallas_call | solution.py:459
  19.3 0.4 collective-permute-start.9
  19.8 2.5 %collective-permute-start.8 = (bf16[32,1280]{1,0:T(8,128)(2,1)S(1)}, bf16[32,1280]{1,0:T(8,128)(2,1)S(1)}, u32[]{:S(2)}, u32[]{:S(2)}) collective-permute-start(bf16[32,1280]{1,0:T(8,128)(2,1)S(1)} %shard_map.105), channel_id=1, source_target_pairs={{0,3},{1,2},{2,1},{3,0},{4,7},{5,6},{6,5},{7,4},{8,11},{9,10},{10,... | collective-permute-start | bytes 245768 | tf_op jit(solution)/shard_map/ppermute | solution.py:24
  22.3 3.8 %collective-permute-done.8.refs_1_ = bf16[32,1280]{1,0:T(8,128)(2,1)S(1)} collective-permute-done((bf16[32,1280]{1,0:T(8,128)(2,1)S(1)}, bf16[32,1280]{1,0:T(8,128)(2,1)S(1)}, u32[]{:S(2)}, u32[]{:S(2)}) %collective-permute-start.8) | collective-permute-done | bytes 81952 | tf_op jit(solution)/shard_map/ppermute | solution.py:24
  26.1 1.6 %collective-permute-start.10 = (bf16[32,1280]{1,0:T(8,128)(2,1)S(1)}, bf16[32,1280]{1,0:T(8,128)(2,1)S(1)}, u32[]{:S(2)}, u32[]{:S(2)}) collective-permute-start(bf16[32,1280]{1,0:T(8,128)(2,1)S(1)} %collective-permute-done.8.refs_1_), channel_id=1, source_target_pairs={{0,8},{4,12},{8,0},{12,4},{1,9},{5,13},{9,1},{13,5},{2,10},{6,14},... | collective-permute-start | bytes 245768 | tf_op jit(solution)/shard_map/ppermute | solution.py:24
  27.8 0.5 %shard_map.103.own_keys = bf16[512,1280]{1,0:T(8,128)(2,1)S(1)} custom-call(bf16[512,256]{1,0:T(8,128)(2,1)S(1)} %get-tuple-element.22.cells.own, bf16[256,1280]{1,0:T(8,128)(2,1)S(1)} %copy-done.3), custom_call_target="tpu_custom_call" | custom-call | flops 335544320 | tf_op jit(solution)/shard_map/pallas_call | solution.py:459
  28.3 0.5 %shard_map.104 = (bf16[512,256]{1,0:T(8,128)(2,1)S(1)}, bf16[512,1280]{1,0:T(8,128)(2,1)S(1)}) custom-call(bf16[512,256]{1,0:T(8,128)(2,1)S(1)} %collective-permute-done.4.other_sent, bf16[256,1280]{1,0:T(8,128)(2,1)S(1)} %copy-done.3), custom_call_target="tpu_custom_call" | custom-call | flops 335544320 | tf_op jit(solution)/shard_map/pallas_call | solution.py:459
  28.8 1.7 %collective-permute-done.10.refs_3_ = bf16[32,1280]{1,0:T(8,128)(2,1)S(1)} collective-permute-done((bf16[32,1280]{1,0:T(8,128)(2,1)S(1)}, bf16[32,1280]{1,0:T(8,128)(2,1)S(1)}, u32[]{:S(2)}, u32[]{:S(2)}) %collective-permute-start.10) | collective-permute-done | bytes 81952 | tf_op jit(solution)/shard_map/ppermute | solution.py:24
  30.6 1.4 %shard_map.107 = (bf16[144,128]{1,0:T(8,128)(2,1)S(1)}, bf16[144,128]{1,0:T(8,128)(2,1)S(1)}) custom-call(bf16[512,256]{1,0:T(8,128)(2,1)S(1)} %get-tuple-element.22.cells.own, bf16[512,256]{1,0:T(8,128)(2,1)S(1)} %get-tuple-element.23.own_sent, bf16[512,1280]{1,0:T(8,128)(2,1)S(1)} %shard_map.103.own_keys, bf16[512,256]{1,0:T(8,128)(2,1)S(1)} %get-tuple-element.24.other, ...), custom_call_target="tpu_custom_call" | custom-call | flops 402653184 | tf_op jit(solution)/shard_map/pallas_call | solution.py:459
  32.0 2.5 %collective-permute-start.13 = (bf16[144,128]{1,0:T(8,128)(2,1)S(1)}, bf16[144,128]{1,0:T(8,128)(2,1)S(1)}, u32[]{:S(2)}, u32[]{:S(2)}) collective-permute-start(bf16[144,128]{1,0:T(8,128)(2,1)S(1)} %get-tuple-element.30), channel_id=1, source_target_pairs={{0,3},{1,2},{2,1},{3,0},{4,7},{5,6},{6,5},{7,4},{8,11},{9,10},{10,... | collective-permute-start | bytes 110600 | tf_op jit(solution)/shard_map/ppermute | solution.py:24
  34.5 1.4 %shard_map.106 = (f32[136,128]{1,0:T(8,128)S(1)}, bf16[144,128]{1,0:T(8,128)(2,1)S(1)}) custom-call(bf16[512,256]{1,0:T(8,128)(2,1)S(1)} %get-tuple-element.22.cells.own, bf16[512,256]{1,0:T(8,128)(2,1)S(1)} %get-tuple-element.23.own_sent, bf16[512,1280]{1,0:T(8,128)(2,1)S(1)} %shard_map.103.own_keys, bf16[512,256]{1,0:T(8,128)(2,1)S(1)} %get-tuple-element.24.other, ...), custom_call_target="tpu_custom_call" | custom-call | flops 402653184 | tf_op jit(solution)/shard_map/pallas_call | solution.py:459
  35.9 1.0 %collective-permute-start.11 = (bf16[144,128]{1,0:T(8,128)(2,1)S(1)}, bf16[144,128]{1,0:T(8,128)(2,1)S(1)}, u32[]{:S(2)}, u32[]{:S(2)}) collective-permute-start(bf16[144,128]{1,0:T(8,128)(2,1)S(1)} %get-tuple-element.28), channel_id=1, source_target_pairs={{0,1},{1,0},{2,3},{3,2},{4,5},{5,4},{6,7},{7,6},{8,9},{9,8},{10,11... | collective-permute-start | bytes 110600 | tf_op jit(solution)/shard_map/ppermute | solution.py:24
  36.9 0.9 %collective-permute-done.13.refs_2_ = bf16[144,128]{1,0:T(8,128)(2,1)S(1)} collective-permute-done((bf16[144,128]{1,0:T(8,128)(2,1)S(1)}, bf16[144,128]{1,0:T(8,128)(2,1)S(1)}, u32[]{:S(2)}, u32[]{:S(2)}) %collective-permute-start.13) | collective-permute-done | bytes 36896 | tf_op jit(solution)/shard_map/ppermute | solution.py:24
  37.8 2.1 %collective-permute-done.11.refs_0_ = bf16[144,128]{1,0:T(8,128)(2,1)S(1)} collective-permute-done((bf16[144,128]{1,0:T(8,128)(2,1)S(1)}, bf16[144,128]{1,0:T(8,128)(2,1)S(1)}, u32[]{:S(2)}, u32[]{:S(2)}) %collective-permute-start.11) | collective-permute-done | bytes 36896 | tf_op jit(solution)/shard_map/ppermute | solution.py:24
  40.0 0.6 %collective-permute-start.14 = (bf16[144,128]{1,0:T(8,128)(2,1)S(1)}, bf16[144,128]{1,0:T(8,128)(2,1)S(1)}, u32[]{:S(2)}, u32[]{:S(2)}) collective-permute-start(bf16[144,128]{1,0:T(8,128)(2,1)S(1)} %get-tuple-element.32), channel_id=1, source_target_pairs={{0,8},{4,12},{8,0},{12,4},{1,9},{5,13},{9,1},{13,5},{2,10},{6,14},... | collective-permute-start | bytes 110600 | tf_op jit(solution)/shard_map/ppermute | solution.py:24
  40.6 3.4 %collective-permute-done.14.arrived = bf16[144,128]{1,0:T(8,128)(2,1)S(1)} collective-permute-done((bf16[144,128]{1,0:T(8,128)(2,1)S(1)}, bf16[144,128]{1,0:T(8,128)(2,1)S(1)}, u32[]{:S(2)}, u32[]{:S(2)}) %collective-permute-start.14) | collective-permute-done | bytes 36896 | tf_op jit(solution)/shard_map/ppermute | solution.py:24
  44.1 0.3 shard_map.110.mine
  44.5 0.8 %collective-permute-done.15.arrived = bf16[128,128]{1,0:T(8,128)(2,1)S(1)} collective-permute-done((bf16[128,128]{1,0:T(8,128)(2,1)S(1)}, bf16[128,128]{1,0:T(8,128)(2,1)S(1)}, u32[]{:S(2)}, u32[]{:S(2)}) %collective-permute-start.15) | collective-permute-done | bytes 32800 | tf_op jit(solution)/shard_map/ppermute | solution.py:24
  45.3 1.4 %fn.1 = bf16[320,128]{1,0:T(8,128)(2,1)} custom-call(bf16[64,1280]{1,0:T(8,128)(2,1)S(1)} %shard_map.110.mine, bf16[128,128]{1,0:T(8,128)(2,1)S(1)} %collective-permute-done.15.arrived, bf16[256,1280]{1,0:T(8,128)(2,1)S(1)} %copy-done, bf16[320,1280]{1,0:T(8,128)(2,1)S(1)} %bitcast.7), custom_call_target="tpu_custom_call" | custom-call | tf_op jit(solution)/shard_map/fn/pallas_call | solution.py:573
  (30 shorter events, 0.5 us)
Async XLA Ops:
  0.0 10.4 %collective-permute-start.5 = (bf16[32,1280]{1,0:T(8,128)(2,1)}, bf16[32,1280]{1,0:T(8,128)(2,1)S(1)}, u32[]{:S(2)}, u32[]{:S(2)}) collective-permute-start(bf16[32,1280]{1,0:T(8,128)(2,1)} %queries.1), channel_id=1, source_target_pairs={{0,4},{4,0},{8,12},{12,8},{1,5},{5,1},{9,13},{13,9},{2,6},{6,2},{1... | collective-permute-start | bytes 245768 | tf_op jit(solution)/shard_map/ppermute | solution.py:24
  1.6 6.8 %collective-permute-start = (bf16[2,32,256]{2,1,0:T(8,128)(2,1)S(1)}, bf16[2,32,256]{2,1,0:T(8,128)(2,1)S(1)}, u32[]{:S(2)}, u32[]{:S(2)}) collective-permute-start(bf16[2,32,256]{2,1,0:T(8,128)(2,1)S(1)} %get-tuple-element.36), channel_id=1, source_target_pairs={{0,1},{1,2},{2,3},{3,0},{4,5},{5,6},{6,7},{7,4},{8,9},{9,10},{10,1... | collective-permute-start | bytes 98312 | tf_op jit(solution)/shard_map/ppermute | solution.py:19
  4.2 4.4 %collective-permute-start.1 = (bf16[2,32,256]{2,1,0:T(8,128)(2,1)S(1)}, bf16[2,32,256]{2,1,0:T(8,128)(2,1)S(1)}, u32[]{:S(2)}, u32[]{:S(2)}) collective-permute-start(bf16[2,32,256]{2,1,0:T(8,128)(2,1)S(1)} %get-tuple-element.35), channel_id=1, source_target_pairs={{0,3},{1,0},{2,1},{3,2},{4,7},{5,4},{6,5},{7,6},{8,11},{9,8},{10,9... | collective-permute-start | bytes 98312 | tf_op jit(solution)/shard_map/ppermute | solution.py:19
  8.7 5.8 %collective-permute-start.2 = (bf16[20,2,256]{2,1,0:T(2,128)(2,1)S(1)}, bf16[20,2,256]{2,1,0:T(2,128)(2,1)S(1)}, u32[]{:S(2)}, u32[]{:S(2)}) collective-permute-start(bf16[20,2,256]{2,1,0:T(2,128)(2,1)S(1)} %get-tuple-element.38), channel_id=1, source_target_pairs={{0,4},{4,0},{8,12},{12,8},{1,5},{5,1},{9,13},{13,9},{2,6},{6,2},{1... | collective-permute-start | bytes 61448 | tf_op jit(solution)/shard_map/ppermute | solution.py:24
  8.8 5.8 %collective-permute-start.3 = (bf16[20,2,256]{2,1,0:T(2,128)(2,1)S(1)}, bf16[20,2,256]{2,1,0:T(2,128)(2,1)S(1)}, u32[]{:S(2)}, u32[]{:S(2)}) collective-permute-start(bf16[20,2,256]{2,1,0:T(2,128)(2,1)S(1)} %get-tuple-element.37), channel_id=1, source_target_pairs={{0,12},{4,8},{8,4},{12,0},{1,13},{5,9},{9,5},{13,1},{2,14},{6,10},... | collective-permute-start | bytes 61448 | tf_op jit(solution)/shard_map/ppermute | solution.py:510
  10.4 8.9 %collective-permute-start.6 = (bf16[32,1280]{1,0:T(8,128)(2,1)S(1)}, bf16[32,1280]{1,0:T(8,128)(2,1)S(1)}, u32[]{:S(2)}, u32[]{:S(2)}) collective-permute-start(bf16[32,1280]{1,0:T(8,128)(2,1)S(1)} %shard_map.105), channel_id=1, source_target_pairs={{0,2},{1,3},{2,0},{3,1},{4,6},{5,7},{6,4},{7,5},{8,10},{9,11},{10,... | collective-permute-start | bytes 245768 | tf_op jit(solution)/shard_map/ppermute | solution.py:24
  12.5 6.8 %collective-permute-start.7 = (bf16[32,1280]{1,0:T(8,128)(2,1)S(1)}, bf16[32,1280]{1,0:T(8,128)(2,1)S(1)}, u32[]{:S(2)}, u32[]{:S(2)}) collective-permute-start(bf16[32,1280]{1,0:T(8,128)(2,1)S(1)} %shard_map.105), channel_id=1, source_target_pairs={{0,1},{1,0},{2,3},{3,2},{4,5},{5,4},{6,7},{7,6},{8,9},{9,8},{10,11... | collective-permute-start | bytes 245768 | tf_op jit(solution)/shard_map/ppermute | solution.py:24
  14.5 1.3 %copy-start.1 = (bf16[3,3,256,256]{3,2,1,0:T(8,128)(2,1)S(1)}, bf16[3,3,256,256]{3,2,1,0:T(8,128)(2,1)}, u32[]{:S(2)}) copy-start(bf16[3,3,256,256]{3,2,1,0:T(8,128)(2,1)} %param.12) | copy-start | bytes 3538948
  15.8 0.7 %copy-start.4 = (f32[256]{0:T(256)S(1)}, f32[256]{0:T(256)}, u32[]{:S(2)}) copy-start(f32[256]{0:T(256)} %param.13) | copy-start | bytes 3076
  16.5 1.5 %copy-start.5 = (f32[256]{0:T(256)S(1)}, f32[256]{0:T(256)}, u32[]{:S(2)}) copy-start(f32[256]{0:T(256)} %param.15) | copy-start | bytes 3076
  18.0 9.7 %copy-start.3 = (bf16[256,1280]{1,0:T(8,128)(2,1)S(1)}, bf16[256,1280]{1,0:T(8,128)(2,1)}, u32[]{:S(2)}) copy-start(bf16[256,1280]{1,0:T(8,128)(2,1)} %weight.3) | copy-start | bytes 1966084
  19.2 9.1 %collective-permute-start.4 = (bf16[512,256]{1,0:T(8,128)(2,1)S(1)}, bf16[512,256]{1,0:T(8,128)(2,1)S(1)}, u32[]{:S(2)}, u32[]{:S(2)}) collective-permute-start(bf16[512,256]{1,0:T(8,128)(2,1)S(1)} %get-tuple-element.23.own_sent), channel_id=1, source_target_pairs={{0,4},{4,0},{8,12},{12,8},{1,5},{5,1},{9,13},{13,9},{2,6},{6,2},{1... | collective-permute-start | bytes 786440 | tf_op jit(solution)/shard_map/ppermute | solution.py:24
  19.3 11.2 %collective-permute-start.9 = (bf16[96,1280]{1,0:T(8,128)(2,1)S(1)}, bf16[96,1280]{1,0:T(8,128)(2,1)S(1)}, u32[]{:S(2)}, u32[]{:S(2)}) collective-permute-start(bf16[96,1280]{1,0:T(8,128)(2,1)S(1)} %pad_maximum_fusion.refs_0_), channel_id=1, source_target_pairs={{0,8},{4,12},{8,0},{12,4},{1,9},{5,13},{9,1},{13,5},{2,10},{6,14},... | collective-permute-start | bytes 737288 | tf_op jit(solution)/shard_map/ppermute | solution.py:24
  19.8 6.3 %collective-permute-start.8 = (bf16[32,1280]{1,0:T(8,128)(2,1)S(1)}, bf16[32,1280]{1,0:T(8,128)(2,1)S(1)}, u32[]{:S(2)}, u32[]{:S(2)}) collective-permute-start(bf16[32,1280]{1,0:T(8,128)(2,1)S(1)} %shard_map.105), channel_id=1, source_target_pairs={{0,3},{1,2},{2,1},{3,0},{4,7},{5,6},{6,5},{7,4},{8,11},{9,10},{10,... | collective-permute-start | bytes 245768 | tf_op jit(solution)/shard_map/ppermute | solution.py:24
  26.1 4.4 %collective-permute-start.10 = (bf16[32,1280]{1,0:T(8,128)(2,1)S(1)}, bf16[32,1280]{1,0:T(8,128)(2,1)S(1)}, u32[]{:S(2)}, u32[]{:S(2)}) collective-permute-start(bf16[32,1280]{1,0:T(8,128)(2,1)S(1)} %collective-permute-done.8.refs_1_), channel_id=1, source_target_pairs={{0,8},{4,12},{8,0},{12,4},{1,9},{5,13},{9,1},{13,5},{2,10},{6,14},... | collective-permute-start | bytes 245768 | tf_op jit(solution)/shard_map/ppermute | solution.py:24
  31.9 5.0 %collective-permute-start.12 = (bf16[144,128]{1,0:T(8,128)(2,1)S(1)}, bf16[144,128]{1,0:T(8,128)(2,1)S(1)}, u32[]{:S(2)}, u32[]{:S(2)}) collective-permute-start(bf16[144,128]{1,0:T(8,128)(2,1)S(1)} %get-tuple-element.29), channel_id=1, source_target_pairs={{0,2},{1,3},{2,0},{3,1},{4,6},{5,7},{6,4},{7,5},{8,10},{9,11},{10,... | collective-permute-start | bytes 110600 | tf_op jit(solution)/shard_map/ppermute | solution.py:24
  32.0 12.1 %copy-start = (bf16[256,1280]{1,0:T(8,128)(2,1)S(1)}, bf16[256,1280]{1,0:T(8,128)(2,1)}, u32[]{:S(2)}) copy-start(bf16[256,1280]{1,0:T(8,128)(2,1)} %value_weight.3) | copy-start | bytes 1966084
  32.0 5.8 %collective-permute-start.13 = (bf16[144,128]{1,0:T(8,128)(2,1)S(1)}, bf16[144,128]{1,0:T(8,128)(2,1)S(1)}, u32[]{:S(2)}, u32[]{:S(2)}) collective-permute-start(bf16[144,128]{1,0:T(8,128)(2,1)S(1)} %get-tuple-element.30), channel_id=1, source_target_pairs={{0,3},{1,2},{2,1},{3,0},{4,7},{5,6},{6,5},{7,4},{8,11},{9,10},{10,... | collective-permute-start | bytes 110600 | tf_op jit(solution)/shard_map/ppermute | solution.py:24
  35.9 9.4 %copy-start.2 = (bf16[1280,320]{0,1:T(8,128)(2,1)S(1)}, bf16[1280,320]{0,1:T(8,128)(2,1)}, u32[]{:S(2)}) copy-start(bf16[1280,320]{0,1:T(8,128)(2,1)} %param.19) | copy-start | bytes 2457604
  35.9 4.0 %collective-permute-start.11 = (bf16[144,128]{1,0:T(8,128)(2,1)S(1)}, bf16[144,128]{1,0:T(8,128)(2,1)S(1)}, u32[]{:S(2)}, u32[]{:S(2)}) collective-permute-start(bf16[144,128]{1,0:T(8,128)(2,1)S(1)} %get-tuple-element.28), channel_id=1, source_target_pairs={{0,1},{1,0},{2,3},{3,2},{4,5},{5,4},{6,7},{7,6},{8,9},{9,8},{10,11... | collective-permute-start | bytes 110600 | tf_op jit(solution)/shard_map/ppermute | solution.py:24
  40.0 4.0 %collective-permute-start.14 = (bf16[144,128]{1,0:T(8,128)(2,1)S(1)}, bf16[144,128]{1,0:T(8,128)(2,1)S(1)}, u32[]{:S(2)}, u32[]{:S(2)}) collective-permute-start(bf16[144,128]{1,0:T(8,128)(2,1)S(1)} %get-tuple-element.32), channel_id=1, source_target_pairs={{0,8},{4,12},{8,0},{12,4},{1,9},{5,13},{9,1},{13,5},{2,10},{6,14},... | collective-permute-start | bytes 110600 | tf_op jit(solution)/shard_map/ppermute | solution.py:24
  44.0 1.3 %collective-permute-start.15 = (bf16[128,128]{1,0:T(8,128)(2,1)S(1)}, bf16[128,128]{1,0:T(8,128)(2,1)S(1)}, u32[]{:S(2)}, u32[]{:S(2)}) collective-permute-start(bf16[128,128]{1,0:T(8,128)(2,1)S(1)} %shard_map.109.normalized), channel_id=1, source_target_pairs={{0,4},{4,0},{8,12},{12,8},{1,5},{5,1},{9,13},{13,9},{2,6},{6,2},{1... | collective-permute-start | bytes 98312 | tf_op jit(solution)/shard_map/ppermute | solution.py:24

commit v10 on v9

--- a/solution.py
+++ b/solution.py
@@ -392,7 +392,7 @@
 def first_score_kernel(own, own_sent, own_keys, other, other_sent, other_keys, *refs):
     *queries, send_2, send_3, held, blocks = refs
     row, across = lax.axis_index("row"), lax.axis_index("col") // 2
-    hold_queries(held, queries[:2], queries[2:], row // 2 != across)
+    hold_queries(held, queries[:3], queries[3:], row // 2 != across)
     scores = masked_scores(held, own_sent, own_keys), masked_scores(held, other_sent, other_keys)
     for parity, block in enumerate(score_blocks(scores, (own, other))):
         write_whole(blocks.at[parity], *block)
@@ -404,7 +404,7 @@
 def last_score_kernel(own, own_sent, own_keys, other, other_sent, other_keys, *refs):
     *queries, kept, send_1, held, blocks = refs
     row, across = lax.axis_index("row"), lax.axis_index("col") // 2
-    hold_queries(held, queries[:2], queries[2:], row // 2 == across)
+    hold_queries(held, queries[:3], queries[3:], row // 2 == across)
     scores = masked_scores(held, own_sent, own_keys), masked_scores(held, other_sent, other_keys)
     for parity, block in enumerate(score_blocks(scores, (own, other))):
         write_whole(blocks.at[parity], *block)
@@ -501,6 +501,7 @@
     bottom = shifted(marked[:HALO], "row", -1)
     one = flipped(queries, "row", 1)
     three = flipped(queries, "row", 3)
+    far_queries = flipped(queries, "col", 2)
 
     edge = lambda cut: jnp.concatenate([top[:, cut], marked[:, cut], bottom[:, cut]], axis=0)
     even = lax.rem(col, 2) == 0
@@ -509,8 +510,8 @@
     rounds = [(k, (k + 1 if k % 2 else k - 1) % cols) for k in range(cols)]
     crossed = lax.ppermute(jnp.where(even, *ends[::-1]), "col", rounds)
 
-    trio = jnp.concatenate([queries, two, one], axis=0)
-    far_trio = flipped(trio, "col", 2)
+    pair = jnp.concatenate([two, one], axis=0)
+    far_pair = flipped(pair, "col", 2)
     far_three = flipped(three, "col", 2)
 
     mid, weight = call(
@@ -539,7 +540,7 @@
         key_kernel, [((cells, width), half)], [own, key_weight],
         limit=4, flops=2 * cells * width * channels,
     )
-    all_queries = [trio, three, far_trio, far_three]
+    all_queries = [queries, pair, three, far_queries, far_pair, far_three]
     score_scratch = [((block, width), half), ((2,) + whole_block, wide)]
     other, other_keys = call(
         other_kernel, [((cells, channels), half), ((cells, width), half)],

time: 46.9 us -> 49.5 us (1.055)
  waiting for transfers between devices: 15 us -> 17.6 us
    ppermute x13 -> x14, waiting for transfers between devices: 12.7 us -> 15.3 us  [flipped(): return lax.ppermute(array, axis, [(i, i ^ bit) for i in range(count)])]
    ppermute x13 -> x14, starting transfers between devices: 13.7 us -> 13.8 us  [flipped(): return lax.ppermute(array, axis, [(i, i ^ bit) for i in range(count)])]
    unnamed x12 -> x13, local copies, waits for them, and re-layouts: 1.97 us -> 1.97 us
  transfers between devices with their start and end apart: 16 -> 17, of which waited for: 8 -> 10; matrix products, arithmetic and copies ran while one was open for 0% -> 0% of each run, Pallas kernels for 14% -> 13%
where the time goes in v10:
time: 49.5 us; the launch traced here: 49.3 us
  starting transfers between devices  20.1 us (41%)
  waiting for transfers between devices  17.6 us (36%)
  Pallas kernels  9.29 us (19%)
  local copies, waits for them, and re-layouts  2.03 us (4%)
    ppermute x14, waiting for transfers between devices, flipped(): return lax.ppermute(array, axis, [(i, i ^ bit) for i in range(count)])  15.3 us
    ppermute x14, starting transfers between devices, flipped(): return lax.ppermute(array, axis, [(i, i ^ bit) for i in range(count)])  13.8 us
    pallas_call x11, Pallas kernels, call(): pl.pallas_call(kernel, out_shape=[pltpu.VMEM(shape, dtype) for shape, dty...  7.92 us
    ppermute x2, starting transfers between devices, shifted(): lax.ppermute(array, axis, [(i, (i + step) % count) for i in range(count)])  4.71 us
    ppermute x2, waiting for transfers between devices, shifted(): lax.ppermute(array, axis, [(i, (i + step) % count) for i in range(count)])  2.3 us
    unnamed x13, local copies, waits for them, and re-layouts  1.97 us
    ppermute x1, starting transfers between devices, kernel_path(): crossed = lax.ppermute(jnp.where(even, *ends[::-1]), 'col', rounds)  1.59 us
    pallas_call x1, Pallas kernels, kernel_path(): pl.pallas_call(finish_kernel, out_shape=jax.ShapeDtypeStruct((out_weight....  1.37 us
  transfers between devices with their start and end apart: 17, of which 10 were waited for; matrix products, arithmetic and copies ran while one was open for 0% of the time, Pallas kernels for 13%

profile of v10, /device:TPU:0, one launch (start us, length us, event | category | flops | bytes accessed | tf_op | source)
XLA Modules:
  0.0 49.3 jit_solution(11103101494464990785)
XLA Ops:
  0.0 0.5 collective-permute-start.5
  0.5 1.1 %shard_map.100 = (bf16[16,32,256]{2,1,0:T(8,128)(2,1)S(1)}, bf16[32,1280]{1,0:T(8,128)(2,1)S(1)}) custom-call(bf16[16,32,256]{2,1,0:T(8,128)(2,1)} %features.1, s32[16,32]{1,0:T(8,128)} %tissue.1, bf16[32,1280]{1,0:T(8,128)(2,1)} %queries.1), custom_call_target="tpu_custom_call" | custom-call | flops 1048576 | tf_op jit(solution)/shard_map/pallas_call | solution.py:459
  1.6 2.6 %collective-permute-start = (bf16[2,32,256]{2,1,0:T(8,128)(2,1)S(1)}, bf16[2,32,256]{2,1,0:T(8,128)(2,1)S(1)}, u32[]{:S(2)}, u32[]{:S(2)}) collective-permute-start(bf16[2,32,256]{2,1,0:T(8,128)(2,1)S(1)} %get-tuple-element.36), channel_id=1, source_target_pairs={{0,1},{1,2},{2,3},{3,0},{4,5},{5,6},{6,7},{7,4},{8,9},{9,10},{10,1... | collective-permute-start | bytes 98312 | tf_op jit(solution)/shard_map/ppermute | solution.py:19
  4.2 2.1 %collective-permute-start.1 = (bf16[2,32,256]{2,1,0:T(8,128)(2,1)S(1)}, bf16[2,32,256]{2,1,0:T(8,128)(2,1)S(1)}, u32[]{:S(2)}, u32[]{:S(2)}) collective-permute-start(bf16[2,32,256]{2,1,0:T(8,128)(2,1)S(1)} %get-tuple-element.35), channel_id=1, source_target_pairs={{0,3},{1,0},{2,1},{3,2},{4,7},{5,4},{6,5},{7,6},{8,11},{9,8},{10,9... | collective-permute-start | bytes 98312 | tf_op jit(solution)/shard_map/ppermute | solution.py:19
  6.3 2.0 %collective-permute-done.top = bf16[2,32,256]{2,1,0:T(8,128)(2,1)S(1)} collective-permute-done((bf16[2,32,256]{2,1,0:T(8,128)(2,1)S(1)}, bf16[2,32,256]{2,1,0:T(8,128)(2,1)S(1)}, u32[]{:S(2)}, u32[]{:S(2)}) %collective-permute-start) | collective-permute-done | bytes 32800 | tf_op jit(solution)/shard_map/ppermute | solution.py:19
  8.8 1.6 %collective-permute-start.3 = (bf16[20,2,256]{2,1,0:T(2,128)(2,1)S(1)}, bf16[20,2,256]{2,1,0:T(2,128)(2,1)S(1)}, u32[]{:S(2)}, u32[]{:S(2)}) collective-permute-start(bf16[20,2,256]{2,1,0:T(2,128)(2,1)S(1)} %get-tuple-element.37), channel_id=1, source_target_pairs={{0,12},{4,8},{8,4},{12,0},{1,13},{5,9},{9,5},{13,1},{2,14},{6,10},... | collective-permute-start | bytes 61448 | tf_op jit(solution)/shard_map/ppermute | solution.py:511
  10.4 2.1 %collective-permute-start.6 = (bf16[32,1280]{1,0:T(8,128)(2,1)S(1)}, bf16[32,1280]{1,0:T(8,128)(2,1)S(1)}, u32[]{:S(2)}, u32[]{:S(2)}) collective-permute-start(bf16[32,1280]{1,0:T(8,128)(2,1)S(1)} %shard_map.105.refs_0_), channel_id=1, source_target_pairs={{0,2},{1,3},{2,0},{3,1},{4,6},{5,7},{6,4},{7,5},{8,10},{9,11},{10,... | collective-permute-start | bytes 245768 | tf_op jit(solution)/shard_map/ppermute | solution.py:24
  12.5 1.3 %copy-done.1 = bf16[3,3,256,256]{3,2,1,0:T(8,128)(2,1)S(1)} copy-done((bf16[3,3,256,256]{3,2,1,0:T(8,128)(2,1)S(1)}, bf16[3,3,256,256]{3,2,1,0:T(8,128)(2,1)}, u32[]{:S(2)}) %copy-start.1) | copy-done | bytes 1179672
  13.8 0.7 %copy-done.4 = f32[256]{0:T(256)S(1)} copy-done((f32[256]{0:T(256)S(1)}, f32[256]{0:T(256)}, u32[]{:S(2)}) %copy-start.4) | copy-done | bytes 1048
  14.5 1.5 %shard_map.101 = (f32[896,256]{1,0:T(8,128)S(1)}, bf16[3,768,256]{2,1,0:T(8,128)(2,1)S(1)}) custom-call(bf16[16,32,256]{2,1,0:T(8,128)(2,1)S(1)} %get-tuple-element.19.marked, bf16[2,32,256]{2,1,0:T(8,128)(2,1)S(1)} %collective-permute-done.top, bf16[2,32,256]{2,1,0:T(8,128)(2,1)S(1)} %collective-permute-done.1.bottom, ...), custom_call_target="tpu_custom_call" | custom-call | flops 704643072 | tf_op jit(solution)/shard_map/pallas_call | solution.py:459
  16.0 1.1 %shard_map.102 = (bf16[512,256]{1,0:T(8,128)(2,1)S(1)}, bf16[512,256]{1,0:T(8,128)(2,1)S(1)}) custom-call(bf16[16,32,256]{2,1,0:T(8,128)(2,1)S(1)} %get-tuple-element.19.marked, f32[896,256]{1,0:T(8,128)S(1)} %get-tuple-element.20.mid, bf16[3,768,256]{2,1,0:T(8,128)(2,1)S(1)} %get-tuple-element.21.second, f32[1,256]{1,0:T(1,128)S(1)} %bitcast.9), custom_call_target="tpu_custom_call" | custom-call | flops 603979776 | tf_op jit(solution)/shard_map/pallas_call | solution.py:459
  17.2 2.1 %collective-permute-start.7 = (bf16[32,1280]{1,0:T(8,128)(2,1)S(1)}, bf16[32,1280]{1,0:T(8,128)(2,1)S(1)}, u32[]{:S(2)}, u32[]{:S(2)}) collective-permute-start(bf16[32,1280]{1,0:T(8,128)(2,1)S(1)} %shard_map.105.refs_0_), channel_id=1, source_target_pairs={{0,1},{1,0},{2,3},{3,2},{4,5},{5,4},{6,7},{7,6},{8,9},{9,8},{10,11... | collective-permute-start | bytes 245768 | tf_op jit(solution)/shard_map/ppermute | solution.py:24
  19.3 1.4 %collective-permute-start.8 = (bf16[32,1280]{1,0:T(8,128)(2,1)S(1)}, bf16[32,1280]{1,0:T(8,128)(2,1)S(1)}, u32[]{:S(2)}, u32[]{:S(2)}) collective-permute-start(bf16[32,1280]{1,0:T(8,128)(2,1)S(1)} %shard_map.105.refs_0_), channel_id=1, source_target_pairs={{0,3},{1,2},{2,1},{3,0},{4,7},{5,6},{6,5},{7,4},{8,11},{9,10},{10,... | collective-permute-start | bytes 245768 | tf_op jit(solution)/shard_map/ppermute | solution.py:24
  20.7 1.6 %collective-permute-done.7 = bf16[32,1280]{1,0:T(8,128)(2,1)S(1)} collective-permute-done((bf16[32,1280]{1,0:T(8,128)(2,1)S(1)}, bf16[32,1280]{1,0:T(8,128)(2,1)S(1)}, u32[]{:S(2)}, u32[]{:S(2)}) %collective-permute-start.7) | collective-permute-done | bytes 81952 | tf_op jit(solution)/shard_map/ppermute | solution.py:24
  22.4 0.8 %collective-permute-start.10 = (bf16[64,1280]{1,0:T(8,128)(2,1)S(1)}, bf16[64,1280]{1,0:T(8,128)(2,1)S(1)}, u32[]{:S(2)}, u32[]{:S(2)}) collective-permute-start(bf16[64,1280]{1,0:T(8,128)(2,1)S(1)} %constant_dynamic-update-slice_fusion.refs_1_), channel_id=1, source_target_pairs={{0,8},{4,12},{8,0},{12,4},{1,9},{5,13},{9,1},{13,5},{2,10},{6,14},... | collective-permute-start | bytes 491528 | tf_op jit(solution)/shard_map/ppermute | solution.py:24
  23.1 1.3 %collective-permute-start.9 = (bf16[32,1280]{1,0:T(8,128)(2,1)S(1)}, bf16[32,1280]{1,0:T(8,128)(2,1)S(1)}, u32[]{:S(2)}, u32[]{:S(2)}) collective-permute-start(bf16[32,1280]{1,0:T(8,128)(2,1)S(1)} %shard_map.105.refs_0_), channel_id=1, source_target_pairs={{0,8},{4,12},{8,0},{12,4},{1,9},{5,13},{9,1},{13,5},{2,10},{6,14},... | collective-permute-start | bytes 245768 | tf_op jit(solution)/shard_map/ppermute | solution.py:24
  24.4 1.2 %collective-permute-done.8.refs_2_ = bf16[32,1280]{1,0:T(8,128)(2,1)S(1)} collective-permute-done((bf16[32,1280]{1,0:T(8,128)(2,1)S(1)}, bf16[32,1280]{1,0:T(8,128)(2,1)S(1)}, u32[]{:S(2)}, u32[]{:S(2)}) %collective-permute-start.8) | collective-permute-done | bytes 81952 | tf_op jit(solution)/shard_map/ppermute | solution.py:24
  25.6 1.1 %collective-permute-start.11 = (bf16[32,1280]{1,0:T(8,128)(2,1)S(1)}, bf16[32,1280]{1,0:T(8,128)(2,1)S(1)}, u32[]{:S(2)}, u32[]{:S(2)}) collective-permute-start(bf16[32,1280]{1,0:T(8,128)(2,1)S(1)} %collective-permute-done.8.refs_2_), channel_id=1, source_target_pairs={{0,8},{4,12},{8,0},{12,4},{1,9},{5,13},{9,1},{13,5},{2,10},{6,14},... | collective-permute-start | bytes 245768 | tf_op jit(solution)/shard_map/ppermute | solution.py:24
  26.8 0.5 %shard_map.103.own_keys = bf16[512,1280]{1,0:T(8,128)(2,1)S(1)} custom-call(bf16[512,256]{1,0:T(8,128)(2,1)S(1)} %get-tuple-element.22.cells.own, bf16[256,1280]{1,0:T(8,128)(2,1)S(1)} %copy-done.3), custom_call_target="tpu_custom_call" | custom-call | flops 335544320 | tf_op jit(solution)/shard_map/pallas_call | solution.py:459
  27.3 0.5 %shard_map.104 = (bf16[512,256]{1,0:T(8,128)(2,1)S(1)}, bf16[512,1280]{1,0:T(8,128)(2,1)S(1)}) custom-call(bf16[512,256]{1,0:T(8,128)(2,1)S(1)} %collective-permute-done.4.other_sent, bf16[256,1280]{1,0:T(8,128)(2,1)S(1)} %copy-done.3), custom_call_target="tpu_custom_call" | custom-call | flops 335544320 | tf_op jit(solution)/shard_map/pallas_call | solution.py:459
  27.8 3.1 %collective-permute-done.9.refs_3_ = bf16[32,1280]{1,0:T(8,128)(2,1)S(1)} collective-permute-done((bf16[32,1280]{1,0:T(8,128)(2,1)S(1)}, bf16[32,1280]{1,0:T(8,128)(2,1)S(1)}, u32[]{:S(2)}, u32[]{:S(2)}) %collective-permute-start.9) | collective-permute-done | bytes 81952 | tf_op jit(solution)/shard_map/ppermute | solution.py:24
  31.0 0.9 %collective-permute-done.11.refs_5_ = bf16[32,1280]{1,0:T(8,128)(2,1)S(1)} collective-permute-done((bf16[32,1280]{1,0:T(8,128)(2,1)S(1)}, bf16[32,1280]{1,0:T(8,128)(2,1)S(1)}, u32[]{:S(2)}, u32[]{:S(2)}) %collective-permute-start.11) | collective-permute-done | bytes 81952 | tf_op jit(solution)/shard_map/ppermute | solution.py:24
  31.9 1.4 %shard_map.107 = (bf16[144,128]{1,0:T(8,128)(2,1)S(1)}, bf16[144,128]{1,0:T(8,128)(2,1)S(1)}) custom-call(bf16[512,256]{1,0:T(8,128)(2,1)S(1)} %get-tuple-element.22.cells.own, bf16[512,256]{1,0:T(8,128)(2,1)S(1)} %get-tuple-element.23.own_sent, bf16[512,1280]{1,0:T(8,128)(2,1)S(1)} %shard_map.103.own_keys, bf16[512,256]{1,0:T(8,128)(2,1)S(1)} %get-tuple-element.24.other, ...), custom_call_target="tpu_custom_call" | custom-call | flops 402653184 | tf_op jit(solution)/shard_map/pallas_call | solution.py:459
  33.2 1.0 %collective-permute-start.13 = (bf16[144,128]{1,0:T(8,128)(2,1)S(1)}, bf16[144,128]{1,0:T(8,128)(2,1)S(1)}, u32[]{:S(2)}, u32[]{:S(2)}) collective-permute-start(bf16[144,128]{1,0:T(8,128)(2,1)S(1)} %get-tuple-element.29), channel_id=1, source_target_pairs={{0,2},{1,3},{2,0},{3,1},{4,6},{5,7},{6,4},{7,5},{8,10},{9,11},{10,... | collective-permute-start | bytes 110600 | tf_op jit(solution)/shard_map/ppermute | solution.py:24
  34.3 2.8 %collective-permute-start.14 = (bf16[144,128]{1,0:T(8,128)(2,1)S(1)}, bf16[144,128]{1,0:T(8,128)(2,1)S(1)}, u32[]{:S(2)}, u32[]{:S(2)}) collective-permute-start(bf16[144,128]{1,0:T(8,128)(2,1)S(1)} %get-tuple-element.30), channel_id=1, source_target_pairs={{0,3},{1,2},{2,1},{3,0},{4,7},{5,6},{6,5},{7,4},{8,11},{9,10},{10,... | collective-permute-start | bytes 110600 | tf_op jit(solution)/shard_map/ppermute | solution.py:24
  37.1 1.4 %shard_map.106 = (f32[136,128]{1,0:T(8,128)S(1)}, bf16[144,128]{1,0:T(8,128)(2,1)S(1)}) custom-call(bf16[512,256]{1,0:T(8,128)(2,1)S(1)} %get-tuple-element.22.cells.own, bf16[512,256]{1,0:T(8,128)(2,1)S(1)} %get-tuple-element.23.own_sent, bf16[512,1280]{1,0:T(8,128)(2,1)S(1)} %shard_map.103.own_keys, bf16[512,256]{1,0:T(8,128)(2,1)S(1)} %get-tuple-element.24.other, ...), custom_call_target="tpu_custom_call" | custom-call | flops 402653184 | tf_op jit(solution)/shard_map/pallas_call | solution.py:459
  38.6 1.5 %collective-permute-done.14.refs_2_ = bf16[144,128]{1,0:T(8,128)(2,1)S(1)} collective-permute-done((bf16[144,128]{1,0:T(8,128)(2,1)S(1)}, bf16[144,128]{1,0:T(8,128)(2,1)S(1)}, u32[]{:S(2)}, u32[]{:S(2)}) %collective-permute-start.14) | collective-permute-done | bytes 36896 | tf_op jit(solution)/shard_map/ppermute | solution.py:24
  40.0 2.5 %collective-permute-done.12.refs_0_ = bf16[144,128]{1,0:T(8,128)(2,1)S(1)} collective-permute-done((bf16[144,128]{1,0:T(8,128)(2,1)S(1)}, bf16[144,128]{1,0:T(8,128)(2,1)S(1)}, u32[]{:S(2)}, u32[]{:S(2)}) %collective-permute-start.12) | collective-permute-done | bytes 36896 | tf_op jit(solution)/shard_map/ppermute | solution.py:24
  42.6 0.4 collective-permute-start.15
  43.0 3.6 %collective-permute-done.15.arrived = bf16[144,128]{1,0:T(8,128)(2,1)S(1)} collective-permute-done((bf16[144,128]{1,0:T(8,128)(2,1)S(1)}, bf16[144,128]{1,0:T(8,128)(2,1)S(1)}, u32[]{:S(2)}, u32[]{:S(2)}) %collective-permute-start.15) | collective-permute-done | bytes 36896 | tf_op jit(solution)/shard_map/ppermute | solution.py:24
  47.1 0.8 %collective-permute-done.16.arrived = bf16[128,128]{1,0:T(8,128)(2,1)S(1)} collective-permute-done((bf16[128,128]{1,0:T(8,128)(2,1)S(1)}, bf16[128,128]{1,0:T(8,128)(2,1)S(1)}, u32[]{:S(2)}, u32[]{:S(2)}) %collective-permute-start.16) | collective-permute-done | bytes 32800 | tf_op jit(solution)/shard_map/ppermute | solution.py:24
  47.9 1.4 %fn.1 = bf16[320,128]{1,0:T(8,128)(2,1)} custom-call(bf16[64,1280]{1,0:T(8,128)(2,1)S(1)} %shard_map.110.mine, bf16[128,128]{1,0:T(8,128)(2,1)S(1)} %collective-permute-done.16.arrived, bf16[256,1280]{1,0:T(8,128)(2,1)S(1)} %copy-done, bf16[320,1280]{1,0:T(8,128)(2,1)S(1)} %bitcast.7), custom_call_target="tpu_custom_call" | custom-call | tf_op jit(solution)/shard_map/fn/pallas_call | solution.py:574
  (33 shorter events, 1.2 us)
Async XLA Ops:
  0.0 10.4 %collective-permute-start.5 = (bf16[32,1280]{1,0:T(8,128)(2,1)}, bf16[32,1280]{1,0:T(8,128)(2,1)S(1)}, u32[]{:S(2)}, u32[]{:S(2)}) collective-permute-start(bf16[32,1280]{1,0:T(8,128)(2,1)} %queries.1), channel_id=1, source_target_pairs={{0,4},{4,0},{8,12},{12,8},{1,5},{5,1},{9,13},{13,9},{2,6},{6,2},{1... | collective-permute-start | bytes 245768 | tf_op jit(solution)/shard_map/ppermute | solution.py:24
  1.6 6.8 %collective-permute-start = (bf16[2,32,256]{2,1,0:T(8,128)(2,1)S(1)}, bf16[2,32,256]{2,1,0:T(8,128)(2,1)S(1)}, u32[]{:S(2)}, u32[]{:S(2)}) collective-permute-start(bf16[2,32,256]{2,1,0:T(8,128)(2,1)S(1)} %get-tuple-element.36), channel_id=1, source_target_pairs={{0,1},{1,2},{2,3},{3,0},{4,5},{5,6},{6,7},{7,4},{8,9},{9,10},{10,1... | collective-permute-start | bytes 98312 | tf_op jit(solution)/shard_map/ppermute | solution.py:19
  4.2 4.4 %collective-permute-start.1 = (bf16[2,32,256]{2,1,0:T(8,128)(2,1)S(1)}, bf16[2,32,256]{2,1,0:T(8,128)(2,1)S(1)}, u32[]{:S(2)}, u32[]{:S(2)}) collective-permute-start(bf16[2,32,256]{2,1,0:T(8,128)(2,1)S(1)} %get-tuple-element.35), channel_id=1, source_target_pairs={{0,3},{1,0},{2,1},{3,2},{4,7},{5,4},{6,5},{7,6},{8,11},{9,8},{10,9... | collective-permute-start | bytes 98312 | tf_op jit(solution)/shard_map/ppermute | solution.py:19
  8.7 3.8 %collective-permute-start.2 = (bf16[20,2,256]{2,1,0:T(2,128)(2,1)S(1)}, bf16[20,2,256]{2,1,0:T(2,128)(2,1)S(1)}, u32[]{:S(2)}, u32[]{:S(2)}) collective-permute-start(bf16[20,2,256]{2,1,0:T(2,128)(2,1)S(1)} %get-tuple-element.38), channel_id=1, source_target_pairs={{0,4},{4,0},{8,12},{12,8},{1,5},{5,1},{9,13},{13,9},{2,6},{6,2},{1... | collective-permute-start | bytes 61448 | tf_op jit(solution)/shard_map/ppermute | solution.py:24
  8.8 3.7 %collective-permute-start.3 = (bf16[20,2,256]{2,1,0:T(2,128)(2,1)S(1)}, bf16[20,2,256]{2,1,0:T(2,128)(2,1)S(1)}, u32[]{:S(2)}, u32[]{:S(2)}) collective-permute-start(bf16[20,2,256]{2,1,0:T(2,128)(2,1)S(1)} %get-tuple-element.37), channel_id=1, source_target_pairs={{0,12},{4,8},{8,4},{12,0},{1,13},{5,9},{9,5},{13,1},{2,14},{6,10},... | collective-permute-start | bytes 61448 | tf_op jit(solution)/shard_map/ppermute | solution.py:511
  10.4 10.3 %collective-permute-start.6 = (bf16[32,1280]{1,0:T(8,128)(2,1)S(1)}, bf16[32,1280]{1,0:T(8,128)(2,1)S(1)}, u32[]{:S(2)}, u32[]{:S(2)}) collective-permute-start(bf16[32,1280]{1,0:T(8,128)(2,1)S(1)} %shard_map.105.refs_0_), channel_id=1, source_target_pairs={{0,2},{1,3},{2,0},{3,1},{4,6},{5,7},{6,4},{7,5},{8,10},{9,11},{10,... | collective-permute-start | bytes 245768 | tf_op jit(solution)/shard_map/ppermute | solution.py:24
  12.5 1.3 %copy-start.1 = (bf16[3,3,256,256]{3,2,1,0:T(8,128)(2,1)S(1)}, bf16[3,3,256,256]{3,2,1,0:T(8,128)(2,1)}, u32[]{:S(2)}) copy-start(bf16[3,3,256,256]{3,2,1,0:T(8,128)(2,1)} %param.12) | copy-start | bytes 3538948
  13.8 0.7 %copy-start.4 = (f32[256]{0:T(256)S(1)}, f32[256]{0:T(256)}, u32[]{:S(2)}) copy-start(f32[256]{0:T(256)} %param.13) | copy-start | bytes 3076
  14.5 1.5 %copy-start.5 = (f32[256]{0:T(256)S(1)}, f32[256]{0:T(256)}, u32[]{:S(2)}) copy-start(f32[256]{0:T(256)} %param.15) | copy-start | bytes 3076
  16.0 10.7 %copy-start.3 = (bf16[256,1280]{1,0:T(8,128)(2,1)S(1)}, bf16[256,1280]{1,0:T(8,128)(2,1)}, u32[]{:S(2)}) copy-start(bf16[256,1280]{1,0:T(8,128)(2,1)} %weight.3) | copy-start | bytes 1966084
  17.2 10.1 %collective-permute-start.4 = (bf16[512,256]{1,0:T(8,128)(2,1)S(1)}, bf16[512,256]{1,0:T(8,128)(2,1)S(1)}, u32[]{:S(2)}, u32[]{:S(2)}) collective-permute-start(bf16[512,256]{1,0:T(8,128)(2,1)S(1)} %get-tuple-element.23.own_sent), channel_id=1, source_target_pairs={{0,4},{4,0},{8,12},{12,8},{1,5},{5,1},{9,13},{13,9},{2,6},{6,2},{1... | collective-permute-start | bytes 786440 | tf_op jit(solution)/shard_map/ppermute | solution.py:24
  17.2 5.1 %collective-permute-start.7 = (bf16[32,1280]{1,0:T(8,128)(2,1)S(1)}, bf16[32,1280]{1,0:T(8,128)(2,1)S(1)}, u32[]{:S(2)}, u32[]{:S(2)}) collective-permute-start(bf16[32,1280]{1,0:T(8,128)(2,1)S(1)} %shard_map.105.refs_0_), channel_id=1, source_target_pairs={{0,1},{1,0},{2,3},{3,2},{4,5},{5,4},{6,7},{7,6},{8,9},{9,8},{10,11... | collective-permute-start | bytes 245768 | tf_op jit(solution)/shard_map/ppermute | solution.py:24
  19.3 6.3 %collective-permute-start.8 = (bf16[32,1280]{1,0:T(8,128)(2,1)S(1)}, bf16[32,1280]{1,0:T(8,128)(2,1)S(1)}, u32[]{:S(2)}, u32[]{:S(2)}) collective-permute-start(bf16[32,1280]{1,0:T(8,128)(2,1)S(1)} %shard_map.105.refs_0_), channel_id=1, source_target_pairs={{0,3},{1,2},{2,1},{3,0},{4,7},{5,6},{6,5},{7,4},{8,11},{9,10},{10,... | collective-permute-start | bytes 245768 | tf_op jit(solution)/shard_map/ppermute | solution.py:24
  22.4 9.5 %collective-permute-start.10 = (bf16[64,1280]{1,0:T(8,128)(2,1)S(1)}, bf16[64,1280]{1,0:T(8,128)(2,1)S(1)}, u32[]{:S(2)}, u32[]{:S(2)}) collective-permute-start(bf16[64,1280]{1,0:T(8,128)(2,1)S(1)} %constant_dynamic-update-slice_fusion.refs_1_), channel_id=1, source_target_pairs={{0,8},{4,12},{8,0},{12,4},{1,9},{5,13},{9,1},{13,5},{2,10},{6,14},... | collective-permute-start | bytes 491528 | tf_op jit(solution)/shard_map/ppermute | solution.py:24
  23.1 7.8 %collective-permute-start.9 = (bf16[32,1280]{1,0:T(8,128)(2,1)S(1)}, bf16[32,1280]{1,0:T(8,128)(2,1)S(1)}, u32[]{:S(2)}, u32[]{:S(2)}) collective-permute-start(bf16[32,1280]{1,0:T(8,128)(2,1)S(1)} %shard_map.105.refs_0_), channel_id=1, source_target_pairs={{0,8},{4,12},{8,0},{12,4},{1,9},{5,13},{9,1},{13,5},{2,10},{6,14},... | collective-permute-start | bytes 245768 | tf_op jit(solution)/shard_map/ppermute | solution.py:24
  25.6 6.2 %collective-permute-start.11 = (bf16[32,1280]{1,0:T(8,128)(2,1)S(1)}, bf16[32,1280]{1,0:T(8,128)(2,1)S(1)}, u32[]{:S(2)}, u32[]{:S(2)}) collective-permute-start(bf16[32,1280]{1,0:T(8,128)(2,1)S(1)} %collective-permute-done.8.refs_2_), channel_id=1, source_target_pairs={{0,8},{4,12},{8,0},{12,4},{1,9},{5,13},{9,1},{13,5},{2,10},{6,14},... | collective-permute-start | bytes 245768 | tf_op jit(solution)/shard_map/ppermute | solution.py:24
  33.2 5.3 %collective-permute-start.13 = (bf16[144,128]{1,0:T(8,128)(2,1)S(1)}, bf16[144,128]{1,0:T(8,128)(2,1)S(1)}, u32[]{:S(2)}, u32[]{:S(2)}) collective-permute-start(bf16[144,128]{1,0:T(8,128)(2,1)S(1)} %get-tuple-element.29), channel_id=1, source_target_pairs={{0,2},{1,3},{2,0},{3,1},{4,6},{5,7},{6,4},{7,5},{8,10},{9,11},{10,... | collective-permute-start | bytes 110600 | tf_op jit(solution)/shard_map/ppermute | solution.py:24
  34.3 12.4 %copy-start = (bf16[256,1280]{1,0:T(8,128)(2,1)S(1)}, bf16[256,1280]{1,0:T(8,128)(2,1)}, u32[]{:S(2)}) copy-start(bf16[256,1280]{1,0:T(8,128)(2,1)} %value_weight.3) | copy-start | bytes 1966084
  34.3 5.8 %collective-permute-start.14 = (bf16[144,128]{1,0:T(8,128)(2,1)S(1)}, bf16[144,128]{1,0:T(8,128)(2,1)S(1)}, u32[]{:S(2)}, u32[]{:S(2)}) collective-permute-start(bf16[144,128]{1,0:T(8,128)(2,1)S(1)} %get-tuple-element.30), channel_id=1, source_target_pairs={{0,3},{1,2},{2,1},{3,0},{4,7},{5,6},{6,5},{7,4},{8,11},{9,10},{10,... | collective-permute-start | bytes 110600 | tf_op jit(solution)/shard_map/ppermute | solution.py:24
  38.5 9.4 %copy-start.2 = (bf16[1280,320]{0,1:T(8,128)(2,1)S(1)}, bf16[1280,320]{0,1:T(8,128)(2,1)}, u32[]{:S(2)}) copy-start(bf16[1280,320]{0,1:T(8,128)(2,1)} %param.19) | copy-start | bytes 2457604
  38.5 4.0 %collective-permute-start.12 = (bf16[144,128]{1,0:T(8,128)(2,1)S(1)}, bf16[144,128]{1,0:T(8,128)(2,1)S(1)}, u32[]{:S(2)}, u32[]{:S(2)}) collective-permute-start(bf16[144,128]{1,0:T(8,128)(2,1)S(1)} %get-tuple-element.28), channel_id=1, source_target_pairs={{0,1},{1,0},{2,3},{3,2},{4,5},{5,4},{6,7},{7,6},{8,9},{9,8},{10,11... | collective-permute-start | bytes 110600 | tf_op jit(solution)/shard_map/ppermute | solution.py:24
  42.6 4.0 %collective-permute-start.15 = (bf16[144,128]{1,0:T(8,128)(2,1)S(1)}, bf16[144,128]{1,0:T(8,128)(2,1)S(1)}, u32[]{:S(2)}, u32[]{:S(2)}) collective-permute-start(bf16[144,128]{1,0:T(8,128)(2,1)S(1)} %get-tuple-element.32), channel_id=1, source_target_pairs={{0,8},{4,12},{8,0},{12,4},{1,9},{5,13},{9,1},{13,5},{2,10},{6,14},... | collective-permute-start | bytes 110600 | tf_op jit(solution)/shard_map/ppermute | solution.py:24
  46.6 1.3 %collective-permute-start.16 = (bf16[128,128]{1,0:T(8,128)(2,1)S(1)}, bf16[128,128]{1,0:T(8,128)(2,1)S(1)}, u32[]{:S(2)}, u32[]{:S(2)}) collective-permute-start(bf16[128,128]{1,0:T(8,128)(2,1)S(1)} %shard_map.109.normalized), channel_id=1, source_target_pairs={{0,4},{4,0},{8,12},{12,8},{1,5},{5,1},{9,13},{13,9},{2,6},{6,2},{1... | collective-permute-start | bytes 98312 | tf_op jit(solution)/shard_map/ppermute | solution.py:24

commit v11 on v10

--- a/solution.py
+++ b/solution.py
@@ -503,9 +503,13 @@
     three = flipped(queries, "row", 3)
     far_queries = flipped(queries, "col", 2)
 
-    edge = lambda cut: jnp.concatenate([top[:, cut], marked[:, cut], bottom[:, cut]], axis=0)
+    sides = slice(breadth - HALO, breadth), slice(0, HALO)
+    middles = [marked[:, cut] for cut in sides]
     even = lax.rem(col, 2) == 0
-    ends = edge(slice(breadth - HALO, breadth)), edge(slice(0, HALO))
+    ends = [
+        jnp.concatenate([top[:, cut], middle, bottom[:, cut]], axis=0)
+        for cut, middle in zip(sides, middles)
+    ]
     paired = flipped(jnp.where(even, *ends), "col", 1)
     rounds = [(k, (k + 1 if k % 2 else k - 1) % cols) for k in range(cols)]
     crossed = lax.ppermute(jnp.where(even, *ends[::-1]), "col", rounds)

time: 49.5 us -> 49.5 us (level)
  no operation moved by 1% of the time
where the time goes in v11:
time: 49.5 us; the launch traced here: 49.3 us
  starting transfers between devices  20.1 us (41%)
  waiting for transfers between devices  17.6 us (36%)
  Pallas kernels  9.29 us (19%)
  local copies, waits for them, and re-layouts  2.03 us (4%)
    ppermute x14, waiting for transfers between devices, flipped(): return lax.ppermute(array, axis, [(i, i ^ bit) for i in range(count)])  15.3 us
    ppermute x14, starting transfers between devices, flipped(): return lax.ppermute(array, axis, [(i, i ^ bit) for i in range(count)])  13.8 us
    pallas_call x11, Pallas kernels, call(): pl.pallas_call(kernel, out_shape=[pltpu.VMEM(shape, dtype) for shape, dty...  7.92 us
    ppermute x2, starting transfers between devices, shifted(): lax.ppermute(array, axis, [(i, (i + step) % count) for i in range(count)])  4.71 us
    ppermute x2, waiting for transfers between devices, shifted(): lax.ppermute(array, axis, [(i, (i + step) % count) for i in range(count)])  2.3 us
    unnamed x13, local copies, waits for them, and re-layouts  1.97 us
    ppermute x1, starting transfers between devices, kernel_path(): crossed = lax.ppermute(jnp.where(even, *ends[::-1]), 'col', rounds)  1.59 us
    pallas_call x1, Pallas kernels, kernel_path(): pl.pallas_call(finish_kernel, out_shape=jax.ShapeDtypeStruct((out_weight....  1.37 us
  transfers between devices with their start and end apart: 17, of which 10 were waited for; matrix products, arithmetic and copies ran while one was open for 0% of the time, Pallas kernels for 13%

profile of v11, /device:TPU:0, one launch (start us, length us, event | category | flops | bytes accessed | tf_op | source)
XLA Modules:
  0.0 49.3 jit_solution(11103101494464990785)
XLA Ops:
  0.0 0.5 collective-permute-start.5
  0.5 1.1 %shard_map.100 = (bf16[16,32,256]{2,1,0:T(8,128)(2,1)S(1)}, bf16[32,1280]{1,0:T(8,128)(2,1)S(1)}) custom-call(bf16[16,32,256]{2,1,0:T(8,128)(2,1)} %features.1, s32[16,32]{1,0:T(8,128)} %tissue.1, bf16[32,1280]{1,0:T(8,128)(2,1)} %queries.1), custom_call_target="tpu_custom_call" | custom-call | flops 1048576 | tf_op jit(solution)/shard_map/pallas_call | solution.py:459
  1.6 2.6 %collective-permute-start = (bf16[2,32,256]{2,1,0:T(8,128)(2,1)S(1)}, bf16[2,32,256]{2,1,0:T(8,128)(2,1)S(1)}, u32[]{:S(2)}, u32[]{:S(2)}) collective-permute-start(bf16[2,32,256]{2,1,0:T(8,128)(2,1)S(1)} %get-tuple-element.36), channel_id=1, source_target_pairs={{0,1},{1,2},{2,3},{3,0},{4,5},{5,6},{6,7},{7,4},{8,9},{9,10},{10,1... | collective-permute-start | bytes 98312 | tf_op jit(solution)/shard_map/ppermute | solution.py:19
  4.2 2.1 %collective-permute-start.1 = (bf16[2,32,256]{2,1,0:T(8,128)(2,1)S(1)}, bf16[2,32,256]{2,1,0:T(8,128)(2,1)S(1)}, u32[]{:S(2)}, u32[]{:S(2)}) collective-permute-start(bf16[2,32,256]{2,1,0:T(8,128)(2,1)S(1)} %get-tuple-element.35), channel_id=1, source_target_pairs={{0,3},{1,0},{2,1},{3,2},{4,7},{5,4},{6,5},{7,6},{8,11},{9,8},{10,9... | collective-permute-start | bytes 98312 | tf_op jit(solution)/shard_map/ppermute | solution.py:19
  6.3 2.0 %collective-permute-done.top = bf16[2,32,256]{2,1,0:T(8,128)(2,1)S(1)} collective-permute-done((bf16[2,32,256]{2,1,0:T(8,128)(2,1)S(1)}, bf16[2,32,256]{2,1,0:T(8,128)(2,1)S(1)}, u32[]{:S(2)}, u32[]{:S(2)}) %collective-permute-start) | collective-permute-done | bytes 32800 | tf_op jit(solution)/shard_map/ppermute | solution.py:19
  8.8 1.6 %collective-permute-start.3 = (bf16[20,2,256]{2,1,0:T(2,128)(2,1)S(1)}, bf16[20,2,256]{2,1,0:T(2,128)(2,1)S(1)}, u32[]{:S(2)}, u32[]{:S(2)}) collective-permute-start(bf16[20,2,256]{2,1,0:T(2,128)(2,1)S(1)} %get-tuple-element.37), channel_id=1, source_target_pairs={{0,12},{4,8},{8,4},{12,0},{1,13},{5,9},{9,5},{13,1},{2,14},{6,10},... | collective-permute-start | bytes 61448 | tf_op jit(solution)/shard_map/ppermute | solution.py:515
  10.4 2.1 %collective-permute-start.6 = (bf16[32,1280]{1,0:T(8,128)(2,1)S(1)}, bf16[32,1280]{1,0:T(8,128)(2,1)S(1)}, u32[]{:S(2)}, u32[]{:S(2)}) collective-permute-start(bf16[32,1280]{1,0:T(8,128)(2,1)S(1)} %shard_map.105.refs_0_), channel_id=1, source_target_pairs={{0,2},{1,3},{2,0},{3,1},{4,6},{5,7},{6,4},{7,5},{8,10},{9,11},{10,... | collective-permute-start | bytes 245768 | tf_op jit(solution)/shard_map/ppermute | solution.py:24
  12.5 1.3 %copy-done.1 = bf16[3,3,256,256]{3,2,1,0:T(8,128)(2,1)S(1)} copy-done((bf16[3,3,256,256]{3,2,1,0:T(8,128)(2,1)S(1)}, bf16[3,3,256,256]{3,2,1,0:T(8,128)(2,1)}, u32[]{:S(2)}) %copy-start.1) | copy-done | bytes 1179672
  13.8 0.7 %copy-done.4 = f32[256]{0:T(256)S(1)} copy-done((f32[256]{0:T(256)S(1)}, f32[256]{0:T(256)}, u32[]{:S(2)}) %copy-start.4) | copy-done | bytes 1048
  14.5 1.5 %shard_map.101 = (f32[896,256]{1,0:T(8,128)S(1)}, bf16[3,768,256]{2,1,0:T(8,128)(2,1)S(1)}) custom-call(bf16[16,32,256]{2,1,0:T(8,128)(2,1)S(1)} %get-tuple-element.19.marked, bf16[2,32,256]{2,1,0:T(8,128)(2,1)S(1)} %collective-permute-done.top, bf16[2,32,256]{2,1,0:T(8,128)(2,1)S(1)} %collective-permute-done.1.bottom, ...), custom_call_target="tpu_custom_call" | custom-call | flops 704643072 | tf_op jit(solution)/shard_map/pallas_call | solution.py:459
  16.0 1.1 %shard_map.102 = (bf16[512,256]{1,0:T(8,128)(2,1)S(1)}, bf16[512,256]{1,0:T(8,128)(2,1)S(1)}) custom-call(bf16[16,32,256]{2,1,0:T(8,128)(2,1)S(1)} %get-tuple-element.19.marked, f32[896,256]{1,0:T(8,128)S(1)} %get-tuple-element.20.mid, bf16[3,768,256]{2,1,0:T(8,128)(2,1)S(1)} %get-tuple-element.21.second, f32[1,256]{1,0:T(1,128)S(1)} %bitcast.9), custom_call_target="tpu_custom_call" | custom-call | flops 603979776 | tf_op jit(solution)/shard_map/pallas_call | solution.py:459
  17.2 2.1 %collective-permute-start.7 = (bf16[32,1280]{1,0:T(8,128)(2,1)S(1)}, bf16[32,1280]{1,0:T(8,128)(2,1)S(1)}, u32[]{:S(2)}, u32[]{:S(2)}) collective-permute-start(bf16[32,1280]{1,0:T(8,128)(2,1)S(1)} %shard_map.105.refs_0_), channel_id=1, source_target_pairs={{0,1},{1,0},{2,3},{3,2},{4,5},{5,4},{6,7},{7,6},{8,9},{9,8},{10,11... | collective-permute-start | bytes 245768 | tf_op jit(solution)/shard_map/ppermute | solution.py:24
  19.3 1.4 %collective-permute-start.8 = (bf16[32,1280]{1,0:T(8,128)(2,1)S(1)}, bf16[32,1280]{1,0:T(8,128)(2,1)S(1)}, u32[]{:S(2)}, u32[]{:S(2)}) collective-permute-start(bf16[32,1280]{1,0:T(8,128)(2,1)S(1)} %shard_map.105.refs_0_), channel_id=1, source_target_pairs={{0,3},{1,2},{2,1},{3,0},{4,7},{5,6},{6,5},{7,4},{8,11},{9,10},{10,... | collective-permute-start | bytes 245768 | tf_op jit(solution)/shard_map/ppermute | solution.py:24
  20.7 1.6 %collective-permute-done.7 = bf16[32,1280]{1,0:T(8,128)(2,1)S(1)} collective-permute-done((bf16[32,1280]{1,0:T(8,128)(2,1)S(1)}, bf16[32,1280]{1,0:T(8,128)(2,1)S(1)}, u32[]{:S(2)}, u32[]{:S(2)}) %collective-permute-start.7) | collective-permute-done | bytes 81952 | tf_op jit(solution)/shard_map/ppermute | solution.py:24
  22.4 0.8 %collective-permute-start.10 = (bf16[64,1280]{1,0:T(8,128)(2,1)S(1)}, bf16[64,1280]{1,0:T(8,128)(2,1)S(1)}, u32[]{:S(2)}, u32[]{:S(2)}) collective-permute-start(bf16[64,1280]{1,0:T(8,128)(2,1)S(1)} %constant_dynamic-update-slice_fusion.refs_1_), channel_id=1, source_target_pairs={{0,8},{4,12},{8,0},{12,4},{1,9},{5,13},{9,1},{13,5},{2,10},{6,14},... | collective-permute-start | bytes 491528 | tf_op jit(solution)/shard_map/ppermute | solution.py:24
  23.1 1.3 %collective-permute-start.9 = (bf16[32,1280]{1,0:T(8,128)(2,1)S(1)}, bf16[32,1280]{1,0:T(8,128)(2,1)S(1)}, u32[]{:S(2)}, u32[]{:S(2)}) collective-permute-start(bf16[32,1280]{1,0:T(8,128)(2,1)S(1)} %shard_map.105.refs_0_), channel_id=1, source_target_pairs={{0,8},{4,12},{8,0},{12,4},{1,9},{5,13},{9,1},{13,5},{2,10},{6,14},... | collective-permute-start | bytes 245768 | tf_op jit(solution)/shard_map/ppermute | solution.py:24
  24.4 1.2 %collective-permute-done.8.refs_2_ = bf16[32,1280]{1,0:T(8,128)(2,1)S(1)} collective-permute-done((bf16[32,1280]{1,0:T(8,128)(2,1)S(1)}, bf16[32,1280]{1,0:T(8,128)(2,1)S(1)}, u32[]{:S(2)}, u32[]{:S(2)}) %collective-permute-start.8) | collective-permute-done | bytes 81952 | tf_op jit(solution)/shard_map/ppermute | solution.py:24
  25.6 1.1 %collective-permute-start.11 = (bf16[32,1280]{1,0:T(8,128)(2,1)S(1)}, bf16[32,1280]{1,0:T(8,128)(2,1)S(1)}, u32[]{:S(2)}, u32[]{:S(2)}) collective-permute-start(bf16[32,1280]{1,0:T(8,128)(2,1)S(1)} %collective-permute-done.8.refs_2_), channel_id=1, source_target_pairs={{0,8},{4,12},{8,0},{12,4},{1,9},{5,13},{9,1},{13,5},{2,10},{6,14},... | collective-permute-start | bytes 245768 | tf_op jit(solution)/shard_map/ppermute | solution.py:24
  26.8 0.5 %shard_map.103.own_keys = bf16[512,1280]{1,0:T(8,128)(2,1)S(1)} custom-call(bf16[512,256]{1,0:T(8,128)(2,1)S(1)} %get-tuple-element.22.cells.own, bf16[256,1280]{1,0:T(8,128)(2,1)S(1)} %copy-done.3), custom_call_target="tpu_custom_call" | custom-call | flops 335544320 | tf_op jit(solution)/shard_map/pallas_call | solution.py:459
  27.3 0.5 %shard_map.104 = (bf16[512,256]{1,0:T(8,128)(2,1)S(1)}, bf16[512,1280]{1,0:T(8,128)(2,1)S(1)}) custom-call(bf16[512,256]{1,0:T(8,128)(2,1)S(1)} %collective-permute-done.4.other_sent, bf16[256,1280]{1,0:T(8,128)(2,1)S(1)} %copy-done.3), custom_call_target="tpu_custom_call" | custom-call | flops 335544320 | tf_op jit(solution)/shard_map/pallas_call | solution.py:459
  27.8 3.1 %collective-permute-done.9.refs_3_ = bf16[32,1280]{1,0:T(8,128)(2,1)S(1)} collective-permute-done((bf16[32,1280]{1,0:T(8,128)(2,1)S(1)}, bf16[32,1280]{1,0:T(8,128)(2,1)S(1)}, u32[]{:S(2)}, u32[]{:S(2)}) %collective-permute-start.9) | collective-permute-done | bytes 81952 | tf_op jit(solution)/shard_map/ppermute | solution.py:24
  31.0 0.9 %collective-permute-done.11.refs_5_ = bf16[32,1280]{1,0:T(8,128)(2,1)S(1)} collective-permute-done((bf16[32,1280]{1,0:T(8,128)(2,1)S(1)}, bf16[32,1280]{1,0:T(8,128)(2,1)S(1)}, u32[]{:S(2)}, u32[]{:S(2)}) %collective-permute-start.11) | collective-permute-done | bytes 81952 | tf_op jit(solution)/shard_map/ppermute | solution.py:24
  31.9 1.4 %shard_map.107 = (bf16[144,128]{1,0:T(8,128)(2,1)S(1)}, bf16[144,128]{1,0:T(8,128)(2,1)S(1)}) custom-call(bf16[512,256]{1,0:T(8,128)(2,1)S(1)} %get-tuple-element.22.cells.own, bf16[512,256]{1,0:T(8,128)(2,1)S(1)} %get-tuple-element.23.own_sent, bf16[512,1280]{1,0:T(8,128)(2,1)S(1)} %shard_map.103.own_keys, bf16[512,256]{1,0:T(8,128)(2,1)S(1)} %get-tuple-element.24.other, ...), custom_call_target="tpu_custom_call" | custom-call | flops 402653184 | tf_op jit(solution)/shard_map/pallas_call | solution.py:459
  33.2 1.0 %collective-permute-start.13 = (bf16[144,128]{1,0:T(8,128)(2,1)S(1)}, bf16[144,128]{1,0:T(8,128)(2,1)S(1)}, u32[]{:S(2)}, u32[]{:S(2)}) collective-permute-start(bf16[144,128]{1,0:T(8,128)(2,1)S(1)} %get-tuple-element.29), channel_id=1, source_target_pairs={{0,2},{1,3},{2,0},{3,1},{4,6},{5,7},{6,4},{7,5},{8,10},{9,11},{10,... | collective-permute-start | bytes 110600 | tf_op jit(solution)/shard_map/ppermute | solution.py:24
  34.3 2.8 %collective-permute-start.14 = (bf16[144,128]{1,0:T(8,128)(2,1)S(1)}, bf16[144,128]{1,0:T(8,128)(2,1)S(1)}, u32[]{:S(2)}, u32[]{:S(2)}) collective-permute-start(bf16[144,128]{1,0:T(8,128)(2,1)S(1)} %get-tuple-element.30), channel_id=1, source_target_pairs={{0,3},{1,2},{2,1},{3,0},{4,7},{5,6},{6,5},{7,4},{8,11},{9,10},{10,... | collective-permute-start | bytes 110600 | tf_op jit(solution)/shard_map/ppermute | solution.py:24
  37.1 1.4 %shard_map.106 = (f32[136,128]{1,0:T(8,128)S(1)}, bf16[144,128]{1,0:T(8,128)(2,1)S(1)}) custom-call(bf16[512,256]{1,0:T(8,128)(2,1)S(1)} %get-tuple-element.22.cells.own, bf16[512,256]{1,0:T(8,128)(2,1)S(1)} %get-tuple-element.23.own_sent, bf16[512,1280]{1,0:T(8,128)(2,1)S(1)} %shard_map.103.own_keys, bf16[512,256]{1,0:T(8,128)(2,1)S(1)} %get-tuple-element.24.other, ...), custom_call_target="tpu_custom_call" | custom-call | flops 402653184 | tf_op jit(solution)/shard_map/pallas_call | solution.py:459
  38.6 1.5 %collective-permute-done.14.refs_2_ = bf16[144,128]{1,0:T(8,128)(2,1)S(1)} collective-permute-done((bf16[144,128]{1,0:T(8,128)(2,1)S(1)}, bf16[144,128]{1,0:T(8,128)(2,1)S(1)}, u32[]{:S(2)}, u32[]{:S(2)}) %collective-permute-start.14) | collective-permute-done | bytes 36896 | tf_op jit(solution)/shard_map/ppermute | solution.py:24
  40.0 2.5 %collective-permute-done.12.refs_0_ = bf16[144,128]{1,0:T(8,128)(2,1)S(1)} collective-permute-done((bf16[144,128]{1,0:T(8,128)(2,1)S(1)}, bf16[144,128]{1,0:T(8,128)(2,1)S(1)}, u32[]{:S(2)}, u32[]{:S(2)}) %collective-permute-start.12) | collective-permute-done | bytes 36896 | tf_op jit(solution)/shard_map/ppermute | solution.py:24
  42.6 0.4 collective-permute-start.15
  43.0 3.6 %collective-permute-done.15.arrived = bf16[144,128]{1,0:T(8,128)(2,1)S(1)} collective-permute-done((bf16[144,128]{1,0:T(8,128)(2,1)S(1)}, bf16[144,128]{1,0:T(8,128)(2,1)S(1)}, u32[]{:S(2)}, u32[]{:S(2)}) %collective-permute-start.15) | collective-permute-done | bytes 36896 | tf_op jit(solution)/shard_map/ppermute | solution.py:24
  47.1 0.8 %collective-permute-done.16.arrived = bf16[128,128]{1,0:T(8,128)(2,1)S(1)} collective-permute-done((bf16[128,128]{1,0:T(8,128)(2,1)S(1)}, bf16[128,128]{1,0:T(8,128)(2,1)S(1)}, u32[]{:S(2)}, u32[]{:S(2)}) %collective-permute-start.16) | collective-permute-done | bytes 32800 | tf_op jit(solution)/shard_map/ppermute | solution.py:24
  47.9 1.4 %fn.1 = bf16[320,128]{1,0:T(8,128)(2,1)} custom-call(bf16[64,1280]{1,0:T(8,128)(2,1)S(1)} %shard_map.110.mine, bf16[128,128]{1,0:T(8,128)(2,1)S(1)} %collective-permute-done.16.arrived, bf16[256,1280]{1,0:T(8,128)(2,1)S(1)} %copy-done, bf16[320,1280]{1,0:T(8,128)(2,1)S(1)} %bitcast.7), custom_call_target="tpu_custom_call" | custom-call | tf_op jit(solution)/shard_map/fn/pallas_call | solution.py:578
  (33 shorter events, 1.2 us)
Async XLA Ops:
  0.0 10.4 %collective-permute-start.5 = (bf16[32,1280]{1,0:T(8,128)(2,1)}, bf16[32,1280]{1,0:T(8,128)(2,1)S(1)}, u32[]{:S(2)}, u32[]{:S(2)}) collective-permute-start(bf16[32,1280]{1,0:T(8,128)(2,1)} %queries.1), channel_id=1, source_target_pairs={{0,4},{4,0},{8,12},{12,8},{1,5},{5,1},{9,13},{13,9},{2,6},{6,2},{1... | collective-permute-start | bytes 245768 | tf_op jit(solution)/shard_map/ppermute | solution.py:24
  1.6 6.8 %collective-permute-start = (bf16[2,32,256]{2,1,0:T(8,128)(2,1)S(1)}, bf16[2,32,256]{2,1,0:T(8,128)(2,1)S(1)}, u32[]{:S(2)}, u32[]{:S(2)}) collective-permute-start(bf16[2,32,256]{2,1,0:T(8,128)(2,1)S(1)} %get-tuple-element.36), channel_id=1, source_target_pairs={{0,1},{1,2},{2,3},{3,0},{4,5},{5,6},{6,7},{7,4},{8,9},{9,10},{10,1... | collective-permute-start | bytes 98312 | tf_op jit(solution)/shard_map/ppermute | solution.py:19
  4.2 4.4 %collective-permute-start.1 = (bf16[2,32,256]{2,1,0:T(8,128)(2,1)S(1)}, bf16[2,32,256]{2,1,0:T(8,128)(2,1)S(1)}, u32[]{:S(2)}, u32[]{:S(2)}) collective-permute-start(bf16[2,32,256]{2,1,0:T(8,128)(2,1)S(1)} %get-tuple-element.35), channel_id=1, source_target_pairs={{0,3},{1,0},{2,1},{3,2},{4,7},{5,4},{6,5},{7,6},{8,11},{9,8},{10,9... | collective-permute-start | bytes 98312 | tf_op jit(solution)/shard_map/ppermute | solution.py:19
  8.7 3.8 %collective-permute-start.2 = (bf16[20,2,256]{2,1,0:T(2,128)(2,1)S(1)}, bf16[20,2,256]{2,1,0:T(2,128)(2,1)S(1)}, u32[]{:S(2)}, u32[]{:S(2)}) collective-permute-start(bf16[20,2,256]{2,1,0:T(2,128)(2,1)S(1)} %get-tuple-element.38), channel_id=1, source_target_pairs={{0,4},{4,0},{8,12},{12,8},{1,5},{5,1},{9,13},{13,9},{2,6},{6,2},{1... | collective-permute-start | bytes 61448 | tf_op jit(solution)/shard_map/ppermute | solution.py:24
  8.8 3.7 %collective-permute-start.3 = (bf16[20,2,256]{2,1,0:T(2,128)(2,1)S(1)}, bf16[20,2,256]{2,1,0:T(2,128)(2,1)S(1)}, u32[]{:S(2)}, u32[]{:S(2)}) collective-permute-start(bf16[20,2,256]{2,1,0:T(2,128)(2,1)S(1)} %get-tuple-element.37), channel_id=1, source_target_pairs={{0,12},{4,8},{8,4},{12,0},{1,13},{5,9},{9,5},{13,1},{2,14},{6,10},... | collective-permute-start | bytes 61448 | tf_op jit(solution)/shard_map/ppermute | solution.py:515
  10.4 10.3 %collective-permute-start.6 = (bf16[32,1280]{1,0:T(8,128)(2,1)S(1)}, bf16[32,1280]{1,0:T(8,128)(2,1)S(1)}, u32[]{:S(2)}, u32[]{:S(2)}) collective-permute-start(bf16[32,1280]{1,0:T(8,128)(2,1)S(1)} %shard_map.105.refs_0_), channel_id=1, source_target_pairs={{0,2},{1,3},{2,0},{3,1},{4,6},{5,7},{6,4},{7,5},{8,10},{9,11},{10,... | collective-permute-start | bytes 245768 | tf_op jit(solution)/shard_map/ppermute | solution.py:24
  12.5 1.3 %copy-start.1 = (bf16[3,3,256,256]{3,2,1,0:T(8,128)(2,1)S(1)}, bf16[3,3,256,256]{3,2,1,0:T(8,128)(2,1)}, u32[]{:S(2)}) copy-start(bf16[3,3,256,256]{3,2,1,0:T(8,128)(2,1)} %param.12) | copy-start | bytes 3538948
  13.8 0.7 %copy-start.4 = (f32[256]{0:T(256)S(1)}, f32[256]{0:T(256)}, u32[]{:S(2)}) copy-start(f32[256]{0:T(256)} %param.13) | copy-start | bytes 3076
  14.5 1.5 %copy-start.5 = (f32[256]{0:T(256)S(1)}, f32[256]{0:T(256)}, u32[]{:S(2)}) copy-start(f32[256]{0:T(256)} %param.15) | copy-start | bytes 3076
  16.0 10.7 %copy-start.3 = (bf16[256,1280]{1,0:T(8,128)(2,1)S(1)}, bf16[256,1280]{1,0:T(8,128)(2,1)}, u32[]{:S(2)}) copy-start(bf16[256,1280]{1,0:T(8,128)(2,1)} %weight.3) | copy-start | bytes 1966084
  17.2 10.1 %collective-permute-start.4 = (bf16[512,256]{1,0:T(8,128)(2,1)S(1)}, bf16[512,256]{1,0:T(8,128)(2,1)S(1)}, u32[]{:S(2)}, u32[]{:S(2)}) collective-permute-start(bf16[512,256]{1,0:T(8,128)(2,1)S(1)} %get-tuple-element.23.own_sent), channel_id=1, source_target_pairs={{0,4},{4,0},{8,12},{12,8},{1,5},{5,1},{9,13},{13,9},{2,6},{6,2},{1... | collective-permute-start | bytes 786440 | tf_op jit(solution)/shard_map/ppermute | solution.py:24
  17.2 5.1 %collective-permute-start.7 = (bf16[32,1280]{1,0:T(8,128)(2,1)S(1)}, bf16[32,1280]{1,0:T(8,128)(2,1)S(1)}, u32[]{:S(2)}, u32[]{:S(2)}) collective-permute-start(bf16[32,1280]{1,0:T(8,128)(2,1)S(1)} %shard_map.105.refs_0_), channel_id=1, source_target_pairs={{0,1},{1,0},{2,3},{3,2},{4,5},{5,4},{6,7},{7,6},{8,9},{9,8},{10,11... | collective-permute-start | bytes 245768 | tf_op jit(solution)/shard_map/ppermute | solution.py:24
  19.3 6.3 %collective-permute-start.8 = (bf16[32,1280]{1,0:T(8,128)(2,1)S(1)}, bf16[32,1280]{1,0:T(8,128)(2,1)S(1)}, u32[]{:S(2)}, u32[]{:S(2)}) collective-permute-start(bf16[32,1280]{1,0:T(8,128)(2,1)S(1)} %shard_map.105.refs_0_), channel_id=1, source_target_pairs={{0,3},{1,2},{2,1},{3,0},{4,7},{5,6},{6,5},{7,4},{8,11},{9,10},{10,... | collective-permute-start | bytes 245768 | tf_op jit(solution)/shard_map/ppermute | solution.py:24
  22.4 9.5 %collective-permute-start.10 = (bf16[64,1280]{1,0:T(8,128)(2,1)S(1)}, bf16[64,1280]{1,0:T(8,128)(2,1)S(1)}, u32[]{:S(2)}, u32[]{:S(2)}) collective-permute-start(bf16[64,1280]{1,0:T(8,128)(2,1)S(1)} %constant_dynamic-update-slice_fusion.refs_1_), channel_id=1, source_target_pairs={{0,8},{4,12},{8,0},{12,4},{1,9},{5,13},{9,1},{13,5},{2,10},{6,14},... | collective-permute-start | bytes 491528 | tf_op jit(solution)/shard_map/ppermute | solution.py:24
  23.1 7.8 %collective-permute-start.9 = (bf16[32,1280]{1,0:T(8,128)(2,1)S(1)}, bf16[32,1280]{1,0:T(8,128)(2,1)S(1)}, u32[]{:S(2)}, u32[]{:S(2)}) collective-permute-start(bf16[32,1280]{1,0:T(8,128)(2,1)S(1)} %shard_map.105.refs_0_), channel_id=1, source_target_pairs={{0,8},{4,12},{8,0},{12,4},{1,9},{5,13},{9,1},{13,5},{2,10},{6,14},... | collective-permute-start | bytes 245768 | tf_op jit(solution)/shard_map/ppermute | solution.py:24
  25.6 6.2 %collective-permute-start.11 = (bf16[32,1280]{1,0:T(8,128)(2,1)S(1)}, bf16[32,1280]{1,0:T(8,128)(2,1)S(1)}, u32[]{:S(2)}, u32[]{:S(2)}) collective-permute-start(bf16[32,1280]{1,0:T(8,128)(2,1)S(1)} %collective-permute-done.8.refs_2_), channel_id=1, source_target_pairs={{0,8},{4,12},{8,0},{12,4},{1,9},{5,13},{9,1},{13,5},{2,10},{6,14},... | collective-permute-start | bytes 245768 | tf_op jit(solution)/shard_map/ppermute | solution.py:24
  33.2 5.3 %collective-permute-start.13 = (bf16[144,128]{1,0:T(8,128)(2,1)S(1)}, bf16[144,128]{1,0:T(8,128)(2,1)S(1)}, u32[]{:S(2)}, u32[]{:S(2)}) collective-permute-start(bf16[144,128]{1,0:T(8,128)(2,1)S(1)} %get-tuple-element.29), channel_id=1, source_target_pairs={{0,2},{1,3},{2,0},{3,1},{4,6},{5,7},{6,4},{7,5},{8,10},{9,11},{10,... | collective-permute-start | bytes 110600 | tf_op jit(solution)/shard_map/ppermute | solution.py:24
  34.3 12.4 %copy-start = (bf16[256,1280]{1,0:T(8,128)(2,1)S(1)}, bf16[256,1280]{1,0:T(8,128)(2,1)}, u32[]{:S(2)}) copy-start(bf16[256,1280]{1,0:T(8,128)(2,1)} %value_weight.3) | copy-start | bytes 1966084
  34.3 5.8 %collective-permute-start.14 = (bf16[144,128]{1,0:T(8,128)(2,1)S(1)}, bf16[144,128]{1,0:T(8,128)(2,1)S(1)}, u32[]{:S(2)}, u32[]{:S(2)}) collective-permute-start(bf16[144,128]{1,0:T(8,128)(2,1)S(1)} %get-tuple-element.30), channel_id=1, source_target_pairs={{0,3},{1,2},{2,1},{3,0},{4,7},{5,6},{6,5},{7,4},{8,11},{9,10},{10,... | collective-permute-start | bytes 110600 | tf_op jit(solution)/shard_map/ppermute | solution.py:24
  38.5 9.4 %copy-start.2 = (bf16[1280,320]{0,1:T(8,128)(2,1)S(1)}, bf16[1280,320]{0,1:T(8,128)(2,1)}, u32[]{:S(2)}) copy-start(bf16[1280,320]{0,1:T(8,128)(2,1)} %param.19) | copy-start | bytes 2457604
  38.5 4.0 %collective-permute-start.12 = (bf16[144,128]{1,0:T(8,128)(2,1)S(1)}, bf16[144,128]{1,0:T(8,128)(2,1)S(1)}, u32[]{:S(2)}, u32[]{:S(2)}) collective-permute-start(bf16[144,128]{1,0:T(8,128)(2,1)S(1)} %get-tuple-element.28), channel_id=1, source_target_pairs={{0,1},{1,0},{2,3},{3,2},{4,5},{5,4},{6,7},{7,6},{8,9},{9,8},{10,11... | collective-permute-start | bytes 110600 | tf_op jit(solution)/shard_map/ppermute | solution.py:24
  42.6 4.0 %collective-permute-start.15 = (bf16[144,128]{1,0:T(8,128)(2,1)S(1)}, bf16[144,128]{1,0:T(8,128)(2,1)S(1)}, u32[]{:S(2)}, u32[]{:S(2)}) collective-permute-start(bf16[144,128]{1,0:T(8,128)(2,1)S(1)} %get-tuple-element.32), channel_id=1, source_target_pairs={{0,8},{4,12},{8,0},{12,4},{1,9},{5,13},{9,1},{13,5},{2,10},{6,14},... | collective-permute-start | bytes 110600 | tf_op jit(solution)/shard_map/ppermute | solution.py:24
  46.6 1.3 %collective-permute-start.16 = (bf16[128,128]{1,0:T(8,128)(2,1)S(1)}, bf16[128,128]{1,0:T(8,128)(2,1)S(1)}, u32[]{:S(2)}, u32[]{:S(2)}) collective-permute-start(bf16[128,128]{1,0:T(8,128)(2,1)S(1)} %shard_map.109.normalized), channel_id=1, source_target_pairs={{0,4},{4,0},{8,12},{12,8},{1,5},{5,1},{9,13},{13,9},{2,6},{6,2},{1... | collective-permute-start | bytes 98312 | tf_op jit(solution)/shard_map/ppermute | solution.py:24

commit v12 on v11

--- a/solution.py
+++ b/solution.py
@@ -514,9 +514,9 @@
     rounds = [(k, (k + 1 if k % 2 else k - 1) % cols) for k in range(cols)]
     crossed = lax.ppermute(jnp.where(even, *ends[::-1]), "col", rounds)
 
-    pair = jnp.concatenate([two, one], axis=0)
-    far_pair = flipped(pair, "col", 2)
-    far_three = flipped(three, "col", 2)
+    rest = jnp.concatenate([one, three], axis=0)
+    far_two = flipped(two, "col", 2)
+    far_rest = flipped(rest, "col", 2)
 
     mid, weight = call(
         conv_kernel,
@@ -544,7 +544,7 @@
         key_kernel, [((cells, width), half)], [own, key_weight],
         limit=4, flops=2 * cells * width * channels,
     )
-    all_queries = [queries, pair, three, far_queries, far_pair, far_three]
+    all_queries = [queries, two, rest, far_queries, far_two, far_rest]
     score_scratch = [((block, width), half), ((2,) + whole_block, wide)]
     other, other_keys = call(
         other_kernel, [((cells, channels), half), ((cells, width), half)],

time: 49.5 us -> 50.3 us (1.016)
  starting transfers between devices: 20.1 us -> 20.8 us
    ppermute x14, starting transfers between devices: 13.8 us -> 14.5 us  [flipped(): return lax.ppermute(array, axis, [(i, i ^ bit) for i in range(count)])]
    ppermute x1, waiting for transfers between devices: 0.01 us -> 0.55 us  [kernel_path(): crossed = lax.ppermute(jnp.where(even, *ends[::-1]), 'col', rounds)]
  transfers between devices with their start and end apart: 17 -> 17, of which waited for: 10 -> 11; matrix products, arithmetic and copies ran while one was open for 0% -> 0% of each run, Pallas kernels for 13% -> 13%
where the time goes in v12:
time: 50.3 us; the launch traced here: 50.1 us
  starting transfers between devices  20.8 us (41%)
  waiting for transfers between devices  17.7 us (35%)
  Pallas kernels  9.28 us (18%)
  local copies, waits for them, and re-layouts  2.03 us (4%)
    ppermute x14, waiting for transfers between devices, flipped(): return lax.ppermute(array, axis, [(i, i ^ bit) for i in range(count)])  14.9 us
    ppermute x14, starting transfers between devices, flipped(): return lax.ppermute(array, axis, [(i, i ^ bit) for i in range(count)])  14.5 us
    pallas_call x11, Pallas kernels, call(): pl.pallas_call(kernel, out_shape=[pltpu.VMEM(shape, dtype) for shape, dty...  7.91 us
    ppermute x2, starting transfers between devices, shifted(): lax.ppermute(array, axis, [(i, (i + step) % count) for i in range(count)])  4.71 us
    ppermute x2, waiting for transfers between devices, shifted(): lax.ppermute(array, axis, [(i, (i + step) % count) for i in range(count)])  2.3 us
    unnamed x13, local copies, waits for them, and re-layouts  1.97 us
    ppermute x1, starting transfers between devices, kernel_path(): crossed = lax.ppermute(jnp.where(even, *ends[::-1]), 'col', rounds)  1.59 us
    pallas_call x1, Pallas kernels, kernel_path(): pl.pallas_call(finish_kernel, out_shape=jax.ShapeDtypeStruct((out_weight....  1.37 us
  transfers between devices with their start and end apart: 17, of which 11 were waited for; matrix products, arithmetic and copies ran while one was open for 0% of the time, Pallas kernels for 13%

profile of v12, /device:TPU:0, one launch (start us, length us, event | category | flops | bytes accessed | tf_op | source)
XLA Modules:
  0.0 50.1 jit_solution(12172255153234535845)
XLA Ops:
  0.0 0.5 collective-permute-start.5
  0.5 1.1 %shard_map.100 = (bf16[16,32,256]{2,1,0:T(8,128)(2,1)S(1)}, bf16[32,1280]{1,0:T(8,128)(2,1)S(1)}) custom-call(bf16[16,32,256]{2,1,0:T(8,128)(2,1)} %features.1, s32[16,32]{1,0:T(8,128)} %tissue.1, bf16[32,1280]{1,0:T(8,128)(2,1)} %queries.1), custom_call_target="tpu_custom_call" | custom-call | flops 1048576 | tf_op jit(solution)/shard_map/pallas_call | solution.py:459
  1.6 2.6 %collective-permute-start = (bf16[2,32,256]{2,1,0:T(8,128)(2,1)S(1)}, bf16[2,32,256]{2,1,0:T(8,128)(2,1)S(1)}, u32[]{:S(2)}, u32[]{:S(2)}) collective-permute-start(bf16[2,32,256]{2,1,0:T(8,128)(2,1)S(1)} %get-tuple-element.36), channel_id=1, source_target_pairs={{0,1},{1,2},{2,3},{3,0},{4,5},{5,6},{6,7},{7,4},{8,9},{9,10},{10,1... | collective-permute-start | bytes 98312 | tf_op jit(solution)/shard_map/ppermute | solution.py:19
  4.2 2.1 %collective-permute-start.1 = (bf16[2,32,256]{2,1,0:T(8,128)(2,1)S(1)}, bf16[2,32,256]{2,1,0:T(8,128)(2,1)S(1)}, u32[]{:S(2)}, u32[]{:S(2)}) collective-permute-start(bf16[2,32,256]{2,1,0:T(8,128)(2,1)S(1)} %get-tuple-element.35), channel_id=1, source_target_pairs={{0,3},{1,0},{2,1},{3,2},{4,7},{5,4},{6,5},{7,6},{8,11},{9,8},{10,9... | collective-permute-start | bytes 98312 | tf_op jit(solution)/shard_map/ppermute | solution.py:19
  6.3 2.0 %collective-permute-done.top = bf16[2,32,256]{2,1,0:T(8,128)(2,1)S(1)} collective-permute-done((bf16[2,32,256]{2,1,0:T(8,128)(2,1)S(1)}, bf16[2,32,256]{2,1,0:T(8,128)(2,1)S(1)}, u32[]{:S(2)}, u32[]{:S(2)}) %collective-permute-start) | collective-permute-done | bytes 32800 | tf_op jit(solution)/shard_map/ppermute | solution.py:19
  8.8 1.6 %collective-permute-start.3 = (bf16[20,2,256]{2,1,0:T(2,128)(2,1)S(1)}, bf16[20,2,256]{2,1,0:T(2,128)(2,1)S(1)}, u32[]{:S(2)}, u32[]{:S(2)}) collective-permute-start(bf16[20,2,256]{2,1,0:T(2,128)(2,1)S(1)} %get-tuple-element.37), channel_id=1, source_target_pairs={{0,12},{4,8},{8,4},{12,0},{1,13},{5,9},{9,5},{13,1},{2,14},{6,10},... | collective-permute-start | bytes 61448 | tf_op jit(solution)/shard_map/ppermute | solution.py:515
  10.4 1.1 %collective-permute-start.7 = (bf16[32,1280]{1,0:T(8,128)(2,1)S(1)}, bf16[32,1280]{1,0:T(8,128)(2,1)S(1)}, u32[]{:S(2)}, u32[]{:S(2)}) collective-permute-start(bf16[32,1280]{1,0:T(8,128)(2,1)S(1)} %shard_map.105.refs_0_), channel_id=1, source_target_pairs={{0,1},{1,0},{2,3},{3,2},{4,5},{5,4},{6,7},{7,6},{8,9},{9,8},{10,11... | collective-permute-start | bytes 245768 | tf_op jit(solution)/shard_map/ppermute | solution.py:24
  11.5 0.5 %collective-permute-done.3.crossed = bf16[20,2,256]{2,1,0:T(2,128)(2,1)S(1)} collective-permute-done((bf16[20,2,256]{2,1,0:T(2,128)(2,1)S(1)}, bf16[20,2,256]{2,1,0:T(2,128)(2,1)S(1)}, u32[]{:S(2)}, u32[]{:S(2)}) %collective-permute-start.3) | collective-permute-done | bytes 20512 | tf_op jit(solution)/shard_map/ppermute | solution.py:515
  12.1 1.3 %copy-done.1 = bf16[3,3,256,256]{3,2,1,0:T(8,128)(2,1)S(1)} copy-done((bf16[3,3,256,256]{3,2,1,0:T(8,128)(2,1)S(1)}, bf16[3,3,256,256]{3,2,1,0:T(8,128)(2,1)}, u32[]{:S(2)}) %copy-start.1) | copy-done | bytes 1179672
  13.3 0.7 %copy-done.4 = f32[256]{0:T(256)S(1)} copy-done((f32[256]{0:T(256)S(1)}, f32[256]{0:T(256)}, u32[]{:S(2)}) %copy-start.4) | copy-done | bytes 1048
  14.0 1.5 %shard_map.101 = (f32[896,256]{1,0:T(8,128)S(1)}, bf16[3,768,256]{2,1,0:T(8,128)(2,1)S(1)}) custom-call(bf16[16,32,256]{2,1,0:T(8,128)(2,1)S(1)} %get-tuple-element.19.marked, bf16[2,32,256]{2,1,0:T(8,128)(2,1)S(1)} %collective-permute-done.top, bf16[2,32,256]{2,1,0:T(8,128)(2,1)S(1)} %collective-permute-done.1.bottom, ...), custom_call_target="tpu_custom_call" | custom-call | flops 704643072 | tf_op jit(solution)/shard_map/pallas_call | solution.py:459
  15.6 1.1 %shard_map.102 = (bf16[512,256]{1,0:T(8,128)(2,1)S(1)}, bf16[512,256]{1,0:T(8,128)(2,1)S(1)}) custom-call(bf16[16,32,256]{2,1,0:T(8,128)(2,1)S(1)} %get-tuple-element.19.marked, f32[896,256]{1,0:T(8,128)S(1)} %get-tuple-element.20.mid, bf16[3,768,256]{2,1,0:T(8,128)(2,1)S(1)} %get-tuple-element.21.second, f32[1,256]{1,0:T(1,128)S(1)} %bitcast.9), custom_call_target="tpu_custom_call" | custom-call | flops 603979776 | tf_op jit(solution)/shard_map/pallas_call | solution.py:459
  16.7 0.5 collective-permute-start.4
  17.2 3.4 %collective-permute-start.8 = (bf16[32,1280]{1,0:T(8,128)(2,1)S(1)}, bf16[32,1280]{1,0:T(8,128)(2,1)S(1)}, u32[]{:S(2)}, u32[]{:S(2)}) collective-permute-start(bf16[32,1280]{1,0:T(8,128)(2,1)S(1)} %shard_map.105.refs_0_), channel_id=1, source_target_pairs={{0,3},{1,2},{2,1},{3,0},{4,7},{5,6},{6,5},{7,4},{8,11},{9,10},{10,... | collective-permute-start | bytes 245768 | tf_op jit(solution)/shard_map/ppermute | solution.py:24
  20.6 3.4 %collective-permute-done.8 = bf16[32,1280]{1,0:T(8,128)(2,1)S(1)} collective-permute-done((bf16[32,1280]{1,0:T(8,128)(2,1)S(1)}, bf16[32,1280]{1,0:T(8,128)(2,1)S(1)}, u32[]{:S(2)}, u32[]{:S(2)}) %collective-permute-start.8) | collective-permute-done | bytes 81952 | tf_op jit(solution)/shard_map/ppermute | solution.py:24
  24.0 1.9 %collective-permute-start.11 = (bf16[64,1280]{1,0:T(8,128)(2,1)S(1)}, bf16[64,1280]{1,0:T(8,128)(2,1)S(1)}, u32[]{:S(2)}, u32[]{:S(2)}) collective-permute-start(bf16[64,1280]{1,0:T(8,128)(2,1)S(1)} %constant_dynamic-update-slice_fusion.refs_2_), channel_id=1, source_target_pairs={{0,8},{4,12},{8,0},{12,4},{1,9},{5,13},{9,1},{13,5},{2,10},{6,14},... | collective-permute-start | bytes 491528 | tf_op jit(solution)/shard_map/ppermute | solution.py:24
  26.0 1.6 %collective-permute-done.6.refs_1_ = bf16[32,1280]{1,0:T(8,128)(2,1)S(1)} collective-permute-done((bf16[32,1280]{1,0:T(8,128)(2,1)S(1)}, bf16[32,1280]{1,0:T(8,128)(2,1)S(1)}, u32[]{:S(2)}, u32[]{:S(2)}) %collective-permute-start.6) | collective-permute-done | bytes 81952 | tf_op jit(solution)/shard_map/ppermute | solution.py:24
  27.6 1.2 %collective-permute-start.10 = (bf16[32,1280]{1,0:T(8,128)(2,1)S(1)}, bf16[32,1280]{1,0:T(8,128)(2,1)S(1)}, u32[]{:S(2)}, u32[]{:S(2)}) collective-permute-start(bf16[32,1280]{1,0:T(8,128)(2,1)S(1)} %collective-permute-done.6.refs_1_), channel_id=1, source_target_pairs={{0,8},{4,12},{8,0},{12,4},{1,9},{5,13},{9,1},{13,5},{2,10},{6,14},... | collective-permute-start | bytes 245768 | tf_op jit(solution)/shard_map/ppermute | solution.py:24
  28.9 0.5 %shard_map.103.own_keys = bf16[512,1280]{1,0:T(8,128)(2,1)S(1)} custom-call(bf16[512,256]{1,0:T(8,128)(2,1)S(1)} %get-tuple-element.22.cells.own, bf16[256,1280]{1,0:T(8,128)(2,1)S(1)} %copy-done.3), custom_call_target="tpu_custom_call" | custom-call | flops 335544320 | tf_op jit(solution)/shard_map/pallas_call | solution.py:459
  29.4 0.5 %shard_map.104 = (bf16[512,256]{1,0:T(8,128)(2,1)S(1)}, bf16[512,1280]{1,0:T(8,128)(2,1)S(1)}) custom-call(bf16[512,256]{1,0:T(8,128)(2,1)S(1)} %collective-permute-done.4.other_sent, bf16[256,1280]{1,0:T(8,128)(2,1)S(1)} %copy-done.3), custom_call_target="tpu_custom_call" | custom-call | flops 335544320 | tf_op jit(solution)/shard_map/pallas_call | solution.py:459
  30.0 1.0 %collective-permute-done.9.refs_3_ = bf16[32,1280]{1,0:T(8,128)(2,1)S(1)} collective-permute-done((bf16[32,1280]{1,0:T(8,128)(2,1)S(1)}, bf16[32,1280]{1,0:T(8,128)(2,1)S(1)}, u32[]{:S(2)}, u32[]{:S(2)}) %collective-permute-start.9) | collective-permute-done | bytes 81952 | tf_op jit(solution)/shard_map/ppermute | solution.py:24
  30.9 1.2 %collective-permute-done.10.refs_4_ = bf16[32,1280]{1,0:T(8,128)(2,1)S(1)} collective-permute-done((bf16[32,1280]{1,0:T(8,128)(2,1)S(1)}, bf16[32,1280]{1,0:T(8,128)(2,1)S(1)}, u32[]{:S(2)}, u32[]{:S(2)}) %collective-permute-start.10) | collective-permute-done | bytes 81952 | tf_op jit(solution)/shard_map/ppermute | solution.py:24
  32.1 1.4 %shard_map.107 = (bf16[144,128]{1,0:T(8,128)(2,1)S(1)}, bf16[144,128]{1,0:T(8,128)(2,1)S(1)}) custom-call(bf16[512,256]{1,0:T(8,128)(2,1)S(1)} %get-tuple-element.22.cells.own, bf16[512,256]{1,0:T(8,128)(2,1)S(1)} %get-tuple-element.23.own_sent, bf16[512,1280]{1,0:T(8,128)(2,1)S(1)} %shard_map.103.own_keys, bf16[512,256]{1,0:T(8,128)(2,1)S(1)} %get-tuple-element.24.other, ...), custom_call_target="tpu_custom_call" | custom-call | flops 402653184 | tf_op jit(solution)/shard_map/pallas_call | solution.py:459
  33.5 3.2 %collective-permute-start.13 = (bf16[144,128]{1,0:T(8,128)(2,1)S(1)}, bf16[144,128]{1,0:T(8,128)(2,1)S(1)}, u32[]{:S(2)}, u32[]{:S(2)}) collective-permute-start(bf16[144,128]{1,0:T(8,128)(2,1)S(1)} %get-tuple-element.29), channel_id=1, source_target_pairs={{0,2},{1,3},{2,0},{3,1},{4,6},{5,7},{6,4},{7,5},{8,10},{9,11},{10,... | collective-permute-start | bytes 110600 | tf_op jit(solution)/shard_map/ppermute | solution.py:24
  36.7 1.2 %collective-permute-start.14 = (bf16[144,128]{1,0:T(8,128)(2,1)S(1)}, bf16[144,128]{1,0:T(8,128)(2,1)S(1)}, u32[]{:S(2)}, u32[]{:S(2)}) collective-permute-start(bf16[144,128]{1,0:T(8,128)(2,1)S(1)} %get-tuple-element.30), channel_id=1, source_target_pairs={{0,3},{1,2},{2,1},{3,0},{4,7},{5,6},{6,5},{7,4},{8,11},{9,10},{10,... | collective-permute-start | bytes 110600 | tf_op jit(solution)/shard_map/ppermute | solution.py:24
  37.9 1.4 %shard_map.106 = (f32[136,128]{1,0:T(8,128)S(1)}, bf16[144,128]{1,0:T(8,128)(2,1)S(1)}) custom-call(bf16[512,256]{1,0:T(8,128)(2,1)S(1)} %get-tuple-element.22.cells.own, bf16[512,256]{1,0:T(8,128)(2,1)S(1)} %get-tuple-element.23.own_sent, bf16[512,1280]{1,0:T(8,128)(2,1)S(1)} %shard_map.103.own_keys, bf16[512,256]{1,0:T(8,128)(2,1)S(1)} %get-tuple-element.24.other, ...), custom_call_target="tpu_custom_call" | custom-call | flops 402653184 | tf_op jit(solution)/shard_map/pallas_call | solution.py:459
  39.4 3.1 %collective-permute-done.14.refs_2_ = bf16[144,128]{1,0:T(8,128)(2,1)S(1)} collective-permute-done((bf16[144,128]{1,0:T(8,128)(2,1)S(1)}, bf16[144,128]{1,0:T(8,128)(2,1)S(1)}, u32[]{:S(2)}, u32[]{:S(2)}) %collective-permute-start.14) | collective-permute-done | bytes 36896 | tf_op jit(solution)/shard_map/ppermute | solution.py:24
  42.4 0.9 %collective-permute-done.12.refs_0_ = bf16[144,128]{1,0:T(8,128)(2,1)S(1)} collective-permute-done((bf16[144,128]{1,0:T(8,128)(2,1)S(1)}, bf16[144,128]{1,0:T(8,128)(2,1)S(1)}, u32[]{:S(2)}, u32[]{:S(2)}) %collective-permute-start.12) | collective-permute-done | bytes 36896 | tf_op jit(solution)/shard_map/ppermute | solution.py:24
  43.4 1.1 %collective-permute-start.15 = (bf16[144,128]{1,0:T(8,128)(2,1)S(1)}, bf16[144,128]{1,0:T(8,128)(2,1)S(1)}, u32[]{:S(2)}, u32[]{:S(2)}) collective-permute-start(bf16[144,128]{1,0:T(8,128)(2,1)S(1)} %get-tuple-element.32), channel_id=1, source_target_pairs={{0,8},{4,12},{8,0},{12,4},{1,9},{5,13},{9,1},{13,5},{2,10},{6,14},... | collective-permute-start | bytes 110600 | tf_op jit(solution)/shard_map/ppermute | solution.py:24
  44.4 3.0 %collective-permute-done.15.arrived = bf16[144,128]{1,0:T(8,128)(2,1)S(1)} collective-permute-done((bf16[144,128]{1,0:T(8,128)(2,1)S(1)}, bf16[144,128]{1,0:T(8,128)(2,1)S(1)}, u32[]{:S(2)}, u32[]{:S(2)}) %collective-permute-start.15) | collective-permute-done | bytes 36896 | tf_op jit(solution)/shard_map/ppermute | solution.py:24
  47.9 0.8 %collective-permute-done.16.arrived = bf16[128,128]{1,0:T(8,128)(2,1)S(1)} collective-permute-done((bf16[128,128]{1,0:T(8,128)(2,1)S(1)}, bf16[128,128]{1,0:T(8,128)(2,1)S(1)}, u32[]{:S(2)}, u32[]{:S(2)}) %collective-permute-start.16) | collective-permute-done | bytes 32800 | tf_op jit(solution)/shard_map/ppermute | solution.py:24
  48.7 1.4 %fn.1 = bf16[320,128]{1,0:T(8,128)(2,1)} custom-call(bf16[64,1280]{1,0:T(8,128)(2,1)S(1)} %shard_map.110.mine, bf16[128,128]{1,0:T(8,128)(2,1)S(1)} %collective-permute-done.16.arrived, bf16[256,1280]{1,0:T(8,128)(2,1)S(1)} %copy-done, bf16[320,1280]{1,0:T(8,128)(2,1)S(1)} %bitcast.7), custom_call_target="tpu_custom_call" | custom-call | tf_op jit(solution)/shard_map/fn/pallas_call | solution.py:578
  (33 shorter events, 1.2 us)
Async XLA Ops:
  0.0 10.4 %collective-permute-start.5 = (bf16[32,1280]{1,0:T(8,128)(2,1)}, bf16[32,1280]{1,0:T(8,128)(2,1)S(1)}, u32[]{:S(2)}, u32[]{:S(2)}) collective-permute-start(bf16[32,1280]{1,0:T(8,128)(2,1)} %queries.1), channel_id=1, source_target_pairs={{0,4},{4,0},{8,12},{12,8},{1,5},{5,1},{9,13},{13,9},{2,6},{6,2},{1... | collective-permute-start | bytes 245768 | tf_op jit(solution)/shard_map/ppermute | solution.py:24
  1.6 6.8 %collective-permute-start = (bf16[2,32,256]{2,1,0:T(8,128)(2,1)S(1)}, bf16[2,32,256]{2,1,0:T(8,128)(2,1)S(1)}, u32[]{:S(2)}, u32[]{:S(2)}) collective-permute-start(bf16[2,32,256]{2,1,0:T(8,128)(2,1)S(1)} %get-tuple-element.36), channel_id=1, source_target_pairs={{0,1},{1,2},{2,3},{3,0},{4,5},{5,6},{6,7},{7,4},{8,9},{9,10},{10,1... | collective-permute-start | bytes 98312 | tf_op jit(solution)/shard_map/ppermute | solution.py:19
  4.2 4.4 %collective-permute-start.1 = (bf16[2,32,256]{2,1,0:T(8,128)(2,1)S(1)}, bf16[2,32,256]{2,1,0:T(8,128)(2,1)S(1)}, u32[]{:S(2)}, u32[]{:S(2)}) collective-permute-start(bf16[2,32,256]{2,1,0:T(8,128)(2,1)S(1)} %get-tuple-element.35), channel_id=1, source_target_pairs={{0,3},{1,0},{2,1},{3,2},{4,7},{5,4},{6,5},{7,6},{8,11},{9,8},{10,9... | collective-permute-start | bytes 98312 | tf_op jit(solution)/shard_map/ppermute | solution.py:19
  8.7 2.8 %collective-permute-start.2 = (bf16[20,2,256]{2,1,0:T(2,128)(2,1)S(1)}, bf16[20,2,256]{2,1,0:T(2,128)(2,1)S(1)}, u32[]{:S(2)}, u32[]{:S(2)}) collective-permute-start(bf16[20,2,256]{2,1,0:T(2,128)(2,1)S(1)} %get-tuple-element.38), channel_id=1, source_target_pairs={{0,4},{4,0},{8,12},{12,8},{1,5},{5,1},{9,13},{13,9},{2,6},{6,2},{1... | collective-permute-start | bytes 61448 | tf_op jit(solution)/shard_map/ppermute | solution.py:24
  8.8 3.3 %collective-permute-start.3 = (bf16[20,2,256]{2,1,0:T(2,128)(2,1)S(1)}, bf16[20,2,256]{2,1,0:T(2,128)(2,1)S(1)}, u32[]{:S(2)}, u32[]{:S(2)}) collective-permute-start(bf16[20,2,256]{2,1,0:T(2,128)(2,1)S(1)} %get-tuple-element.37), channel_id=1, source_target_pairs={{0,12},{4,8},{8,4},{12,0},{1,13},{5,9},{9,5},{13,1},{2,14},{6,10},... | collective-permute-start | bytes 61448 | tf_op jit(solution)/shard_map/ppermute | solution.py:515
  10.4 10.2 %collective-permute-start.7 = (bf16[32,1280]{1,0:T(8,128)(2,1)S(1)}, bf16[32,1280]{1,0:T(8,128)(2,1)S(1)}, u32[]{:S(2)}, u32[]{:S(2)}) collective-permute-start(bf16[32,1280]{1,0:T(8,128)(2,1)S(1)} %shard_map.105.refs_0_), channel_id=1, source_target_pairs={{0,1},{1,0},{2,3},{3,2},{4,5},{5,4},{6,7},{7,6},{8,9},{9,8},{10,11... | collective-permute-start | bytes 245768 | tf_op jit(solution)/shard_map/ppermute | solution.py:24
  12.1 1.3 %copy-start.1 = (bf16[3,3,256,256]{3,2,1,0:T(8,128)(2,1)S(1)}, bf16[3,3,256,256]{3,2,1,0:T(8,128)(2,1)}, u32[]{:S(2)}) copy-start(bf16[3,3,256,256]{3,2,1,0:T(8,128)(2,1)} %param.12) | copy-start | bytes 3538948
  13.3 0.7 %copy-start.4 = (f32[256]{0:T(256)S(1)}, f32[256]{0:T(256)}, u32[]{:S(2)}) copy-start(f32[256]{0:T(256)} %param.13) | copy-start | bytes 3076
  14.0 1.5 %copy-start.5 = (f32[256]{0:T(256)S(1)}, f32[256]{0:T(256)}, u32[]{:S(2)}) copy-start(f32[256]{0:T(256)} %param.15) | copy-start | bytes 3076
  15.5 13.3 %copy-start.3 = (bf16[256,1280]{1,0:T(8,128)(2,1)S(1)}, bf16[256,1280]{1,0:T(8,128)(2,1)}, u32[]{:S(2)}) copy-start(bf16[256,1280]{1,0:T(8,128)(2,1)} %weight.3) | copy-start | bytes 1966084
  16.7 12.7 %collective-permute-start.4 = (bf16[512,256]{1,0:T(8,128)(2,1)S(1)}, bf16[512,256]{1,0:T(8,128)(2,1)S(1)}, u32[]{:S(2)}, u32[]{:S(2)}) collective-permute-start(bf16[512,256]{1,0:T(8,128)(2,1)S(1)} %get-tuple-element.23.own_sent), channel_id=1, source_target_pairs={{0,4},{4,0},{8,12},{12,8},{1,5},{5,1},{9,13},{13,9},{2,6},{6,2},{1... | collective-permute-start | bytes 786440 | tf_op jit(solution)/shard_map/ppermute | solution.py:24
  17.2 6.8 %collective-permute-start.8 = (bf16[32,1280]{1,0:T(8,128)(2,1)S(1)}, bf16[32,1280]{1,0:T(8,128)(2,1)S(1)}, u32[]{:S(2)}, u32[]{:S(2)}) collective-permute-start(bf16[32,1280]{1,0:T(8,128)(2,1)S(1)} %shard_map.105.refs_0_), channel_id=1, source_target_pairs={{0,3},{1,2},{2,1},{3,0},{4,7},{5,6},{6,5},{7,4},{8,11},{9,10},{10,... | collective-permute-start | bytes 245768 | tf_op jit(solution)/shard_map/ppermute | solution.py:24
  20.6 7.1 %collective-permute-start.6 = (bf16[32,1280]{1,0:T(8,128)(2,1)S(1)}, bf16[32,1280]{1,0:T(8,128)(2,1)S(1)}, u32[]{:S(2)}, u32[]{:S(2)}) collective-permute-start(bf16[32,1280]{1,0:T(8,128)(2,1)S(1)} %shard_map.105.refs_0_), channel_id=1, source_target_pairs={{0,2},{1,3},{2,0},{3,1},{4,6},{5,7},{6,4},{7,5},{8,10},{9,11},{10,... | collective-permute-start | bytes 245768 | tf_op jit(solution)/shard_map/ppermute | solution.py:24
  24.0 8.1 %collective-permute-start.11 = (bf16[64,1280]{1,0:T(8,128)(2,1)S(1)}, bf16[64,1280]{1,0:T(8,128)(2,1)S(1)}, u32[]{:S(2)}, u32[]{:S(2)}) collective-permute-start(bf16[64,1280]{1,0:T(8,128)(2,1)S(1)} %constant_dynamic-update-slice_fusion.refs_2_), channel_id=1, source_target_pairs={{0,8},{4,12},{8,0},{12,4},{1,9},{5,13},{9,1},{13,5},{2,10},{6,14},... | collective-permute-start | bytes 491528 | tf_op jit(solution)/shard_map/ppermute | solution.py:24
  25.9 5.0 %collective-permute-start.9 = (bf16[32,1280]{1,0:T(8,128)(2,1)S(1)}, bf16[32,1280]{1,0:T(8,128)(2,1)S(1)}, u32[]{:S(2)}, u32[]{:S(2)}) collective-permute-start(bf16[32,1280]{1,0:T(8,128)(2,1)S(1)} %shard_map.105.refs_0_), channel_id=1, source_target_pairs={{0,8},{4,12},{8,0},{12,4},{1,9},{5,13},{9,1},{13,5},{2,10},{6,14},... | collective-permute-start | bytes 245768 | tf_op jit(solution)/shard_map/ppermute | solution.py:24
  27.6 4.5 %collective-permute-start.10 = (bf16[32,1280]{1,0:T(8,128)(2,1)S(1)}, bf16[32,1280]{1,0:T(8,128)(2,1)S(1)}, u32[]{:S(2)}, u32[]{:S(2)}) collective-permute-start(bf16[32,1280]{1,0:T(8,128)(2,1)S(1)} %collective-permute-done.6.refs_1_), channel_id=1, source_target_pairs={{0,8},{4,12},{8,0},{12,4},{1,9},{5,13},{9,1},{13,5},{2,10},{6,14},... | collective-permute-start | bytes 245768 | tf_op jit(solution)/shard_map/ppermute | solution.py:24
  33.5 5.9 %collective-permute-start.13 = (bf16[144,128]{1,0:T(8,128)(2,1)S(1)}, bf16[144,128]{1,0:T(8,128)(2,1)S(1)}, u32[]{:S(2)}, u32[]{:S(2)}) collective-permute-start(bf16[144,128]{1,0:T(8,128)(2,1)S(1)} %get-tuple-element.29), channel_id=1, source_target_pairs={{0,2},{1,3},{2,0},{3,1},{4,6},{5,7},{6,4},{7,5},{8,10},{9,11},{10,... | collective-permute-start | bytes 110600 | tf_op jit(solution)/shard_map/ppermute | solution.py:24
  36.7 10.8 %copy-start = (bf16[256,1280]{1,0:T(8,128)(2,1)S(1)}, bf16[256,1280]{1,0:T(8,128)(2,1)}, u32[]{:S(2)}) copy-start(bf16[256,1280]{1,0:T(8,128)(2,1)} %value_weight.3) | copy-start | bytes 1966084
  36.7 5.8 %collective-permute-start.14 = (bf16[144,128]{1,0:T(8,128)(2,1)S(1)}, bf16[144,128]{1,0:T(8,128)(2,1)S(1)}, u32[]{:S(2)}, u32[]{:S(2)}) collective-permute-start(bf16[144,128]{1,0:T(8,128)(2,1)S(1)} %get-tuple-element.30), channel_id=1, source_target_pairs={{0,3},{1,2},{2,1},{3,0},{4,7},{5,6},{6,5},{7,4},{8,11},{9,10},{10,... | collective-permute-start | bytes 110600 | tf_op jit(solution)/shard_map/ppermute | solution.py:24
  39.3 9.4 %copy-start.2 = (bf16[1280,320]{0,1:T(8,128)(2,1)S(1)}, bf16[1280,320]{0,1:T(8,128)(2,1)}, u32[]{:S(2)}) copy-start(bf16[1280,320]{0,1:T(8,128)(2,1)} %param.19) | copy-start | bytes 2457604
  39.3 4.0 %collective-permute-start.12 = (bf16[144,128]{1,0:T(8,128)(2,1)S(1)}, bf16[144,128]{1,0:T(8,128)(2,1)S(1)}, u32[]{:S(2)}, u32[]{:S(2)}) collective-permute-start(bf16[144,128]{1,0:T(8,128)(2,1)S(1)} %get-tuple-element.28), channel_id=1, source_target_pairs={{0,1},{1,0},{2,3},{3,2},{4,5},{5,4},{6,7},{7,6},{8,9},{9,8},{10,11... | collective-permute-start | bytes 110600 | tf_op jit(solution)/shard_map/ppermute | solution.py:24
  43.4 4.0 %collective-permute-start.15 = (bf16[144,128]{1,0:T(8,128)(2,1)S(1)}, bf16[144,128]{1,0:T(8,128)(2,1)S(1)}, u32[]{:S(2)}, u32[]{:S(2)}) collective-permute-start(bf16[144,128]{1,0:T(8,128)(2,1)S(1)} %get-tuple-element.32), channel_id=1, source_target_pairs={{0,8},{4,12},{8,0},{12,4},{1,9},{5,13},{9,1},{13,5},{2,10},{6,14},... | collective-permute-start | bytes 110600 | tf_op jit(solution)/shard_map/ppermute | solution.py:24
  47.4 1.3 %collective-permute-start.16 = (bf16[128,128]{1,0:T(8,128)(2,1)S(1)}, bf16[128,128]{1,0:T(8,128)(2,1)S(1)}, u32[]{:S(2)}, u32[]{:S(2)}) collective-permute-start(bf16[128,128]{1,0:T(8,128)(2,1)S(1)} %shard_map.109.normalized), channel_id=1, source_target_pairs={{0,4},{4,0},{8,12},{12,8},{1,5},{5,1},{9,13},{13,9},{2,6},{6,2},{1... | collective-permute-start | bytes 98312 | tf_op jit(solution)/shard_map/ppermute | solution.py:24

commit v13 on v12

--- a/solution.py
+++ b/solution.py
@@ -165,11 +165,16 @@
     return 0.5 * value * (1.0 + lax.erf(value * math.sqrt(0.5)))
 
 
-def mark_kernel(features, tissue, queries, out, queries_out, features_held, tissue_held, done):
+def mark_kernel(
+    features, tissue, queries, weight, bias,
+    out, queries_out, weight_out, bias_out, features_held, tissue_held, done,
+):
     copies = [
         pltpu.make_async_copy(tissue, tissue_held, done.at[0]),
         pltpu.make_async_copy(features, features_held, done.at[1]),
         pltpu.make_async_copy(queries, queries_out, done.at[2]),
+        pltpu.make_async_copy(bias, bias_out, done.at[3]),
+        pltpu.make_async_copy(weight, weight_out, done.at[4]),
     ]
     for copy in copies:
         copy.start()
@@ -192,7 +197,8 @@
         out[k] = jnp.where(
             keep[k * breadth : (k + 1) * breadth] > 0.0, features_held[k].astype(jnp.float32), FAR
         ).astype(jnp.bfloat16)
-    copies[2].wait()
+    for copy in copies[2:]:
+        copy.wait()
 
 
 def halve_kernel(own, other, out):
@@ -489,11 +495,16 @@
     score_flops = 4 * cells * block * (width + channels)
 
     beside = flipped(latent_queries, "col", 1)
-    marked, queries = call(
-        mark_kernel, [(features.shape, half), ((size, width), half)],
-        [features, tissue, latent_queries],
-        [(features.shape, half), (tissue.shape, jnp.int32), pltpu.SemaphoreType.DMA((3,))],
-        far=(0, 1, 2), flops=1 << 20,
+    weight_shape = (3, 3 * channels, channels)
+    marked, queries, first_weight, first_bias = call(
+        mark_kernel,
+        [(features.shape, half), ((size, width), half), (weight_shape, half), ((1, channels), wide)],
+        [
+            features, tissue, latent_queries,
+            conv_first.reshape(weight_shape), bias_first.reshape(1, channels),
+        ],
+        [(features.shape, half), (tissue.shape, jnp.int32), pltpu.SemaphoreType.DMA((5,))],
+        limit=6, far=(0, 1, 2, 3, 4), flops=1 << 20,
     )
     (queries,) = call(halve_kernel, [((size, width), half)], [queries, beside])
     two = flipped(queries, "row", 2)
@@ -523,7 +534,7 @@
         [((count + 2 * EDGE, channels), wide), ((3, 3 * channels, channels), half)],
         [
             marked, top, bottom, paired, crossed,
-            conv_first.reshape(3, 3 * channels, channels), bias_first.reshape(1, channels),
+            first_weight, first_bias,
             conv_second.reshape(3, 3 * channels, channels),
         ],
         [

time: 50.3 us -> 48.8 us (0.970)
  local copies, waits for them, and re-layouts: 2.03 us -> 0.08 us
    unnamed x13 -> x9, local copies, waits for them, and re-layouts: 1.97 us -> 0.02 us
  transfers between devices with their start and end apart: 17 -> 17, of which waited for: 11 -> 11; matrix products, arithmetic and copies ran while one was open for 0% -> 0% of each run, Pallas kernels for 13% -> 14%
where the time goes in v13:
time: 48.8 us; the launch traced here: 48.6 us
  starting transfers between devices  20.8 us (43%)
  waiting for transfers between devices  17.8 us (36%)
  Pallas kernels  9.72 us (20%)
    ppermute x14, waiting for transfers between devices, flipped(): return lax.ppermute(array, axis, [(i, i ^ bit) for i in range(count)])  14.9 us
    ppermute x14, starting transfers between devices, flipped(): return lax.ppermute(array, axis, [(i, i ^ bit) for i in range(count)])  14.5 us
    pallas_call x11, Pallas kernels, call(): pl.pallas_call(kernel, out_shape=[pltpu.VMEM(shape, dtype) for shape, dty...  8.35 us
    ppermute x2, starting transfers between devices, shifted(): lax.ppermute(array, axis, [(i, (i + step) % count) for i in range(count)])  4.71 us
    ppermute x2, waiting for transfers between devices, shifted(): lax.ppermute(array, axis, [(i, (i + step) % count) for i in range(count)])  2.3 us
    ppermute x1, starting transfers between devices, kernel_path(): crossed = lax.ppermute(jnp.where(even, *ends[::-1]), 'col', rounds)  1.59 us
    pallas_call x1, Pallas kernels, kernel_path(): pl.pallas_call(finish_kernel, out_shape=jax.ShapeDtypeStruct((out_weight....  1.37 us
  transfers between devices with their start and end apart: 17, of which 11 were waited for; matrix products, arithmetic and copies ran while one was open for 0% of the time, Pallas kernels for 14%

profile of v13, /device:TPU:0, one launch (start us, length us, event | category | flops | bytes accessed | tf_op | source)
XLA Modules:
  0.0 48.6 jit_solution(7956172736213843369)
XLA Ops:
  0.0 0.5 %collective-permute-start.5 = (bf16[32,1280]{1,0:T(8,128)(2,1)}, bf16[32,1280]{1,0:T(8,128)(2,1)S(1)}, u32[]{:S(2)}, u32[]{:S(2)}) collective-permute-start(bf16[32,1280]{1,0:T(8,128)(2,1)} %queries.1), channel_id=1, source_target_pairs={{0,4},{4,0},{8,12},{12,8},{1,5},{5,1},{9,13},{13,9},{2,6},{6,2},{1... | collective-permute-start | bytes 245768 | tf_op jit(solution)/shard_map/ppermute | solution.py:24
  0.5 1.5 %shard_map.100 = (bf16[16,32,256]{2,1,0:T(8,128)(2,1)S(1)}, bf16[32,1280]{1,0:T(8,128)(2,1)S(1)}, bf16[3,768,256]{2,1,0:T(8,128)(2,1)S(1)}, f32[1,256]{1,0:T(1,128)S(1)}) custom-call(bf16[16,32,256]{2,1,0:T(8,128)(2,1)} %features.1, s32[16,32]{1,0:T(8,128)} %tissue.1, bf16[32,1280]{1,0:T(8,128)(2,1)} %queries.1, bf16[3,768,256]{2,1,0:T(8,128)(2,1)} %bitcast.9, ...), custom_call_target="tpu_custom_call" | custom-call | flops 1048576 | tf_op jit(solution)/shard_map/pallas_call | solution.py:465
  2.0 2.6 %collective-permute-start = (bf16[2,32,256]{2,1,0:T(8,128)(2,1)S(1)}, bf16[2,32,256]{2,1,0:T(8,128)(2,1)S(1)}, u32[]{:S(2)}, u32[]{:S(2)}) collective-permute-start(bf16[2,32,256]{2,1,0:T(8,128)(2,1)S(1)} %get-tuple-element.40), channel_id=1, source_target_pairs={{0,1},{1,2},{2,3},{3,0},{4,5},{5,6},{6,7},{7,4},{8,9},{9,10},{10,1... | collective-permute-start | bytes 98312 | tf_op jit(solution)/shard_map/ppermute | solution.py:19
  4.6 2.1 %collective-permute-start.1 = (bf16[2,32,256]{2,1,0:T(8,128)(2,1)S(1)}, bf16[2,32,256]{2,1,0:T(8,128)(2,1)S(1)}, u32[]{:S(2)}, u32[]{:S(2)}) collective-permute-start(bf16[2,32,256]{2,1,0:T(8,128)(2,1)S(1)} %get-tuple-element.39), channel_id=1, source_target_pairs={{0,3},{1,0},{2,1},{3,2},{4,7},{5,4},{6,5},{7,6},{8,11},{9,8},{10,9... | collective-permute-start | bytes 98312 | tf_op jit(solution)/shard_map/ppermute | solution.py:19
  6.7 2.0 %collective-permute-done.top = bf16[2,32,256]{2,1,0:T(8,128)(2,1)S(1)} collective-permute-done((bf16[2,32,256]{2,1,0:T(8,128)(2,1)S(1)}, bf16[2,32,256]{2,1,0:T(8,128)(2,1)S(1)}, u32[]{:S(2)}, u32[]{:S(2)}) %collective-permute-start) | collective-permute-done | bytes 32800 | tf_op jit(solution)/shard_map/ppermute | solution.py:19
  8.8 0.3 collective-permute-done.1.bottom
  9.2 1.6 %collective-permute-start.3 = (bf16[20,2,256]{2,1,0:T(2,128)(2,1)S(1)}, bf16[20,2,256]{2,1,0:T(2,128)(2,1)S(1)}, u32[]{:S(2)}, u32[]{:S(2)}) collective-permute-start(bf16[20,2,256]{2,1,0:T(2,128)(2,1)S(1)} %get-tuple-element.41), channel_id=1, source_target_pairs={{0,12},{4,8},{8,4},{12,0},{1,13},{5,9},{9,5},{13,1},{2,14},{6,10},... | collective-permute-start | bytes 61448 | tf_op jit(solution)/shard_map/ppermute | solution.py:526
  10.8 1.1 %collective-permute-start.7 = (bf16[32,1280]{1,0:T(8,128)(2,1)S(1)}, bf16[32,1280]{1,0:T(8,128)(2,1)S(1)}, u32[]{:S(2)}, u32[]{:S(2)}) collective-permute-start(bf16[32,1280]{1,0:T(8,128)(2,1)S(1)} %shard_map.105.refs_0_), channel_id=1, source_target_pairs={{0,1},{1,0},{2,3},{3,2},{4,5},{5,4},{6,7},{7,6},{8,9},{9,8},{10,11... | collective-permute-start | bytes 245768 | tf_op jit(solution)/shard_map/ppermute | solution.py:24
  11.9 0.5 %collective-permute-done.3.crossed = bf16[20,2,256]{2,1,0:T(2,128)(2,1)S(1)} collective-permute-done((bf16[20,2,256]{2,1,0:T(2,128)(2,1)S(1)}, bf16[20,2,256]{2,1,0:T(2,128)(2,1)S(1)}, u32[]{:S(2)}, u32[]{:S(2)}) %collective-permute-start.3) | collective-permute-done | bytes 20512 | tf_op jit(solution)/shard_map/ppermute | solution.py:526
  12.5 1.5 %shard_map.101 = (f32[896,256]{1,0:T(8,128)S(1)}, bf16[3,768,256]{2,1,0:T(8,128)(2,1)S(1)}) custom-call(bf16[16,32,256]{2,1,0:T(8,128)(2,1)S(1)} %get-tuple-element.21.marked, bf16[2,32,256]{2,1,0:T(8,128)(2,1)S(1)} %collective-permute-done.top, bf16[2,32,256]{2,1,0:T(8,128)(2,1)S(1)} %collective-permute-done.1.bottom, ...), custom_call_target="tpu_custom_call" | custom-call | flops 704643072 | tf_op jit(solution)/shard_map/pallas_call | solution.py:465
  14.0 1.2 %shard_map.102 = (bf16[512,256]{1,0:T(8,128)(2,1)S(1)}, bf16[512,256]{1,0:T(8,128)(2,1)S(1)}) custom-call(bf16[16,32,256]{2,1,0:T(8,128)(2,1)S(1)} %get-tuple-element.21.marked, f32[896,256]{1,0:T(8,128)S(1)} %get-tuple-element.24.mid, bf16[3,768,256]{2,1,0:T(8,128)(2,1)S(1)} %get-tuple-element.25.second, f32[1,256]{1,0:T(1,128)S(1)} %bitcast.7), custom_call_target="tpu_custom_call" | custom-call | flops 603979776 | tf_op jit(solution)/shard_map/pallas_call | solution.py:465
  15.2 0.5 %collective-permute-start.4 = (bf16[512,256]{1,0:T(8,128)(2,1)S(1)}, bf16[512,256]{1,0:T(8,128)(2,1)S(1)}, u32[]{:S(2)}, u32[]{:S(2)}) collective-permute-start(bf16[512,256]{1,0:T(8,128)(2,1)S(1)} %get-tuple-element.27.own_sent), channel_id=1, source_target_pairs={{0,4},{4,0},{8,12},{12,8},{1,5},{5,1},{9,13},{13,9},{2,6},{6,2},{1... | collective-permute-start | bytes 786440 | tf_op jit(solution)/shard_map/ppermute | solution.py:24
  15.7 3.4 %collective-permute-start.8 = (bf16[32,1280]{1,0:T(8,128)(2,1)S(1)}, bf16[32,1280]{1,0:T(8,128)(2,1)S(1)}, u32[]{:S(2)}, u32[]{:S(2)}) collective-permute-start(bf16[32,1280]{1,0:T(8,128)(2,1)S(1)} %shard_map.105.refs_0_), channel_id=1, source_target_pairs={{0,3},{1,2},{2,1},{3,0},{4,7},{5,6},{6,5},{7,4},{8,11},{9,10},{10,... | collective-permute-start | bytes 245768 | tf_op jit(solution)/shard_map/ppermute | solution.py:24
  19.1 3.4 %collective-permute-done.8 = bf16[32,1280]{1,0:T(8,128)(2,1)S(1)} collective-permute-done((bf16[32,1280]{1,0:T(8,128)(2,1)S(1)}, bf16[32,1280]{1,0:T(8,128)(2,1)S(1)}, u32[]{:S(2)}, u32[]{:S(2)}) %collective-permute-start.8) | collective-permute-done | bytes 81952 | tf_op jit(solution)/shard_map/ppermute | solution.py:24
  22.5 1.9 %collective-permute-start.11 = (bf16[64,1280]{1,0:T(8,128)(2,1)S(1)}, bf16[64,1280]{1,0:T(8,128)(2,1)S(1)}, u32[]{:S(2)}, u32[]{:S(2)}) collective-permute-start(bf16[64,1280]{1,0:T(8,128)(2,1)S(1)} %constant_dynamic-update-slice_fusion.refs_2_), channel_id=1, source_target_pairs={{0,8},{4,12},{8,0},{12,4},{1,9},{5,13},{9,1},{13,5},{2,10},{6,14},... | collective-permute-start | bytes 491528 | tf_op jit(solution)/shard_map/ppermute | solution.py:24
  24.5 1.6 %collective-permute-done.6.refs_1_ = bf16[32,1280]{1,0:T(8,128)(2,1)S(1)} collective-permute-done((bf16[32,1280]{1,0:T(8,128)(2,1)S(1)}, bf16[32,1280]{1,0:T(8,128)(2,1)S(1)}, u32[]{:S(2)}, u32[]{:S(2)}) %collective-permute-start.6) | collective-permute-done | bytes 81952 | tf_op jit(solution)/shard_map/ppermute | solution.py:24
  26.1 1.2 %collective-permute-start.10 = (bf16[32,1280]{1,0:T(8,128)(2,1)S(1)}, bf16[32,1280]{1,0:T(8,128)(2,1)S(1)}, u32[]{:S(2)}, u32[]{:S(2)}) collective-permute-start(bf16[32,1280]{1,0:T(8,128)(2,1)S(1)} %collective-permute-done.6.refs_1_), channel_id=1, source_target_pairs={{0,8},{4,12},{8,0},{12,4},{1,9},{5,13},{9,1},{13,5},{2,10},{6,14},... | collective-permute-start | bytes 245768 | tf_op jit(solution)/shard_map/ppermute | solution.py:24
  27.4 0.5 %shard_map.103.own_keys = bf16[512,1280]{1,0:T(8,128)(2,1)S(1)} custom-call(bf16[512,256]{1,0:T(8,128)(2,1)S(1)} %get-tuple-element.26.cells.own, bf16[256,1280]{1,0:T(8,128)(2,1)S(1)} %copy-done.2), custom_call_target="tpu_custom_call" | custom-call | flops 335544320 | tf_op jit(solution)/shard_map/pallas_call | solution.py:465
  27.9 0.5 %shard_map.104 = (bf16[512,256]{1,0:T(8,128)(2,1)S(1)}, bf16[512,1280]{1,0:T(8,128)(2,1)S(1)}) custom-call(bf16[512,256]{1,0:T(8,128)(2,1)S(1)} %collective-permute-done.4.other_sent, bf16[256,1280]{1,0:T(8,128)(2,1)S(1)} %copy-done.2), custom_call_target="tpu_custom_call" | custom-call | flops 335544320 | tf_op jit(solution)/shard_map/pallas_call | solution.py:465
  28.4 1.0 %collective-permute-done.9.refs_3_ = bf16[32,1280]{1,0:T(8,128)(2,1)S(1)} collective-permute-done((bf16[32,1280]{1,0:T(8,128)(2,1)S(1)}, bf16[32,1280]{1,0:T(8,128)(2,1)S(1)}, u32[]{:S(2)}, u32[]{:S(2)}) %collective-permute-start.9) | collective-permute-done | bytes 81952 | tf_op jit(solution)/shard_map/ppermute | solution.py:24
  29.4 1.2 %collective-permute-done.10.refs_4_ = bf16[32,1280]{1,0:T(8,128)(2,1)S(1)} collective-permute-done((bf16[32,1280]{1,0:T(8,128)(2,1)S(1)}, bf16[32,1280]{1,0:T(8,128)(2,1)S(1)}, u32[]{:S(2)}, u32[]{:S(2)}) %collective-permute-start.10) | collective-permute-done | bytes 81952 | tf_op jit(solution)/shard_map/ppermute | solution.py:24
  30.6 1.4 %shard_map.107 = (bf16[144,128]{1,0:T(8,128)(2,1)S(1)}, bf16[144,128]{1,0:T(8,128)(2,1)S(1)}) custom-call(bf16[512,256]{1,0:T(8,128)(2,1)S(1)} %get-tuple-element.26.cells.own, bf16[512,256]{1,0:T(8,128)(2,1)S(1)} %get-tuple-element.27.own_sent, bf16[512,1280]{1,0:T(8,128)(2,1)S(1)} %shard_map.103.own_keys, bf16[512,256]{1,0:T(8,128)(2,1)S(1)} %get-tuple-element.28.other, ...), custom_call_target="tpu_custom_call" | custom-call | flops 402653184 | tf_op jit(solution)/shard_map/pallas_call | solution.py:465
  31.9 3.2 %collective-permute-start.13 = (bf16[144,128]{1,0:T(8,128)(2,1)S(1)}, bf16[144,128]{1,0:T(8,128)(2,1)S(1)}, u32[]{:S(2)}, u32[]{:S(2)}) collective-permute-start(bf16[144,128]{1,0:T(8,128)(2,1)S(1)} %get-tuple-element.33), channel_id=1, source_target_pairs={{0,2},{1,3},{2,0},{3,1},{4,6},{5,7},{6,4},{7,5},{8,10},{9,11},{10,... | collective-permute-start | bytes 110600 | tf_op jit(solution)/shard_map/ppermute | solution.py:24
  35.2 1.3 %collective-permute-start.14 = (bf16[144,128]{1,0:T(8,128)(2,1)S(1)}, bf16[144,128]{1,0:T(8,128)(2,1)S(1)}, u32[]{:S(2)}, u32[]{:S(2)}) collective-permute-start(bf16[144,128]{1,0:T(8,128)(2,1)S(1)} %get-tuple-element.34), channel_id=1, source_target_pairs={{0,3},{1,2},{2,1},{3,0},{4,7},{5,6},{6,5},{7,4},{8,11},{9,10},{10,... | collective-permute-start | bytes 110600 | tf_op jit(solution)/shard_map/ppermute | solution.py:24
  36.4 1.4 %shard_map.106 = (f32[136,128]{1,0:T(8,128)S(1)}, bf16[144,128]{1,0:T(8,128)(2,1)S(1)}) custom-call(bf16[512,256]{1,0:T(8,128)(2,1)S(1)} %get-tuple-element.26.cells.own, bf16[512,256]{1,0:T(8,128)(2,1)S(1)} %get-tuple-element.27.own_sent, bf16[512,1280]{1,0:T(8,128)(2,1)S(1)} %shard_map.103.own_keys, bf16[512,256]{1,0:T(8,128)(2,1)S(1)} %get-tuple-element.28.other, ...), custom_call_target="tpu_custom_call" | custom-call | flops 402653184 | tf_op jit(solution)/shard_map/pallas_call | solution.py:465
  37.9 3.0 %collective-permute-done.14.refs_2_ = bf16[144,128]{1,0:T(8,128)(2,1)S(1)} collective-permute-done((bf16[144,128]{1,0:T(8,128)(2,1)S(1)}, bf16[144,128]{1,0:T(8,128)(2,1)S(1)}, u32[]{:S(2)}, u32[]{:S(2)}) %collective-permute-start.14) | collective-permute-done | bytes 36896 | tf_op jit(solution)/shard_map/ppermute | solution.py:24
  40.9 0.9 %collective-permute-done.12.refs_0_ = bf16[144,128]{1,0:T(8,128)(2,1)S(1)} collective-permute-done((bf16[144,128]{1,0:T(8,128)(2,1)S(1)}, bf16[144,128]{1,0:T(8,128)(2,1)S(1)}, u32[]{:S(2)}, u32[]{:S(2)}) %collective-permute-start.12) | collective-permute-done | bytes 36896 | tf_op jit(solution)/shard_map/ppermute | solution.py:24
  41.9 1.0 %collective-permute-start.15 = (bf16[144,128]{1,0:T(8,128)(2,1)S(1)}, bf16[144,128]{1,0:T(8,128)(2,1)S(1)}, u32[]{:S(2)}, u32[]{:S(2)}) collective-permute-start(bf16[144,128]{1,0:T(8,128)(2,1)S(1)} %get-tuple-element.36), channel_id=1, source_target_pairs={{0,8},{4,12},{8,0},{12,4},{1,9},{5,13},{9,1},{13,5},{2,10},{6,14},... | collective-permute-start | bytes 110600 | tf_op jit(solution)/shard_map/ppermute | solution.py:24
  42.9 3.0 %collective-permute-done.15.arrived = bf16[144,128]{1,0:T(8,128)(2,1)S(1)} collective-permute-done((bf16[144,128]{1,0:T(8,128)(2,1)S(1)}, bf16[144,128]{1,0:T(8,128)(2,1)S(1)}, u32[]{:S(2)}, u32[]{:S(2)}) %collective-permute-start.15) | collective-permute-done | bytes 36896 | tf_op jit(solution)/shard_map/ppermute | solution.py:24
  46.0 0.3 shard_map.110.mine
  46.4 0.8 %collective-permute-done.16.arrived = bf16[128,128]{1,0:T(8,128)(2,1)S(1)} collective-permute-done((bf16[128,128]{1,0:T(8,128)(2,1)S(1)}, bf16[128,128]{1,0:T(8,128)(2,1)S(1)}, u32[]{:S(2)}, u32[]{:S(2)}) %collective-permute-start.16) | collective-permute-done | bytes 32800 | tf_op jit(solution)/shard_map/ppermute | solution.py:24
  47.2 1.4 %fn.1 = bf16[320,128]{1,0:T(8,128)(2,1)} custom-call(bf16[64,1280]{1,0:T(8,128)(2,1)S(1)} %shard_map.110.mine, bf16[128,128]{1,0:T(8,128)(2,1)S(1)} %collective-permute-done.16.arrived, bf16[256,1280]{1,0:T(8,128)(2,1)S(1)} %copy-done, bf16[320,1280]{1,0:T(8,128)(2,1)S(1)} %bitcast.6), custom_call_target="tpu_custom_call" | custom-call | tf_op jit(solution)/shard_map/fn/pallas_call | solution.py:589
  (29 shorter events, 0.6 us)
Async XLA Ops:
  0.0 10.8 %collective-permute-start.5 = (bf16[32,1280]{1,0:T(8,128)(2,1)}, bf16[32,1280]{1,0:T(8,128)(2,1)S(1)}, u32[]{:S(2)}, u32[]{:S(2)}) collective-permute-start(bf16[32,1280]{1,0:T(8,128)(2,1)} %queries.1), channel_id=1, source_target_pairs={{0,4},{4,0},{8,12},{12,8},{1,5},{5,1},{9,13},{13,9},{2,6},{6,2},{1... | collective-permute-start | bytes 245768 | tf_op jit(solution)/shard_map/ppermute | solution.py:24
  2.0 6.8 %collective-permute-start = (bf16[2,32,256]{2,1,0:T(8,128)(2,1)S(1)}, bf16[2,32,256]{2,1,0:T(8,128)(2,1)S(1)}, u32[]{:S(2)}, u32[]{:S(2)}) collective-permute-start(bf16[2,32,256]{2,1,0:T(8,128)(2,1)S(1)} %get-tuple-element.40), channel_id=1, source_target_pairs={{0,1},{1,2},{2,3},{3,0},{4,5},{5,6},{6,7},{7,4},{8,9},{9,10},{10,1... | collective-permute-start | bytes 98312 | tf_op jit(solution)/shard_map/ppermute | solution.py:19
  4.6 4.4 %collective-permute-start.1 = (bf16[2,32,256]{2,1,0:T(8,128)(2,1)S(1)}, bf16[2,32,256]{2,1,0:T(8,128)(2,1)S(1)}, u32[]{:S(2)}, u32[]{:S(2)}) collective-permute-start(bf16[2,32,256]{2,1,0:T(8,128)(2,1)S(1)} %get-tuple-element.39), channel_id=1, source_target_pairs={{0,3},{1,0},{2,1},{3,2},{4,7},{5,4},{6,5},{7,6},{8,11},{9,8},{10,9... | collective-permute-start | bytes 98312 | tf_op jit(solution)/shard_map/ppermute | solution.py:19
  9.1 2.8 %collective-permute-start.2 = (bf16[20,2,256]{2,1,0:T(2,128)(2,1)S(1)}, bf16[20,2,256]{2,1,0:T(2,128)(2,1)S(1)}, u32[]{:S(2)}, u32[]{:S(2)}) collective-permute-start(bf16[20,2,256]{2,1,0:T(2,128)(2,1)S(1)} %get-tuple-element.42), channel_id=1, source_target_pairs={{0,4},{4,0},{8,12},{12,8},{1,5},{5,1},{9,13},{13,9},{2,6},{6,2},{1... | collective-permute-start | bytes 61448 | tf_op jit(solution)/shard_map/ppermute | solution.py:24
  9.2 3.3 %collective-permute-start.3 = (bf16[20,2,256]{2,1,0:T(2,128)(2,1)S(1)}, bf16[20,2,256]{2,1,0:T(2,128)(2,1)S(1)}, u32[]{:S(2)}, u32[]{:S(2)}) collective-permute-start(bf16[20,2,256]{2,1,0:T(2,128)(2,1)S(1)} %get-tuple-element.41), channel_id=1, source_target_pairs={{0,12},{4,8},{8,4},{12,0},{1,13},{5,9},{9,5},{13,1},{2,14},{6,10},... | collective-permute-start | bytes 61448 | tf_op jit(solution)/shard_map/ppermute | solution.py:526
  10.8 8.2 %collective-permute-start.7 = (bf16[32,1280]{1,0:T(8,128)(2,1)S(1)}, bf16[32,1280]{1,0:T(8,128)(2,1)S(1)}, u32[]{:S(2)}, u32[]{:S(2)}) collective-permute-start(bf16[32,1280]{1,0:T(8,128)(2,1)S(1)} %shard_map.105.refs_0_), channel_id=1, source_target_pairs={{0,1},{1,0},{2,3},{3,2},{4,5},{5,4},{6,7},{7,6},{8,9},{9,8},{10,11... | collective-permute-start | bytes 245768 | tf_op jit(solution)/shard_map/ppermute | solution.py:24
  12.5 1.5 %copy-start.3 = (f32[256]{0:T(256)S(1)}, f32[256]{0:T(256)}, u32[]{:S(2)}) copy-start(f32[256]{0:T(256)} %param.15) | copy-start | bytes 3076
  14.0 13.4 %copy-start.2 = (bf16[256,1280]{1,0:T(8,128)(2,1)S(1)}, bf16[256,1280]{1,0:T(8,128)(2,1)}, u32[]{:S(2)}) copy-start(bf16[256,1280]{1,0:T(8,128)(2,1)} %weight.3) | copy-start | bytes 1966084
  15.2 12.7 %collective-permute-start.4 = (bf16[512,256]{1,0:T(8,128)(2,1)S(1)}, bf16[512,256]{1,0:T(8,128)(2,1)S(1)}, u32[]{:S(2)}, u32[]{:S(2)}) collective-permute-start(bf16[512,256]{1,0:T(8,128)(2,1)S(1)} %get-tuple-element.27.own_sent), channel_id=1, source_target_pairs={{0,4},{4,0},{8,12},{12,8},{1,5},{5,1},{9,13},{13,9},{2,6},{6,2},{1... | collective-permute-start | bytes 786440 | tf_op jit(solution)/shard_map/ppermute | solution.py:24
  15.7 6.8 %collective-permute-start.8 = (bf16[32,1280]{1,0:T(8,128)(2,1)S(1)}, bf16[32,1280]{1,0:T(8,128)(2,1)S(1)}, u32[]{:S(2)}, u32[]{:S(2)}) collective-permute-start(bf16[32,1280]{1,0:T(8,128)(2,1)S(1)} %shard_map.105.refs_0_), channel_id=1, source_target_pairs={{0,3},{1,2},{2,1},{3,0},{4,7},{5,6},{6,5},{7,4},{8,11},{9,10},{10,... | collective-permute-start | bytes 245768 | tf_op jit(solution)/shard_map/ppermute | solution.py:24
  19.0 7.1 %collective-permute-start.6 = (bf16[32,1280]{1,0:T(8,128)(2,1)S(1)}, bf16[32,1280]{1,0:T(8,128)(2,1)S(1)}, u32[]{:S(2)}, u32[]{:S(2)}) collective-permute-start(bf16[32,1280]{1,0:T(8,128)(2,1)S(1)} %shard_map.105.refs_0_), channel_id=1, source_target_pairs={{0,2},{1,3},{2,0},{3,1},{4,6},{5,7},{6,4},{7,5},{8,10},{9,11},{10,... | collective-permute-start | bytes 245768 | tf_op jit(solution)/shard_map/ppermute | solution.py:24
  22.5 8.1 %collective-permute-start.11 = (bf16[64,1280]{1,0:T(8,128)(2,1)S(1)}, bf16[64,1280]{1,0:T(8,128)(2,1)S(1)}, u32[]{:S(2)}, u32[]{:S(2)}) collective-permute-start(bf16[64,1280]{1,0:T(8,128)(2,1)S(1)} %constant_dynamic-update-slice_fusion.refs_2_), channel_id=1, source_target_pairs={{0,8},{4,12},{8,0},{12,4},{1,9},{5,13},{9,1},{13,5},{2,10},{6,14},... | collective-permute-start | bytes 491528 | tf_op jit(solution)/shard_map/ppermute | solution.py:24
  24.4 5.0 %collective-permute-start.9 = (bf16[32,1280]{1,0:T(8,128)(2,1)S(1)}, bf16[32,1280]{1,0:T(8,128)(2,1)S(1)}, u32[]{:S(2)}, u32[]{:S(2)}) collective-permute-start(bf16[32,1280]{1,0:T(8,128)(2,1)S(1)} %shard_map.105.refs_0_), channel_id=1, source_target_pairs={{0,8},{4,12},{8,0},{12,4},{1,9},{5,13},{9,1},{13,5},{2,10},{6,14},... | collective-permute-start | bytes 245768 | tf_op jit(solution)/shard_map/ppermute | solution.py:24
  26.1 4.5 %collective-permute-start.10 = (bf16[32,1280]{1,0:T(8,128)(2,1)S(1)}, bf16[32,1280]{1,0:T(8,128)(2,1)S(1)}, u32[]{:S(2)}, u32[]{:S(2)}) collective-permute-start(bf16[32,1280]{1,0:T(8,128)(2,1)S(1)} %collective-permute-done.6.refs_1_), channel_id=1, source_target_pairs={{0,8},{4,12},{8,0},{12,4},{1,9},{5,13},{9,1},{13,5},{2,10},{6,14},... | collective-permute-start | bytes 245768 | tf_op jit(solution)/shard_map/ppermute | solution.py:24
  31.9 5.9 %collective-permute-start.13 = (bf16[144,128]{1,0:T(8,128)(2,1)S(1)}, bf16[144,128]{1,0:T(8,128)(2,1)S(1)}, u32[]{:S(2)}, u32[]{:S(2)}) collective-permute-start(bf16[144,128]{1,0:T(8,128)(2,1)S(1)} %get-tuple-element.33), channel_id=1, source_target_pairs={{0,2},{1,3},{2,0},{3,1},{4,6},{5,7},{6,4},{7,5},{8,10},{9,11},{10,... | collective-permute-start | bytes 110600 | tf_op jit(solution)/shard_map/ppermute | solution.py:24
  35.2 10.8 %copy-start = (bf16[256,1280]{1,0:T(8,128)(2,1)S(1)}, bf16[256,1280]{1,0:T(8,128)(2,1)}, u32[]{:S(2)}) copy-start(bf16[256,1280]{1,0:T(8,128)(2,1)} %value_weight.3) | copy-start | bytes 1966084
  35.2 5.8 %collective-permute-start.14 = (bf16[144,128]{1,0:T(8,128)(2,1)S(1)}, bf16[144,128]{1,0:T(8,128)(2,1)S(1)}, u32[]{:S(2)}, u32[]{:S(2)}) collective-permute-start(bf16[144,128]{1,0:T(8,128)(2,1)S(1)} %get-tuple-element.34), channel_id=1, source_target_pairs={{0,3},{1,2},{2,1},{3,0},{4,7},{5,6},{6,5},{7,4},{8,11},{9,10},{10,... | collective-permute-start | bytes 110600 | tf_op jit(solution)/shard_map/ppermute | solution.py:24
  37.8 9.4 %copy-start.1 = (bf16[1280,320]{0,1:T(8,128)(2,1)S(1)}, bf16[1280,320]{0,1:T(8,128)(2,1)}, u32[]{:S(2)}) copy-start(bf16[1280,320]{0,1:T(8,128)(2,1)} %param.19) | copy-start | bytes 2457604
  37.8 4.0 %collective-permute-start.12 = (bf16[144,128]{1,0:T(8,128)(2,1)S(1)}, bf16[144,128]{1,0:T(8,128)(2,1)S(1)}, u32[]{:S(2)}, u32[]{:S(2)}) collective-permute-start(bf16[144,128]{1,0:T(8,128)(2,1)S(1)} %get-tuple-element.32), channel_id=1, source_target_pairs={{0,1},{1,0},{2,3},{3,2},{4,5},{5,4},{6,7},{7,6},{8,9},{9,8},{10,11... | collective-permute-start | bytes 110600 | tf_op jit(solution)/shard_map/ppermute | solution.py:24
  41.9 4.0 %collective-permute-start.15 = (bf16[144,128]{1,0:T(8,128)(2,1)S(1)}, bf16[144,128]{1,0:T(8,128)(2,1)S(1)}, u32[]{:S(2)}, u32[]{:S(2)}) collective-permute-start(bf16[144,128]{1,0:T(8,128)(2,1)S(1)} %get-tuple-element.36), channel_id=1, source_target_pairs={{0,8},{4,12},{8,0},{12,4},{1,9},{5,13},{9,1},{13,5},{2,10},{6,14},... | collective-permute-start | bytes 110600 | tf_op jit(solution)/shard_map/ppermute | solution.py:24
  45.9 1.3 %collective-permute-start.16 = (bf16[128,128]{1,0:T(8,128)(2,1)S(1)}, bf16[128,128]{1,0:T(8,128)(2,1)S(1)}, u32[]{:S(2)}, u32[]{:S(2)}) collective-permute-start(bf16[128,128]{1,0:T(8,128)(2,1)S(1)} %shard_map.109.normalized), channel_id=1, source_target_pairs={{0,4},{4,0},{8,12},{12,8},{1,5},{5,1},{9,13},{13,9},{2,6},{6,2},{1... | collective-permute-start | bytes 98312 | tf_op jit(solution)/shard_map/ppermute | solution.py:24
